TPU v7x, 32 devices: a whole 2x2x4 slice. The times are simulated.
32 devices in a mesh: clip: 16 (over z, y, core), seq: 2 (over x).
Axes of the slice: x: 2, y: 2, z: 4, core: 2. Of those that a mesh axis runs over, the one named last changes fastest.
Arguments:
- patches: bfloat16 [4096, 1280], P('clip'), may hold values from -6 to 6
- clip_tokens: int32 [16], P('clip'), may hold values from 16 to 64
- positions: int32 [16, 64], P('clip'), may hold values from 0 to 255, as said below
- norm_gain: float32 [1280], replicated, may hold values from 0.5 to 1.5
- norm_bias: float32 [1280], replicated, may hold values from -3 to 3
- w_qkv: bfloat16 [1280, 3, 1280], P(None, None, 'seq'), may hold values from -0.9503289 to 0.9503289
- b_qkv: float32 [3, 1280], P(None, 'seq'), may hold values from -3 to 3
- w_proj: bfloat16 [1280, 1280], P('seq'), may hold values from -0.15625 to 0.15625
- b_proj: float32 [1280], replicated, may hold values from -3 to 3
- merge_gain: float32 [1280], replicated, may hold values from 0.5 to 1.5
- merge_bias: float32 [1280], replicated, may hold values from -3 to 3
- grad_placed: bfloat16 [4096, 5120], P(('clip', 'seq')), may hold values from -0.09375 to 0.09375
Outputs:
- placed: bfloat16 [4096, 5120], P(('clip', 'seq'))
- grad_qkv: float32 [2, 1920, 1280], P('seq', 'clip')
Inputs may be any that keep to these rules, and one draw needn't show every extreme that they name: The positions of one clip are distinct.
All inputs are finite; a program needn't handle non-finite values.
Results may differ from a plain program's by a relative error of at most 0.01.
Values may be sent and summed in bfloat16 or wider, within the bound.
No kernel may reach another device: no remote copies, remote signals or barrier semaphores. Data moves between devices by JAX's collectives and lax.ppermute only.
A program may use at most 64 MiB of HBM per device.

v0:
```python
import functools

import jax
import jax.numpy as jnp
from jax import lax
from jax.experimental import pallas as pl
from jax.experimental.pallas import tpu as pltpu
from jax.sharding import PartitionSpec as P


HEAD = 80


EPSILON = 1e-06


def normalize(values, gain_row, bias_row):
    center = values - jnp.mean(values, axis=-1, keepdims=True)
    inverse = lax.rsqrt(jnp.mean(center * center, axis=-1, keepdims=True) + EPSILON)
    unit_rows = center * inverse
    return (unit_rows * gain_row + bias_row, unit_rows, inverse)


def normalize_back(upstream, unit_rows, inverse, gain_row):
    scaled = upstream * gain_row
    return inverse * (
        scaled
        - jnp.mean(scaled, axis=-1, keepdims=True)
        - unit_rows * jnp.mean(scaled * unit_rows, axis=-1, keepdims=True)
    )


def leading(left, right):
    return lax.dot_general(
        left, right, (((0,), (0,)), ((), ())), preferred_element_type=jnp.float32
    )


def trailing(left, right):
    return lax.dot_general(
        left, right, (((1,), (1,)), ((), ())), preferred_element_type=jnp.float32
    )


def general_body(
    patches,
    clip_tokens,
    positions,
    norm_gain,
    norm_bias,
    w_qkv,
    b_qkv,
    w_proj,
    b_proj,
    merge_gain,
    merge_bias,
    grad_placed,
):
    block_rows = patches.shape[0]
    model_width = patches.shape[1]
    local_width = w_qkv.shape[2]
    local_heads = local_width // HEAD
    live_count = clip_tokens[0]
    places = positions[0]
    widened = patches.astype(jnp.float32)
    normed = normalize(widened, norm_gain, norm_bias)[0].astype(jnp.bfloat16)
    triple = jnp.dot(
        normed, w_qkv.reshape(model_width, 3 * local_width), preferred_element_type=jnp.float32
    )
    triple = (triple.reshape(block_rows, 3, local_width) + b_qkv).astype(jnp.bfloat16)
    query_rows = triple[:, 0].reshape(block_rows, local_heads, HEAD)
    key_rows = triple[:, 1].reshape(block_rows, local_heads, HEAD)
    value_rows = triple[:, 2].reshape(block_rows, local_heads, HEAD)
    scaling = HEAD ** (-0.5)
    scores = (
        jnp.einsum("qhd,khd->hqk", query_rows, key_rows, preferred_element_type=jnp.float32)
        * scaling
    )
    live_keys = jnp.arange(block_rows, dtype=jnp.int32) < 4 * live_count
    scores = jnp.where(live_keys[None, None, :], scores, -1e30)
    highest = jnp.max(scores, axis=-1, keepdims=True)
    powers = jnp.exp(scores - highest)
    weights = powers / jnp.sum(powers, axis=-1, keepdims=True)
    weights_low = weights.astype(jnp.bfloat16)
    attended = jnp.einsum(
        "hqk,khd->qhd", weights_low, value_rows, preferred_element_type=jnp.float32
    )
    attended = attended.reshape(block_rows, local_width).astype(jnp.bfloat16)
    partial_value = jnp.dot(attended, w_proj, preferred_element_type=jnp.float32)
    summed_share = lax.psum_scatter(
        partial_value.astype(jnp.bfloat16), "seq", scatter_dimension=0, tiled=True
    ).astype(jnp.float32)
    share_count = summed_share.shape[0]
    own_start = lax.axis_index("seq") * share_count
    own_patches = lax.dynamic_slice_in_dim(widened, own_start, share_count, 0)
    output_share = summed_share + b_proj + own_patches
    output = lax.all_gather(output_share.astype(jnp.bfloat16), "seq", axis=0, tiled=True).astype(
        output_share.dtype
    )
    merged_full, unit_rows, inverse = normalize(output, merge_gain, merge_bias)
    merged = merged_full.reshape(block_rows // 4, 4 * model_width).astype(jnp.bfloat16)
    live_tokens = jnp.arange(block_rows // 4, dtype=jnp.int32) < live_count
    share_rows = grad_placed.shape[0]
    rows_here = lax.axis_index("seq") * share_rows + jnp.arange(share_rows, dtype=jnp.int32)
    selector = ((places[None, :] == rows_here[:, None]) & live_tokens[None, :]).astype(jnp.bfloat16)
    placed = jnp.dot(selector, merged, preferred_element_type=jnp.float32).astype(jnp.bfloat16)
    own_grad = leading(selector, grad_placed)
    token_grad = lax.psum(own_grad.astype(jnp.bfloat16), "seq").astype(jnp.float32)
    upstream = token_grad.reshape(block_rows, model_width)
    row_grad = normalize_back(upstream, unit_rows, inverse, merge_gain).astype(jnp.bfloat16)
    attn_grad = lax.dot_general(
        row_grad, w_proj, (((1,), (1,)), ((), ())), preferred_element_type=jnp.float32
    )
    attn_grad = attn_grad.astype(jnp.bfloat16).reshape(block_rows, local_heads, HEAD)
    prob_grad = jnp.einsum(
        "qhd,khd->hqk", attn_grad, value_rows, preferred_element_type=jnp.float32
    )
    value_grad = jnp.einsum(
        "hqk,qhd->khd", weights_low, attn_grad, preferred_element_type=jnp.float32
    )
    score_grad = (
        weights * (prob_grad - jnp.sum(prob_grad * weights, axis=-1, keepdims=True)) * scaling
    )
    score_grad = score_grad.astype(jnp.bfloat16)
    query_grad = jnp.einsum(
        "hqk,khd->qhd", score_grad, key_rows, preferred_element_type=jnp.float32
    )
    key_grad = jnp.einsum(
        "hqk,qhd->khd", score_grad, query_rows, preferred_element_type=jnp.float32
    )
    triple_grad = jnp.stack([query_grad, key_grad, value_grad], axis=1)
    triple_grad = triple_grad.reshape(block_rows, 3 * local_width).astype(jnp.bfloat16)
    full_term = leading(triple_grad, normed)
    summed = lax.psum_scatter(full_term, "clip", scatter_dimension=0, tiled=True)
    return (placed, summed[None])


def place_masks(live_ref, places_ref, share_rows, rows):
    tokens = places_ref.shape[1]
    token = lax.broadcasted_iota(jnp.int32, (tokens, rows), 0)
    owner = lax.broadcasted_iota(jnp.int32, (tokens, rows), 1) // 4
    spread = jnp.where((token == owner) & (token < live_ref[0]), 1.0, 0.0)
    shifted = jnp.broadcast_to(places_ref[...].astype(jnp.float32) + 1.0, (8, tokens))
    row = jnp.dot(shifted, spread, precision=lax.Precision.HIGHEST)[:1] - 1.0
    first = lax.axis_index("seq") * share_rows
    window = lax.broadcasted_iota(jnp.int32, (share_rows, rows), 0) + first
    patch = lax.broadcasted_iota(jnp.int32, (share_rows, rows), 1)
    hit = window.astype(jnp.float32) == row
    return [
        jnp.where(hit & (lax.rem(patch, 4) == k), 1.0, 0.0).astype(jnp.bfloat16) for k in range(4)
    ]


def pull_kernel(live_ref, places_ref, grad_ref, out_ref):
    width = out_ref.shape[1]
    masks = place_masks(live_ref, places_ref, grad_ref.shape[0], out_ref.shape[0])
    total = None
    for k in range(4):
        term = leading(masks[k], grad_ref[:, k * width : (k + 1) * width])
        total = term if total is None else total + term
    out_ref[...] = total.astype(out_ref.dtype)


def place_kernel(live_ref, places_ref, merged_ref, _, out_ref):
    width = merged_ref.shape[1]
    masks = place_masks(live_ref, places_ref, out_ref.shape[0], merged_ref.shape[0])
    for k in range(4):
        term = jnp.dot(masks[k], merged_ref[...], preferred_element_type=jnp.float32)
        out_ref[:, k * width : (k + 1) * width] = term.astype(out_ref.dtype)


def begin(sources, targets, sems, first=0):
    copies = [
        pltpu.make_async_copy(source, target, sems.at[first + k])
        for k, (source, target) in enumerate(zip(sources, targets, strict=True))
    ]
    for copy in copies:
        copy.start()
    return copies


def forward_kernel(
    live_ref,
    gain_ref,
    bias_ref,
    b_ref,
    patches_hbm,
    w_hbm,
    proj_hbm,
    normed_ref,
    triple_ref,
    probs_ref,
    partial_ref,
    patches_ref,
    w_ref,
    proj_ref,
    attended_ref,
    sems,
):
    rows = patches_ref.shape[0]
    came = begin(
        (patches_hbm, w_hbm.at[0], w_hbm.at[1], w_hbm.at[2], proj_hbm),
        (patches_ref, w_ref.at[0], w_ref.at[1], w_ref.at[2], proj_ref),
        sems,
    )
    came[0].wait()
    normed_ref[...] = normalize(
        patches_ref[...].astype(jnp.float32), gain_ref[...][None, :], bias_ref[...][None, :]
    )[0].astype(jnp.bfloat16)
    for t in range(3):
        came[1 + t].wait()
        part = jnp.dot(normed_ref[...], w_ref[t], preferred_element_type=jnp.float32)
        triple_ref[t] = (part + b_ref[t : t + 1, :]).astype(jnp.bfloat16)
    live = lax.broadcasted_iota(jnp.int32, (rows, rows), 1) < 4 * live_ref[0]
    steep = HEAD ** (-0.5) * 1.4426950408889634
    for h in range(probs_ref.shape[0]):
        cols = slice(h * HEAD, (h + 1) * HEAD)
        scores = trailing(triple_ref[0, :, cols], triple_ref[1, :, cols])
        scores = jnp.where(live, scores, -1e30)
        powers = jnp.exp2((scores - jnp.max(scores, axis=-1, keepdims=True)) * steep)
        weights = powers * (1.0 / jnp.sum(powers, axis=-1, keepdims=True))
        weights = weights.astype(jnp.bfloat16)
        probs_ref[h] = weights
        attended_ref[:, cols] = jnp.dot(
            weights, triple_ref[2, :, cols], preferred_element_type=jnp.float32
        ).astype(jnp.bfloat16)
    came[4].wait()
    partial_ref[...] = jnp.dot(
        attended_ref[...], proj_ref[...], preferred_element_type=jnp.float32
    ).astype(jnp.bfloat16)


def backward_kernel(
    b_ref,
    gain_ref,
    bias_ref,
    own_ref,
    other_ref,
    patches_ref,
    up_own_ref,
    up_other_ref,
    proj_ref,
    triple_ref,
    probs_ref,
    merged_ref,
    *refs,
):
    outs, (back_ref, slots_ref) = refs[:8], refs[8:]
    gain = gain_ref[...][None, :]
    output = (
        own_ref[...].astype(jnp.float32)
        + other_ref[...].astype(jnp.float32)
        + b_ref[...][None, :]
        + patches_ref[...].astype(jnp.float32)
    )
    merged, unit_rows, inverse = normalize(output, gain, bias_ref[...][None, :])
    merged_ref[...] = merged.astype(jnp.bfloat16)
    upstream = up_own_ref[...].astype(jnp.float32) + up_other_ref[...].astype(jnp.float32)
    row_grad = normalize_back(upstream, unit_rows, inverse, gain).astype(jnp.bfloat16)
    back_ref[...] = trailing(row_grad, proj_ref[...]).astype(jnp.bfloat16)
    scaling = HEAD ** (-0.5)
    heads = probs_ref.shape[0]
    per_block = slots_ref.shape[2] // HEAD
    me = lax.axis_index("clip")
    turn = lax.bitwise_and(lax.shift_right_logical(me, 1), 3)
    away = 1 - lax.shift_right_logical(me, 3)

    def put(t, h, value):
        piece = t * heads + h
        block, sub = piece // per_block, piece % per_block
        slot = lax.bitwise_xor(turn, block % 4)
        side = lax.bitwise_xor(away, block // 4)
        slots_ref[side, slot, sub * HEAD : (sub + 1) * HEAD, :] = value.astype(jnp.bfloat16)

    for h in range(heads):
        cols = slice(h * HEAD, (h + 1) * HEAD)
        back = back_ref[:, cols]
        weights = probs_ref[h]
        put(2, h, leading(back, weights))
        prob_grad = trailing(back, triple_ref[2, :, cols])
        wide = weights.astype(jnp.float32)
        inner = jnp.sum(prob_grad * wide, axis=-1, keepdims=True)
        score_grad = (wide * (prob_grad - inner)).astype(jnp.bfloat16)
        query_grad = lax.dot_general(
            triple_ref[1, :, cols],
            score_grad,
            (((0,), (1,)), ((), ())),
            preferred_element_type=jnp.float32,
        )
        put(0, h, query_grad * scaling)
        put(1, h, leading(triple_ref[0, :, cols], score_grad) * scaling)
    for k, out_ref in enumerate(outs):
        out_ref[...] = slots_ref[k // 4, k % 4]


def product_kernel(*refs):
    t_refs, n_refs = refs[:4], refs[4:8]
    keep_ref, send_ref, sum_ref = refs[-3:]
    half = keep_ref.shape[0]
    core = lax.bitwise_and(lax.axis_index("clip"), 1)
    total = None
    for t_ref, n_ref in zip(t_refs, n_refs, strict=True):
        term = jnp.dot(t_ref[...], n_ref[...], preferred_element_type=jnp.float32)
        total = term if total is None else total + term
    sum_ref[...] = total
    keep_ref[...] = sum_ref[pl.ds(pl.multiple_of(core * half, 8), half), :]
    other = sum_ref[pl.ds(pl.multiple_of((1 - core) * half, 8), half), :]
    send_ref[...] = other.astype(jnp.bfloat16)


def call(kernel, outs, kinds, flops, args, scratch=(), limit=30):
    spec = {
        "s": pl.BlockSpec(memory_space=pltpu.SMEM),
        "v": pl.BlockSpec(memory_space=pltpu.VMEM),
        "a": pl.BlockSpec(memory_space=pl.ANY),
    }
    return pl.pallas_call(
        kernel,
        out_shape=outs,
        in_specs=[spec[kind] for kind in kinds],
        out_specs=jax.tree.map(lambda _: spec["v"], outs),
        scratch_shapes=list(scratch),
        cost_estimate=pl.CostEstimate(flops=flops, bytes_accessed=4_000_000, transcendentals=0),
        compiler_params=pltpu.CompilerParams(vmem_limit_bytes=limit * 1024 * 1024),
    )(*args)


def fast_body(
    n_clip,
    patches,
    clip_tokens,
    positions,
    norm_gain,
    norm_bias,
    w_qkv,
    b_qkv,
    w_proj,
    b_proj,
    merge_gain,
    merge_bias,
    grad_placed,
):
    rows, width = patches.shape
    local = w_qkv.shape[2]
    heads = local // HEAD
    share_rows = grad_placed.shape[0]
    low = jnp.bfloat16
    shape = jax.ShapeDtypeStruct
    full = shape((rows, width), low)

    def swap(value):
        return lax.ppermute(value, "seq", [(0, 1), (1, 0)])

    def flip(value, bits):
        return lax.ppermute(value, "clip", [(i, i ^ bits) for i in range(n_clip)])

    up_own = call(
        pull_kernel,
        full,
        "svv",
        8 * rows * share_rows * width,
        (clip_tokens, positions, grad_placed),
    )
    up_other = swap(up_own)
    normed, triple, probs, partial = call(
        forward_kernel,
        (full, shape((3, rows, local), low), shape((heads, rows, rows), low), full),
        "svvvaaa",
        8 * rows * width * local,
        (
            clip_tokens,
            norm_gain,
            norm_bias,
            b_qkv,
            patches,
            jnp.transpose(w_qkv, (1, 0, 2)),
            w_proj,
        ),
        (
            pltpu.VMEM((rows, width), low),
            pltpu.VMEM((3, width, local), low),
            pltpu.VMEM((local, width), low),
            pltpu.VMEM((rows, local), low),
            pltpu.SemaphoreType.DMA((5,)),
        ),
        limit=52,
    )
    other = swap(partial)
    normed_of = [normed] + [flip(normed, q << 1) for q in (1, 2, 3)]
    block = 3 * local // 8
    merged, *sent = call(
        backward_kernel,
        (full,) + (shape((block, rows), low),) * 8,
        "v" * 11,
        6 * rows * width * local,
        (
            b_proj,
            merge_gain,
            merge_bias,
            partial,
            other,
            patches,
            up_own,
            up_other,
            w_proj,
            triple,
            probs,
        ),
        (pltpu.VMEM((rows, local), low), pltpu.VMEM((2, 4, block, rows), low)),
    )

    def exchange(sent):
        return [sent[0]] + [flip(sent[q], q << 1) for q in (1, 2, 3)]

    def product(taken, after=()):
        return call(
            product_kernel,
            (shape((block // 2, width), jnp.float32), shape((block // 2, width), low)),
            "v" * 8 + "a" * len(after),
            8 * block * rows * width,
            (*taken, *normed_of, *after),
            (pltpu.VMEM((block, width), jnp.float32),),
        )

    far_taken = exchange(sent[:4])
    near_taken = exchange(sent[4:])
    far_keep, far_send = product(far_taken)
    far_came = flip(far_send, 1)
    far_sum = (far_keep + far_came.astype(jnp.float32)).astype(low)
    crossing = flip(far_sum, 8)
    near_keep, near_send = product(near_taken, (far_sum,))
    near_came = flip(near_send, 1)
    placed = call(
        place_kernel,
        shape((share_rows, 4 * width), low),
        "svva",
        8 * rows * share_rows * width,
        (clip_tokens, positions, merged, far_sum),
    )
    summed = near_keep + near_came.astype(jnp.float32) + crossing.astype(jnp.float32)
    return (placed, summed[None])


def solution(mesh):
    n_clip, n_seq = mesh.shape["clip"], mesh.shape["seq"]
    fast = n_clip == 2 * 4 * 2 and n_seq == 2
    body = functools.partial(fast_body, n_clip) if fast else general_body
    return jax.shard_map(
        body,
        mesh=mesh,
        in_specs=(
            P("clip", None),
            P("clip"),
            P("clip", None),
            P(),
            P(),
            P(None, None, "seq"),
            P(None, "seq"),
            P("seq", None),
            P(),
            P(),
            P(),
            P(("clip", "seq"), None),
        ),
        out_specs=(P(("clip", "seq"), None), P("seq", "clip", None)),
        check_vma=False,
    )
```

profile of v0, /device:TPU:0, one launch (start us, length us, event | category | flops | bytes accessed | tf_op | source)
XLA Modules:
  0.0 82.7 jit_solution(4467655343602366060)
XLA Ops:
  0.6 0.0 copy-start.1
  1.4 0.0 copy-start.2
  1.4 1.3 %copy-done.2 = bf16[128,5120]{1,0:T(8,128)(2,1)S(1)} copy-done((bf16[128,5120]{1,0:T(8,128)(2,1)S(1)}, bf16[128,5120]{1,0:T(8,128)(2,1)}, u32[]{:S(2)}) %copy-start.2) | copy-done | bytes 1310744
  2.7 0.0 copy-start.11
  2.7 0.7 copy-done.11
  3.3 0.0 copy-start.5
  3.3 0.0 copy-start.6
  3.3 0.0 copy-start.7
  3.3 1.1 %shard_map.132.up_own_ref = bf16[256,1280]{1,0:T(8,128)(2,1)S(1)} custom-call(s32[1]{0:T(128)S(6)} %copy.14.live_ref, s32[1,64]{1,0:T(1,128)S(1)} %copy-done.11, bf16[128,5120]{1,0:T(8,128)(2,1)S(1)} %copy-done.2), custom_call_target="tpu_custom_call" | custom-call | flops 335544320 | bytes 4000000 | tf_op jit(solution)/shard_map/pallas_call | solution.py:317
  4.4 3.0 %collective-permute-start.1 = (bf16[256,1280]{1,0:T(8,128)(2,1)S(1)}, bf16[256,1280]{1,0:T(8,128)(2,1)S(1)}, u32[]{:S(2)}, u32[]{:S(2)}) collective-permute-start(bf16[256,1280]{1,0:T(8,128)(2,1)S(1)} %shard_map.132.up_own_ref), channel_id=1, source_target_pairs={{0,1},{1,0},{2,3},{3,2},{4,5},{5,4},{6,7},{7,6},{8,9},{9,8},{10,11... | collective-permute-start | bytes 1966088 | tf_op jit(solution)/shard_map/ppermute | solution.py:352
  7.4 0.0 copy-done.1
  7.4 0.0 copy-done.5
  7.4 0.0 copy-done.6
  7.5 0.0 copy-done.7
  7.5 0.0 copy-start
  7.5 0.0 copy-start.8
  7.5 0.0 copy-start.9
  7.5 0.0 copy-start.10
  7.5 7.5 %shard_map.131 = (bf16[256,1280]{1,0:T(8,128)(2,1)S(1)}, bf16[3,256,640]{2,1,0:T(8,128)(2,1)}, bf16[8,256,256]{2,1,0:T(8,128)(2,1)}, bf16[256,1280]{1,0:T(8,128)(2,1)S(1)}) custom-call(s32[1]{0:T(128)S(6)} %copy.14.live_ref, f32[1280]{0:T(1024)S(1)} %copy-done.6, f32[1280]{0:T(1024)S(1)} %copy-done.7, f32[3,640]{1,0:T(4,128)S(1)} %copy-done.5, ...), custom_call_target="tpu_custom_call" | custom-call | flops 1677721600 | bytes 4000000 | tf_op jit(solution)/shard_map/pallas_call | solution.py:317
  15.0 0.1 collective-permute-start
  15.1 3.0 %collective-permute-start.7 = (bf16[256,1280]{1,0:T(8,128)(2,1)S(1)}, bf16[256,1280]{1,0:T(8,128)(2,1)S(1)}, u32[]{:S(2)}, u32[]{:S(2)}) collective-permute-start(bf16[256,1280]{1,0:T(8,128)(2,1)S(1)} %get-tuple-element.27.refs_4_), channel_id=1, source_target_pairs={{0,12},{2,14},{4,8},{6,10},{8,4},{10,6},{12,0},{14,2},{16,28},{18,... | collective-permute-start | bytes 1966088 | tf_op jit(solution)/shard_map/ppermute | solution.py:355
  18.1 0.4 collective-permute-start.6
  18.6 0.1 collective-permute-start.5
  18.7 4.3 %collective-permute-done.1.up_other_ref = bf16[256,1280]{1,0:T(8,128)(2,1)S(1)} collective-permute-done((bf16[256,1280]{1,0:T(8,128)(2,1)S(1)}, bf16[256,1280]{1,0:T(8,128)(2,1)S(1)}, u32[]{:S(2)}, u32[]{:S(2)}) %collective-permute-start.1) | collective-permute-done | bytes 655392 | tf_op jit(solution)/shard_map/ppermute | solution.py:352
  23.0 13.2 %collective-permute-done.other_ref = bf16[256,1280]{1,0:T(8,128)(2,1)S(1)} collective-permute-done((bf16[256,1280]{1,0:T(8,128)(2,1)S(1)}, bf16[256,1280]{1,0:T(8,128)(2,1)S(1)}, u32[]{:S(2)}, u32[]{:S(2)}) %collective-permute-start) | collective-permute-done | bytes 655392 | tf_op jit(solution)/shard_map/ppermute | solution.py:352
  36.2 0.0 copy-done
  36.2 0.0 copy-done.8
  36.2 0.0 copy-done.9
  36.2 0.0 copy-done.10
  36.2 0.0 copy-start.3
  36.3 1.2 %copy-done.3 = bf16[8,256,256]{2,1,0:T(8,128)(2,1)S(1)} copy-done((bf16[8,256,256]{2,1,0:T(8,128)(2,1)S(1)}, bf16[8,256,256]{2,1,0:T(8,128)(2,1)}, u32[]{:S(2)}) %copy-start.3) | copy-done | bytes 1048600
  37.5 0.0 copy-start.4
  37.5 1.2 %copy-done.4 = bf16[3,256,640]{2,1,0:T(8,128)(2,1)S(1)} copy-done((bf16[3,256,640]{2,1,0:T(8,128)(2,1)S(1)}, bf16[3,256,640]{2,1,0:T(8,128)(2,1)}, u32[]{:S(2)}) %copy-start.4) | copy-done | bytes 983064
  38.7 5.1 %shard_map.133 = (bf16[256,1280]{1,0:T(8,128)(2,1)S(1)}, bf16[240,256]{1,0:T(8,128)(2,1)S(1)}, bf16[240,256]{1,0:T(8,128)(2,1)S(1)}, bf16[240,256]{1,0:T(8,128)(...) custom-call(f32[1280]{0:T(1024)S(1)} %copy-done.8, ...), custom_call_target="tpu_custom_call" | custom-call | flops 1258291200 | bytes 4000000 | tf_op jit(solution)/shard_map/pallas_call | solution.py:317
  43.7 1.8 %collective-permute-start.2 = (bf16[240,256]{1,0:T(8,128)(2,1)S(1)}, bf16[240,256]{1,0:T(8,128)(2,1)S(1)}, u32[]{:S(2)}, u32[]{:S(2)}) collective-permute-start(bf16[240,256]{1,0:T(8,128)(2,1)S(1)} %get-tuple-element.24), channel_id=1, source_target_pairs={{0,4},{2,6},{4,0},{6,2},{8,12},{10,14},{12,8},{14,10},{16,20},{18,... | collective-permute-start | bytes 368648 | tf_op jit(solution)/shard_map/ppermute | solution.py:355
  45.6 1.6 %collective-permute-start.3 = (bf16[240,256]{1,0:T(8,128)(2,1)S(1)}, bf16[240,256]{1,0:T(8,128)(2,1)S(1)}, u32[]{:S(2)}, u32[]{:S(2)}) collective-permute-start(bf16[240,256]{1,0:T(8,128)(2,1)S(1)} %get-tuple-element.25), channel_id=1, source_target_pairs={{0,8},{2,10},{4,12},{6,14},{8,0},{10,2},{12,4},{14,6},{16,24},{18,... | collective-permute-start | bytes 368648 | tf_op jit(solution)/shard_map/ppermute | solution.py:355
  47.1 0.0 collective-permute-done.7.refs_7_
  47.2 0.1 collective-permute-start.4
  47.3 0.0 collective-permute-done.6.refs_6_
  47.3 0.0 collective-permute-done.5.refs_5_
  47.3 2.2 %collective-permute-done.2.refs_1_ = bf16[240,256]{1,0:T(8,128)(2,1)S(1)} collective-permute-done((bf16[240,256]{1,0:T(8,128)(2,1)S(1)}, bf16[240,256]{1,0:T(8,128)(2,1)S(1)}, u32[]{:S(2)}, u32[]{:S(2)}) %collective-permute-start.2) | collective-permute-done | bytes 122912 | tf_op jit(solution)/shard_map/ppermute | solution.py:355
  49.5 1.4 %collective-permute-done.3.refs_2_ = bf16[240,256]{1,0:T(8,128)(2,1)S(1)} collective-permute-done((bf16[240,256]{1,0:T(8,128)(2,1)S(1)}, bf16[240,256]{1,0:T(8,128)(2,1)S(1)}, u32[]{:S(2)}, u32[]{:S(2)}) %collective-permute-start.3) | collective-permute-done | bytes 122912 | tf_op jit(solution)/shard_map/ppermute | solution.py:355
  50.8 2.1 %collective-permute-done.4.refs_3_ = bf16[240,256]{1,0:T(8,128)(2,1)S(1)} collective-permute-done((bf16[240,256]{1,0:T(8,128)(2,1)S(1)}, bf16[240,256]{1,0:T(8,128)(2,1)S(1)}, u32[]{:S(2)}, u32[]{:S(2)}) %collective-permute-start.4) | collective-permute-done | bytes 122912 | tf_op jit(solution)/shard_map/ppermute | solution.py:355
  52.9 1.0 %shard_map.134 = (f32[120,1280]{1,0:T(8,128)S(1)}, bf16[120,1280]{1,0:T(8,128)(2,1)S(1)}) custom-call(bf16[240,256]{1,0:T(8,128)(2,1)S(1)} %get-tuple-element.23.refs_0_, bf16[240,256]{1,0:T(8,128)(2,1)S(1)} %collective-permute-done.2.refs_1_, bf16[240,256]{1,0:T(8,128)(2,1)S(1)} %collective-permute-done.3.refs_2_, ...), custom_call_target="tpu_custom_call" | custom-call | flops 629145600 | bytes 4000000 | tf_op jit(solution)/shard_map/pallas_call | solution.py:317
  53.9 0.1 collective-permute-start.8
  54.0 0.8 collective-permute-start.9
  54.7 1.6 %collective-permute-start.10 = (bf16[240,256]{1,0:T(8,128)(2,1)S(1)}, bf16[240,256]{1,0:T(8,128)(2,1)S(1)}, u32[]{:S(2)}, u32[]{:S(2)}) collective-permute-start(bf16[240,256]{1,0:T(8,128)(2,1)S(1)} %get-tuple-element.32), channel_id=1, source_target_pairs={{0,8},{2,10},{4,12},{6,14},{8,0},{10,2},{12,4},{14,6},{16,24},{18,... | collective-permute-start | bytes 368648 | tf_op jit(solution)/shard_map/ppermute | solution.py:355
  56.3 1.2 %collective-permute-start.11 = (bf16[240,256]{1,0:T(8,128)(2,1)S(1)}, bf16[240,256]{1,0:T(8,128)(2,1)S(1)}, u32[]{:S(2)}, u32[]{:S(2)}) collective-permute-start(bf16[240,256]{1,0:T(8,128)(2,1)S(1)} %get-tuple-element.33), channel_id=1, source_target_pairs={{0,12},{2,14},{4,8},{6,10},{8,4},{10,6},{12,0},{14,2},{16,28},{18,... | collective-permute-start | bytes 368648 | tf_op jit(solution)/shard_map/ppermute | solution.py:355
  57.5 0.0 collective-permute-done.8
  57.5 0.1 add_convert_fusion._.refs_8_
  57.6 2.1 %collective-permute-done.9.refs_1_ = bf16[240,256]{1,0:T(8,128)(2,1)S(1)} collective-permute-done((bf16[240,256]{1,0:T(8,128)(2,1)S(1)}, bf16[240,256]{1,0:T(8,128)(2,1)S(1)}, u32[]{:S(2)}, u32[]{:S(2)}) %collective-permute-start.9) | collective-permute-done | bytes 122912 | tf_op jit(solution)/shard_map/ppermute | solution.py:355
  59.7 1.2 %collective-permute-done.10.refs_2_ = bf16[240,256]{1,0:T(8,128)(2,1)S(1)} collective-permute-done((bf16[240,256]{1,0:T(8,128)(2,1)S(1)}, bf16[240,256]{1,0:T(8,128)(2,1)S(1)}, u32[]{:S(2)}, u32[]{:S(2)}) %collective-permute-start.10) | collective-permute-done | bytes 122912 | tf_op jit(solution)/shard_map/ppermute | solution.py:355
  60.9 2.6 %collective-permute-done.11.refs_3_ = bf16[240,256]{1,0:T(8,128)(2,1)S(1)} collective-permute-done((bf16[240,256]{1,0:T(8,128)(2,1)S(1)}, bf16[240,256]{1,0:T(8,128)(2,1)S(1)}, u32[]{:S(2)}, u32[]{:S(2)}) %collective-permute-start.11) | collective-permute-done | bytes 122912 | tf_op jit(solution)/shard_map/ppermute | solution.py:355
  63.5 0.0 copy-start.12
  63.5 0.9 %shard_map.136 = (f32[120,1280]{1,0:T(8,128)S(1)}, bf16[120,1280]{1,0:T(8,128)(2,1)S(1)}) custom-call(bf16[240,256]{1,0:T(8,128)(2,1)S(1)} %get-tuple-element.30.refs_0_, bf16[240,256]{1,0:T(8,128)(2,1)S(1)} %collective-permute-done.9.refs_1_, bf16[240,256]{1,0:T(8,128)(2,1)S(1)} %collective-permute-done.10.refs_2_, ...), custom_call_target="tpu_custom_call" | custom-call | flops 629145600 | bytes 4000000 | tf_op jit(solution)/shard_map/pallas_call | solution.py:317
  64.5 0.1 collective-permute-start.12
  64.5 2.7 %collective-permute-start.13 = (bf16[120,1280]{1,0:T(8,128)(2,1)S(1)}, bf16[120,1280]{1,0:T(8,128)(2,1)S(1)}, u32[]{:S(2)}, u32[]{:S(2)}) collective-permute-start(bf16[120,1280]{1,0:T(8,128)(2,1)S(1)} %add_convert_fusion._.refs_8_), channel_id=1, source_target_pairs={{0,16},{2,18},{4,20},{6,22},{8,24},{10,26},{12,28},{14,30},{16,0},... | collective-permute-start | bytes 921608 | tf_op jit(solution)/shard_map/ppermute | solution.py:355
  67.3 0.0 copy-done.12
  67.3 1.7 %shard_map.135 = bf16[128,5120]{1,0:T(8,128)(2,1)} custom-call(s32[1]{0:T(128)S(6)} %copy.14.live_ref, s32[1,64]{1,0:T(1,128)S(1)} %copy-done.12, bf16[256,1280]{1,0:T(8,128)(2,1)S(1)} %get-tuple-element.22.merged_ref, bf16[120,1280]{1,0:T(8,128)(2,1)S(1)} %add_convert_fusion._.refs_8_), custom_call_target="tpu_custom_call" | custom-call | flops 335544320 | bytes 4000000 | tf_op jit(solution)/shard_map/pallas_call | solution.py:317
  69.0 0.0 collective-permute-done.12
  69.0 12.7 %collective-permute-done.13 = bf16[120,1280]{1,0:T(8,128)(2,1)S(1)} collective-permute-done((bf16[120,1280]{1,0:T(8,128)(2,1)S(1)}, bf16[120,1280]{1,0:T(8,128)(2,1)S(1)}, u32[]{:S(2)}, u32[]{:S(2)}) %collective-permute-start.13) | collective-permute-done | bytes 307232 | tf_op jit(solution)/shard_map/ppermute | solution.py:355
  81.7 0.9 %add_bitcast_fusion = f32[1,120,1280]{2,1,0:T(8,128)} fusion(bf16[120,1280]{1,0:T(8,128)(2,1)S(1)} %collective-permute-done.13, f32[120,1280]{1,0:T(8,128)S(1)} %get-tuple-element.34, bf16[120,1280]{1,0:T(8,128)(2,1)S(1)} %collective-permute-done.12), kind=kLoop, calls=%fused_computation | loop fusion | flops 614400 | bytes 1843200 | tf_op jit(solution)/shard_map/broadcast_in_dim | solution.py:441
Async XLA Ops:
  0.6 6.8 %copy-start.1 = (bf16[256,1280]{1,0:T(8,128)(2,1)S(1)}, bf16[256,1280]{1,0:T(8,128)(2,1)}, u32[]{:S(2)}) copy-start(bf16[256,1280]{1,0:T(8,128)(2,1)} %patches_ref.1) | copy-start | bytes 1966084
  1.4 1.3 %copy-start.2 = (bf16[128,5120]{1,0:T(8,128)(2,1)S(1)}, bf16[128,5120]{1,0:T(8,128)(2,1)}, u32[]{:S(2)}) copy-start(bf16[128,5120]{1,0:T(8,128)(2,1)} %grad_ref.1) | copy-start | bytes 3932164
  2.7 0.7 copy-start.11
  3.3 4.1 %copy-start.5 = (f32[3,640]{1,0:T(4,128)S(1)}, f32[3,640]{1,0:T(4,128)}, u32[]{:S(2)}) copy-start(f32[3,640]{1,0:T(4,128)} %b_ref.2) | copy-start | bytes 23044
  3.3 4.1 %copy-start.6 = (f32[1280]{0:T(1024)S(1)}, f32[1280]{0:T(1024)}, u32[]{:S(2)}) copy-start(f32[1280]{0:T(1024)} %gain_ref.2) | copy-start | bytes 15364
  3.3 4.1 %copy-start.7 = (f32[1280]{0:T(1024)S(1)}, f32[1280]{0:T(1024)}, u32[]{:S(2)}) copy-start(f32[1280]{0:T(1024)} %bias_ref.2) | copy-start | bytes 15364
  4.4 18.6 %collective-permute-start.1 = (bf16[256,1280]{1,0:T(8,128)(2,1)S(1)}, bf16[256,1280]{1,0:T(8,128)(2,1)S(1)}, u32[]{:S(2)}, u32[]{:S(2)}) collective-permute-start(bf16[256,1280]{1,0:T(8,128)(2,1)S(1)} %shard_map.132.up_own_ref), channel_id=1, source_target_pairs={{0,1},{1,0},{2,3},{3,2},{4,5},{5,4},{6,7},{7,6},{8,9},{9,8},{10,11... | collective-permute-start | bytes 1966088 | tf_op jit(solution)/shard_map/ppermute | solution.py:352
  7.5 28.8 %copy-start = (bf16[640,1280]{1,0:T(8,128)(2,1)S(1)}, bf16[640,1280]{1,0:T(8,128)(2,1)}, u32[]{:S(2)}) copy-start(bf16[640,1280]{1,0:T(8,128)(2,1)} %proj_ref.1) | copy-start | bytes 4915204
  7.5 28.8 %copy-start.8 = (f32[1280]{0:T(1024)S(1)}, f32[1280]{0:T(1024)}, u32[]{:S(2)}) copy-start(f32[1280]{0:T(1024)} %b_ref.3) | copy-start | bytes 15364
  7.5 28.7 %copy-start.9 = (f32[1280]{0:T(1024)S(1)}, f32[1280]{0:T(1024)}, u32[]{:S(2)}) copy-start(f32[1280]{0:T(1024)} %gain_ref.3) | copy-start | bytes 15364
  7.5 28.7 %copy-start.10 = (f32[1280]{0:T(1024)S(1)}, f32[1280]{0:T(1024)}, u32[]{:S(2)}) copy-start(f32[1280]{0:T(1024)} %bias_ref.3) | copy-start | bytes 15364
  15.0 21.2 %collective-permute-start = (bf16[256,1280]{1,0:T(8,128)(2,1)S(1)}, bf16[256,1280]{1,0:T(8,128)(2,1)S(1)}, u32[]{:S(2)}, u32[]{:S(2)}) collective-permute-start(bf16[256,1280]{1,0:T(8,128)(2,1)S(1)} %get-tuple-element.19.own_ref), channel_id=1, source_target_pairs={{0,1},{1,0},{2,3},{3,2},{4,5},{5,4},{6,7},{7,6},{8,9},{9,8},{10,11... | collective-permute-start | bytes 1966088 | tf_op jit(solution)/shard_map/ppermute | solution.py:352
  15.1 32.0 %collective-permute-start.7 = (bf16[256,1280]{1,0:T(8,128)(2,1)S(1)}, bf16[256,1280]{1,0:T(8,128)(2,1)S(1)}, u32[]{:S(2)}, u32[]{:S(2)}) collective-permute-start(bf16[256,1280]{1,0:T(8,128)(2,1)S(1)} %get-tuple-element.27.refs_4_), channel_id=1, source_target_pairs={{0,12},{2,14},{4,8},{6,10},{8,4},{10,6},{12,0},{14,2},{16,28},{18,... | collective-permute-start | bytes 1966088 | tf_op jit(solution)/shard_map/ppermute | solution.py:355
  18.1 29.2 %collective-permute-start.6 = (bf16[256,1280]{1,0:T(8,128)(2,1)S(1)}, bf16[256,1280]{1,0:T(8,128)(2,1)S(1)}, u32[]{:S(2)}, u32[]{:S(2)}) collective-permute-start(bf16[256,1280]{1,0:T(8,128)(2,1)S(1)} %get-tuple-element.27.refs_4_), channel_id=1, source_target_pairs={{0,8},{2,10},{4,12},{6,14},{8,0},{10,2},{12,4},{14,6},{16,24},{18,... | collective-permute-start | bytes 1966088 | tf_op jit(solution)/shard_map/ppermute | solution.py:355
  18.6 28.7 %collective-permute-start.5 = (bf16[256,1280]{1,0:T(8,128)(2,1)S(1)}, bf16[256,1280]{1,0:T(8,128)(2,1)S(1)}, u32[]{:S(2)}, u32[]{:S(2)}) collective-permute-start(bf16[256,1280]{1,0:T(8,128)(2,1)S(1)} %get-tuple-element.27.refs_4_), channel_id=1, source_target_pairs={{0,4},{2,6},{4,0},{6,2},{8,12},{10,14},{12,8},{14,10},{16,20},{18,... | collective-permute-start | bytes 1966088 | tf_op jit(solution)/shard_map/ppermute | solution.py:355
  36.2 1.2 %copy-start.3 = (bf16[8,256,256]{2,1,0:T(8,128)(2,1)S(1)}, bf16[8,256,256]{2,1,0:T(8,128)(2,1)}, u32[]{:S(2)}) copy-start(bf16[8,256,256]{2,1,0:T(8,128)(2,1)} %get-tuple-element.21.probs_ref) | copy-start | bytes 3145732
  37.5 1.2 %copy-start.4 = (bf16[3,256,640]{2,1,0:T(8,128)(2,1)S(1)}, bf16[3,256,640]{2,1,0:T(8,128)(2,1)}, u32[]{:S(2)}) copy-start(bf16[3,256,640]{2,1,0:T(8,128)(2,1)} %get-tuple-element.20.triple_ref) | copy-start | bytes 2949124
  43.7 5.7 %collective-permute-start.2 = (bf16[240,256]{1,0:T(8,128)(2,1)S(1)}, bf16[240,256]{1,0:T(8,128)(2,1)S(1)}, u32[]{:S(2)}, u32[]{:S(2)}) collective-permute-start(bf16[240,256]{1,0:T(8,128)(2,1)S(1)} %get-tuple-element.24), channel_id=1, source_target_pairs={{0,4},{2,6},{4,0},{6,2},{8,12},{10,14},{12,8},{14,10},{16,20},{18,... | collective-permute-start | bytes 368648 | tf_op jit(solution)/shard_map/ppermute | solution.py:355
  45.6 5.3 %collective-permute-start.3 = (bf16[240,256]{1,0:T(8,128)(2,1)S(1)}, bf16[240,256]{1,0:T(8,128)(2,1)S(1)}, u32[]{:S(2)}, u32[]{:S(2)}) collective-permute-start(bf16[240,256]{1,0:T(8,128)(2,1)S(1)} %get-tuple-element.25), channel_id=1, source_target_pairs={{0,8},{2,10},{4,12},{6,14},{8,0},{10,2},{12,4},{14,6},{16,24},{18,... | collective-permute-start | bytes 368648 | tf_op jit(solution)/shard_map/ppermute | solution.py:355
  47.2 5.8 %collective-permute-start.4 = (bf16[240,256]{1,0:T(8,128)(2,1)S(1)}, bf16[240,256]{1,0:T(8,128)(2,1)S(1)}, u32[]{:S(2)}, u32[]{:S(2)}) collective-permute-start(bf16[240,256]{1,0:T(8,128)(2,1)S(1)} %get-tuple-element.26), channel_id=1, source_target_pairs={{0,12},{2,14},{4,8},{6,10},{8,4},{10,6},{12,0},{14,2},{16,28},{18,... | collective-permute-start | bytes 368648 | tf_op jit(solution)/shard_map/ppermute | solution.py:355
  53.9 3.6 %collective-permute-start.8 = (bf16[120,1280]{1,0:T(8,128)(2,1)S(1)}, bf16[120,1280]{1,0:T(8,128)(2,1)S(1)}, u32[]{:S(2)}, u32[]{:S(2)}) collective-permute-start(bf16[120,1280]{1,0:T(8,128)(2,1)S(1)} %get-tuple-element.29), channel_id=1, source_target_pairs={{0,2},{2,0},{4,6},{6,4},{8,10},{10,8},{12,14},{14,12},{16,18},{18,... | collective-permute-start | bytes 921608 | tf_op jit(solution)/shard_map/ppermute | solution.py:355
  54.0 5.7 %collective-permute-start.9 = (bf16[240,256]{1,0:T(8,128)(2,1)S(1)}, bf16[240,256]{1,0:T(8,128)(2,1)S(1)}, u32[]{:S(2)}, u32[]{:S(2)}) collective-permute-start(bf16[240,256]{1,0:T(8,128)(2,1)S(1)} %get-tuple-element.31), channel_id=1, source_target_pairs={{0,4},{2,6},{4,0},{6,2},{8,12},{10,14},{12,8},{14,10},{16,20},{18,... | collective-permute-start | bytes 368648 | tf_op jit(solution)/shard_map/ppermute | solution.py:355
  54.7 6.2 %collective-permute-start.10 = (bf16[240,256]{1,0:T(8,128)(2,1)S(1)}, bf16[240,256]{1,0:T(8,128)(2,1)S(1)}, u32[]{:S(2)}, u32[]{:S(2)}) collective-permute-start(bf16[240,256]{1,0:T(8,128)(2,1)S(1)} %get-tuple-element.32), channel_id=1, source_target_pairs={{0,8},{2,10},{4,12},{6,14},{8,0},{10,2},{12,4},{14,6},{16,24},{18,... | collective-permute-start | bytes 368648 | tf_op jit(solution)/shard_map/ppermute | solution.py:355
  56.3 7.2 %collective-permute-start.11 = (bf16[240,256]{1,0:T(8,128)(2,1)S(1)}, bf16[240,256]{1,0:T(8,128)(2,1)S(1)}, u32[]{:S(2)}, u32[]{:S(2)}) collective-permute-start(bf16[240,256]{1,0:T(8,128)(2,1)S(1)} %get-tuple-element.33), channel_id=1, source_target_pairs={{0,12},{2,14},{4,8},{6,10},{8,4},{10,6},{12,0},{14,2},{16,28},{18,... | collective-permute-start | bytes 368648 | tf_op jit(solution)/shard_map/ppermute | solution.py:355
  63.5 3.8 %copy-start.12 = (s32[1,64]{1,0:T(1,128)S(1)}, s32[1,64]{1,0:T(1,128)}, u32[]{:S(2)}) copy-start(s32[1,64]{1,0:T(1,128)} %places_ref.3) | copy-start | bytes 772
  64.5 4.6 %collective-permute-start.12 = (bf16[120,1280]{1,0:T(8,128)(2,1)S(1)}, bf16[120,1280]{1,0:T(8,128)(2,1)S(1)}, u32[]{:S(2)}, u32[]{:S(2)}) collective-permute-start(bf16[120,1280]{1,0:T(8,128)(2,1)S(1)} %get-tuple-element.35), channel_id=1, source_target_pairs={{0,2},{2,0},{4,6},{6,4},{8,10},{10,8},{12,14},{14,12},{16,18},{18,... | collective-permute-start | bytes 921608 | tf_op jit(solution)/shard_map/ppermute | solution.py:355
  64.5 17.2 %collective-permute-start.13 = (bf16[120,1280]{1,0:T(8,128)(2,1)S(1)}, bf16[120,1280]{1,0:T(8,128)(2,1)S(1)}, u32[]{:S(2)}, u32[]{:S(2)}) collective-permute-start(bf16[120,1280]{1,0:T(8,128)(2,1)S(1)} %add_convert_fusion._.refs_8_), channel_id=1, source_target_pairs={{0,16},{2,18},{4,20},{6,22},{8,24},{10,26},{12,28},{14,30},{16,0},... | collective-permute-start | bytes 921608 | tf_op jit(solution)/shard_map/ppermute | solution.py:355
where the time goes:
time: 82.9 us; the launch traced here: 82.7 us
  waiting for transfers between devices  41.8 us (50%)
  Pallas kernels  17.3 us (21%)
  starting transfers between devices  16.7 us (20%)
  local copies, waits for them, and re-layouts  4.43 us (5%)
  between operations  1.49 us (2%)
  other arithmetic  0.99 us (1%)
    ppermute x12, waiting for transfers between devices, flip(): return lax.ppermute(value, 'clip', [(i, i ^ bits) for i in range(n_clip)])  24.2 us
    ppermute x2, waiting for transfers between devices, swap(): return lax.ppermute(value, 'seq', [(0, 1), (1, 0)])  17.5 us
    pallas_call x6, Pallas kernels, call(): pl.pallas_call(kernel, out_shape=outs, in_specs=[spec[kind] for kind in k...  17.3 us
    ppermute x12, starting transfers between devices, flip(): return lax.ppermute(value, 'clip', [(i, i ^ bits) for i in range(n_clip)])  13.6 us
    unnamed x26, local copies, waits for them, and re-layouts  4.43 us
    ppermute x2, starting transfers between devices, swap(): return lax.ppermute(value, 'seq', [(0, 1), (1, 0)])  3.14 us
  transfers between devices with their start and end apart: 14, of which 9 were waited for; matrix products, arithmetic and copies ran while one was open for 0% of the time, Pallas kernels for 17%

commit v1 on v0

--- a/solution.py
+++ b/solution.py
@@ -135,12 +135,12 @@
     return (placed, summed[None])
 
 
-def place_masks(live_ref, places_ref, share_rows, rows):
-    tokens = places_ref.shape[1]
+def place_masks(live_ref, places, share_rows, rows, first_row):
+    tokens = places.shape[1]
     token = lax.broadcasted_iota(jnp.int32, (tokens, rows), 0)
-    owner = lax.broadcasted_iota(jnp.int32, (tokens, rows), 1) // 4
+    owner = (lax.broadcasted_iota(jnp.int32, (tokens, rows), 1) + first_row) // 4
     spread = jnp.where((token == owner) & (token < live_ref[0]), 1.0, 0.0)
-    shifted = jnp.broadcast_to(places_ref[...].astype(jnp.float32) + 1.0, (8, tokens))
+    shifted = jnp.broadcast_to(places.astype(jnp.float32) + 1.0, (8, tokens))
     row = jnp.dot(shifted, spread, precision=lax.Precision.HIGHEST)[:1] - 1.0
     first = lax.axis_index("seq") * share_rows
     window = lax.broadcasted_iota(jnp.int32, (share_rows, rows), 0) + first
@@ -151,24 +151,6 @@
     ]
 
 
-def pull_kernel(live_ref, places_ref, grad_ref, out_ref):
-    width = out_ref.shape[1]
-    masks = place_masks(live_ref, places_ref, grad_ref.shape[0], out_ref.shape[0])
-    total = None
-    for k in range(4):
-        term = leading(masks[k], grad_ref[:, k * width : (k + 1) * width])
-        total = term if total is None else total + term
-    out_ref[...] = total.astype(out_ref.dtype)
-
-
-def place_kernel(live_ref, places_ref, merged_ref, _, out_ref):
-    width = merged_ref.shape[1]
-    masks = place_masks(live_ref, places_ref, out_ref.shape[0], merged_ref.shape[0])
-    for k in range(4):
-        term = jnp.dot(masks[k], merged_ref[...], preferred_element_type=jnp.float32)
-        out_ref[:, k * width : (k + 1) * width] = term.astype(out_ref.dtype)
-
-
 def begin(sources, targets, sems, first=0):
     copies = [
         pltpu.make_async_copy(source, target, sems.at[first + k])
@@ -179,43 +161,64 @@
     return copies
 
 
-def forward_kernel(
+def half_start(half, own):
+    seq = lax.axis_index("seq")
+    return pl.multiple_of((seq if own else 1 - seq) * half, 128)
+
+
+def prepare_kernel(
     live_ref,
     gain_ref,
     bias_ref,
-    b_ref,
     patches_hbm,
-    w_hbm,
-    proj_hbm,
+    places_hbm,
+    grad_hbm,
     normed_ref,
-    triple_ref,
-    probs_ref,
-    partial_ref,
+    keep_ref,
+    send_ref,
     patches_ref,
-    w_ref,
-    proj_ref,
-    attended_ref,
+    places_ref,
+    grad_ref,
     sems,
 ):
-    rows = patches_ref.shape[0]
-    came = begin(
-        (patches_hbm, w_hbm.at[0], w_hbm.at[1], w_hbm.at[2], proj_hbm),
-        (patches_ref, w_ref.at[0], w_ref.at[1], w_ref.at[2], proj_ref),
-        sems,
-    )
+    width = send_ref.shape[1]
+    half = send_ref.shape[0]
+    came = begin((patches_hbm, places_hbm, grad_hbm), (patches_ref, places_ref, grad_ref), sems)
     came[0].wait()
     normed_ref[...] = normalize(
         patches_ref[...].astype(jnp.float32), gain_ref[...][None, :], bias_ref[...][None, :]
     )[0].astype(jnp.bfloat16)
-    for t in range(3):
-        came[1 + t].wait()
-        part = jnp.dot(normed_ref[...], w_ref[t], preferred_element_type=jnp.float32)
-        triple_ref[t] = (part + b_ref[t : t + 1, :]).astype(jnp.bfloat16)
-    live = lax.broadcasted_iota(jnp.int32, (rows, rows), 1) < 4 * live_ref[0]
+    came[1].wait()
+    came[2].wait()
+    for out_ref, own in ((send_ref, False), (keep_ref, True)):
+        masks = place_masks(
+            live_ref, places_ref[...], grad_ref.shape[0], half, half_start(half, own)
+        )
+        total = None
+        for k in range(4):
+            term = leading(masks[k], grad_ref[:, k * width : (k + 1) * width])
+            total = term if total is None else total + term
+        out_ref[...] = total.astype(out_ref.dtype)
+
+
+def place_kernel(live_ref, places_ref, own_ref, other_ref, _, out_ref):
+    half, width = own_ref.shape
+    share_rows = out_ref.shape[0]
+    own = place_masks(live_ref, places_ref[...], share_rows, half, half_start(half, True))
+    other = place_masks(live_ref, places_ref[...], share_rows, half, half_start(half, False))
+    for k in range(4):
+        term = jnp.dot(own[k], own_ref[...], preferred_element_type=jnp.float32)
+        term += jnp.dot(other[k], other_ref[...], preferred_element_type=jnp.float32)
+        out_ref[:, k * width : (k + 1) * width] = term.astype(out_ref.dtype)
+
+
+def attend(live_ref, triple_ref, start, probs_ref, attended_ref):
+    half, rows = probs_ref.shape[1:]
+    live = lax.broadcasted_iota(jnp.int32, (half, rows), 1) < 4 * live_ref[0]
     steep = HEAD ** (-0.5) * 1.4426950408889634
     for h in range(probs_ref.shape[0]):
         cols = slice(h * HEAD, (h + 1) * HEAD)
-        scores = trailing(triple_ref[0, :, cols], triple_ref[1, :, cols])
+        scores = trailing(triple_ref[0, pl.ds(start, half), cols], triple_ref[1, :, cols])
         scores = jnp.where(live, scores, -1e30)
         powers = jnp.exp2((scores - jnp.max(scores, axis=-1, keepdims=True)) * steep)
         weights = powers * (1.0 / jnp.sum(powers, axis=-1, keepdims=True))
@@ -224,59 +227,81 @@
         attended_ref[:, cols] = jnp.dot(
             weights, triple_ref[2, :, cols], preferred_element_type=jnp.float32
         ).astype(jnp.bfloat16)
+
+
+def first_kernel(
+    live_ref,
+    b_ref,
+    normed_hbm,
+    w_hbm,
+    proj_hbm,
+    triple_ref,
+    probs_ref,
+    send_ref,
+    normed_ref,
+    w_ref,
+    proj_ref,
+    attended_ref,
+    sems,
+):
+    came = begin(
+        (normed_hbm, w_hbm.at[0], w_hbm.at[1], w_hbm.at[2], proj_hbm),
+        (normed_ref, w_ref.at[0], w_ref.at[1], w_ref.at[2], proj_ref),
+        sems,
+    )
+    came[0].wait()
+    for t in range(3):
+        came[1 + t].wait()
+        part = jnp.dot(normed_ref[...], w_ref[t], preferred_element_type=jnp.float32)
+        triple_ref[t] = (part + b_ref[t : t + 1, :]).astype(jnp.bfloat16)
+    start = half_start(send_ref.shape[0], False)
+    attend(live_ref, triple_ref, start, probs_ref, attended_ref)
     came[4].wait()
-    partial_ref[...] = jnp.dot(
+    send_ref[...] = jnp.dot(
         attended_ref[...], proj_ref[...], preferred_element_type=jnp.float32
     ).astype(jnp.bfloat16)
 
 
-def backward_kernel(
+def second_kernel(live_ref, triple_ref, proj_ref, probs_ref, keep_ref, attended_ref):
+    start = half_start(keep_ref.shape[0], True)
+    attend(live_ref, triple_ref, start, probs_ref, attended_ref)
+    keep_ref[...] = jnp.dot(attended_ref[...], proj_ref[...], preferred_element_type=jnp.float32)
+
+
+def middle_kernel(
     b_ref,
     gain_ref,
     bias_ref,
-    own_ref,
-    other_ref,
+    keep_ref,
+    came_ref,
     patches_ref,
-    up_own_ref,
-    up_other_ref,
-    proj_ref,
-    triple_ref,
-    probs_ref,
+    up_keep_ref,
+    up_came_ref,
     merged_ref,
-    *refs,
-):
-    outs, (back_ref, slots_ref) = refs[:8], refs[8:]
+    back_ref,
+):
+    half = keep_ref.shape[0]
     gain = gain_ref[...][None, :]
     output = (
-        own_ref[...].astype(jnp.float32)
-        + other_ref[...].astype(jnp.float32)
+        keep_ref[...]
+        + came_ref[...].astype(jnp.float32)
         + b_ref[...][None, :]
-        + patches_ref[...].astype(jnp.float32)
+        + patches_ref[pl.ds(half_start(half, True), half), :].astype(jnp.float32)
     )
     merged, unit_rows, inverse = normalize(output, gain, bias_ref[...][None, :])
     merged_ref[...] = merged.astype(jnp.bfloat16)
-    upstream = up_own_ref[...].astype(jnp.float32) + up_other_ref[...].astype(jnp.float32)
-    row_grad = normalize_back(upstream, unit_rows, inverse, gain).astype(jnp.bfloat16)
-    back_ref[...] = trailing(row_grad, proj_ref[...]).astype(jnp.bfloat16)
+    upstream = up_keep_ref[...].astype(jnp.float32) + up_came_ref[...].astype(jnp.float32)
+    back_ref[...] = normalize_back(upstream, unit_rows, inverse, gain).astype(jnp.bfloat16)
+
+
+def attend_back(row_ref, proj_ref, triple_ref, probs_ref, back_ref, start, put):
+    half = row_ref.shape[0]
+    back_ref[...] = trailing(row_ref[...], proj_ref[...]).astype(jnp.bfloat16)
     scaling = HEAD ** (-0.5)
-    heads = probs_ref.shape[0]
-    per_block = slots_ref.shape[2] // HEAD
-    me = lax.axis_index("clip")
-    turn = lax.bitwise_and(lax.shift_right_logical(me, 1), 3)
-    away = 1 - lax.shift_right_logical(me, 3)
-
-    def put(t, h, value):
-        piece = t * heads + h
-        block, sub = piece // per_block, piece % per_block
-        slot = lax.bitwise_xor(turn, block % 4)
-        side = lax.bitwise_xor(away, block // 4)
-        slots_ref[side, slot, sub * HEAD : (sub + 1) * HEAD, :] = value.astype(jnp.bfloat16)
-
-    for h in range(heads):
+    for h in range(probs_ref.shape[0]):
         cols = slice(h * HEAD, (h + 1) * HEAD)
         back = back_ref[:, cols]
         weights = probs_ref[h]
-        put(2, h, leading(back, weights))
         prob_grad = trailing(back, triple_ref[2, :, cols])
         wide = weights.astype(jnp.float32)
         inner = jnp.sum(prob_grad * wide, axis=-1, keepdims=True)
@@ -287,8 +312,53 @@
             (((0,), (1,)), ((), ())),
             preferred_element_type=jnp.float32,
         )
-        put(0, h, query_grad * scaling)
-        put(1, h, leading(triple_ref[0, :, cols], score_grad) * scaling)
+        key_grad = leading(triple_ref[0, pl.ds(start, half), cols], score_grad)
+        put(h, query_grad * scaling, key_grad * scaling, leading(back, weights))
+
+
+def own_back_kernel(
+    row_ref, proj_ref, triple_ref, probs_ref, query_ref, key_ref, value_ref, back_ref
+):
+    def put(h, query_grad, key_grad, value_grad):
+        rows = slice(h * HEAD, (h + 1) * HEAD)
+        query_ref[rows, :] = query_grad.astype(jnp.bfloat16)
+        key_ref[rows, :] = key_grad
+        value_ref[rows, :] = value_grad
+
+    start = half_start(row_ref.shape[0], True)
+    attend_back(row_ref, proj_ref, triple_ref, probs_ref, back_ref, start, put)
+
+
+def other_back_kernel(
+    row_ref, proj_ref, triple_ref, probs_ref, query_ref, key_ref, value_ref, *refs
+):
+    outs, (back_ref, slots_ref) = refs[:8], refs[8:]
+    half = row_ref.shape[0]
+    heads = probs_ref.shape[0]
+    per_block = slots_ref.shape[2] // HEAD
+    me = lax.axis_index("clip")
+    turn = lax.bitwise_and(lax.shift_right_logical(me, 1), 3)
+    away = 1 - lax.shift_right_logical(me, 3)
+    mine, start = half_start(half, True), half_start(half, False)
+
+    def where(t, h):
+        piece = t * heads + h
+        block, sub = piece // per_block, piece % per_block
+        slot = lax.bitwise_xor(turn, block % 4)
+        side = lax.bitwise_xor(away, block // 4)
+        return side, slot, slice(sub * HEAD, (sub + 1) * HEAD)
+
+    def put(h, query_grad, key_grad, value_grad):
+        rows = slice(h * HEAD, (h + 1) * HEAD)
+        side, slot, place = where(0, h)
+        slots_ref[side, slot, place, pl.ds(mine, half)] = query_ref[rows, :]
+        slots_ref[side, slot, place, pl.ds(start, half)] = query_grad.astype(jnp.bfloat16)
+        side, slot, place = where(1, h)
+        slots_ref[side, slot, place, :] = (key_ref[rows, :] + key_grad).astype(jnp.bfloat16)
+        side, slot, place = where(2, h)
+        slots_ref[side, slot, place, :] = (value_ref[rows, :] + value_grad).astype(jnp.bfloat16)
+
+    attend_back(row_ref, proj_ref, triple_ref, probs_ref, back_ref, start, put)
     for k, out_ref in enumerate(outs):
         out_ref[...] = slots_ref[k // 4, k % 4]
 
@@ -354,59 +424,89 @@
     def flip(value, bits):
         return lax.ppermute(value, "clip", [(i, i ^ bits) for i in range(n_clip)])
 
-    up_own = call(
-        pull_kernel,
-        full,
-        "svv",
+    half = rows // 2
+    part, wide = shape((half, width), low), shape((half, width), jnp.float32)
+    probs_half = shape((heads, half, rows), low)
+    attended = pltpu.VMEM((half, local), low)
+    block = 3 * local // 8
+    normed, up_keep, up_send = call(
+        prepare_kernel,
+        (full, part, part),
+        "svvaaa",
         8 * rows * share_rows * width,
-        (clip_tokens, positions, grad_placed),
-    )
-    up_other = swap(up_own)
-    normed, triple, probs, partial = call(
-        forward_kernel,
-        (full, shape((3, rows, local), low), shape((heads, rows, rows), low), full),
-        "svvvaaa",
-        8 * rows * width * local,
+        (clip_tokens, norm_gain, norm_bias, patches, positions, grad_placed),
         (
-            clip_tokens,
-            norm_gain,
-            norm_bias,
-            b_qkv,
-            patches,
-            jnp.transpose(w_qkv, (1, 0, 2)),
-            w_proj,
+            pltpu.VMEM((rows, width), low),
+            pltpu.VMEM(positions.shape, jnp.int32),
+            pltpu.VMEM(grad_placed.shape, low),
+            pltpu.SemaphoreType.DMA((3,)),
         ),
+        limit=62,
+    )
+    up_came = swap(up_send)
+    normed_of = [normed] + [flip(normed, q << 1) for q in (1, 2)]
+    normed_of += [flip(normed, 3 << 1)]
+    triple, other_probs, part_send = call(
+        first_kernel,
+        (shape((3, rows, local), low), probs_half, part),
+        "svaaa",
+        7 * rows * width * local,
+        (clip_tokens, b_qkv, normed, jnp.transpose(w_qkv, (1, 0, 2)), w_proj),
         (
             pltpu.VMEM((rows, width), low),
             pltpu.VMEM((3, width, local), low),
             pltpu.VMEM((local, width), low),
-            pltpu.VMEM((rows, local), low),
+            attended,
             pltpu.SemaphoreType.DMA((5,)),
         ),
-        limit=52,
-    )
-    other = swap(partial)
-    normed_of = [normed] + [flip(normed, q << 1) for q in (1, 2, 3)]
-    block = 3 * local // 8
-    merged, *sent = call(
-        backward_kernel,
-        (full,) + (shape((block, rows), low),) * 8,
-        "v" * 11,
-        6 * rows * width * local,
+        limit=51,
+    )
+    part_came = swap(part_send)
+    own_probs, part_keep = call(
+        second_kernel,
+        (probs_half, wide),
+        "svv",
+        3 * half * width * local,
+        (clip_tokens, triple, w_proj),
+        (attended,),
+    )
+    merged, own_rows = call(
+        middle_kernel,
+        (part, part),
+        "v" * 8,
+        100 * half * width,
         (
             b_proj,
             merge_gain,
             merge_bias,
-            partial,
-            other,
+            part_keep,
+            part_came,
             patches,
-            up_own,
-            up_other,
-            w_proj,
-            triple,
-            probs,
+            up_keep,
+            up_came,
         ),
-        (pltpu.VMEM((rows, local), low), pltpu.VMEM((2, 4, block, rows), low)),
+    )
+    other_rows = swap(own_rows)
+    other_merged = swap(merged)
+    query_own, key_own, value_own = call(
+        own_back_kernel,
+        (
+            shape((local, half), low),
+            shape((local, rows), jnp.float32),
+            shape((local, rows), jnp.float32),
+        ),
+        "vvvv",
+        4 * half * width * local,
+        (own_rows, w_proj, triple, own_probs),
+        (attended,),
+    )
+    sent = call(
+        other_back_kernel,
+        (shape((block, rows), low),) * 8,
+        "v" * 7,
+        4 * half * width * local,
+        (other_rows, w_proj, triple, other_probs, query_own, key_own, value_own),
+        (attended, pltpu.VMEM((2, 4, block, rows), low)),
     )
 
     def exchange(sent):
@@ -433,9 +533,9 @@
     placed = call(
         place_kernel,
         shape((share_rows, 4 * width), low),
-        "svva",
+        "svvva",
         8 * rows * share_rows * width,
-        (clip_tokens, positions, merged, far_sum),
+        (clip_tokens, positions, merged, other_merged, far_sum),
     )
     summed = near_keep + near_came.astype(jnp.float32) + crossing.astype(jnp.float32)
     return (placed, summed[None])

time: 82.9 us -> 83.5 us (level)
  Pallas kernels: 17.3 us -> 24.4 us
  waiting for transfers between devices: 41.8 us -> 35.3 us
  starting transfers between devices: 16.7 us -> 20 us
  local copies, waits for them, and re-layouts: 4.43 us -> 1.13 us
    pallas_call x6 -> x9, Pallas kernels: 17.3 us -> 24.4 us  [call(): pl.pallas_call(kernel, out_shape=outs, in_specs=[spec[kind] for kind in k...]
    ppermute x2 -> x4, waiting for transfers between devices: 17.5 us -> 11.9 us  [swap(): return lax.ppermute(value, 'seq', [(0, 1), (1, 0)])]
    ppermute x2 -> x4, starting transfers between devices: 3.14 us -> 6.62 us  [swap(): return lax.ppermute(value, 'seq', [(0, 1), (1, 0)])]
    unnamed x26 -> x20, local copies, waits for them, and re-layouts: 4.43 us -> 1.13 us
  transfers between devices with their start and end apart: 14 -> 16, of which waited for: 9 -> 11; matrix products, arithmetic and copies ran while one was open for 0% -> 0% of each run, Pallas kernels for 17% -> 16%
where the time goes in v1:
time: 83.5 us; the launch traced here: 83.2 us
  waiting for transfers between devices  35.3 us (42%)
  Pallas kernels  24.4 us (29%)
  starting transfers between devices  20 us (24%)
  between operations  1.46 us (2%)
  local copies, waits for them, and re-layouts  1.13 us (1%)
  other arithmetic  0.98 us (1%)
    pallas_call x9, Pallas kernels, call(): pl.pallas_call(kernel, out_shape=outs, in_specs=[spec[kind] for kind in k...  24.4 us
    ppermute x12, waiting for transfers between devices, flip(): return lax.ppermute(value, 'clip', [(i, i ^ bits) for i in range(n_clip)])  23.4 us
    ppermute x12, starting transfers between devices, flip(): return lax.ppermute(value, 'clip', [(i, i ^ bits) for i in range(n_clip)])  13.4 us
    ppermute x4, waiting for transfers between devices, swap(): return lax.ppermute(value, 'seq', [(0, 1), (1, 0)])  11.9 us
    ppermute x4, starting transfers between devices, swap(): return lax.ppermute(value, 'seq', [(0, 1), (1, 0)])  6.62 us
  transfers between devices with their start and end apart: 16, of which 11 were waited for; matrix products, arithmetic and copies ran while one was open for 0% of the time, Pallas kernels for 16%

profile of v1, /device:TPU:0, one launch (start us, length us, event | category | flops | bytes accessed | tf_op | source)
XLA Modules:
  0.0 83.2 jit_solution(13023542726812910283)
XLA Ops:
  0.6 0.0 copy-start.4
  1.3 4.3 %shard_map.131 = (bf16[256,1280]{1,0:T(8,128)(2,1)}, bf16[128,1280]{1,0:T(8,128)(2,1)}, bf16[128,1280]{1,0:T(8,128)(2,1)}) custom-call(s32[1]{0:T(128)S(6)} %copy.14.live_ref, f32[1280]{0:T(1024)} %gain_ref.2, f32[1280]{0:T(1024)} %bias_ref.2, bf16[256,1280]{1,0:T(8,128)(2,1)} %patches_ref.1, s32[1,64]{1,0:T(1,128)} %places_ref.1, bf16[128,5120]{1,0:T(8,128)(2,1)} %grad_hbm.1), custom_call_target="tpu_custom_call" | custom-call | flops 335544320 | bytes 4000000 | tf_op jit(solution)/shard_map/pallas_call | solution.py:387
  5.6 0.0 copy-done.4
  5.6 0.0 copy-start.1
  5.7 1.1 %copy-done.1 = bf16[256,1280]{1,0:T(8,128)(2,1)S(1)} copy-done((bf16[256,1280]{1,0:T(8,128)(2,1)S(1)}, bf16[256,1280]{1,0:T(8,128)(2,1)}, u32[]{:S(2)}) %copy-start.1) | copy-done | bytes 655384
  6.7 0.0 copy-start.9
  6.7 0.0 copy-start
  6.7 5.5 %shard_map.132 = (bf16[3,256,640]{2,1,0:T(8,128)(2,1)S(1)}, bf16[8,128,256]{2,1,0:T(8,128)(2,1)S(1)}, bf16[128,1280]{1,0:T(8,128)(2,1)S(1)}) custom-call(s32[1]{0:T(128)S(6)} %copy.14.live_ref, f32[3,640]{1,0:T(4,128)S(1)} %copy-done.4, bf16[256,1280]{1,0:T(8,128)(2,1)S(1)} %copy-done.1, bf16[3,1280,640]{2,1,0:T(8,128)(2,1)} %bitcast.3, ...), custom_call_target="tpu_custom_call" | custom-call | flops 1468006400 | bytes 4000000 | tf_op jit(solution)/shard_map/pallas_call | solution.py:387
  12.3 0.0 copy-start.2
  12.3 0.0 copy-start.3
  12.3 0.0 copy-start.5
  12.3 0.0 copy-start.6
  12.3 0.0 copy-start.7
  12.3 3.0 %collective-permute-start = (bf16[128,1280]{1,0:T(8,128)(2,1)S(1)}, bf16[128,1280]{1,0:T(8,128)(2,1)S(1)}, u32[]{:S(2)}, u32[]{:S(2)}) collective-permute-start(bf16[128,1280]{1,0:T(8,128)(2,1)S(1)} %get-tuple-element.30), channel_id=1, source_target_pairs={{0,1},{1,0},{2,3},{3,2},{4,5},{5,4},{6,7},{7,6},{8,9},{9,8},{10,11... | collective-permute-start | bytes 983048 | tf_op jit(solution)/shard_map/ppermute | solution.py:422
  15.4 0.0 copy-done.9
  15.4 0.1 collective-permute-start.1
  15.5 2.0 %collective-permute-start.7 = (bf16[256,1280]{1,0:T(8,128)(2,1)S(1)}, bf16[256,1280]{1,0:T(8,128)(2,1)S(1)}, u32[]{:S(2)}, u32[]{:S(2)}) collective-permute-start(bf16[256,1280]{1,0:T(8,128)(2,1)S(1)} %copy-done.1), channel_id=1, source_target_pairs={{0,4},{2,6},{4,0},{6,2},{8,12},{10,14},{12,8},{14,10},{16,20},{18,... | collective-permute-start | bytes 1966088 | tf_op jit(solution)/shard_map/ppermute | solution.py:425
  17.4 1.6 %collective-permute-start.8 = (bf16[256,1280]{1,0:T(8,128)(2,1)S(1)}, bf16[256,1280]{1,0:T(8,128)(2,1)S(1)}, u32[]{:S(2)}, u32[]{:S(2)}) collective-permute-start(bf16[256,1280]{1,0:T(8,128)(2,1)S(1)} %copy-done.1), channel_id=1, source_target_pairs={{0,8},{2,10},{4,12},{6,14},{8,0},{10,2},{12,4},{14,6},{16,24},{18,... | collective-permute-start | bytes 1966088 | tf_op jit(solution)/shard_map/ppermute | solution.py:425
  19.0 0.0 collective-permute-start.9
  19.0 0.0 copy-done
  19.0 2.8 %shard_map.133 = (bf16[8,128,256]{2,1,0:T(8,128)(2,1)S(1)}, f32[128,1280]{1,0:T(8,128)S(1)}) custom-call(s32[1]{0:T(128)S(6)} %copy.14.live_ref, bf16[3,256,640]{2,1,0:T(8,128)(2,1)S(1)} %get-tuple-element.28.triple_ref, bf16[640,1280]{1,0:T(8,128)(2,1)S(1)} %copy-done), custom_call_target="tpu_custom_call" | custom-call | flops 314572800 | bytes 4000000 | tf_op jit(solution)/shard_map/pallas_call | solution.py:387
  21.8 2.1 %collective-permute-done.came_ref = bf16[128,1280]{1,0:T(8,128)(2,1)S(1)} collective-permute-done((bf16[128,1280]{1,0:T(8,128)(2,1)S(1)}, bf16[128,1280]{1,0:T(8,128)(2,1)S(1)}, u32[]{:S(2)}, u32[]{:S(2)}) %collective-permute-start) | collective-permute-done | bytes 327712 | tf_op jit(solution)/shard_map/ppermute | solution.py:422
  23.9 6.2 %collective-permute-done.1.up_came_ref = bf16[128,1280]{1,0:T(8,128)(2,1)S(1)} collective-permute-done((bf16[128,1280]{1,0:T(8,128)(2,1)S(1)}, bf16[128,1280]{1,0:T(8,128)(2,1)S(1)}, u32[]{:S(2)}, u32[]{:S(2)}) %collective-permute-start.1) | collective-permute-done | bytes 327712 | tf_op jit(solution)/shard_map/ppermute | solution.py:422
  30.1 0.0 copy-done.2
  30.1 0.0 copy-done.3
  30.1 0.0 copy-done.5
  30.1 0.0 copy-done.6
  30.1 0.0 copy-done.7
  30.1 0.6 shard_map.134
  30.7 1.8 %collective-permute-start.3 = (bf16[128,1280]{1,0:T(8,128)(2,1)S(1)}, bf16[128,1280]{1,0:T(8,128)(2,1)S(1)}, u32[]{:S(2)}, u32[]{:S(2)}) collective-permute-start(bf16[128,1280]{1,0:T(8,128)(2,1)S(1)} %get-tuple-element.34.row_ref), channel_id=1, source_target_pairs={{0,1},{1,0},{2,3},{3,2},{4,5},{5,4},{6,7},{7,6},{8,9},{9,8},{10,11... | collective-permute-start | bytes 983048 | tf_op jit(solution)/shard_map/ppermute | solution.py:422
  32.5 3.5 %shard_map.135 = (bf16[640,128]{1,0:T(8,128)(2,1)S(1)}, f32[640,256]{1,0:T(8,128)S(1)}, f32[640,256]{1,0:T(8,128)S(1)}) custom-call(bf16[128,1280]{1,0:T(8,128)(2,1)S(1)} %get-tuple-element.34.row_ref, bf16[640,1280]{1,0:T(8,128)(2,1)S(1)} %copy-done, bf16[3,256,640]{2,1,0:T(8,128)(2,1)S(1)} %get-tuple-element.28.triple_ref, ...), custom_call_target="tpu_custom_call" | custom-call | flops 419430400 | bytes 4000000 | tf_op jit(solution)/shard_map/pallas_call | solution.py:387
  36.1 3.6 %collective-permute-done.3.row_ref = bf16[128,1280]{1,0:T(8,128)(2,1)S(1)} collective-permute-done((bf16[128,1280]{1,0:T(8,128)(2,1)S(1)}, bf16[128,1280]{1,0:T(8,128)(2,1)S(1)}, u32[]{:S(2)}, u32[]{:S(2)}) %collective-permute-start.3) | collective-permute-done | bytes 327712 | tf_op jit(solution)/shard_map/ppermute | solution.py:422
  39.6 3.6 %shard_map.136 = (bf16[240,256]{1,0:T(8,128)(2,1)S(1)}, bf16[240,256]{1,0:T(8,128)(2,1)S(1)}, bf16[240,256]{1,0:T(8,128)(2,1)S(1)}, bf16[240,256]{1,0:T(8,128)(2...) custom-call(bf16[128,1280]{1,0:T(8,128)(2,1)S(1)} %collective-permut, ...), custom_call_target="tpu_custom_call" | custom-call | flops 419430400 | bytes 4000000 | tf_op jit(solution)/shard_map/pallas_call | solution.py:387
  43.3 1.6 %collective-permute-start.4 = (bf16[240,256]{1,0:T(8,128)(2,1)S(1)}, bf16[240,256]{1,0:T(8,128)(2,1)S(1)}, u32[]{:S(2)}, u32[]{:S(2)}) collective-permute-start(bf16[240,256]{1,0:T(8,128)(2,1)S(1)} %get-tuple-element.41), channel_id=1, source_target_pairs={{0,4},{2,6},{4,0},{6,2},{8,12},{10,14},{12,8},{14,10},{16,20},{18,... | collective-permute-start | bytes 368648 | tf_op jit(solution)/shard_map/ppermute | solution.py:425
  44.8 1.6 %collective-permute-start.5 = (bf16[240,256]{1,0:T(8,128)(2,1)S(1)}, bf16[240,256]{1,0:T(8,128)(2,1)S(1)}, u32[]{:S(2)}, u32[]{:S(2)}) collective-permute-start(bf16[240,256]{1,0:T(8,128)(2,1)S(1)} %get-tuple-element.42), channel_id=1, source_target_pairs={{0,8},{2,10},{4,12},{6,14},{8,0},{10,2},{12,4},{14,6},{16,24},{18,... | collective-permute-start | bytes 368648 | tf_op jit(solution)/shard_map/ppermute | solution.py:425
  46.4 0.0 collective-permute-done.7.refs_5_
  46.4 0.4 collective-permute-start.6
  46.8 0.0 collective-permute-done.8.refs_6_
  46.8 1.4 %collective-permute-done.9.refs_7_ = bf16[256,1280]{1,0:T(8,128)(2,1)S(1)} collective-permute-done((bf16[256,1280]{1,0:T(8,128)(2,1)S(1)}, bf16[256,1280]{1,0:T(8,128)(2,1)S(1)}, u32[]{:S(2)}, u32[]{:S(2)}) %collective-permute-start.9) | collective-permute-done | bytes 655392 | tf_op jit(solution)/shard_map/ppermute | solution.py:425
  48.3 2.6 %collective-permute-done.4.refs_1_ = bf16[240,256]{1,0:T(8,128)(2,1)S(1)} collective-permute-done((bf16[240,256]{1,0:T(8,128)(2,1)S(1)}, bf16[240,256]{1,0:T(8,128)(2,1)S(1)}, u32[]{:S(2)}, u32[]{:S(2)}) %collective-permute-start.4) | collective-permute-done | bytes 122912 | tf_op jit(solution)/shard_map/ppermute | solution.py:425
  50.8 0.2 collective-permute-done.5.refs_2_
  51.1 1.1 %collective-permute-done.6.refs_3_ = bf16[240,256]{1,0:T(8,128)(2,1)S(1)} collective-permute-done((bf16[240,256]{1,0:T(8,128)(2,1)S(1)}, bf16[240,256]{1,0:T(8,128)(2,1)S(1)}, u32[]{:S(2)}, u32[]{:S(2)}) %collective-permute-start.6) | collective-permute-done | bytes 122912 | tf_op jit(solution)/shard_map/ppermute | solution.py:425
  52.2 1.0 %shard_map.137 = (f32[120,1280]{1,0:T(8,128)S(1)}, bf16[120,1280]{1,0:T(8,128)(2,1)S(1)}) custom-call(bf16[240,256]{1,0:T(8,128)(2,1)S(1)} %get-tuple-element.40.refs_0_, bf16[240,256]{1,0:T(8,128)(2,1)S(1)} %collective-permute-done.4.refs_1_, bf16[240,256]{1,0:T(8,128)(2,1)S(1)} %collective-permute-done.5.refs_2_, ...), custom_call_target="tpu_custom_call" | custom-call | flops 629145600 | bytes 4000000 | tf_op jit(solution)/shard_map/pallas_call | solution.py:387
  53.1 0.1 collective-permute-start.10
  53.2 1.7 %collective-permute-start.2 = (bf16[128,1280]{1,0:T(8,128)(2,1)S(1)}, bf16[128,1280]{1,0:T(8,128)(2,1)S(1)}, u32[]{:S(2)}, u32[]{:S(2)}) collective-permute-start(bf16[128,1280]{1,0:T(8,128)(2,1)S(1)} %get-tuple-element.33.own_ref), channel_id=1, source_target_pairs={{0,1},{1,0},{2,3},{3,2},{4,5},{5,4},{6,7},{7,6},{8,9},{9,8},{10,11... | collective-permute-start | bytes 983048 | tf_op jit(solution)/shard_map/ppermute | solution.py:422
  54.9 1.5 %collective-permute-start.11 = (bf16[240,256]{1,0:T(8,128)(2,1)S(1)}, bf16[240,256]{1,0:T(8,128)(2,1)S(1)}, u32[]{:S(2)}, u32[]{:S(2)}) collective-permute-start(bf16[240,256]{1,0:T(8,128)(2,1)S(1)} %get-tuple-element.47), channel_id=1, source_target_pairs={{0,4},{2,6},{4,0},{6,2},{8,12},{10,14},{12,8},{14,10},{16,20},{18,... | collective-permute-start | bytes 368648 | tf_op jit(solution)/shard_map/ppermute | solution.py:425
  56.4 1.6 %collective-permute-start.12 = (bf16[240,256]{1,0:T(8,128)(2,1)S(1)}, bf16[240,256]{1,0:T(8,128)(2,1)S(1)}, u32[]{:S(2)}, u32[]{:S(2)}) collective-permute-start(bf16[240,256]{1,0:T(8,128)(2,1)S(1)} %get-tuple-element.48), channel_id=1, source_target_pairs={{0,8},{2,10},{4,12},{6,14},{8,0},{10,2},{12,4},{14,6},{16,24},{18,... | collective-permute-start | bytes 368648 | tf_op jit(solution)/shard_map/ppermute | solution.py:425
  58.0 0.4 collective-permute-start.13
  58.4 0.0 collective-permute-done.10
  58.4 0.1 add_convert_fusion._.refs_8_
  58.5 1.8 %collective-permute-done.11.refs_1_ = bf16[240,256]{1,0:T(8,128)(2,1)S(1)} collective-permute-done((bf16[240,256]{1,0:T(8,128)(2,1)S(1)}, bf16[240,256]{1,0:T(8,128)(2,1)S(1)}, u32[]{:S(2)}, u32[]{:S(2)}) %collective-permute-start.11) | collective-permute-done | bytes 122912 | tf_op jit(solution)/shard_map/ppermute | solution.py:425
  60.3 2.3 %collective-permute-done.12.refs_2_ = bf16[240,256]{1,0:T(8,128)(2,1)S(1)} collective-permute-done((bf16[240,256]{1,0:T(8,128)(2,1)S(1)}, bf16[240,256]{1,0:T(8,128)(2,1)S(1)}, u32[]{:S(2)}, u32[]{:S(2)}) %collective-permute-start.12) | collective-permute-done | bytes 122912 | tf_op jit(solution)/shard_map/ppermute | solution.py:425
  62.6 1.5 %collective-permute-done.13.refs_3_ = bf16[240,256]{1,0:T(8,128)(2,1)S(1)} collective-permute-done((bf16[240,256]{1,0:T(8,128)(2,1)S(1)}, bf16[240,256]{1,0:T(8,128)(2,1)S(1)}, u32[]{:S(2)}, u32[]{:S(2)}) %collective-permute-start.13) | collective-permute-done | bytes 122912 | tf_op jit(solution)/shard_map/ppermute | solution.py:425
  64.1 0.0 copy-start.8
  64.1 1.0 %shard_map.139 = (f32[120,1280]{1,0:T(8,128)S(1)}, bf16[120,1280]{1,0:T(8,128)(2,1)S(1)}) custom-call(bf16[240,256]{1,0:T(8,128)(2,1)S(1)} %get-tuple-element.46.refs_0_, bf16[240,256]{1,0:T(8,128)(2,1)S(1)} %collective-permute-done.11.refs_1_, bf16[240,256]{1,0:T(8,128)(2,1)S(1)} %collective-permute-done.12.refs_2_, ...), custom_call_target="tpu_custom_call" | custom-call | flops 629145600 | bytes 4000000 | tf_op jit(solution)/shard_map/pallas_call | solution.py:387
  65.1 0.1 collective-permute-start.14
  65.1 2.6 %collective-permute-start.15 = (bf16[120,1280]{1,0:T(8,128)(2,1)S(1)}, bf16[120,1280]{1,0:T(8,128)(2,1)S(1)}, u32[]{:S(2)}, u32[]{:S(2)}) collective-permute-start(bf16[120,1280]{1,0:T(8,128)(2,1)S(1)} %add_convert_fusion._.refs_8_), channel_id=1, source_target_pairs={{0,16},{2,18},{4,20},{6,22},{8,24},{10,26},{12,28},{14,30},{16,0},... | collective-permute-start | bytes 921608 | tf_op jit(solution)/shard_map/ppermute | solution.py:425
  67.8 0.0 collective-permute-done.2.other_ref
  67.8 0.0 copy-done.8
  67.8 2.1 %shard_map.138 = bf16[128,5120]{1,0:T(8,128)(2,1)} custom-call(s32[1]{0:T(128)S(6)} %copy.14.live_ref, s32[1,64]{1,0:T(1,128)S(1)} %copy-done.8, bf16[128,1280]{1,0:T(8,128)(2,1)S(1)} %get-tuple-element.33.own_ref, bf16[128,1280]{1,0:T(8,128)(2,1)S(1)} %collective-permute-done.2.other_ref, bf16[120,1280]{1,0:T(8,128)(2,1)S(1)} %add_convert_fusion._.refs_8_), custom_call_target="tpu_custom_call" | custom-call | flops 335544320 | bytes 4000000 | tf_op jit(solution)/shard_map/pallas_call | solution.py:387
  69.9 0.0 collective-permute-done.14
  69.9 12.4 %collective-permute-done.15 = bf16[120,1280]{1,0:T(8,128)(2,1)S(1)} collective-permute-done((bf16[120,1280]{1,0:T(8,128)(2,1)S(1)}, bf16[120,1280]{1,0:T(8,128)(2,1)S(1)}, u32[]{:S(2)}, u32[]{:S(2)}) %collective-permute-start.15) | collective-permute-done | bytes 307232 | tf_op jit(solution)/shard_map/ppermute | solution.py:425
  82.3 0.9 %add_bitcast_fusion = f32[1,120,1280]{2,1,0:T(8,128)} fusion(bf16[120,1280]{1,0:T(8,128)(2,1)S(1)} %collective-permute-done.15, f32[120,1280]{1,0:T(8,128)S(1)} %get-tuple-element.50, bf16[120,1280]{1,0:T(8,128)(2,1)S(1)} %collective-permute-done.14), kind=kLoop, calls=%fused_computation | loop fusion | flops 614400 | bytes 1843200 | tf_op jit(solution)/shard_map/broadcast_in_dim | solution.py:541
Async XLA Ops:
  0.6 5.0 %copy-start.4 = (f32[3,640]{1,0:T(4,128)S(1)}, f32[3,640]{1,0:T(4,128)}, u32[]{:S(2)}) copy-start(f32[3,640]{1,0:T(4,128)} %b_ref.2) | copy-start | bytes 23044
  5.6 1.1 %copy-start.1 = (bf16[256,1280]{1,0:T(8,128)(2,1)S(1)}, bf16[256,1280]{1,0:T(8,128)(2,1)}, u32[]{:S(2)}) copy-start(bf16[256,1280]{1,0:T(8,128)(2,1)} %get-tuple-element.27.normed_hbm.refs_4_) | copy-start | bytes 1966084
  6.7 8.6 %copy-start.9 = (bf16[128,1280]{1,0:T(8,128)(2,1)S(1)}, bf16[128,1280]{1,0:T(8,128)(2,1)}, u32[]{:S(2)}) copy-start(bf16[128,1280]{1,0:T(8,128)(2,1)} %get-tuple-element.32) | copy-start | bytes 983044
  6.7 12.3 %copy-start = (bf16[640,1280]{1,0:T(8,128)(2,1)S(1)}, bf16[640,1280]{1,0:T(8,128)(2,1)}, u32[]{:S(2)}) copy-start(bf16[640,1280]{1,0:T(8,128)(2,1)} %proj_ref.5) | copy-start | bytes 4915204
  12.3 17.8 %copy-start.2 = (bf16[256,1280]{1,0:T(8,128)(2,1)S(1)}, bf16[256,1280]{1,0:T(8,128)(2,1)}, u32[]{:S(2)}) copy-start(bf16[256,1280]{1,0:T(8,128)(2,1)} %patches_ref.1) | copy-start | bytes 1966084
  12.3 17.8 %copy-start.3 = (bf16[128,1280]{1,0:T(8,128)(2,1)S(1)}, bf16[128,1280]{1,0:T(8,128)(2,1)}, u32[]{:S(2)}) copy-start(bf16[128,1280]{1,0:T(8,128)(2,1)} %get-tuple-element.31.up_keep_ref) | copy-start | bytes 983044
  12.3 17.8 %copy-start.5 = (f32[1280]{0:T(1024)S(1)}, f32[1280]{0:T(1024)}, u32[]{:S(2)}) copy-start(f32[1280]{0:T(1024)} %b_ref.3) | copy-start | bytes 15364
  12.3 17.8 %copy-start.6 = (f32[1280]{0:T(1024)S(1)}, f32[1280]{0:T(1024)}, u32[]{:S(2)}) copy-start(f32[1280]{0:T(1024)} %gain_ref.3) | copy-start | bytes 15364
  12.3 17.8 %copy-start.7 = (f32[1280]{0:T(1024)S(1)}, f32[1280]{0:T(1024)}, u32[]{:S(2)}) copy-start(f32[1280]{0:T(1024)} %bias_ref.3) | copy-start | bytes 15364
  12.3 11.6 %collective-permute-start = (bf16[128,1280]{1,0:T(8,128)(2,1)S(1)}, bf16[128,1280]{1,0:T(8,128)(2,1)S(1)}, u32[]{:S(2)}, u32[]{:S(2)}) collective-permute-start(bf16[128,1280]{1,0:T(8,128)(2,1)S(1)} %get-tuple-element.30), channel_id=1, source_target_pairs={{0,1},{1,0},{2,3},{3,2},{4,5},{5,4},{6,7},{7,6},{8,9},{9,8},{10,11... | collective-permute-start | bytes 983048 | tf_op jit(solution)/shard_map/ppermute | solution.py:422
  15.4 14.7 %collective-permute-start.1 = (bf16[128,1280]{1,0:T(8,128)(2,1)S(1)}, bf16[128,1280]{1,0:T(8,128)(2,1)S(1)}, u32[]{:S(2)}, u32[]{:S(2)}) collective-permute-start(bf16[128,1280]{1,0:T(8,128)(2,1)S(1)} %copy-done.9), channel_id=1, source_target_pairs={{0,1},{1,0},{2,3},{3,2},{4,5},{5,4},{6,7},{7,6},{8,9},{9,8},{10,11... | collective-permute-start | bytes 983048 | tf_op jit(solution)/shard_map/ppermute | solution.py:422
  15.5 30.9 %collective-permute-start.7 = (bf16[256,1280]{1,0:T(8,128)(2,1)S(1)}, bf16[256,1280]{1,0:T(8,128)(2,1)S(1)}, u32[]{:S(2)}, u32[]{:S(2)}) collective-permute-start(bf16[256,1280]{1,0:T(8,128)(2,1)S(1)} %copy-done.1), channel_id=1, source_target_pairs={{0,4},{2,6},{4,0},{6,2},{8,12},{10,14},{12,8},{14,10},{16,20},{18,... | collective-permute-start | bytes 1966088 | tf_op jit(solution)/shard_map/ppermute | solution.py:425
  17.4 29.4 %collective-permute-start.8 = (bf16[256,1280]{1,0:T(8,128)(2,1)S(1)}, bf16[256,1280]{1,0:T(8,128)(2,1)S(1)}, u32[]{:S(2)}, u32[]{:S(2)}) collective-permute-start(bf16[256,1280]{1,0:T(8,128)(2,1)S(1)} %copy-done.1), channel_id=1, source_target_pairs={{0,8},{2,10},{4,12},{6,14},{8,0},{10,2},{12,4},{14,6},{16,24},{18,... | collective-permute-start | bytes 1966088 | tf_op jit(solution)/shard_map/ppermute | solution.py:425
  19.0 29.2 %collective-permute-start.9 = (bf16[256,1280]{1,0:T(8,128)(2,1)S(1)}, bf16[256,1280]{1,0:T(8,128)(2,1)S(1)}, u32[]{:S(2)}, u32[]{:S(2)}) collective-permute-start(bf16[256,1280]{1,0:T(8,128)(2,1)S(1)} %copy-done.1), channel_id=1, source_target_pairs={{0,12},{2,14},{4,8},{6,10},{8,4},{10,6},{12,0},{14,2},{16,28},{18,... | collective-permute-start | bytes 1966088 | tf_op jit(solution)/shard_map/ppermute | solution.py:425
  30.7 8.9 %collective-permute-start.3 = (bf16[128,1280]{1,0:T(8,128)(2,1)S(1)}, bf16[128,1280]{1,0:T(8,128)(2,1)S(1)}, u32[]{:S(2)}, u32[]{:S(2)}) collective-permute-start(bf16[128,1280]{1,0:T(8,128)(2,1)S(1)} %get-tuple-element.34.row_ref), channel_id=1, source_target_pairs={{0,1},{1,0},{2,3},{3,2},{4,5},{5,4},{6,7},{7,6},{8,9},{9,8},{10,11... | collective-permute-start | bytes 983048 | tf_op jit(solution)/shard_map/ppermute | solution.py:422
  43.3 7.6 %collective-permute-start.4 = (bf16[240,256]{1,0:T(8,128)(2,1)S(1)}, bf16[240,256]{1,0:T(8,128)(2,1)S(1)}, u32[]{:S(2)}, u32[]{:S(2)}) collective-permute-start(bf16[240,256]{1,0:T(8,128)(2,1)S(1)} %get-tuple-element.41), channel_id=1, source_target_pairs={{0,4},{2,6},{4,0},{6,2},{8,12},{10,14},{12,8},{14,10},{16,20},{18,... | collective-permute-start | bytes 368648 | tf_op jit(solution)/shard_map/ppermute | solution.py:425
  44.8 6.2 %collective-permute-start.5 = (bf16[240,256]{1,0:T(8,128)(2,1)S(1)}, bf16[240,256]{1,0:T(8,128)(2,1)S(1)}, u32[]{:S(2)}, u32[]{:S(2)}) collective-permute-start(bf16[240,256]{1,0:T(8,128)(2,1)S(1)} %get-tuple-element.42), channel_id=1, source_target_pairs={{0,8},{2,10},{4,12},{6,14},{8,0},{10,2},{12,4},{14,6},{16,24},{18,... | collective-permute-start | bytes 368648 | tf_op jit(solution)/shard_map/ppermute | solution.py:425
  46.4 5.8 %collective-permute-start.6 = (bf16[240,256]{1,0:T(8,128)(2,1)S(1)}, bf16[240,256]{1,0:T(8,128)(2,1)S(1)}, u32[]{:S(2)}, u32[]{:S(2)}) collective-permute-start(bf16[240,256]{1,0:T(8,128)(2,1)S(1)} %get-tuple-element.43), channel_id=1, source_target_pairs={{0,12},{2,14},{4,8},{6,10},{8,4},{10,6},{12,0},{14,2},{16,28},{18,... | collective-permute-start | bytes 368648 | tf_op jit(solution)/shard_map/ppermute | solution.py:425
  53.1 5.3 %collective-permute-start.10 = (bf16[120,1280]{1,0:T(8,128)(2,1)S(1)}, bf16[120,1280]{1,0:T(8,128)(2,1)S(1)}, u32[]{:S(2)}, u32[]{:S(2)}) collective-permute-start(bf16[120,1280]{1,0:T(8,128)(2,1)S(1)} %get-tuple-element.45), channel_id=1, source_target_pairs={{0,2},{2,0},{4,6},{6,4},{8,10},{10,8},{12,14},{14,12},{16,18},{18,... | collective-permute-start | bytes 921608 | tf_op jit(solution)/shard_map/ppermute | solution.py:425
  53.2 14.6 %collective-permute-start.2 = (bf16[128,1280]{1,0:T(8,128)(2,1)S(1)}, bf16[128,1280]{1,0:T(8,128)(2,1)S(1)}, u32[]{:S(2)}, u32[]{:S(2)}) collective-permute-start(bf16[128,1280]{1,0:T(8,128)(2,1)S(1)} %get-tuple-element.33.own_ref), channel_id=1, source_target_pairs={{0,1},{1,0},{2,3},{3,2},{4,5},{5,4},{6,7},{7,6},{8,9},{9,8},{10,11... | collective-permute-start | bytes 983048 | tf_op jit(solution)/shard_map/ppermute | solution.py:422
  54.9 5.4 %collective-permute-start.11 = (bf16[240,256]{1,0:T(8,128)(2,1)S(1)}, bf16[240,256]{1,0:T(8,128)(2,1)S(1)}, u32[]{:S(2)}, u32[]{:S(2)}) collective-permute-start(bf16[240,256]{1,0:T(8,128)(2,1)S(1)} %get-tuple-element.47), channel_id=1, source_target_pairs={{0,4},{2,6},{4,0},{6,2},{8,12},{10,14},{12,8},{14,10},{16,20},{18,... | collective-permute-start | bytes 368648 | tf_op jit(solution)/shard_map/ppermute | solution.py:425
  56.4 6.2 %collective-permute-start.12 = (bf16[240,256]{1,0:T(8,128)(2,1)S(1)}, bf16[240,256]{1,0:T(8,128)(2,1)S(1)}, u32[]{:S(2)}, u32[]{:S(2)}) collective-permute-start(bf16[240,256]{1,0:T(8,128)(2,1)S(1)} %get-tuple-element.48), channel_id=1, source_target_pairs={{0,8},{2,10},{4,12},{6,14},{8,0},{10,2},{12,4},{14,6},{16,24},{18,... | collective-permute-start | bytes 368648 | tf_op jit(solution)/shard_map/ppermute | solution.py:425
  58.0 6.1 %collective-permute-start.13 = (bf16[240,256]{1,0:T(8,128)(2,1)S(1)}, bf16[240,256]{1,0:T(8,128)(2,1)S(1)}, u32[]{:S(2)}, u32[]{:S(2)}) collective-permute-start(bf16[240,256]{1,0:T(8,128)(2,1)S(1)} %get-tuple-element.49), channel_id=1, source_target_pairs={{0,12},{2,14},{4,8},{6,10},{8,4},{10,6},{12,0},{14,2},{16,28},{18,... | collective-permute-start | bytes 368648 | tf_op jit(solution)/shard_map/ppermute | solution.py:425
  64.1 3.7 %copy-start.8 = (s32[1,64]{1,0:T(1,128)S(1)}, s32[1,64]{1,0:T(1,128)}, u32[]{:S(2)}) copy-start(s32[1,64]{1,0:T(1,128)} %places_ref.1) | copy-start | bytes 772
  65.1 4.8 %collective-permute-start.14 = (bf16[120,1280]{1,0:T(8,128)(2,1)S(1)}, bf16[120,1280]{1,0:T(8,128)(2,1)S(1)}, u32[]{:S(2)}, u32[]{:S(2)}) collective-permute-start(bf16[120,1280]{1,0:T(8,128)(2,1)S(1)} %get-tuple-element.51), channel_id=1, source_target_pairs={{0,2},{2,0},{4,6},{6,4},{8,10},{10,8},{12,14},{14,12},{16,18},{18,... | collective-permute-start | bytes 921608 | tf_op jit(solution)/shard_map/ppermute | solution.py:425
  65.1 17.2 %collective-permute-start.15 = (bf16[120,1280]{1,0:T(8,128)(2,1)S(1)}, bf16[120,1280]{1,0:T(8,128)(2,1)S(1)}, u32[]{:S(2)}, u32[]{:S(2)}) collective-permute-start(bf16[120,1280]{1,0:T(8,128)(2,1)S(1)} %add_convert_fusion._.refs_8_), channel_id=1, source_target_pairs={{0,16},{2,18},{4,20},{6,22},{8,24},{10,26},{12,28},{14,30},{16,0},... | collective-permute-start | bytes 921608 | tf_op jit(solution)/shard_map/ppermute | solution.py:425

commit v2 on v1

--- a/solution.py
+++ b/solution.py
@@ -168,37 +168,52 @@
 
 def prepare_kernel(
     live_ref,
-    gain_ref,
-    bias_ref,
+    gain_hbm,
+    bias_hbm,
     patches_hbm,
     places_hbm,
     grad_hbm,
+    normed_hbm,
+    keep_hbm,
+    send_hbm,
+    gain_ref,
+    bias_ref,
+    patches_ref,
+    places_ref,
+    grad_ref,
     normed_ref,
     keep_ref,
     send_ref,
-    patches_ref,
-    places_ref,
-    grad_ref,
     sems,
 ):
-    width = send_ref.shape[1]
-    half = send_ref.shape[0]
-    came = begin((patches_hbm, places_hbm, grad_hbm), (patches_ref, places_ref, grad_ref), sems)
+    half, width = send_ref.shape
+    came = begin(
+        (places_hbm, grad_hbm, gain_hbm, bias_hbm, patches_hbm),
+        (places_ref, grad_ref, gain_ref, bias_ref, patches_ref),
+        sems,
+    )
     came[0].wait()
+    masks = [
+        place_masks(live_ref, places_ref[...], grad_ref.shape[0], half, half_start(half, own))
+        for own in (False, True)
+    ]
+    came[1].wait()
+    went = []
+    for out_ref, out_hbm, masks_of in ((send_ref, send_hbm, masks[0]), (keep_ref, keep_hbm, masks[1])):
+        total = None
+        for k in range(4):
+            term = leading(masks_of[k], grad_ref[:, k * width : (k + 1) * width])
+            total = term if total is None else total + term
+        out_ref[...] = total.astype(out_ref.dtype)
+        went += begin((out_ref,), (out_hbm,), sems, 5 + len(went))
+    for copy in came[2:]:
+        copy.wait()
     normed_ref[...] = normalize(
         patches_ref[...].astype(jnp.float32), gain_ref[...][None, :], bias_ref[...][None, :]
     )[0].astype(jnp.bfloat16)
-    came[1].wait()
-    came[2].wait()
-    for out_ref, own in ((send_ref, False), (keep_ref, True)):
-        masks = place_masks(
-            live_ref, places_ref[...], grad_ref.shape[0], half, half_start(half, own)
-        )
-        total = None
-        for k in range(4):
-            term = leading(masks[k], grad_ref[:, k * width : (k + 1) * width])
-            total = term if total is None else total + term
-        out_ref[...] = total.astype(out_ref.dtype)
+    went += begin((normed_ref,), (normed_hbm,), sems, 7)
+    for copy in went:
+        copy.wait()
 
 
 def place_kernel(live_ref, places_ref, own_ref, other_ref, _, out_ref):
@@ -378,7 +393,7 @@
     send_ref[...] = other.astype(jnp.bfloat16)
 
 
-def call(kernel, outs, kinds, flops, args, scratch=(), limit=30):
+def call(kernel, outs, kinds, flops, args, scratch=(), limit=30, out_kind="v"):
     spec = {
         "s": pl.BlockSpec(memory_space=pltpu.SMEM),
         "v": pl.BlockSpec(memory_space=pltpu.VMEM),
@@ -388,7 +403,7 @@
         kernel,
         out_shape=outs,
         in_specs=[spec[kind] for kind in kinds],
-        out_specs=jax.tree.map(lambda _: spec["v"], outs),
+        out_specs=jax.tree.map(lambda _: spec[out_kind], outs),
         scratch_shapes=list(scratch),
         cost_estimate=pl.CostEstimate(flops=flops, bytes_accessed=4_000_000, transcendentals=0),
         compiler_params=pltpu.CompilerParams(vmem_limit_bytes=limit * 1024 * 1024),
@@ -432,16 +447,22 @@
     normed, up_keep, up_send = call(
         prepare_kernel,
         (full, part, part),
-        "svvaaa",
+        "saaaaa",
         8 * rows * share_rows * width,
         (clip_tokens, norm_gain, norm_bias, patches, positions, grad_placed),
         (
+            pltpu.VMEM(norm_gain.shape, jnp.float32),
+            pltpu.VMEM(norm_bias.shape, jnp.float32),
             pltpu.VMEM((rows, width), low),
             pltpu.VMEM(positions.shape, jnp.int32),
             pltpu.VMEM(grad_placed.shape, low),
-            pltpu.SemaphoreType.DMA((3,)),
+            pltpu.VMEM((rows, width), low),
+            pltpu.VMEM((half, width), low),
+            pltpu.VMEM((half, width), low),
+            pltpu.SemaphoreType.DMA((8,)),
         ),
         limit=62,
+        out_kind="a",
     )
     up_came = swap(up_send)
     normed_of = [normed] + [flip(normed, q << 1) for q in (1, 2)]

time: 83.5 us -> 82.7 us (level)
  no operation moved by 1% of the time
where the time goes in v2:
time: 82.7 us; the launch traced here: 82.4 us
  waiting for transfers between devices  35.3 us (43%)
  Pallas kernels  23.6 us (29%)
  starting transfers between devices  20 us (24%)
  between operations  1.46 us (2%)
  local copies, waits for them, and re-layouts  1.13 us (1%)
  other arithmetic  0.98 us (1%)
    pallas_call x9, Pallas kernels, call(): pl.pallas_call(kernel, out_shape=outs, in_specs=[spec[kind] for kind in k...  23.6 us
    ppermute x12, waiting for transfers between devices, flip(): return lax.ppermute(value, 'clip', [(i, i ^ bits) for i in range(n_clip)])  23.4 us
    ppermute x12, starting transfers between devices, flip(): return lax.ppermute(value, 'clip', [(i, i ^ bits) for i in range(n_clip)])  13.4 us
    ppermute x4, waiting for transfers between devices, swap(): return lax.ppermute(value, 'seq', [(0, 1), (1, 0)])  11.9 us
    ppermute x4, starting transfers between devices, swap(): return lax.ppermute(value, 'seq', [(0, 1), (1, 0)])  6.61 us
  transfers between devices with their start and end apart: 16, of which 11 were waited for; matrix products, arithmetic and copies ran while one was open for 0% of the time, Pallas kernels for 16%

profile of v2, /device:TPU:0, one launch (start us, length us, event | category | flops | bytes accessed | tf_op | source)
XLA Modules:
  0.0 82.4 jit_solution(5578366137838986145)
XLA Ops:
  0.6 0.0 copy-start.4
  1.3 3.5 %shard_map.131 = (bf16[256,1280]{1,0:T(8,128)(2,1)}, bf16[128,1280]{1,0:T(8,128)(2,1)}, bf16[128,1280]{1,0:T(8,128)(2,1)}) custom-call(s32[1]{0:T(128)S(6)} %copy.14.live_ref, f32[1280]{0:T(1024)} %gain_hbm.1, f32[1280]{0:T(1024)} %bias_hbm.1, bf16[256,1280]{1,0:T(8,128)(2,1)} %patches_ref.1, s32[1,64]{1,0:T(1,128)} %places_ref.1, bf16[128,5120]{1,0:T(8,128)(2,1)} %grad_hbm.1), custom_call_target="tpu_custom_call" | custom-call | flops 335544320 | bytes 4000000 | tf_op jit(solution)/shard_map/pallas_call | solution.py:402
  4.8 0.0 copy-done.4
  4.9 0.0 copy-start.1
  4.9 1.1 %copy-done.1 = bf16[256,1280]{1,0:T(8,128)(2,1)S(1)} copy-done((bf16[256,1280]{1,0:T(8,128)(2,1)S(1)}, bf16[256,1280]{1,0:T(8,128)(2,1)}, u32[]{:S(2)}) %copy-start.1) | copy-done | bytes 655384
  5.9 0.0 copy-start.9
  6.0 0.0 copy-start
  6.0 5.5 %shard_map.132 = (bf16[3,256,640]{2,1,0:T(8,128)(2,1)S(1)}, bf16[8,128,256]{2,1,0:T(8,128)(2,1)S(1)}, bf16[128,1280]{1,0:T(8,128)(2,1)S(1)}) custom-call(s32[1]{0:T(128)S(6)} %copy.14.live_ref, f32[3,640]{1,0:T(4,128)S(1)} %copy-done.4, bf16[256,1280]{1,0:T(8,128)(2,1)S(1)} %copy-done.1, bf16[3,1280,640]{2,1,0:T(8,128)(2,1)} %bitcast.3, ...), custom_call_target="tpu_custom_call" | custom-call | flops 1468006400 | bytes 4000000 | tf_op jit(solution)/shard_map/pallas_call | solution.py:402
  11.5 0.0 copy-start.2
  11.5 0.0 copy-start.3
  11.5 0.0 copy-start.5
  11.5 0.0 copy-start.6
  11.5 0.0 copy-start.7
  11.6 3.0 %collective-permute-start = (bf16[128,1280]{1,0:T(8,128)(2,1)S(1)}, bf16[128,1280]{1,0:T(8,128)(2,1)S(1)}, u32[]{:S(2)}, u32[]{:S(2)}) collective-permute-start(bf16[128,1280]{1,0:T(8,128)(2,1)S(1)} %get-tuple-element.30), channel_id=1, source_target_pairs={{0,1},{1,0},{2,3},{3,2},{4,5},{5,4},{6,7},{7,6},{8,9},{9,8},{10,11... | collective-permute-start | bytes 983048 | tf_op jit(solution)/shard_map/ppermute | solution.py:437
  14.6 0.0 copy-done.9
  14.6 0.1 collective-permute-start.1
  14.7 2.0 %collective-permute-start.7 = (bf16[256,1280]{1,0:T(8,128)(2,1)S(1)}, bf16[256,1280]{1,0:T(8,128)(2,1)S(1)}, u32[]{:S(2)}, u32[]{:S(2)}) collective-permute-start(bf16[256,1280]{1,0:T(8,128)(2,1)S(1)} %copy-done.1), channel_id=1, source_target_pairs={{0,4},{2,6},{4,0},{6,2},{8,12},{10,14},{12,8},{14,10},{16,20},{18,... | collective-permute-start | bytes 1966088 | tf_op jit(solution)/shard_map/ppermute | solution.py:440
  16.6 1.6 %collective-permute-start.8 = (bf16[256,1280]{1,0:T(8,128)(2,1)S(1)}, bf16[256,1280]{1,0:T(8,128)(2,1)S(1)}, u32[]{:S(2)}, u32[]{:S(2)}) collective-permute-start(bf16[256,1280]{1,0:T(8,128)(2,1)S(1)} %copy-done.1), channel_id=1, source_target_pairs={{0,8},{2,10},{4,12},{6,14},{8,0},{10,2},{12,4},{14,6},{16,24},{18,... | collective-permute-start | bytes 1966088 | tf_op jit(solution)/shard_map/ppermute | solution.py:440
  18.2 0.0 collective-permute-start.9
  18.2 0.0 copy-done
  18.2 2.8 %shard_map.133 = (bf16[8,128,256]{2,1,0:T(8,128)(2,1)S(1)}, f32[128,1280]{1,0:T(8,128)S(1)}) custom-call(s32[1]{0:T(128)S(6)} %copy.14.live_ref, bf16[3,256,640]{2,1,0:T(8,128)(2,1)S(1)} %get-tuple-element.28.triple_ref, bf16[640,1280]{1,0:T(8,128)(2,1)S(1)} %copy-done), custom_call_target="tpu_custom_call" | custom-call | flops 314572800 | bytes 4000000 | tf_op jit(solution)/shard_map/pallas_call | solution.py:402
  21.0 2.1 %collective-permute-done.came_ref = bf16[128,1280]{1,0:T(8,128)(2,1)S(1)} collective-permute-done((bf16[128,1280]{1,0:T(8,128)(2,1)S(1)}, bf16[128,1280]{1,0:T(8,128)(2,1)S(1)}, u32[]{:S(2)}, u32[]{:S(2)}) %collective-permute-start) | collective-permute-done | bytes 327712 | tf_op jit(solution)/shard_map/ppermute | solution.py:437
  23.2 6.2 %collective-permute-done.1.up_came_ref = bf16[128,1280]{1,0:T(8,128)(2,1)S(1)} collective-permute-done((bf16[128,1280]{1,0:T(8,128)(2,1)S(1)}, bf16[128,1280]{1,0:T(8,128)(2,1)S(1)}, u32[]{:S(2)}, u32[]{:S(2)}) %collective-permute-start.1) | collective-permute-done | bytes 327712 | tf_op jit(solution)/shard_map/ppermute | solution.py:437
  29.3 0.0 copy-done.2
  29.3 0.0 copy-done.3
  29.3 0.0 copy-done.5
  29.3 0.0 copy-done.6
  29.3 0.0 copy-done.7
  29.4 0.6 shard_map.134
  29.9 1.8 %collective-permute-start.3 = (bf16[128,1280]{1,0:T(8,128)(2,1)S(1)}, bf16[128,1280]{1,0:T(8,128)(2,1)S(1)}, u32[]{:S(2)}, u32[]{:S(2)}) collective-permute-start(bf16[128,1280]{1,0:T(8,128)(2,1)S(1)} %get-tuple-element.34.row_ref), channel_id=1, source_target_pairs={{0,1},{1,0},{2,3},{3,2},{4,5},{5,4},{6,7},{7,6},{8,9},{9,8},{10,11... | collective-permute-start | bytes 983048 | tf_op jit(solution)/shard_map/ppermute | solution.py:437
  31.7 3.5 %shard_map.135 = (bf16[640,128]{1,0:T(8,128)(2,1)S(1)}, f32[640,256]{1,0:T(8,128)S(1)}, f32[640,256]{1,0:T(8,128)S(1)}) custom-call(bf16[128,1280]{1,0:T(8,128)(2,1)S(1)} %get-tuple-element.34.row_ref, bf16[640,1280]{1,0:T(8,128)(2,1)S(1)} %copy-done, bf16[3,256,640]{2,1,0:T(8,128)(2,1)S(1)} %get-tuple-element.28.triple_ref, ...), custom_call_target="tpu_custom_call" | custom-call | flops 419430400 | bytes 4000000 | tf_op jit(solution)/shard_map/pallas_call | solution.py:402
  35.3 3.6 %collective-permute-done.3.row_ref = bf16[128,1280]{1,0:T(8,128)(2,1)S(1)} collective-permute-done((bf16[128,1280]{1,0:T(8,128)(2,1)S(1)}, bf16[128,1280]{1,0:T(8,128)(2,1)S(1)}, u32[]{:S(2)}, u32[]{:S(2)}) %collective-permute-start.3) | collective-permute-done | bytes 327712 | tf_op jit(solution)/shard_map/ppermute | solution.py:437
  38.9 3.6 %shard_map.136 = (bf16[240,256]{1,0:T(8,128)(2,1)S(1)}, bf16[240,256]{1,0:T(8,128)(2,1)S(1)}, bf16[240,256]{1,0:T(8,128)(2,1)S(1)}, bf16[240,256]{1,0:T(8,128)(2...) custom-call(bf16[128,1280]{1,0:T(8,128)(2,1)S(1)} %collective-permut, ...), custom_call_target="tpu_custom_call" | custom-call | flops 419430400 | bytes 4000000 | tf_op jit(solution)/shard_map/pallas_call | solution.py:402
  42.5 1.6 %collective-permute-start.4 = (bf16[240,256]{1,0:T(8,128)(2,1)S(1)}, bf16[240,256]{1,0:T(8,128)(2,1)S(1)}, u32[]{:S(2)}, u32[]{:S(2)}) collective-permute-start(bf16[240,256]{1,0:T(8,128)(2,1)S(1)} %get-tuple-element.41), channel_id=1, source_target_pairs={{0,4},{2,6},{4,0},{6,2},{8,12},{10,14},{12,8},{14,10},{16,20},{18,... | collective-permute-start | bytes 368648 | tf_op jit(solution)/shard_map/ppermute | solution.py:440
  44.1 1.6 %collective-permute-start.5 = (bf16[240,256]{1,0:T(8,128)(2,1)S(1)}, bf16[240,256]{1,0:T(8,128)(2,1)S(1)}, u32[]{:S(2)}, u32[]{:S(2)}) collective-permute-start(bf16[240,256]{1,0:T(8,128)(2,1)S(1)} %get-tuple-element.42), channel_id=1, source_target_pairs={{0,8},{2,10},{4,12},{6,14},{8,0},{10,2},{12,4},{14,6},{16,24},{18,... | collective-permute-start | bytes 368648 | tf_op jit(solution)/shard_map/ppermute | solution.py:440
  45.6 0.0 collective-permute-done.7.refs_5_
  45.6 0.4 collective-permute-start.6
  46.1 0.0 collective-permute-done.8.refs_6_
  46.1 1.4 %collective-permute-done.9.refs_7_ = bf16[256,1280]{1,0:T(8,128)(2,1)S(1)} collective-permute-done((bf16[256,1280]{1,0:T(8,128)(2,1)S(1)}, bf16[256,1280]{1,0:T(8,128)(2,1)S(1)}, u32[]{:S(2)}, u32[]{:S(2)}) %collective-permute-start.9) | collective-permute-done | bytes 655392 | tf_op jit(solution)/shard_map/ppermute | solution.py:440
  47.5 2.6 %collective-permute-done.4.refs_1_ = bf16[240,256]{1,0:T(8,128)(2,1)S(1)} collective-permute-done((bf16[240,256]{1,0:T(8,128)(2,1)S(1)}, bf16[240,256]{1,0:T(8,128)(2,1)S(1)}, u32[]{:S(2)}, u32[]{:S(2)}) %collective-permute-start.4) | collective-permute-done | bytes 122912 | tf_op jit(solution)/shard_map/ppermute | solution.py:440
  50.1 0.2 collective-permute-done.5.refs_2_
  50.3 1.1 %collective-permute-done.6.refs_3_ = bf16[240,256]{1,0:T(8,128)(2,1)S(1)} collective-permute-done((bf16[240,256]{1,0:T(8,128)(2,1)S(1)}, bf16[240,256]{1,0:T(8,128)(2,1)S(1)}, u32[]{:S(2)}, u32[]{:S(2)}) %collective-permute-start.6) | collective-permute-done | bytes 122912 | tf_op jit(solution)/shard_map/ppermute | solution.py:440
  51.4 1.0 %shard_map.137 = (f32[120,1280]{1,0:T(8,128)S(1)}, bf16[120,1280]{1,0:T(8,128)(2,1)S(1)}) custom-call(bf16[240,256]{1,0:T(8,128)(2,1)S(1)} %get-tuple-element.40.refs_0_, bf16[240,256]{1,0:T(8,128)(2,1)S(1)} %collective-permute-done.4.refs_1_, bf16[240,256]{1,0:T(8,128)(2,1)S(1)} %collective-permute-done.5.refs_2_, ...), custom_call_target="tpu_custom_call" | custom-call | flops 629145600 | bytes 4000000 | tf_op jit(solution)/shard_map/pallas_call | solution.py:402
  52.4 0.1 collective-permute-start.10
  52.4 1.7 %collective-permute-start.2 = (bf16[128,1280]{1,0:T(8,128)(2,1)S(1)}, bf16[128,1280]{1,0:T(8,128)(2,1)S(1)}, u32[]{:S(2)}, u32[]{:S(2)}) collective-permute-start(bf16[128,1280]{1,0:T(8,128)(2,1)S(1)} %get-tuple-element.33.own_ref), channel_id=1, source_target_pairs={{0,1},{1,0},{2,3},{3,2},{4,5},{5,4},{6,7},{7,6},{8,9},{9,8},{10,11... | collective-permute-start | bytes 983048 | tf_op jit(solution)/shard_map/ppermute | solution.py:437
  54.1 1.5 %collective-permute-start.11 = (bf16[240,256]{1,0:T(8,128)(2,1)S(1)}, bf16[240,256]{1,0:T(8,128)(2,1)S(1)}, u32[]{:S(2)}, u32[]{:S(2)}) collective-permute-start(bf16[240,256]{1,0:T(8,128)(2,1)S(1)} %get-tuple-element.47), channel_id=1, source_target_pairs={{0,4},{2,6},{4,0},{6,2},{8,12},{10,14},{12,8},{14,10},{16,20},{18,... | collective-permute-start | bytes 368648 | tf_op jit(solution)/shard_map/ppermute | solution.py:440
  55.6 1.6 %collective-permute-start.12 = (bf16[240,256]{1,0:T(8,128)(2,1)S(1)}, bf16[240,256]{1,0:T(8,128)(2,1)S(1)}, u32[]{:S(2)}, u32[]{:S(2)}) collective-permute-start(bf16[240,256]{1,0:T(8,128)(2,1)S(1)} %get-tuple-element.48), channel_id=1, source_target_pairs={{0,8},{2,10},{4,12},{6,14},{8,0},{10,2},{12,4},{14,6},{16,24},{18,... | collective-permute-start | bytes 368648 | tf_op jit(solution)/shard_map/ppermute | solution.py:440
  57.2 0.4 collective-permute-start.13
  57.6 0.0 collective-permute-done.10
  57.6 0.1 add_convert_fusion._.refs_8_
  57.7 1.8 %collective-permute-done.11.refs_1_ = bf16[240,256]{1,0:T(8,128)(2,1)S(1)} collective-permute-done((bf16[240,256]{1,0:T(8,128)(2,1)S(1)}, bf16[240,256]{1,0:T(8,128)(2,1)S(1)}, u32[]{:S(2)}, u32[]{:S(2)}) %collective-permute-start.11) | collective-permute-done | bytes 122912 | tf_op jit(solution)/shard_map/ppermute | solution.py:440
  59.5 2.3 %collective-permute-done.12.refs_2_ = bf16[240,256]{1,0:T(8,128)(2,1)S(1)} collective-permute-done((bf16[240,256]{1,0:T(8,128)(2,1)S(1)}, bf16[240,256]{1,0:T(8,128)(2,1)S(1)}, u32[]{:S(2)}, u32[]{:S(2)}) %collective-permute-start.12) | collective-permute-done | bytes 122912 | tf_op jit(solution)/shard_map/ppermute | solution.py:440
  61.8 1.5 %collective-permute-done.13.refs_3_ = bf16[240,256]{1,0:T(8,128)(2,1)S(1)} collective-permute-done((bf16[240,256]{1,0:T(8,128)(2,1)S(1)}, bf16[240,256]{1,0:T(8,128)(2,1)S(1)}, u32[]{:S(2)}, u32[]{:S(2)}) %collective-permute-start.13) | collective-permute-done | bytes 122912 | tf_op jit(solution)/shard_map/ppermute | solution.py:440
  63.3 0.0 copy-start.8
  63.3 1.0 %shard_map.139 = (f32[120,1280]{1,0:T(8,128)S(1)}, bf16[120,1280]{1,0:T(8,128)(2,1)S(1)}) custom-call(bf16[240,256]{1,0:T(8,128)(2,1)S(1)} %get-tuple-element.46.refs_0_, bf16[240,256]{1,0:T(8,128)(2,1)S(1)} %collective-permute-done.11.refs_1_, bf16[240,256]{1,0:T(8,128)(2,1)S(1)} %collective-permute-done.12.refs_2_, ...), custom_call_target="tpu_custom_call" | custom-call | flops 629145600 | bytes 4000000 | tf_op jit(solution)/shard_map/pallas_call | solution.py:402
  64.3 0.1 collective-permute-start.14
  64.4 2.6 %collective-permute-start.15 = (bf16[120,1280]{1,0:T(8,128)(2,1)S(1)}, bf16[120,1280]{1,0:T(8,128)(2,1)S(1)}, u32[]{:S(2)}, u32[]{:S(2)}) collective-permute-start(bf16[120,1280]{1,0:T(8,128)(2,1)S(1)} %add_convert_fusion._.refs_8_), channel_id=1, source_target_pairs={{0,16},{2,18},{4,20},{6,22},{8,24},{10,26},{12,28},{14,30},{16,0},... | collective-permute-start | bytes 921608 | tf_op jit(solution)/shard_map/ppermute | solution.py:440
  67.0 0.0 collective-permute-done.2.other_ref
  67.0 0.0 copy-done.8
  67.0 2.1 %shard_map.138 = bf16[128,5120]{1,0:T(8,128)(2,1)} custom-call(s32[1]{0:T(128)S(6)} %copy.14.live_ref, s32[1,64]{1,0:T(1,128)S(1)} %copy-done.8, bf16[128,1280]{1,0:T(8,128)(2,1)S(1)} %get-tuple-element.33.own_ref, bf16[128,1280]{1,0:T(8,128)(2,1)S(1)} %collective-permute-done.2.other_ref, bf16[120,1280]{1,0:T(8,128)(2,1)S(1)} %add_convert_fusion._.refs_8_), custom_call_target="tpu_custom_call" | custom-call | flops 335544320 | bytes 4000000 | tf_op jit(solution)/shard_map/pallas_call | solution.py:402
  69.1 0.0 collective-permute-done.14
  69.1 12.4 %collective-permute-done.15 = bf16[120,1280]{1,0:T(8,128)(2,1)S(1)} collective-permute-done((bf16[120,1280]{1,0:T(8,128)(2,1)S(1)}, bf16[120,1280]{1,0:T(8,128)(2,1)S(1)}, u32[]{:S(2)}, u32[]{:S(2)}) %collective-permute-start.15) | collective-permute-done | bytes 307232 | tf_op jit(solution)/shard_map/ppermute | solution.py:440
  81.5 0.9 %add_bitcast_fusion = f32[1,120,1280]{2,1,0:T(8,128)} fusion(bf16[120,1280]{1,0:T(8,128)(2,1)S(1)} %collective-permute-done.15, f32[120,1280]{1,0:T(8,128)S(1)} %get-tuple-element.50, bf16[120,1280]{1,0:T(8,128)(2,1)S(1)} %collective-permute-done.14), kind=kLoop, calls=%fused_computation | loop fusion | flops 614400 | bytes 1843200 | tf_op jit(solution)/shard_map/broadcast_in_dim | solution.py:562
Async XLA Ops:
  0.6 4.2 %copy-start.4 = (f32[3,640]{1,0:T(4,128)S(1)}, f32[3,640]{1,0:T(4,128)}, u32[]{:S(2)}) copy-start(f32[3,640]{1,0:T(4,128)} %b_ref.2) | copy-start | bytes 23044
  4.9 1.1 %copy-start.1 = (bf16[256,1280]{1,0:T(8,128)(2,1)S(1)}, bf16[256,1280]{1,0:T(8,128)(2,1)}, u32[]{:S(2)}) copy-start(bf16[256,1280]{1,0:T(8,128)(2,1)} %get-tuple-element.27.normed_hbm.refs_4_) | copy-start | bytes 1966084
  5.9 8.6 %copy-start.9 = (bf16[128,1280]{1,0:T(8,128)(2,1)S(1)}, bf16[128,1280]{1,0:T(8,128)(2,1)}, u32[]{:S(2)}) copy-start(bf16[128,1280]{1,0:T(8,128)(2,1)} %get-tuple-element.32) | copy-start | bytes 983044
  6.0 12.3 %copy-start = (bf16[640,1280]{1,0:T(8,128)(2,1)S(1)}, bf16[640,1280]{1,0:T(8,128)(2,1)}, u32[]{:S(2)}) copy-start(bf16[640,1280]{1,0:T(8,128)(2,1)} %proj_ref.5) | copy-start | bytes 4915204
  11.5 17.8 %copy-start.2 = (bf16[256,1280]{1,0:T(8,128)(2,1)S(1)}, bf16[256,1280]{1,0:T(8,128)(2,1)}, u32[]{:S(2)}) copy-start(bf16[256,1280]{1,0:T(8,128)(2,1)} %patches_ref.1) | copy-start | bytes 1966084
  11.5 17.8 %copy-start.3 = (bf16[128,1280]{1,0:T(8,128)(2,1)S(1)}, bf16[128,1280]{1,0:T(8,128)(2,1)}, u32[]{:S(2)}) copy-start(bf16[128,1280]{1,0:T(8,128)(2,1)} %get-tuple-element.31.up_keep_ref) | copy-start | bytes 983044
  11.5 17.8 %copy-start.5 = (f32[1280]{0:T(1024)S(1)}, f32[1280]{0:T(1024)}, u32[]{:S(2)}) copy-start(f32[1280]{0:T(1024)} %b_ref.3) | copy-start | bytes 15364
  11.5 17.8 %copy-start.6 = (f32[1280]{0:T(1024)S(1)}, f32[1280]{0:T(1024)}, u32[]{:S(2)}) copy-start(f32[1280]{0:T(1024)} %gain_ref.1) | copy-start | bytes 15364
  11.5 17.8 %copy-start.7 = (f32[1280]{0:T(1024)S(1)}, f32[1280]{0:T(1024)}, u32[]{:S(2)}) copy-start(f32[1280]{0:T(1024)} %bias_ref.1) | copy-start | bytes 15364
  11.6 11.6 %collective-permute-start = (bf16[128,1280]{1,0:T(8,128)(2,1)S(1)}, bf16[128,1280]{1,0:T(8,128)(2,1)S(1)}, u32[]{:S(2)}, u32[]{:S(2)}) collective-permute-start(bf16[128,1280]{1,0:T(8,128)(2,1)S(1)} %get-tuple-element.30), channel_id=1, source_target_pairs={{0,1},{1,0},{2,3},{3,2},{4,5},{5,4},{6,7},{7,6},{8,9},{9,8},{10,11... | collective-permute-start | bytes 983048 | tf_op jit(solution)/shard_map/ppermute | solution.py:437
  14.6 14.7 %collective-permute-start.1 = (bf16[128,1280]{1,0:T(8,128)(2,1)S(1)}, bf16[128,1280]{1,0:T(8,128)(2,1)S(1)}, u32[]{:S(2)}, u32[]{:S(2)}) collective-permute-start(bf16[128,1280]{1,0:T(8,128)(2,1)S(1)} %copy-done.9), channel_id=1, source_target_pairs={{0,1},{1,0},{2,3},{3,2},{4,5},{5,4},{6,7},{7,6},{8,9},{9,8},{10,11... | collective-permute-start | bytes 983048 | tf_op jit(solution)/shard_map/ppermute | solution.py:437
  14.7 31.0 %collective-permute-start.7 = (bf16[256,1280]{1,0:T(8,128)(2,1)S(1)}, bf16[256,1280]{1,0:T(8,128)(2,1)S(1)}, u32[]{:S(2)}, u32[]{:S(2)}) collective-permute-start(bf16[256,1280]{1,0:T(8,128)(2,1)S(1)} %copy-done.1), channel_id=1, source_target_pairs={{0,4},{2,6},{4,0},{6,2},{8,12},{10,14},{12,8},{14,10},{16,20},{18,... | collective-permute-start | bytes 1966088 | tf_op jit(solution)/shard_map/ppermute | solution.py:440
  16.6 29.4 %collective-permute-start.8 = (bf16[256,1280]{1,0:T(8,128)(2,1)S(1)}, bf16[256,1280]{1,0:T(8,128)(2,1)S(1)}, u32[]{:S(2)}, u32[]{:S(2)}) collective-permute-start(bf16[256,1280]{1,0:T(8,128)(2,1)S(1)} %copy-done.1), channel_id=1, source_target_pairs={{0,8},{2,10},{4,12},{6,14},{8,0},{10,2},{12,4},{14,6},{16,24},{18,... | collective-permute-start | bytes 1966088 | tf_op jit(solution)/shard_map/ppermute | solution.py:440
  18.2 29.2 %collective-permute-start.9 = (bf16[256,1280]{1,0:T(8,128)(2,1)S(1)}, bf16[256,1280]{1,0:T(8,128)(2,1)S(1)}, u32[]{:S(2)}, u32[]{:S(2)}) collective-permute-start(bf16[256,1280]{1,0:T(8,128)(2,1)S(1)} %copy-done.1), channel_id=1, source_target_pairs={{0,12},{2,14},{4,8},{6,10},{8,4},{10,6},{12,0},{14,2},{16,28},{18,... | collective-permute-start | bytes 1966088 | tf_op jit(solution)/shard_map/ppermute | solution.py:440
  29.9 8.9 %collective-permute-start.3 = (bf16[128,1280]{1,0:T(8,128)(2,1)S(1)}, bf16[128,1280]{1,0:T(8,128)(2,1)S(1)}, u32[]{:S(2)}, u32[]{:S(2)}) collective-permute-start(bf16[128,1280]{1,0:T(8,128)(2,1)S(1)} %get-tuple-element.34.row_ref), channel_id=1, source_target_pairs={{0,1},{1,0},{2,3},{3,2},{4,5},{5,4},{6,7},{7,6},{8,9},{9,8},{10,11... | collective-permute-start | bytes 983048 | tf_op jit(solution)/shard_map/ppermute | solution.py:437
  42.5 7.6 %collective-permute-start.4 = (bf16[240,256]{1,0:T(8,128)(2,1)S(1)}, bf16[240,256]{1,0:T(8,128)(2,1)S(1)}, u32[]{:S(2)}, u32[]{:S(2)}) collective-permute-start(bf16[240,256]{1,0:T(8,128)(2,1)S(1)} %get-tuple-element.41), channel_id=1, source_target_pairs={{0,4},{2,6},{4,0},{6,2},{8,12},{10,14},{12,8},{14,10},{16,20},{18,... | collective-permute-start | bytes 368648 | tf_op jit(solution)/shard_map/ppermute | solution.py:440
  44.1 6.2 %collective-permute-start.5 = (bf16[240,256]{1,0:T(8,128)(2,1)S(1)}, bf16[240,256]{1,0:T(8,128)(2,1)S(1)}, u32[]{:S(2)}, u32[]{:S(2)}) collective-permute-start(bf16[240,256]{1,0:T(8,128)(2,1)S(1)} %get-tuple-element.42), channel_id=1, source_target_pairs={{0,8},{2,10},{4,12},{6,14},{8,0},{10,2},{12,4},{14,6},{16,24},{18,... | collective-permute-start | bytes 368648 | tf_op jit(solution)/shard_map/ppermute | solution.py:440
  45.6 5.8 %collective-permute-start.6 = (bf16[240,256]{1,0:T(8,128)(2,1)S(1)}, bf16[240,256]{1,0:T(8,128)(2,1)S(1)}, u32[]{:S(2)}, u32[]{:S(2)}) collective-permute-start(bf16[240,256]{1,0:T(8,128)(2,1)S(1)} %get-tuple-element.43), channel_id=1, source_target_pairs={{0,12},{2,14},{4,8},{6,10},{8,4},{10,6},{12,0},{14,2},{16,28},{18,... | collective-permute-start | bytes 368648 | tf_op jit(solution)/shard_map/ppermute | solution.py:440
  52.4 5.3 %collective-permute-start.10 = (bf16[120,1280]{1,0:T(8,128)(2,1)S(1)}, bf16[120,1280]{1,0:T(8,128)(2,1)S(1)}, u32[]{:S(2)}, u32[]{:S(2)}) collective-permute-start(bf16[120,1280]{1,0:T(8,128)(2,1)S(1)} %get-tuple-element.45), channel_id=1, source_target_pairs={{0,2},{2,0},{4,6},{6,4},{8,10},{10,8},{12,14},{14,12},{16,18},{18,... | collective-permute-start | bytes 921608 | tf_op jit(solution)/shard_map/ppermute | solution.py:440
  52.4 14.6 %collective-permute-start.2 = (bf16[128,1280]{1,0:T(8,128)(2,1)S(1)}, bf16[128,1280]{1,0:T(8,128)(2,1)S(1)}, u32[]{:S(2)}, u32[]{:S(2)}) collective-permute-start(bf16[128,1280]{1,0:T(8,128)(2,1)S(1)} %get-tuple-element.33.own_ref), channel_id=1, source_target_pairs={{0,1},{1,0},{2,3},{3,2},{4,5},{5,4},{6,7},{7,6},{8,9},{9,8},{10,11... | collective-permute-start | bytes 983048 | tf_op jit(solution)/shard_map/ppermute | solution.py:437
  54.1 5.4 %collective-permute-start.11 = (bf16[240,256]{1,0:T(8,128)(2,1)S(1)}, bf16[240,256]{1,0:T(8,128)(2,1)S(1)}, u32[]{:S(2)}, u32[]{:S(2)}) collective-permute-start(bf16[240,256]{1,0:T(8,128)(2,1)S(1)} %get-tuple-element.47), channel_id=1, source_target_pairs={{0,4},{2,6},{4,0},{6,2},{8,12},{10,14},{12,8},{14,10},{16,20},{18,... | collective-permute-start | bytes 368648 | tf_op jit(solution)/shard_map/ppermute | solution.py:440
  55.6 6.2 %collective-permute-start.12 = (bf16[240,256]{1,0:T(8,128)(2,1)S(1)}, bf16[240,256]{1,0:T(8,128)(2,1)S(1)}, u32[]{:S(2)}, u32[]{:S(2)}) collective-permute-start(bf16[240,256]{1,0:T(8,128)(2,1)S(1)} %get-tuple-element.48), channel_id=1, source_target_pairs={{0,8},{2,10},{4,12},{6,14},{8,0},{10,2},{12,4},{14,6},{16,24},{18,... | collective-permute-start | bytes 368648 | tf_op jit(solution)/shard_map/ppermute | solution.py:440
  57.2 6.1 %collective-permute-start.13 = (bf16[240,256]{1,0:T(8,128)(2,1)S(1)}, bf16[240,256]{1,0:T(8,128)(2,1)S(1)}, u32[]{:S(2)}, u32[]{:S(2)}) collective-permute-start(bf16[240,256]{1,0:T(8,128)(2,1)S(1)} %get-tuple-element.49), channel_id=1, source_target_pairs={{0,12},{2,14},{4,8},{6,10},{8,4},{10,6},{12,0},{14,2},{16,28},{18,... | collective-permute-start | bytes 368648 | tf_op jit(solution)/shard_map/ppermute | solution.py:440
  63.3 3.7 %copy-start.8 = (s32[1,64]{1,0:T(1,128)S(1)}, s32[1,64]{1,0:T(1,128)}, u32[]{:S(2)}) copy-start(s32[1,64]{1,0:T(1,128)} %places_ref.1) | copy-start | bytes 772
  64.3 4.8 %collective-permute-start.14 = (bf16[120,1280]{1,0:T(8,128)(2,1)S(1)}, bf16[120,1280]{1,0:T(8,128)(2,1)S(1)}, u32[]{:S(2)}, u32[]{:S(2)}) collective-permute-start(bf16[120,1280]{1,0:T(8,128)(2,1)S(1)} %get-tuple-element.51), channel_id=1, source_target_pairs={{0,2},{2,0},{4,6},{6,4},{8,10},{10,8},{12,14},{14,12},{16,18},{18,... | collective-permute-start | bytes 921608 | tf_op jit(solution)/shard_map/ppermute | solution.py:440
  64.4 17.2 %collective-permute-start.15 = (bf16[120,1280]{1,0:T(8,128)(2,1)S(1)}, bf16[120,1280]{1,0:T(8,128)(2,1)S(1)}, u32[]{:S(2)}, u32[]{:S(2)}) collective-permute-start(bf16[120,1280]{1,0:T(8,128)(2,1)S(1)} %add_convert_fusion._.refs_8_), channel_id=1, source_target_pairs={{0,16},{2,18},{4,20},{6,22},{8,24},{10,26},{12,28},{14,30},{16,0},... | collective-permute-start | bytes 921608 | tf_op jit(solution)/shard_map/ppermute | solution.py:440

commit v3 on v2

--- a/solution.py
+++ b/solution.py
@@ -166,6 +166,24 @@
     return pl.multiple_of((seq if own else 1 - seq) * half, 128)
 
 
+def norm_low(patches_ref, gain_ref, bias_ref):
+    return normalize(
+        patches_ref[...].astype(jnp.float32), gain_ref[...][None, :], bias_ref[...][None, :]
+    )[0].astype(jnp.bfloat16)
+
+
+def pull(live_ref, places_ref, grad_ref, out_ref, own):
+    half, width = out_ref.shape
+    masks = place_masks(
+        live_ref, places_ref[...], grad_ref.shape[0], half, half_start(half, own)
+    )
+    total = None
+    for k in range(4):
+        term = leading(masks[k], grad_ref[:, k * width : (k + 1) * width])
+        total = term if total is None else total + term
+    out_ref[...] = total.astype(out_ref.dtype)
+
+
 def prepare_kernel(
     live_ref,
     gain_hbm,
@@ -174,7 +192,6 @@
     places_hbm,
     grad_hbm,
     normed_hbm,
-    keep_hbm,
     send_hbm,
     gain_ref,
     bias_ref,
@@ -182,36 +199,22 @@
     places_ref,
     grad_ref,
     normed_ref,
-    keep_ref,
     send_ref,
     sems,
 ):
-    half, width = send_ref.shape
     came = begin(
-        (places_hbm, grad_hbm, gain_hbm, bias_hbm, patches_hbm),
-        (places_ref, grad_ref, gain_ref, bias_ref, patches_ref),
+        (gain_hbm, bias_hbm, patches_hbm, places_hbm, grad_hbm),
+        (gain_ref, bias_ref, patches_ref, places_ref, grad_ref),
         sems,
     )
-    came[0].wait()
-    masks = [
-        place_masks(live_ref, places_ref[...], grad_ref.shape[0], half, half_start(half, own))
-        for own in (False, True)
-    ]
-    came[1].wait()
-    went = []
-    for out_ref, out_hbm, masks_of in ((send_ref, send_hbm, masks[0]), (keep_ref, keep_hbm, masks[1])):
-        total = None
-        for k in range(4):
-            term = leading(masks_of[k], grad_ref[:, k * width : (k + 1) * width])
-            total = term if total is None else total + term
-        out_ref[...] = total.astype(out_ref.dtype)
-        went += begin((out_ref,), (out_hbm,), sems, 5 + len(went))
-    for copy in came[2:]:
+    for copy in came[:3]:
         copy.wait()
-    normed_ref[...] = normalize(
-        patches_ref[...].astype(jnp.float32), gain_ref[...][None, :], bias_ref[...][None, :]
-    )[0].astype(jnp.bfloat16)
-    went += begin((normed_ref,), (normed_hbm,), sems, 7)
+    normed_ref[...] = norm_low(patches_ref, gain_ref, bias_ref)
+    went = begin((normed_ref,), (normed_hbm,), sems, 5)
+    for copy in came[3:]:
+        copy.wait()
+    pull(live_ref, places_ref, grad_ref, send_ref, False)
+    went += begin((send_ref,), (send_hbm,), sems, 6)
     for copy in went:
         copy.wait()
 
@@ -247,24 +250,28 @@
 def first_kernel(
     live_ref,
     b_ref,
-    normed_hbm,
+    gain_ref,
+    bias_ref,
+    patches_hbm,
     w_hbm,
     proj_hbm,
     triple_ref,
     probs_ref,
     send_ref,
-    normed_ref,
+    patches_ref,
     w_ref,
     proj_ref,
     attended_ref,
+    normed_ref,
     sems,
 ):
     came = begin(
-        (normed_hbm, w_hbm.at[0], w_hbm.at[1], w_hbm.at[2], proj_hbm),
-        (normed_ref, w_ref.at[0], w_ref.at[1], w_ref.at[2], proj_ref),
+        (patches_hbm, w_hbm.at[0], w_hbm.at[1], w_hbm.at[2], proj_hbm),
+        (patches_ref, w_ref.at[0], w_ref.at[1], w_ref.at[2], proj_ref),
         sems,
     )
     came[0].wait()
+    normed_ref[...] = norm_low(patches_ref, gain_ref, bias_ref)
     for t in range(3):
         came[1 + t].wait()
         part = jnp.dot(normed_ref[...], w_ref[t], preferred_element_type=jnp.float32)
@@ -277,10 +284,21 @@
     ).astype(jnp.bfloat16)
 
 
-def second_kernel(live_ref, triple_ref, proj_ref, probs_ref, keep_ref, attended_ref):
+def second_kernel(
+    live_ref,
+    places_ref,
+    grad_ref,
+    triple_ref,
+    proj_ref,
+    probs_ref,
+    keep_ref,
+    up_ref,
+    attended_ref,
+):
     start = half_start(keep_ref.shape[0], True)
     attend(live_ref, triple_ref, start, probs_ref, attended_ref)
     keep_ref[...] = jnp.dot(attended_ref[...], proj_ref[...], preferred_element_type=jnp.float32)
+    pull(live_ref, places_ref, grad_ref, up_ref, True)
 
 
 def middle_kernel(
@@ -444,9 +462,9 @@
     probs_half = shape((heads, half, rows), low)
     attended = pltpu.VMEM((half, local), low)
     block = 3 * local // 8
-    normed, up_keep, up_send = call(
+    normed, up_send = call(
         prepare_kernel,
-        (full, part, part),
+        (full, part),
         "saaaaa",
         8 * rows * share_rows * width,
         (clip_tokens, norm_gain, norm_bias, patches, positions, grad_placed),
@@ -458,8 +476,7 @@
             pltpu.VMEM(grad_placed.shape, low),
             pltpu.VMEM((rows, width), low),
             pltpu.VMEM((half, width), low),
-            pltpu.VMEM((half, width), low),
-            pltpu.SemaphoreType.DMA((8,)),
+            pltpu.SemaphoreType.DMA((7,)),
         ),
         limit=62,
         out_kind="a",
@@ -470,25 +487,34 @@
     triple, other_probs, part_send = call(
         first_kernel,
         (shape((3, rows, local), low), probs_half, part),
-        "svaaa",
+        "svvvaaa",
         7 * rows * width * local,
-        (clip_tokens, b_qkv, normed, jnp.transpose(w_qkv, (1, 0, 2)), w_proj),
+        (
+            clip_tokens,
+            b_qkv,
+            norm_gain,
+            norm_bias,
+            patches,
+            jnp.transpose(w_qkv, (1, 0, 2)),
+            w_proj,
+        ),
         (
             pltpu.VMEM((rows, width), low),
             pltpu.VMEM((3, width, local), low),
             pltpu.VMEM((local, width), low),
             attended,
+            pltpu.VMEM((rows, width), low),
             pltpu.SemaphoreType.DMA((5,)),
         ),
         limit=51,
     )
     part_came = swap(part_send)
-    own_probs, part_keep = call(
+    own_probs, part_keep, up_keep = call(
         second_kernel,
-        (probs_half, wide),
-        "svv",
+        (probs_half, wide, part),
+        "svvvv",
         3 * half * width * local,
-        (clip_tokens, triple, w_proj),
+        (clip_tokens, positions, grad_placed, triple, w_proj),
         (attended,),
     )
     merged, own_rows = call(

time: 82.7 us -> 87 us (1.052)
  local copies, waits for them, and re-layouts: 1.13 us -> 7.46 us
  waiting for transfers between devices: 35.3 us -> 32.6 us
    unnamed x20 -> x34, local copies, waits for them, and re-layouts: 1.13 us -> 7.46 us
    ppermute x4, waiting for transfers between devices: 11.9 us -> 5.91 us  [swap(): return lax.ppermute(value, 'seq', [(0, 1), (1, 0)])]
    ppermute x12, waiting for transfers between devices: 23.4 us -> 26.7 us  [flip(): return lax.ppermute(value, 'clip', [(i, i ^ bits) for i in range(n_clip)])]
  transfers between devices with their start and end apart: 16 -> 16, of which waited for: 11 -> 10; matrix products, arithmetic and copies ran while one was open for 0% -> 0% of each run, Pallas kernels for 16% -> 20%
where the time goes in v3:
time: 87 us; the launch traced here: 86.5 us
  waiting for transfers between devices  32.6 us (37%)
  Pallas kernels  24.2 us (28%)
  starting transfers between devices  19.9 us (23%)
  local copies, waits for them, and re-layouts  7.46 us (9%)
  between operations  1.43 us (2%)
  other arithmetic  0.98 us (1%)
    ppermute x12, waiting for transfers between devices, flip(): return lax.ppermute(value, 'clip', [(i, i ^ bits) for i in range(n_clip)])  26.7 us
    pallas_call x9, Pallas kernels, call(): pl.pallas_call(kernel, out_shape=outs, in_specs=[spec[kind] for kind in k...  24.2 us
    ppermute x12, starting transfers between devices, flip(): return lax.ppermute(value, 'clip', [(i, i ^ bits) for i in range(n_clip)])  13.4 us
    unnamed x34, local copies, waits for them, and re-layouts  7.46 us
    ppermute x4, starting transfers between devices, swap(): return lax.ppermute(value, 'seq', [(0, 1), (1, 0)])  6.56 us
    ppermute x4, waiting for transfers between devices, swap(): return lax.ppermute(value, 'seq', [(0, 1), (1, 0)])  5.91 us
  transfers between devices with their start and end apart: 16, of which 10 were waited for; matrix products, arithmetic and copies ran while one was open for 0% of the time, Pallas kernels for 20%

profile of v3, /device:TPU:0, one launch (start us, length us, event | category | flops | bytes accessed | tf_op | source)
XLA Modules:
  0.0 86.5 jit_solution(17131035781462987171)
XLA Ops:
  1.3 0.0 copy-start.4
  1.3 1.1 %copy-done.4 = bf16[256,1280]{1,0:T(8,128)(2,1)S(1)} copy-done((bf16[256,1280]{1,0:T(8,128)(2,1)S(1)}, bf16[256,1280]{1,0:T(8,128)(2,1)}, u32[]{:S(2)}) %copy-start.4) | copy-done | bytes 655384
  2.4 0.7 copy-done.10
  3.1 0.7 copy-done.11
  3.8 0.7 copy-done.12
  4.5 6.2 %shard_map.131 = (bf16[3,256,640]{2,1,0:T(8,128)(2,1)S(1)}, bf16[8,128,256]{2,1,0:T(8,128)(2,1)S(1)}, bf16[128,1280]{1,0:T(8,128)(2,1)}) custom-call(s32[1]{0:T(128)S(6)} %copy.14.live_ref, f32[3,640]{1,0:T(4,128)S(1)} %copy-done.12, f32[1280]{0:T(1024)S(1)} %copy-done.10, f32[1280]{0:T(1024)S(1)} %copy-done.11, bf16[256,1280]{1,0:T(8,128)(2,1)S(1)} %copy-done.4, ...), custom_call_target="tpu_custom_call" | custom-call | flops 1468006400 | bytes 4000000 | tf_op jit(solution)/shard_map/pallas_call | solution.py:420
  10.6 0.0 copy-start.1
  10.6 0.9 %copy-done.1 = bf16[3,256,640]{2,1,0:T(8,128)(2,1)} copy-done((bf16[3,256,640]{2,1,0:T(8,128)(2,1)}, bf16[3,256,640]{2,1,0:T(8,128)(2,1)S(1)}, u32[]{:S(2)}) %copy-start.1) | copy-done | bytes 983064
  11.6 0.8 copy-done.8
  12.4 3.0 %collective-permute-start = (bf16[128,1280]{1,0:T(8,128)(2,1)}, bf16[128,1280]{1,0:T(8,128)(2,1)S(1)}, u32[]{:S(2)}, u32[]{:S(2)}) collective-permute-start(bf16[128,1280]{1,0:T(8,128)(2,1)} %get-tuple-element.29), channel_id=1, source_target_pairs={{0,1},{1,0},{2,3},{3,2},{4,5},{5,4},{6,7},{7,6},{8,9},{9,8},{10,11... | collective-permute-start | bytes 983048 | tf_op jit(solution)/shard_map/ppermute | solution.py:455
  15.4 3.0 %shard_map.133 = (bf16[256,1280]{1,0:T(8,128)(2,1)}, bf16[128,1280]{1,0:T(8,128)(2,1)}) custom-call(s32[1]{0:T(128)S(6)} %copy.14.live_ref, f32[1280]{0:T(1024)} %gain_hbm.1, f32[1280]{0:T(1024)} %bias_hbm.1, bf16[256,1280]{1,0:T(8,128)(2,1)} %patches_ref.1, s32[1,64]{1,0:T(1,128)} %places_ref.3, bf16[128,5120]{1,0:T(8,128)(2,1)} %grad_hbm.1), custom_call_target="tpu_custom_call" | custom-call | flops 335544320 | bytes 4000000 | tf_op jit(solution)/shard_map/pallas_call | solution.py:420
  18.4 0.2 collective-permute-start.1
  18.6 1.9 %collective-permute-start.7 = (bf16[256,1280]{1,0:T(8,128)(2,1)}, bf16[256,1280]{1,0:T(8,128)(2,1)S(1)}, u32[]{:S(2)}, u32[]{:S(2)}) collective-permute-start(bf16[256,1280]{1,0:T(8,128)(2,1)} %get-tuple-element.43.refs_4_), channel_id=1, source_target_pairs={{0,4},{2,6},{4,0},{6,2},{8,12},{10,14},{12,8},{14,10},{16,20},{18,... | collective-permute-start | bytes 1966088 | tf_op jit(solution)/shard_map/ppermute | solution.py:458
  20.5 1.6 %collective-permute-start.8 = (bf16[256,1280]{1,0:T(8,128)(2,1)}, bf16[256,1280]{1,0:T(8,128)(2,1)S(1)}, u32[]{:S(2)}, u32[]{:S(2)}) collective-permute-start(bf16[256,1280]{1,0:T(8,128)(2,1)} %get-tuple-element.43.refs_4_), channel_id=1, source_target_pairs={{0,8},{2,10},{4,12},{6,14},{8,0},{10,2},{12,4},{14,6},{16,24},{18,... | collective-permute-start | bytes 1966088 | tf_op jit(solution)/shard_map/ppermute | solution.py:458
  22.1 0.0 collective-permute-start.9
  22.1 0.0 copy-done
  22.1 0.0 copy-done.16
  22.1 0.0 copy-start.2
  22.1 1.2 %copy-done.2 = bf16[3,256,640]{2,1,0:T(8,128)(2,1)S(1)} copy-done((bf16[3,256,640]{2,1,0:T(8,128)(2,1)S(1)}, bf16[3,256,640]{2,1,0:T(8,128)(2,1)}, u32[]{:S(2)}) %copy-start.2) | copy-done | bytes 983064
  23.3 1.3 %copy-done.6 = bf16[128,5120]{1,0:T(8,128)(2,1)S(1)} copy-done((bf16[128,5120]{1,0:T(8,128)(2,1)S(1)}, bf16[128,5120]{1,0:T(8,128)(2,1)}, u32[]{:S(2)}) %copy-start.6) | copy-done | bytes 1310744
  24.6 3.3 %shard_map.132 = (bf16[8,128,256]{2,1,0:T(8,128)(2,1)S(1)}, f32[128,1280]{1,0:T(8,128)S(1)}, bf16[128,1280]{1,0:T(8,128)(2,1)S(1)}) custom-call(s32[1]{0:T(128)S(6)} %copy.14.live_ref, s32[1,64]{1,0:T(1,128)S(1)} %copy-done.16, bf16[128,5120]{1,0:T(8,128)(2,1)S(1)} %copy-done.6, bf16[3,256,640]{2,1,0:T(8,128)(2,1)S(1)} %copy-done.2, ...), custom_call_target="tpu_custom_call" | custom-call | flops 314572800 | bytes 4000000 | tf_op jit(solution)/shard_map/pallas_call | solution.py:420
  28.0 0.0 copy-start.3
  28.0 0.0 collective-permute-done.came_ref
  28.0 2.3 %collective-permute-done.1.up_came_ref = bf16[128,1280]{1,0:T(8,128)(2,1)S(1)} collective-permute-done((bf16[128,1280]{1,0:T(8,128)(2,1)}, bf16[128,1280]{1,0:T(8,128)(2,1)S(1)}, u32[]{:S(2)}, u32[]{:S(2)}) %collective-permute-start.1) | collective-permute-done | bytes 327712 | tf_op jit(solution)/shard_map/ppermute | solution.py:455
  30.3 0.0 copy-done.5
  30.3 0.0 copy-done.13
  30.3 0.0 copy-done.14
  30.3 0.0 copy-done.15
  30.3 0.6 shard_map.134
  30.9 1.8 %collective-permute-start.3 = (bf16[128,1280]{1,0:T(8,128)(2,1)S(1)}, bf16[128,1280]{1,0:T(8,128)(2,1)S(1)}, u32[]{:S(2)}, u32[]{:S(2)}) collective-permute-start(bf16[128,1280]{1,0:T(8,128)(2,1)S(1)} %get-tuple-element.33.row_ref), channel_id=1, source_target_pairs={{0,1},{1,0},{2,3},{3,2},{4,5},{5,4},{6,7},{7,6},{8,9},{9,8},{10,11... | collective-permute-start | bytes 983048 | tf_op jit(solution)/shard_map/ppermute | solution.py:455
  32.7 0.0 copy-done.3
  32.7 3.5 %shard_map.135 = (bf16[640,128]{1,0:T(8,128)(2,1)S(1)}, f32[640,256]{1,0:T(8,128)S(1)}, f32[640,256]{1,0:T(8,128)S(1)}) custom-call(bf16[128,1280]{1,0:T(8,128)(2,1)S(1)} %get-tuple-element.33.row_ref, bf16[640,1280]{1,0:T(8,128)(2,1)S(1)} %copy-done, bf16[3,256,640]{2,1,0:T(8,128)(2,1)S(1)} %copy-done.3, bf16[8,128,256]{2,1,0:T(8,128)(2,1)S(1)} %get-tuple-element.35.probs_ref), custom_call_target="tpu_custom_call" | custom-call | flops 419430400 | bytes 4000000 | tf_op jit(solution)/shard_map/pallas_call | solution.py:420
  36.2 3.6 %collective-permute-done.3.row_ref = bf16[128,1280]{1,0:T(8,128)(2,1)S(1)} collective-permute-done((bf16[128,1280]{1,0:T(8,128)(2,1)S(1)}, bf16[128,1280]{1,0:T(8,128)(2,1)S(1)}, u32[]{:S(2)}, u32[]{:S(2)}) %collective-permute-start.3) | collective-permute-done | bytes 327712 | tf_op jit(solution)/shard_map/ppermute | solution.py:455
  39.8 0.0 copy-done.9
  39.8 3.6 %shard_map.136 = (bf16[240,256]{1,0:T(8,128)(2,1)S(1)}, bf16[240,256]{1,0:T(8,128)(2,1)S(1)}, bf16[240,256]{1,0:T(8,128)(2,1)S(1)}, bf16[240,256]{1,0:T(8,128)(2...) custom-call(bf16[128,1280]{1,0:T(8,128)(2,1)S(1)} %collective-permut, ...), custom_call_target="tpu_custom_call" | custom-call | flops 419430400 | bytes 4000000 | tf_op jit(solution)/shard_map/pallas_call | solution.py:420
  43.5 1.5 %collective-permute-start.4 = (bf16[240,256]{1,0:T(8,128)(2,1)S(1)}, bf16[240,256]{1,0:T(8,128)(2,1)S(1)}, u32[]{:S(2)}, u32[]{:S(2)}) collective-permute-start(bf16[240,256]{1,0:T(8,128)(2,1)S(1)} %get-tuple-element.40), channel_id=1, source_target_pairs={{0,4},{2,6},{4,0},{6,2},{8,12},{10,14},{12,8},{14,10},{16,20},{18,... | collective-permute-start | bytes 368648 | tf_op jit(solution)/shard_map/ppermute | solution.py:458
  45.0 1.6 %collective-permute-start.5 = (bf16[240,256]{1,0:T(8,128)(2,1)S(1)}, bf16[240,256]{1,0:T(8,128)(2,1)S(1)}, u32[]{:S(2)}, u32[]{:S(2)}) collective-permute-start(bf16[240,256]{1,0:T(8,128)(2,1)S(1)} %get-tuple-element.41), channel_id=1, source_target_pairs={{0,8},{2,10},{4,12},{6,14},{8,0},{10,2},{12,4},{14,6},{16,24},{18,... | collective-permute-start | bytes 368648 | tf_op jit(solution)/shard_map/ppermute | solution.py:458
  46.6 0.0 collective-permute-done.7.refs_5_
  46.6 0.4 collective-permute-start.6
  47.0 0.0 collective-permute-done.8.refs_6_
  47.0 5.0 %collective-permute-done.9.refs_7_ = bf16[256,1280]{1,0:T(8,128)(2,1)S(1)} collective-permute-done((bf16[256,1280]{1,0:T(8,128)(2,1)}, bf16[256,1280]{1,0:T(8,128)(2,1)S(1)}, u32[]{:S(2)}, u32[]{:S(2)}) %collective-permute-start.9) | collective-permute-done | bytes 655392 | tf_op jit(solution)/shard_map/ppermute | solution.py:458
  52.0 2.3 %collective-permute-done.4.refs_1_ = bf16[240,256]{1,0:T(8,128)(2,1)S(1)} collective-permute-done((bf16[240,256]{1,0:T(8,128)(2,1)S(1)}, bf16[240,256]{1,0:T(8,128)(2,1)S(1)}, u32[]{:S(2)}, u32[]{:S(2)}) %collective-permute-start.4) | collective-permute-done | bytes 122912 | tf_op jit(solution)/shard_map/ppermute | solution.py:458
  54.3 0.2 collective-permute-done.5.refs_2_
  54.5 1.1 %collective-permute-done.6.refs_3_ = bf16[240,256]{1,0:T(8,128)(2,1)S(1)} collective-permute-done((bf16[240,256]{1,0:T(8,128)(2,1)S(1)}, bf16[240,256]{1,0:T(8,128)(2,1)S(1)}, u32[]{:S(2)}, u32[]{:S(2)}) %collective-permute-start.6) | collective-permute-done | bytes 122912 | tf_op jit(solution)/shard_map/ppermute | solution.py:458
  55.6 0.0 copy-done.7
  55.6 0.9 %shard_map.137 = (f32[120,1280]{1,0:T(8,128)S(1)}, bf16[120,1280]{1,0:T(8,128)(2,1)S(1)}) custom-call(bf16[240,256]{1,0:T(8,128)(2,1)S(1)} %get-tuple-element.39.refs_0_, bf16[240,256]{1,0:T(8,128)(2,1)S(1)} %collective-permute-done.4.refs_1_, bf16[240,256]{1,0:T(8,128)(2,1)S(1)} %collective-permute-done.5.refs_2_, ...), custom_call_target="tpu_custom_call" | custom-call | flops 629145600 | bytes 4000000 | tf_op jit(solution)/shard_map/pallas_call | solution.py:420
  56.6 0.1 collective-permute-start.10
  56.7 1.6 %collective-permute-start.2 = (bf16[128,1280]{1,0:T(8,128)(2,1)S(1)}, bf16[128,1280]{1,0:T(8,128)(2,1)S(1)}, u32[]{:S(2)}, u32[]{:S(2)}) collective-permute-start(bf16[128,1280]{1,0:T(8,128)(2,1)S(1)} %get-tuple-element.32.own_ref), channel_id=1, source_target_pairs={{0,1},{1,0},{2,3},{3,2},{4,5},{5,4},{6,7},{7,6},{8,9},{9,8},{10,11... | collective-permute-start | bytes 983048 | tf_op jit(solution)/shard_map/ppermute | solution.py:455
  58.2 1.5 %collective-permute-start.11 = (bf16[240,256]{1,0:T(8,128)(2,1)S(1)}, bf16[240,256]{1,0:T(8,128)(2,1)S(1)}, u32[]{:S(2)}, u32[]{:S(2)}) collective-permute-start(bf16[240,256]{1,0:T(8,128)(2,1)S(1)} %get-tuple-element.47), channel_id=1, source_target_pairs={{0,4},{2,6},{4,0},{6,2},{8,12},{10,14},{12,8},{14,10},{16,20},{18,... | collective-permute-start | bytes 368648 | tf_op jit(solution)/shard_map/ppermute | solution.py:458
  59.7 1.6 %collective-permute-start.12 = (bf16[240,256]{1,0:T(8,128)(2,1)S(1)}, bf16[240,256]{1,0:T(8,128)(2,1)S(1)}, u32[]{:S(2)}, u32[]{:S(2)}) collective-permute-start(bf16[240,256]{1,0:T(8,128)(2,1)S(1)} %get-tuple-element.48), channel_id=1, source_target_pairs={{0,8},{2,10},{4,12},{6,14},{8,0},{10,2},{12,4},{14,6},{16,24},{18,... | collective-permute-start | bytes 368648 | tf_op jit(solution)/shard_map/ppermute | solution.py:458
  61.3 0.4 collective-permute-start.13
  61.7 0.0 collective-permute-done.10
  61.7 0.1 add_convert_fusion._.refs_8_
  61.8 1.8 %collective-permute-done.11.refs_1_ = bf16[240,256]{1,0:T(8,128)(2,1)S(1)} collective-permute-done((bf16[240,256]{1,0:T(8,128)(2,1)S(1)}, bf16[240,256]{1,0:T(8,128)(2,1)S(1)}, u32[]{:S(2)}, u32[]{:S(2)}) %collective-permute-start.11) | collective-permute-done | bytes 122912 | tf_op jit(solution)/shard_map/ppermute | solution.py:458
  63.6 2.3 %collective-permute-done.12.refs_2_ = bf16[240,256]{1,0:T(8,128)(2,1)S(1)} collective-permute-done((bf16[240,256]{1,0:T(8,128)(2,1)S(1)}, bf16[240,256]{1,0:T(8,128)(2,1)S(1)}, u32[]{:S(2)}, u32[]{:S(2)}) %collective-permute-start.12) | collective-permute-done | bytes 122912 | tf_op jit(solution)/shard_map/ppermute | solution.py:458
  65.9 1.5 %collective-permute-done.13.refs_3_ = bf16[240,256]{1,0:T(8,128)(2,1)S(1)} collective-permute-done((bf16[240,256]{1,0:T(8,128)(2,1)S(1)}, bf16[240,256]{1,0:T(8,128)(2,1)S(1)}, u32[]{:S(2)}, u32[]{:S(2)}) %collective-permute-start.13) | collective-permute-done | bytes 122912 | tf_op jit(solution)/shard_map/ppermute | solution.py:458
  67.4 0.9 %shard_map.139 = (f32[120,1280]{1,0:T(8,128)S(1)}, bf16[120,1280]{1,0:T(8,128)(2,1)S(1)}) custom-call(bf16[240,256]{1,0:T(8,128)(2,1)S(1)} %get-tuple-element.46.refs_0_, bf16[240,256]{1,0:T(8,128)(2,1)S(1)} %collective-permute-done.11.refs_1_, bf16[240,256]{1,0:T(8,128)(2,1)S(1)} %collective-permute-done.12.refs_2_, ...), custom_call_target="tpu_custom_call" | custom-call | flops 629145600 | bytes 4000000 | tf_op jit(solution)/shard_map/pallas_call | solution.py:420
  68.4 0.1 collective-permute-start.14
  68.5 2.7 %collective-permute-start.15 = (bf16[120,1280]{1,0:T(8,128)(2,1)S(1)}, bf16[120,1280]{1,0:T(8,128)(2,1)S(1)}, u32[]{:S(2)}, u32[]{:S(2)}) collective-permute-start(bf16[120,1280]{1,0:T(8,128)(2,1)S(1)} %add_convert_fusion._.refs_8_), channel_id=1, source_target_pairs={{0,16},{2,18},{4,20},{6,22},{8,24},{10,26},{12,28},{14,30},{16,0},... | collective-permute-start | bytes 921608 | tf_op jit(solution)/shard_map/ppermute | solution.py:458
  71.1 0.0 collective-permute-done.2.other_ref
  71.1 2.1 %shard_map.138 = bf16[128,5120]{1,0:T(8,128)(2,1)} custom-call(s32[1]{0:T(128)S(6)} %copy.14.live_ref, s32[1,64]{1,0:T(1,128)S(1)} %copy-done.16, bf16[128,1280]{1,0:T(8,128)(2,1)S(1)} %get-tuple-element.32.own_ref, bf16[128,1280]{1,0:T(8,128)(2,1)S(1)} %collective-permute-done.2.other_ref, bf16[120,1280]{1,0:T(8,128)(2,1)S(1)} %add_convert_fusion._.refs_8_), custom_call_target="tpu_custom_call" | custom-call | flops 335544320 | bytes 4000000 | tf_op jit(solution)/shard_map/pallas_call | solution.py:420
  73.2 0.0 collective-permute-done.14
  73.2 12.4 %collective-permute-done.15 = bf16[120,1280]{1,0:T(8,128)(2,1)S(1)} collective-permute-done((bf16[120,1280]{1,0:T(8,128)(2,1)S(1)}, bf16[120,1280]{1,0:T(8,128)(2,1)S(1)}, u32[]{:S(2)}, u32[]{:S(2)}) %collective-permute-start.15) | collective-permute-done | bytes 307232 | tf_op jit(solution)/shard_map/ppermute | solution.py:458
  85.6 0.9 %add_bitcast_fusion = f32[1,120,1280]{2,1,0:T(8,128)} fusion(bf16[120,1280]{1,0:T(8,128)(2,1)S(1)} %collective-permute-done.15, f32[120,1280]{1,0:T(8,128)S(1)} %get-tuple-element.50, bf16[120,1280]{1,0:T(8,128)(2,1)S(1)} %collective-permute-done.14), kind=kLoop, calls=%fused_computation | loop fusion | flops 614400 | bytes 1843200 | tf_op jit(solution)/shard_map/broadcast_in_dim | solution.py:588
  (13 shorter events, 0.0 us)
Async XLA Ops:
  1.3 1.1 %copy-start.4 = (bf16[256,1280]{1,0:T(8,128)(2,1)S(1)}, bf16[256,1280]{1,0:T(8,128)(2,1)}, u32[]{:S(2)}) copy-start(bf16[256,1280]{1,0:T(8,128)(2,1)} %patches_ref.1) | copy-start | bytes 1966084
  2.4 0.7 copy-start.10
  3.1 0.7 copy-start.11
  3.8 0.7 copy-start.12
  10.6 0.9 %copy-start.1 = (bf16[3,256,640]{2,1,0:T(8,128)(2,1)}, bf16[3,256,640]{2,1,0:T(8,128)(2,1)S(1)}, u32[]{:S(2)}) copy-start(bf16[3,256,640]{2,1,0:T(8,128)(2,1)S(1)} %get-tuple-element.27.triple_ref) | copy-start | bytes 2949124
  11.6 0.8 copy-start.8
  12.4 9.7 %copy-start = (bf16[640,1280]{1,0:T(8,128)(2,1)S(1)}, bf16[640,1280]{1,0:T(8,128)(2,1)}, u32[]{:S(2)}) copy-start(bf16[640,1280]{1,0:T(8,128)(2,1)} %proj_ref.5) | copy-start | bytes 4915204
  12.4 9.7 %copy-start.16 = (s32[1,64]{1,0:T(1,128)S(1)}, s32[1,64]{1,0:T(1,128)}, u32[]{:S(2)}) copy-start(s32[1,64]{1,0:T(1,128)} %places_ref.3) | copy-start | bytes 772
  12.4 15.6 %collective-permute-start = (bf16[128,1280]{1,0:T(8,128)(2,1)}, bf16[128,1280]{1,0:T(8,128)(2,1)S(1)}, u32[]{:S(2)}, u32[]{:S(2)}) collective-permute-start(bf16[128,1280]{1,0:T(8,128)(2,1)} %get-tuple-element.29), channel_id=1, source_target_pairs={{0,1},{1,0},{2,3},{3,2},{4,5},{5,4},{6,7},{7,6},{8,9},{9,8},{10,11... | collective-permute-start | bytes 983048 | tf_op jit(solution)/shard_map/ppermute | solution.py:455
  18.4 11.9 %collective-permute-start.1 = (bf16[128,1280]{1,0:T(8,128)(2,1)}, bf16[128,1280]{1,0:T(8,128)(2,1)S(1)}, u32[]{:S(2)}, u32[]{:S(2)}) collective-permute-start(bf16[128,1280]{1,0:T(8,128)(2,1)} %get-tuple-element.31), channel_id=1, source_target_pairs={{0,1},{1,0},{2,3},{3,2},{4,5},{5,4},{6,7},{7,6},{8,9},{9,8},{10,11... | collective-permute-start | bytes 983048 | tf_op jit(solution)/shard_map/ppermute | solution.py:455
  18.6 28.0 %collective-permute-start.7 = (bf16[256,1280]{1,0:T(8,128)(2,1)}, bf16[256,1280]{1,0:T(8,128)(2,1)S(1)}, u32[]{:S(2)}, u32[]{:S(2)}) collective-permute-start(bf16[256,1280]{1,0:T(8,128)(2,1)} %get-tuple-element.43.refs_4_), channel_id=1, source_target_pairs={{0,4},{2,6},{4,0},{6,2},{8,12},{10,14},{12,8},{14,10},{16,20},{18,... | collective-permute-start | bytes 1966088 | tf_op jit(solution)/shard_map/ppermute | solution.py:458
  20.5 26.5 %collective-permute-start.8 = (bf16[256,1280]{1,0:T(8,128)(2,1)}, bf16[256,1280]{1,0:T(8,128)(2,1)S(1)}, u32[]{:S(2)}, u32[]{:S(2)}) collective-permute-start(bf16[256,1280]{1,0:T(8,128)(2,1)} %get-tuple-element.43.refs_4_), channel_id=1, source_target_pairs={{0,8},{2,10},{4,12},{6,14},{8,0},{10,2},{12,4},{14,6},{16,24},{18,... | collective-permute-start | bytes 1966088 | tf_op jit(solution)/shard_map/ppermute | solution.py:458
  22.1 29.9 %collective-permute-start.9 = (bf16[256,1280]{1,0:T(8,128)(2,1)}, bf16[256,1280]{1,0:T(8,128)(2,1)S(1)}, u32[]{:S(2)}, u32[]{:S(2)}) collective-permute-start(bf16[256,1280]{1,0:T(8,128)(2,1)} %get-tuple-element.43.refs_4_), channel_id=1, source_target_pairs={{0,12},{2,14},{4,8},{6,10},{8,4},{10,6},{12,0},{14,2},{16,28},{18,... | collective-permute-start | bytes 1966088 | tf_op jit(solution)/shard_map/ppermute | solution.py:458
  22.1 1.2 %copy-start.2 = (bf16[3,256,640]{2,1,0:T(8,128)(2,1)S(1)}, bf16[3,256,640]{2,1,0:T(8,128)(2,1)}, u32[]{:S(2)}) copy-start(bf16[3,256,640]{2,1,0:T(8,128)(2,1)} %copy-done.1) | copy-start | bytes 2949124
  23.3 1.3 %copy-start.6 = (bf16[128,5120]{1,0:T(8,128)(2,1)S(1)}, bf16[128,5120]{1,0:T(8,128)(2,1)}, u32[]{:S(2)}) copy-start(bf16[128,5120]{1,0:T(8,128)(2,1)} %grad_hbm.1) | copy-start | bytes 3932164
  24.6 5.7 %copy-start.5 = (bf16[256,1280]{1,0:T(8,128)(2,1)S(1)}, bf16[256,1280]{1,0:T(8,128)(2,1)}, u32[]{:S(2)}) copy-start(bf16[256,1280]{1,0:T(8,128)(2,1)} %patches_ref.1) | copy-start | bytes 1966084
  24.6 5.7 %copy-start.13 = (f32[1280]{0:T(1024)S(1)}, f32[1280]{0:T(1024)}, u32[]{:S(2)}) copy-start(f32[1280]{0:T(1024)} %b_ref.3) | copy-start | bytes 15364
  24.6 5.7 %copy-start.14 = (f32[1280]{0:T(1024)S(1)}, f32[1280]{0:T(1024)}, u32[]{:S(2)}) copy-start(f32[1280]{0:T(1024)} %gain_ref.3) | copy-start | bytes 15364
  24.6 5.7 %copy-start.15 = (f32[1280]{0:T(1024)S(1)}, f32[1280]{0:T(1024)}, u32[]{:S(2)}) copy-start(f32[1280]{0:T(1024)} %bias_ref.3) | copy-start | bytes 15364
  28.0 4.8 %copy-start.3 = (bf16[3,256,640]{2,1,0:T(8,128)(2,1)S(1)}, bf16[3,256,640]{2,1,0:T(8,128)(2,1)}, u32[]{:S(2)}) copy-start(bf16[3,256,640]{2,1,0:T(8,128)(2,1)} %copy-done.1) | copy-start | bytes 2949124
  30.9 8.9 %collective-permute-start.3 = (bf16[128,1280]{1,0:T(8,128)(2,1)S(1)}, bf16[128,1280]{1,0:T(8,128)(2,1)S(1)}, u32[]{:S(2)}, u32[]{:S(2)}) collective-permute-start(bf16[128,1280]{1,0:T(8,128)(2,1)S(1)} %get-tuple-element.33.row_ref), channel_id=1, source_target_pairs={{0,1},{1,0},{2,3},{3,2},{4,5},{5,4},{6,7},{7,6},{8,9},{9,8},{10,11... | collective-permute-start | bytes 983048 | tf_op jit(solution)/shard_map/ppermute | solution.py:455
  32.7 7.1 %copy-start.9 = (bf16[8,128,256]{2,1,0:T(8,128)(2,1)S(1)}, bf16[8,128,256]{2,1,0:T(8,128)(2,1)}, u32[]{:S(2)}) copy-start(bf16[8,128,256]{2,1,0:T(8,128)(2,1)} %copy-done.8) | copy-start | bytes 1572868
  39.8 15.8 %copy-start.7 = (bf16[256,1280]{1,0:T(8,128)(2,1)S(1)}, bf16[256,1280]{1,0:T(8,128)(2,1)}, u32[]{:S(2)}) copy-start(bf16[256,1280]{1,0:T(8,128)(2,1)} %get-tuple-element.43.refs_4_) | copy-start | bytes 1966084
  43.5 10.8 %collective-permute-start.4 = (bf16[240,256]{1,0:T(8,128)(2,1)S(1)}, bf16[240,256]{1,0:T(8,128)(2,1)S(1)}, u32[]{:S(2)}, u32[]{:S(2)}) collective-permute-start(bf16[240,256]{1,0:T(8,128)(2,1)S(1)} %get-tuple-element.40), channel_id=1, source_target_pairs={{0,4},{2,6},{4,0},{6,2},{8,12},{10,14},{12,8},{14,10},{16,20},{18,... | collective-permute-start | bytes 368648 | tf_op jit(solution)/shard_map/ppermute | solution.py:458
  45.0 9.5 %collective-permute-start.5 = (bf16[240,256]{1,0:T(8,128)(2,1)S(1)}, bf16[240,256]{1,0:T(8,128)(2,1)S(1)}, u32[]{:S(2)}, u32[]{:S(2)}) collective-permute-start(bf16[240,256]{1,0:T(8,128)(2,1)S(1)} %get-tuple-element.41), channel_id=1, source_target_pairs={{0,8},{2,10},{4,12},{6,14},{8,0},{10,2},{12,4},{14,6},{16,24},{18,... | collective-permute-start | bytes 368648 | tf_op jit(solution)/shard_map/ppermute | solution.py:458
  46.6 9.0 %collective-permute-start.6 = (bf16[240,256]{1,0:T(8,128)(2,1)S(1)}, bf16[240,256]{1,0:T(8,128)(2,1)S(1)}, u32[]{:S(2)}, u32[]{:S(2)}) collective-permute-start(bf16[240,256]{1,0:T(8,128)(2,1)S(1)} %get-tuple-element.42), channel_id=1, source_target_pairs={{0,12},{2,14},{4,8},{6,10},{8,4},{10,6},{12,0},{14,2},{16,28},{18,... | collective-permute-start | bytes 368648 | tf_op jit(solution)/shard_map/ppermute | solution.py:458
  56.6 5.1 %collective-permute-start.10 = (bf16[120,1280]{1,0:T(8,128)(2,1)S(1)}, bf16[120,1280]{1,0:T(8,128)(2,1)S(1)}, u32[]{:S(2)}, u32[]{:S(2)}) collective-permute-start(bf16[120,1280]{1,0:T(8,128)(2,1)S(1)} %get-tuple-element.45), channel_id=1, source_target_pairs={{0,2},{2,0},{4,6},{6,4},{8,10},{10,8},{12,14},{14,12},{16,18},{18,... | collective-permute-start | bytes 921608 | tf_op jit(solution)/shard_map/ppermute | solution.py:458
  56.7 14.5 %collective-permute-start.2 = (bf16[128,1280]{1,0:T(8,128)(2,1)S(1)}, bf16[128,1280]{1,0:T(8,128)(2,1)S(1)}, u32[]{:S(2)}, u32[]{:S(2)}) collective-permute-start(bf16[128,1280]{1,0:T(8,128)(2,1)S(1)} %get-tuple-element.32.own_ref), channel_id=1, source_target_pairs={{0,1},{1,0},{2,3},{3,2},{4,5},{5,4},{6,7},{7,6},{8,9},{9,8},{10,11... | collective-permute-start | bytes 983048 | tf_op jit(solution)/shard_map/ppermute | solution.py:455
  58.2 5.4 %collective-permute-start.11 = (bf16[240,256]{1,0:T(8,128)(2,1)S(1)}, bf16[240,256]{1,0:T(8,128)(2,1)S(1)}, u32[]{:S(2)}, u32[]{:S(2)}) collective-permute-start(bf16[240,256]{1,0:T(8,128)(2,1)S(1)} %get-tuple-element.47), channel_id=1, source_target_pairs={{0,4},{2,6},{4,0},{6,2},{8,12},{10,14},{12,8},{14,10},{16,20},{18,... | collective-permute-start | bytes 368648 | tf_op jit(solution)/shard_map/ppermute | solution.py:458
  59.7 6.2 %collective-permute-start.12 = (bf16[240,256]{1,0:T(8,128)(2,1)S(1)}, bf16[240,256]{1,0:T(8,128)(2,1)S(1)}, u32[]{:S(2)}, u32[]{:S(2)}) collective-permute-start(bf16[240,256]{1,0:T(8,128)(2,1)S(1)} %get-tuple-element.48), channel_id=1, source_target_pairs={{0,8},{2,10},{4,12},{6,14},{8,0},{10,2},{12,4},{14,6},{16,24},{18,... | collective-permute-start | bytes 368648 | tf_op jit(solution)/shard_map/ppermute | solution.py:458
  61.3 6.1 %collective-permute-start.13 = (bf16[240,256]{1,0:T(8,128)(2,1)S(1)}, bf16[240,256]{1,0:T(8,128)(2,1)S(1)}, u32[]{:S(2)}, u32[]{:S(2)}) collective-permute-start(bf16[240,256]{1,0:T(8,128)(2,1)S(1)} %get-tuple-element.49), channel_id=1, source_target_pairs={{0,12},{2,14},{4,8},{6,10},{8,4},{10,6},{12,0},{14,2},{16,28},{18,... | collective-permute-start | bytes 368648 | tf_op jit(solution)/shard_map/ppermute | solution.py:458
  68.4 4.8 %collective-permute-start.14 = (bf16[120,1280]{1,0:T(8,128)(2,1)S(1)}, bf16[120,1280]{1,0:T(8,128)(2,1)S(1)}, u32[]{:S(2)}, u32[]{:S(2)}) collective-permute-start(bf16[120,1280]{1,0:T(8,128)(2,1)S(1)} %get-tuple-element.51), channel_id=1, source_target_pairs={{0,2},{2,0},{4,6},{6,4},{8,10},{10,8},{12,14},{14,12},{16,18},{18,... | collective-permute-start | bytes 921608 | tf_op jit(solution)/shard_map/ppermute | solution.py:458
  68.5 17.2 %collective-permute-start.15 = (bf16[120,1280]{1,0:T(8,128)(2,1)S(1)}, bf16[120,1280]{1,0:T(8,128)(2,1)S(1)}, u32[]{:S(2)}, u32[]{:S(2)}) collective-permute-start(bf16[120,1280]{1,0:T(8,128)(2,1)S(1)} %add_convert_fusion._.refs_8_), channel_id=1, source_target_pairs={{0,16},{2,18},{4,20},{6,22},{8,24},{10,26},{12,28},{14,30},{16,0},... | collective-permute-start | bytes 921608 | tf_op jit(solution)/shard_map/ppermute | solution.py:458

commit v4 on v3

--- a/solution.py
+++ b/solution.py
@@ -230,20 +230,20 @@
         out_ref[:, k * width : (k + 1) * width] = term.astype(out_ref.dtype)
 
 
-def attend(live_ref, triple_ref, start, probs_ref, attended_ref):
+def attend(live_ref, query_ref, pair_ref, probs_ref, attended_ref):
     half, rows = probs_ref.shape[1:]
     live = lax.broadcasted_iota(jnp.int32, (half, rows), 1) < 4 * live_ref[0]
     steep = HEAD ** (-0.5) * 1.4426950408889634
     for h in range(probs_ref.shape[0]):
         cols = slice(h * HEAD, (h + 1) * HEAD)
-        scores = trailing(triple_ref[0, pl.ds(start, half), cols], triple_ref[1, :, cols])
+        scores = trailing(query_ref[:, cols], pair_ref[0, :, cols])
         scores = jnp.where(live, scores, -1e30)
         powers = jnp.exp2((scores - jnp.max(scores, axis=-1, keepdims=True)) * steep)
         weights = powers * (1.0 / jnp.sum(powers, axis=-1, keepdims=True))
         weights = weights.astype(jnp.bfloat16)
         probs_ref[h] = weights
         attended_ref[:, cols] = jnp.dot(
-            weights, triple_ref[2, :, cols], preferred_element_type=jnp.float32
+            weights, pair_ref[1, :, cols], preferred_element_type=jnp.float32
         ).astype(jnp.bfloat16)
 
 
@@ -255,7 +255,10 @@
     patches_hbm,
     w_hbm,
     proj_hbm,
-    triple_ref,
+    query_ref,
+    pair_ref,
+    own_ref,
+    wq_ref,
     probs_ref,
     send_ref,
     patches_ref,
@@ -267,17 +270,24 @@
 ):
     came = begin(
         (patches_hbm, w_hbm.at[0], w_hbm.at[1], w_hbm.at[2], proj_hbm),
-        (patches_ref, w_ref.at[0], w_ref.at[1], w_ref.at[2], proj_ref),
+        (patches_ref, wq_ref, w_ref.at[0], w_ref.at[1], proj_ref),
         sems,
     )
     came[0].wait()
     normed_ref[...] = norm_low(patches_ref, gain_ref, bias_ref)
-    for t in range(3):
+    half = send_ref.shape[0]
+    start = half_start(half, False)
+    came[1].wait()
+    part = jnp.dot(
+        normed_ref[pl.ds(start, half), :], wq_ref[...], preferred_element_type=jnp.float32
+    )
+    query_ref[...] = (part + b_ref[0:1, :]).astype(jnp.bfloat16)
+    own_ref[...] = normed_ref[pl.ds(half_start(half, True), half), :]
+    for t in (1, 2):
         came[1 + t].wait()
-        part = jnp.dot(normed_ref[...], w_ref[t], preferred_element_type=jnp.float32)
-        triple_ref[t] = (part + b_ref[t : t + 1, :]).astype(jnp.bfloat16)
-    start = half_start(send_ref.shape[0], False)
-    attend(live_ref, triple_ref, start, probs_ref, attended_ref)
+        part = jnp.dot(normed_ref[...], w_ref[t - 1], preferred_element_type=jnp.float32)
+        pair_ref[t - 1] = (part + b_ref[t : t + 1, :]).astype(jnp.bfloat16)
+    attend(live_ref, query_ref, pair_ref, probs_ref, attended_ref)
     came[4].wait()
     send_ref[...] = jnp.dot(
         attended_ref[...], proj_ref[...], preferred_element_type=jnp.float32
@@ -288,17 +298,22 @@
     live_ref,
     places_ref,
     grad_ref,
-    triple_ref,
+    b_ref,
+    own_ref,
+    w_ref,
+    pair_ref,
     proj_ref,
+    query_ref,
     probs_ref,
     keep_ref,
     up_ref,
     attended_ref,
 ):
-    start = half_start(keep_ref.shape[0], True)
-    attend(live_ref, triple_ref, start, probs_ref, attended_ref)
+    pull(live_ref, places_ref, grad_ref, up_ref, True)
+    part = jnp.dot(own_ref[...], w_ref[...], preferred_element_type=jnp.float32)
+    query_ref[...] = (part + b_ref[0:1, :]).astype(jnp.bfloat16)
+    attend(live_ref, query_ref, pair_ref, probs_ref, attended_ref)
     keep_ref[...] = jnp.dot(attended_ref[...], proj_ref[...], preferred_element_type=jnp.float32)
-    pull(live_ref, places_ref, grad_ref, up_ref, True)
 
 
 def middle_kernel(
@@ -327,30 +342,29 @@
     back_ref[...] = normalize_back(upstream, unit_rows, inverse, gain).astype(jnp.bfloat16)
 
 
-def attend_back(row_ref, proj_ref, triple_ref, probs_ref, back_ref, start, put):
-    half = row_ref.shape[0]
+def attend_back(row_ref, proj_ref, query_ref, pair_ref, probs_ref, back_ref, put):
     back_ref[...] = trailing(row_ref[...], proj_ref[...]).astype(jnp.bfloat16)
     scaling = HEAD ** (-0.5)
     for h in range(probs_ref.shape[0]):
         cols = slice(h * HEAD, (h + 1) * HEAD)
         back = back_ref[:, cols]
         weights = probs_ref[h]
-        prob_grad = trailing(back, triple_ref[2, :, cols])
+        prob_grad = trailing(back, pair_ref[1, :, cols])
         wide = weights.astype(jnp.float32)
         inner = jnp.sum(prob_grad * wide, axis=-1, keepdims=True)
         score_grad = (wide * (prob_grad - inner)).astype(jnp.bfloat16)
         query_grad = lax.dot_general(
-            triple_ref[1, :, cols],
+            pair_ref[0, :, cols],
             score_grad,
             (((0,), (1,)), ((), ())),
             preferred_element_type=jnp.float32,
         )
-        key_grad = leading(triple_ref[0, pl.ds(start, half), cols], score_grad)
+        key_grad = leading(query_ref[:, cols], score_grad)
         put(h, query_grad * scaling, key_grad * scaling, leading(back, weights))
 
 
 def own_back_kernel(
-    row_ref, proj_ref, triple_ref, probs_ref, query_ref, key_ref, value_ref, back_ref
+    row_ref, proj_ref, q_ref, pair_ref, probs_ref, query_ref, key_ref, value_ref, back_ref
 ):
     def put(h, query_grad, key_grad, value_grad):
         rows = slice(h * HEAD, (h + 1) * HEAD)
@@ -358,12 +372,11 @@
         key_ref[rows, :] = key_grad
         value_ref[rows, :] = value_grad
 
-    start = half_start(row_ref.shape[0], True)
-    attend_back(row_ref, proj_ref, triple_ref, probs_ref, back_ref, start, put)
+    attend_back(row_ref, proj_ref, q_ref, pair_ref, probs_ref, back_ref, put)
 
 
 def other_back_kernel(
-    row_ref, proj_ref, triple_ref, probs_ref, query_ref, key_ref, value_ref, *refs
+    row_ref, proj_ref, q_ref, pair_ref, probs_ref, query_ref, key_ref, value_ref, *refs
 ):
     outs, (back_ref, slots_ref) = refs[:8], refs[8:]
     half = row_ref.shape[0]
@@ -391,7 +404,7 @@
         side, slot, place = where(2, h)
         slots_ref[side, slot, place, :] = (value_ref[rows, :] + value_grad).astype(jnp.bfloat16)
 
-    attend_back(row_ref, proj_ref, triple_ref, probs_ref, back_ref, start, put)
+    attend_back(row_ref, proj_ref, q_ref, pair_ref, probs_ref, back_ref, put)
     for k, out_ref in enumerate(outs):
         out_ref[...] = slots_ref[k // 4, k % 4]
 
@@ -460,6 +473,7 @@
     half = rows // 2
     part, wide = shape((half, width), low), shape((half, width), jnp.float32)
     probs_half = shape((heads, half, rows), low)
+    query = shape((half, local), low)
     attended = pltpu.VMEM((half, local), low)
     block = 3 * local // 8
     normed, up_send = call(
@@ -484,9 +498,9 @@
     up_came = swap(up_send)
     normed_of = [normed] + [flip(normed, q << 1) for q in (1, 2)]
     normed_of += [flip(normed, 3 << 1)]
-    triple, other_probs, part_send = call(
+    other_query, pair, own_normed, w_query, other_probs, part_send = call(
         first_kernel,
-        (shape((3, rows, local), low), probs_half, part),
+        (query, shape((2, rows, local), low), part, shape((width, local), low), probs_half, part),
         "svvvaaa",
         7 * rows * width * local,
         (
@@ -500,21 +514,30 @@
         ),
         (
             pltpu.VMEM((rows, width), low),
-            pltpu.VMEM((3, width, local), low),
+            pltpu.VMEM((2, width, local), low),
             pltpu.VMEM((local, width), low),
             attended,
             pltpu.VMEM((rows, width), low),
             pltpu.SemaphoreType.DMA((5,)),
         ),
-        limit=51,
+        limit=49,
     )
     part_came = swap(part_send)
-    own_probs, part_keep, up_keep = call(
+    own_query, own_probs, part_keep, up_keep = call(
         second_kernel,
-        (probs_half, wide, part),
-        "svvvv",
-        3 * half * width * local,
-        (clip_tokens, positions, grad_placed, triple, w_proj),
+        (query, probs_half, wide, part),
+        "svvvvvvv",
+        5 * half * width * local,
+        (
+            clip_tokens,
+            positions,
+            grad_placed,
+            b_qkv,
+            own_normed,
+            w_query,
+            pair,
+            w_proj,
+        ),
         (attended,),
     )
     merged, own_rows = call(
@@ -542,17 +565,26 @@
             shape((local, rows), jnp.float32),
             shape((local, rows), jnp.float32),
         ),
-        "vvvv",
+        "vvvvv",
         4 * half * width * local,
-        (own_rows, w_proj, triple, own_probs),
+        (own_rows, w_proj, own_query, pair, own_probs),
         (attended,),
     )
     sent = call(
         other_back_kernel,
         (shape((block, rows), low),) * 8,
-        "v" * 7,
+        "v" * 8,
         4 * half * width * local,
-        (other_rows, w_proj, triple, other_probs, query_own, key_own, value_own),
+        (
+            other_rows,
+            w_proj,
+            other_query,
+            pair,
+            other_probs,
+            query_own,
+            key_own,
+            value_own,
+        ),
         (attended, pltpu.VMEM((2, 4, block, rows), low)),
     )
 

time: 87 us -> 88.5 us (1.017)
  local copies, waits for them, and re-layouts: 7.46 us -> 10.6 us
  waiting for transfers between devices: 32.6 us -> 30.4 us
    unnamed x34 -> x44, local copies, waits for them, and re-layouts: 7.46 us -> 10.6 us
    ppermute x4, waiting for transfers between devices: 5.91 us -> 4.68 us  [swap(): return lax.ppermute(value, 'seq', [(0, 1), (1, 0)])]
    ppermute x12, waiting for transfers between devices: 26.7 us -> 25.7 us  [flip(): return lax.ppermute(value, 'clip', [(i, i ^ bits) for i in range(n_clip)])]
where the time goes in v4:
time: 88.5 us; the launch traced here: 88 us
  waiting for transfers between devices  30.4 us (34%)
  Pallas kernels  24.8 us (28%)
  starting transfers between devices  19.9 us (22%)
  local copies, waits for them, and re-layouts  10.6 us (12%)
  between operations  1.44 us (2%)
  other arithmetic  0.99 us (1%)
    ppermute x12, waiting for transfers between devices, flip(): return lax.ppermute(value, 'clip', [(i, i ^ bits) for i in range(n_clip)])  25.7 us
    pallas_call x9, Pallas kernels, call(): pl.pallas_call(kernel, out_shape=outs, in_specs=[spec[kind] for kind in k...  24.8 us
    ppermute x12, starting transfers between devices, flip(): return lax.ppermute(value, 'clip', [(i, i ^ bits) for i in range(n_clip)])  13.4 us
    unnamed x44, local copies, waits for them, and re-layouts  10.6 us
    ppermute x4, starting transfers between devices, swap(): return lax.ppermute(value, 'seq', [(0, 1), (1, 0)])  6.5 us
    ppermute x4, waiting for transfers between devices, swap(): return lax.ppermute(value, 'seq', [(0, 1), (1, 0)])  4.68 us
  transfers between devices with their start and end apart: 16, of which 10 were waited for; matrix products, arithmetic and copies ran while one was open for 0% of the time, Pallas kernels for 20%

profile of v4, /device:TPU:0, one launch (start us, length us, event | category | flops | bytes accessed | tf_op | source)
XLA Modules:
  0.0 88.0 jit_solution(11366236981087910533)
XLA Ops:
  1.3 0.0 copy-start.1
  1.3 1.1 %copy-done.1 = bf16[256,1280]{1,0:T(8,128)(2,1)S(1)} copy-done((bf16[256,1280]{1,0:T(8,128)(2,1)S(1)}, bf16[256,1280]{1,0:T(8,128)(2,1)}, u32[]{:S(2)}) %copy-start.1) | copy-done | bytes 655384
  2.4 0.7 copy-done.14
  3.1 0.7 copy-done.16
  3.8 0.7 copy-done.17
  4.5 5.9 %shard_map.131 = (bf16[128,640]{1,0:T(8,128)(2,1)S(1)}, bf16[2,256,640]{2,1,0:T(8,128)(2,1)S(1)}, bf16[128,1280]{1,0:T(8,128)(2,1)S(1)}, bf16[1280,640]{1,0:T(8,...) custom-call(s32[1]{0:T(128)S(6)} %copy.14.live_ref, f32[3,640]{1,0:T(4,128)S(1)} %copy-done.14, ...), custom_call_target="tpu_custom_call" | custom-call | flops 1468006400 | bytes 4000000 | tf_op jit(solution)/shard_map/pallas_call | solution.py:433
  10.3 0.0 copy-start.3
  10.4 0.8 copy-done.3
  11.2 1.2 %copy-done.8 = bf16[1280,640]{1,0:T(8,128)(2,1)} copy-done((bf16[1280,640]{1,0:T(8,128)(2,1)}, bf16[1280,640]{1,0:T(8,128)(2,1)S(1)}, u32[]{:S(2)}) %copy-start.8) | copy-done | bytes 1638424
  12.4 0.8 copy-done.10
  13.2 0.7 copy-done.12
  13.9 2.9 %collective-permute-start = (bf16[128,1280]{1,0:T(8,128)(2,1)}, bf16[128,1280]{1,0:T(8,128)(2,1)}, u32[]{:S(2)}, u32[]{:S(2)}) collective-permute-start(bf16[128,1280]{1,0:T(8,128)(2,1)} %get-tuple-element.35), channel_id=1, source_target_pairs={{0,1},{1,0},{2,3},{3,2},{4,5},{5,4},{6,7},{7,6},{8,9},{9,8},{10,11... | collective-permute-start | bytes 983048 | tf_op jit(solution)/shard_map/ppermute | solution.py:468
  16.8 3.0 %shard_map.133 = (bf16[256,1280]{1,0:T(8,128)(2,1)}, bf16[128,1280]{1,0:T(8,128)(2,1)}) custom-call(s32[1]{0:T(128)S(6)} %copy.14.live_ref, f32[1280]{0:T(1024)} %gain_hbm.1, f32[1280]{0:T(1024)} %bias_hbm.1, bf16[256,1280]{1,0:T(8,128)(2,1)} %patches_ref.1, s32[1,64]{1,0:T(1,128)} %places_ref.3, bf16[128,5120]{1,0:T(8,128)(2,1)} %grad_hbm.1), custom_call_target="tpu_custom_call" | custom-call | flops 335544320 | bytes 4000000 | tf_op jit(solution)/shard_map/pallas_call | solution.py:433
  19.8 0.2 collective-permute-start.1
  20.0 1.9 %collective-permute-start.7 = (bf16[256,1280]{1,0:T(8,128)(2,1)}, bf16[256,1280]{1,0:T(8,128)(2,1)S(1)}, u32[]{:S(2)}, u32[]{:S(2)}) collective-permute-start(bf16[256,1280]{1,0:T(8,128)(2,1)} %get-tuple-element.51.refs_4_), channel_id=1, source_target_pairs={{0,4},{2,6},{4,0},{6,2},{8,12},{10,14},{12,8},{14,10},{16,20},{18,... | collective-permute-start | bytes 1966088 | tf_op jit(solution)/shard_map/ppermute | solution.py:471
  22.0 1.6 %collective-permute-start.8 = (bf16[256,1280]{1,0:T(8,128)(2,1)}, bf16[256,1280]{1,0:T(8,128)(2,1)S(1)}, u32[]{:S(2)}, u32[]{:S(2)}) collective-permute-start(bf16[256,1280]{1,0:T(8,128)(2,1)} %get-tuple-element.51.refs_4_), channel_id=1, source_target_pairs={{0,8},{2,10},{4,12},{6,14},{8,0},{10,2},{12,4},{14,6},{16,24},{18,... | collective-permute-start | bytes 1966088 | tf_op jit(solution)/shard_map/ppermute | solution.py:471
  23.5 0.0 collective-permute-start.9
  23.5 0.0 copy-done
  23.5 0.0 copy-done.15
  23.5 0.0 copy-done.21
  23.6 0.0 copy-start.4
  23.6 1.1 %copy-done.4 = bf16[2,256,640]{2,1,0:T(8,128)(2,1)S(1)} copy-done((bf16[2,256,640]{2,1,0:T(8,128)(2,1)S(1)}, bf16[2,256,640]{2,1,0:T(8,128)(2,1)}, u32[]{:S(2)}) %copy-start.4) | copy-done | bytes 655384
  24.6 1.3 %copy-done.6 = bf16[128,5120]{1,0:T(8,128)(2,1)S(1)} copy-done((bf16[128,5120]{1,0:T(8,128)(2,1)S(1)}, bf16[128,5120]{1,0:T(8,128)(2,1)}, u32[]{:S(2)}) %copy-start.6) | copy-done | bytes 1310744
  26.0 1.4 %copy-done.9 = bf16[1280,640]{1,0:T(8,128)(2,1)S(1)} copy-done((bf16[1280,640]{1,0:T(8,128)(2,1)S(1)}, bf16[1280,640]{1,0:T(8,128)(2,1)}, u32[]{:S(2)}) %copy-start.9) | copy-done | bytes 1638424
  27.4 3.2 %shard_map.132 = (bf16[128,640]{1,0:T(8,128)(2,1)S(1)}, bf16[8,128,256]{2,1,0:T(8,128)(2,1)S(1)}, f32[128,1280]{1,0:T(8,128)S(1)}, bf16[128,1280]{1,0:T(8,128)(2,1)S(1)}) custom-call(s32[1]{0:T(128)S(6)} %copy.14.live_ref, s32[1,64]{1,0:T(1,128)S(1)} %copy-done.21, bf16[128,5120]{1,0:T(8,128)(2,1)S(1)} %copy-done.6, f32[3,640]{1,0:T(4,128)S(1)} %copy-done.15, ...), custom_call_target="tpu_custom_call" | custom-call | flops 524288000 | bytes 4000000 | tf_op jit(solution)/shard_map/pallas_call | solution.py:433
  30.6 0.0 copy-start.5
  30.6 0.0 collective-permute-done.came_ref
  30.7 1.1 %collective-permute-done.1.up_came_ref = bf16[128,1280]{1,0:T(8,128)(2,1)S(1)} collective-permute-done((bf16[128,1280]{1,0:T(8,128)(2,1)}, bf16[128,1280]{1,0:T(8,128)(2,1)S(1)}, u32[]{:S(2)}, u32[]{:S(2)}) %collective-permute-start.1) | collective-permute-done | bytes 327712 | tf_op jit(solution)/shard_map/ppermute | solution.py:468
  31.8 0.0 copy-done.2
  31.8 0.0 copy-done.20
  31.8 1.5 %shard_map.134 = (bf16[128,1280]{1,0:T(8,128)(2,1)S(1)}, bf16[128,1280]{1,0:T(8,128)(2,1)S(1)}) custom-call(f32[1280]{0:T(1024)S(1)} %copy-done.18, f32[1280]{0:T(1024)S(1)} %copy-done.19, f32[1280]{0:T(1024)S(1)} %copy-done.20, f32[128,1280]{1,0:T(8,128)S(1)} %get-tuple-element.34.keep_ref, bf16[128,1280]{1,0:T(8,128)(2,1)} %collective-permute-done.came_ref, ...), custom_call_target="tpu_custom_call" | custom-call | flops 16384000 | bytes 4000000 | tf_op jit(solution)/shard_map/pallas_call | solution.py:433
  33.3 1.8 %collective-permute-start.3 = (bf16[128,1280]{1,0:T(8,128)(2,1)S(1)}, bf16[128,1280]{1,0:T(8,128)(2,1)S(1)}, u32[]{:S(2)}, u32[]{:S(2)}) collective-permute-start(bf16[128,1280]{1,0:T(8,128)(2,1)S(1)} %get-tuple-element.39.row_ref), channel_id=1, source_target_pairs={{0,1},{1,0},{2,3},{3,2},{4,5},{5,4},{6,7},{7,6},{8,9},{9,8},{10,11... | collective-permute-start | bytes 983048 | tf_op jit(solution)/shard_map/ppermute | solution.py:468
  35.1 3.5 %shard_map.135 = (bf16[640,128]{1,0:T(8,128)(2,1)S(1)}, f32[640,256]{1,0:T(8,128)S(1)}, f32[640,256]{1,0:T(8,128)S(1)}) custom-call(bf16[128,1280]{1,0:T(8,128)(2,1)S(1)} %get-tuple-element.39.row_ref, bf16[640,1280]{1,0:T(8,128)(2,1)S(1)} %copy-done, bf16[128,640]{1,0:T(8,128)(2,1)S(1)} %get-tuple-element.42.q_ref, bf16[2,256,640]{2,1,0:T(8,128)(2,1)S(1)} %copy-done.5, ...), custom_call_target="tpu_custom_call" | custom-call | flops 419430400 | bytes 4000000 | tf_op jit(solution)/shard_map/pallas_call | solution.py:433
  38.7 3.6 %collective-permute-done.3.row_ref = bf16[128,1280]{1,0:T(8,128)(2,1)S(1)} collective-permute-done((bf16[128,1280]{1,0:T(8,128)(2,1)S(1)}, bf16[128,1280]{1,0:T(8,128)(2,1)S(1)}, u32[]{:S(2)}, u32[]{:S(2)}) %collective-permute-start.3) | collective-permute-done | bytes 327712 | tf_op jit(solution)/shard_map/ppermute | solution.py:468
  42.3 0.0 copy-done.13
  42.3 3.6 %shard_map.136 = (bf16[240,256]{1,0:T(8,128)(2,1)S(1)}, bf16[240,256]{1,0:T(8,128)(2,1)S(1)}, bf16[240,256]{1,0:T(8,128)(2,1)S(1)}, bf16[240,256]{1,0:T(8,128)(2...) custom-call(bf16[128,1280]{1,0:T(8,128)(2,1)S(1)} %collective-permut, ...), custom_call_target="tpu_custom_call" | custom-call | flops 419430400 | bytes 4000000 | tf_op jit(solution)/shard_map/pallas_call | solution.py:433
  45.9 1.6 %collective-permute-start.4 = (bf16[240,256]{1,0:T(8,128)(2,1)S(1)}, bf16[240,256]{1,0:T(8,128)(2,1)S(1)}, u32[]{:S(2)}, u32[]{:S(2)}) collective-permute-start(bf16[240,256]{1,0:T(8,128)(2,1)S(1)} %get-tuple-element.48), channel_id=1, source_target_pairs={{0,4},{2,6},{4,0},{6,2},{8,12},{10,14},{12,8},{14,10},{16,20},{18,... | collective-permute-start | bytes 368648 | tf_op jit(solution)/shard_map/ppermute | solution.py:471
  47.5 1.6 %collective-permute-start.5 = (bf16[240,256]{1,0:T(8,128)(2,1)S(1)}, bf16[240,256]{1,0:T(8,128)(2,1)S(1)}, u32[]{:S(2)}, u32[]{:S(2)}) collective-permute-start(bf16[240,256]{1,0:T(8,128)(2,1)S(1)} %get-tuple-element.49), channel_id=1, source_target_pairs={{0,8},{2,10},{4,12},{6,14},{8,0},{10,2},{12,4},{14,6},{16,24},{18,... | collective-permute-start | bytes 368648 | tf_op jit(solution)/shard_map/ppermute | solution.py:471
  49.1 0.0 collective-permute-done.7.refs_5_
  49.1 0.4 collective-permute-start.6
  49.5 0.0 collective-permute-done.8.refs_6_
  49.5 4.0 %collective-permute-done.9.refs_7_ = bf16[256,1280]{1,0:T(8,128)(2,1)S(1)} collective-permute-done((bf16[256,1280]{1,0:T(8,128)(2,1)}, bf16[256,1280]{1,0:T(8,128)(2,1)S(1)}, u32[]{:S(2)}, u32[]{:S(2)}) %collective-permute-start.9) | collective-permute-done | bytes 655392 | tf_op jit(solution)/shard_map/ppermute | solution.py:471
  53.4 2.3 %collective-permute-done.4.refs_1_ = bf16[240,256]{1,0:T(8,128)(2,1)S(1)} collective-permute-done((bf16[240,256]{1,0:T(8,128)(2,1)S(1)}, bf16[240,256]{1,0:T(8,128)(2,1)S(1)}, u32[]{:S(2)}, u32[]{:S(2)}) %collective-permute-start.4) | collective-permute-done | bytes 122912 | tf_op jit(solution)/shard_map/ppermute | solution.py:471
  55.7 0.2 collective-permute-done.5.refs_2_
  56.0 1.1 %collective-permute-done.6.refs_3_ = bf16[240,256]{1,0:T(8,128)(2,1)S(1)} collective-permute-done((bf16[240,256]{1,0:T(8,128)(2,1)S(1)}, bf16[240,256]{1,0:T(8,128)(2,1)S(1)}, u32[]{:S(2)}, u32[]{:S(2)}) %collective-permute-start.6) | collective-permute-done | bytes 122912 | tf_op jit(solution)/shard_map/ppermute | solution.py:471
  57.1 0.9 %shard_map.137 = (f32[120,1280]{1,0:T(8,128)S(1)}, bf16[120,1280]{1,0:T(8,128)(2,1)S(1)}) custom-call(bf16[240,256]{1,0:T(8,128)(2,1)S(1)} %get-tuple-element.47.refs_0_, bf16[240,256]{1,0:T(8,128)(2,1)S(1)} %collective-permute-done.4.refs_1_, bf16[240,256]{1,0:T(8,128)(2,1)S(1)} %collective-permute-done.5.refs_2_, ...), custom_call_target="tpu_custom_call" | custom-call | flops 629145600 | bytes 4000000 | tf_op jit(solution)/shard_map/pallas_call | solution.py:433
  58.1 0.1 collective-permute-start.10
  58.1 1.5 %collective-permute-start.2 = (bf16[128,1280]{1,0:T(8,128)(2,1)S(1)}, bf16[128,1280]{1,0:T(8,128)(2,1)S(1)}, u32[]{:S(2)}, u32[]{:S(2)}) collective-permute-start(bf16[128,1280]{1,0:T(8,128)(2,1)S(1)} %get-tuple-element.38.own_ref), channel_id=1, source_target_pairs={{0,1},{1,0},{2,3},{3,2},{4,5},{5,4},{6,7},{7,6},{8,9},{9,8},{10,11... | collective-permute-start | bytes 983048 | tf_op jit(solution)/shard_map/ppermute | solution.py:468
  59.7 1.5 %collective-permute-start.11 = (bf16[240,256]{1,0:T(8,128)(2,1)S(1)}, bf16[240,256]{1,0:T(8,128)(2,1)S(1)}, u32[]{:S(2)}, u32[]{:S(2)}) collective-permute-start(bf16[240,256]{1,0:T(8,128)(2,1)S(1)} %get-tuple-element.55), channel_id=1, source_target_pairs={{0,4},{2,6},{4,0},{6,2},{8,12},{10,14},{12,8},{14,10},{16,20},{18,... | collective-permute-start | bytes 368648 | tf_op jit(solution)/shard_map/ppermute | solution.py:471
  61.2 1.6 %collective-permute-start.12 = (bf16[240,256]{1,0:T(8,128)(2,1)S(1)}, bf16[240,256]{1,0:T(8,128)(2,1)S(1)}, u32[]{:S(2)}, u32[]{:S(2)}) collective-permute-start(bf16[240,256]{1,0:T(8,128)(2,1)S(1)} %get-tuple-element.56), channel_id=1, source_target_pairs={{0,8},{2,10},{4,12},{6,14},{8,0},{10,2},{12,4},{14,6},{16,24},{18,... | collective-permute-start | bytes 368648 | tf_op jit(solution)/shard_map/ppermute | solution.py:471
  62.8 0.4 collective-permute-start.13
  63.2 0.0 collective-permute-done.10
  63.2 0.1 add_convert_fusion._.refs_8_
  63.3 1.8 %collective-permute-done.11.refs_1_ = bf16[240,256]{1,0:T(8,128)(2,1)S(1)} collective-permute-done((bf16[240,256]{1,0:T(8,128)(2,1)S(1)}, bf16[240,256]{1,0:T(8,128)(2,1)S(1)}, u32[]{:S(2)}, u32[]{:S(2)}) %collective-permute-start.11) | collective-permute-done | bytes 122912 | tf_op jit(solution)/shard_map/ppermute | solution.py:471
  65.1 2.3 %collective-permute-done.12.refs_2_ = bf16[240,256]{1,0:T(8,128)(2,1)S(1)} collective-permute-done((bf16[240,256]{1,0:T(8,128)(2,1)S(1)}, bf16[240,256]{1,0:T(8,128)(2,1)S(1)}, u32[]{:S(2)}, u32[]{:S(2)}) %collective-permute-start.12) | collective-permute-done | bytes 122912 | tf_op jit(solution)/shard_map/ppermute | solution.py:471
  67.4 1.5 %collective-permute-done.13.refs_3_ = bf16[240,256]{1,0:T(8,128)(2,1)S(1)} collective-permute-done((bf16[240,256]{1,0:T(8,128)(2,1)S(1)}, bf16[240,256]{1,0:T(8,128)(2,1)S(1)}, u32[]{:S(2)}, u32[]{:S(2)}) %collective-permute-start.13) | collective-permute-done | bytes 122912 | tf_op jit(solution)/shard_map/ppermute | solution.py:471
  68.9 0.9 %shard_map.139 = (f32[120,1280]{1,0:T(8,128)S(1)}, bf16[120,1280]{1,0:T(8,128)(2,1)S(1)}) custom-call(bf16[240,256]{1,0:T(8,128)(2,1)S(1)} %get-tuple-element.54.refs_0_, bf16[240,256]{1,0:T(8,128)(2,1)S(1)} %collective-permute-done.11.refs_1_, bf16[240,256]{1,0:T(8,128)(2,1)S(1)} %collective-permute-done.12.refs_2_, ...), custom_call_target="tpu_custom_call" | custom-call | flops 629145600 | bytes 4000000 | tf_op jit(solution)/shard_map/pallas_call | solution.py:433
  69.8 0.1 collective-permute-start.14
  69.9 2.7 %collective-permute-start.15 = (bf16[120,1280]{1,0:T(8,128)(2,1)S(1)}, bf16[120,1280]{1,0:T(8,128)(2,1)S(1)}, u32[]{:S(2)}, u32[]{:S(2)}) collective-permute-start(bf16[120,1280]{1,0:T(8,128)(2,1)S(1)} %add_convert_fusion._.refs_8_), channel_id=1, source_target_pairs={{0,16},{2,18},{4,20},{6,22},{8,24},{10,26},{12,28},{14,30},{16,0},... | collective-permute-start | bytes 921608 | tf_op jit(solution)/shard_map/ppermute | solution.py:471
  72.6 0.0 collective-permute-done.2.other_ref
  72.6 2.1 %shard_map.138 = bf16[128,5120]{1,0:T(8,128)(2,1)} custom-call(s32[1]{0:T(128)S(6)} %copy.14.live_ref, s32[1,64]{1,0:T(1,128)S(1)} %copy-done.21, bf16[128,1280]{1,0:T(8,128)(2,1)S(1)} %get-tuple-element.38.own_ref, bf16[128,1280]{1,0:T(8,128)(2,1)S(1)} %collective-permute-done.2.other_ref, bf16[120,1280]{1,0:T(8,128)(2,1)S(1)} %add_convert_fusion._.refs_8_), custom_call_target="tpu_custom_call" | custom-call | flops 335544320 | bytes 4000000 | tf_op jit(solution)/shard_map/pallas_call | solution.py:433
  74.7 0.0 collective-permute-done.14
  74.7 12.4 %collective-permute-done.15 = bf16[120,1280]{1,0:T(8,128)(2,1)S(1)} collective-permute-done((bf16[120,1280]{1,0:T(8,128)(2,1)S(1)}, bf16[120,1280]{1,0:T(8,128)(2,1)S(1)}, u32[]{:S(2)}, u32[]{:S(2)}) %collective-permute-start.15) | collective-permute-done | bytes 307232 | tf_op jit(solution)/shard_map/ppermute | solution.py:471
  87.1 0.9 %add_bitcast_fusion = f32[1,120,1280]{2,1,0:T(8,128)} fusion(bf16[120,1280]{1,0:T(8,128)(2,1)S(1)} %collective-permute-done.15, f32[120,1280]{1,0:T(8,128)S(1)} %get-tuple-element.58, bf16[120,1280]{1,0:T(8,128)(2,1)S(1)} %collective-permute-done.14), kind=kLoop, calls=%fused_computation | loop fusion | flops 614400 | bytes 1843200 | tf_op jit(solution)/shard_map/broadcast_in_dim | solution.py:620
  (23 shorter events, 0.0 us)
Async XLA Ops:
  1.3 1.1 %copy-start.1 = (bf16[256,1280]{1,0:T(8,128)(2,1)S(1)}, bf16[256,1280]{1,0:T(8,128)(2,1)}, u32[]{:S(2)}) copy-start(bf16[256,1280]{1,0:T(8,128)(2,1)} %patches_ref.1) | copy-start | bytes 1966084
  2.4 0.7 copy-start.14
  3.1 0.7 copy-start.16
  3.8 0.7 copy-start.17
  10.3 0.8 copy-start.3
  11.2 1.2 %copy-start.8 = (bf16[1280,640]{1,0:T(8,128)(2,1)}, bf16[1280,640]{1,0:T(8,128)(2,1)S(1)}, u32[]{:S(2)}) copy-start(bf16[1280,640]{1,0:T(8,128)(2,1)S(1)} %get-tuple-element.32.w_ref) | copy-start | bytes 4915204
  12.4 0.8 copy-start.10
  13.2 0.7 copy-start.12
  13.9 9.7 %copy-start = (bf16[640,1280]{1,0:T(8,128)(2,1)S(1)}, bf16[640,1280]{1,0:T(8,128)(2,1)}, u32[]{:S(2)}) copy-start(bf16[640,1280]{1,0:T(8,128)(2,1)} %proj_ref.5) | copy-start | bytes 4915204
  13.9 9.7 %copy-start.15 = (f32[3,640]{1,0:T(4,128)S(1)}, f32[3,640]{1,0:T(4,128)}, u32[]{:S(2)}) copy-start(f32[3,640]{1,0:T(4,128)} %b_ref.4) | copy-start | bytes 23044
  13.9 9.7 %copy-start.21 = (s32[1,64]{1,0:T(1,128)S(1)}, s32[1,64]{1,0:T(1,128)}, u32[]{:S(2)}) copy-start(s32[1,64]{1,0:T(1,128)} %places_ref.3) | copy-start | bytes 772
  13.9 16.8 %collective-permute-start = (bf16[128,1280]{1,0:T(8,128)(2,1)}, bf16[128,1280]{1,0:T(8,128)(2,1)}, u32[]{:S(2)}, u32[]{:S(2)}) collective-permute-start(bf16[128,1280]{1,0:T(8,128)(2,1)} %get-tuple-element.35), channel_id=1, source_target_pairs={{0,1},{1,0},{2,3},{3,2},{4,5},{5,4},{6,7},{7,6},{8,9},{9,8},{10,11... | collective-permute-start | bytes 983048 | tf_op jit(solution)/shard_map/ppermute | solution.py:468
  19.8 11.9 %collective-permute-start.1 = (bf16[128,1280]{1,0:T(8,128)(2,1)}, bf16[128,1280]{1,0:T(8,128)(2,1)S(1)}, u32[]{:S(2)}, u32[]{:S(2)}) collective-permute-start(bf16[128,1280]{1,0:T(8,128)(2,1)} %get-tuple-element.37), channel_id=1, source_target_pairs={{0,1},{1,0},{2,3},{3,2},{4,5},{5,4},{6,7},{7,6},{8,9},{9,8},{10,11... | collective-permute-start | bytes 983048 | tf_op jit(solution)/shard_map/ppermute | solution.py:468
  20.0 29.0 %collective-permute-start.7 = (bf16[256,1280]{1,0:T(8,128)(2,1)}, bf16[256,1280]{1,0:T(8,128)(2,1)S(1)}, u32[]{:S(2)}, u32[]{:S(2)}) collective-permute-start(bf16[256,1280]{1,0:T(8,128)(2,1)} %get-tuple-element.51.refs_4_), channel_id=1, source_target_pairs={{0,4},{2,6},{4,0},{6,2},{8,12},{10,14},{12,8},{14,10},{16,20},{18,... | collective-permute-start | bytes 1966088 | tf_op jit(solution)/shard_map/ppermute | solution.py:471
  22.0 27.5 %collective-permute-start.8 = (bf16[256,1280]{1,0:T(8,128)(2,1)}, bf16[256,1280]{1,0:T(8,128)(2,1)S(1)}, u32[]{:S(2)}, u32[]{:S(2)}) collective-permute-start(bf16[256,1280]{1,0:T(8,128)(2,1)} %get-tuple-element.51.refs_4_), channel_id=1, source_target_pairs={{0,8},{2,10},{4,12},{6,14},{8,0},{10,2},{12,4},{14,6},{16,24},{18,... | collective-permute-start | bytes 1966088 | tf_op jit(solution)/shard_map/ppermute | solution.py:471
  23.5 29.9 %collective-permute-start.9 = (bf16[256,1280]{1,0:T(8,128)(2,1)}, bf16[256,1280]{1,0:T(8,128)(2,1)S(1)}, u32[]{:S(2)}, u32[]{:S(2)}) collective-permute-start(bf16[256,1280]{1,0:T(8,128)(2,1)} %get-tuple-element.51.refs_4_), channel_id=1, source_target_pairs={{0,12},{2,14},{4,8},{6,10},{8,4},{10,6},{12,0},{14,2},{16,28},{18,... | collective-permute-start | bytes 1966088 | tf_op jit(solution)/shard_map/ppermute | solution.py:471
  23.6 1.1 %copy-start.4 = (bf16[2,256,640]{2,1,0:T(8,128)(2,1)S(1)}, bf16[2,256,640]{2,1,0:T(8,128)(2,1)}, u32[]{:S(2)}) copy-start(bf16[2,256,640]{2,1,0:T(8,128)(2,1)} %copy-done.3) | copy-start | bytes 1966084
  24.6 1.3 %copy-start.6 = (bf16[128,5120]{1,0:T(8,128)(2,1)S(1)}, bf16[128,5120]{1,0:T(8,128)(2,1)}, u32[]{:S(2)}) copy-start(bf16[128,5120]{1,0:T(8,128)(2,1)} %grad_hbm.1) | copy-start | bytes 3932164
  26.0 1.4 %copy-start.9 = (bf16[1280,640]{1,0:T(8,128)(2,1)S(1)}, bf16[1280,640]{1,0:T(8,128)(2,1)}, u32[]{:S(2)}) copy-start(bf16[1280,640]{1,0:T(8,128)(2,1)} %copy-done.8) | copy-start | bytes 4915204
  27.4 4.4 %copy-start.2 = (bf16[256,1280]{1,0:T(8,128)(2,1)S(1)}, bf16[256,1280]{1,0:T(8,128)(2,1)}, u32[]{:S(2)}) copy-start(bf16[256,1280]{1,0:T(8,128)(2,1)} %patches_ref.1) | copy-start | bytes 1966084
  27.4 4.4 %copy-start.18 = (f32[1280]{0:T(1024)S(1)}, f32[1280]{0:T(1024)}, u32[]{:S(2)}) copy-start(f32[1280]{0:T(1024)} %b_ref.5) | copy-start | bytes 15364
  27.4 4.4 %copy-start.19 = (f32[1280]{0:T(1024)S(1)}, f32[1280]{0:T(1024)}, u32[]{:S(2)}) copy-start(f32[1280]{0:T(1024)} %gain_ref.3) | copy-start | bytes 15364
  27.4 4.4 %copy-start.20 = (f32[1280]{0:T(1024)S(1)}, f32[1280]{0:T(1024)}, u32[]{:S(2)}) copy-start(f32[1280]{0:T(1024)} %bias_ref.3) | copy-start | bytes 15364
  30.6 4.5 %copy-start.5 = (bf16[2,256,640]{2,1,0:T(8,128)(2,1)S(1)}, bf16[2,256,640]{2,1,0:T(8,128)(2,1)}, u32[]{:S(2)}) copy-start(bf16[2,256,640]{2,1,0:T(8,128)(2,1)} %copy-done.3) | copy-start | bytes 1966084
  33.3 8.9 %collective-permute-start.3 = (bf16[128,1280]{1,0:T(8,128)(2,1)S(1)}, bf16[128,1280]{1,0:T(8,128)(2,1)S(1)}, u32[]{:S(2)}, u32[]{:S(2)}) collective-permute-start(bf16[128,1280]{1,0:T(8,128)(2,1)S(1)} %get-tuple-element.39.row_ref), channel_id=1, source_target_pairs={{0,1},{1,0},{2,3},{3,2},{4,5},{5,4},{6,7},{7,6},{8,9},{9,8},{10,11... | collective-permute-start | bytes 983048 | tf_op jit(solution)/shard_map/ppermute | solution.py:468
  35.1 7.1 %copy-start.11 = (bf16[8,128,256]{2,1,0:T(8,128)(2,1)S(1)}, bf16[8,128,256]{2,1,0:T(8,128)(2,1)}, u32[]{:S(2)}) copy-start(bf16[8,128,256]{2,1,0:T(8,128)(2,1)} %copy-done.10) | copy-start | bytes 1572868
  35.1 7.1 %copy-start.13 = (bf16[128,640]{1,0:T(8,128)(2,1)S(1)}, bf16[128,640]{1,0:T(8,128)(2,1)}, u32[]{:S(2)}) copy-start(bf16[128,640]{1,0:T(8,128)(2,1)} %copy-done.12) | copy-start | bytes 491524
  42.3 14.8 %copy-start.7 = (bf16[256,1280]{1,0:T(8,128)(2,1)S(1)}, bf16[256,1280]{1,0:T(8,128)(2,1)}, u32[]{:S(2)}) copy-start(bf16[256,1280]{1,0:T(8,128)(2,1)} %get-tuple-element.51.refs_4_) | copy-start | bytes 1966084
  45.9 9.9 %collective-permute-start.4 = (bf16[240,256]{1,0:T(8,128)(2,1)S(1)}, bf16[240,256]{1,0:T(8,128)(2,1)S(1)}, u32[]{:S(2)}, u32[]{:S(2)}) collective-permute-start(bf16[240,256]{1,0:T(8,128)(2,1)S(1)} %get-tuple-element.48), channel_id=1, source_target_pairs={{0,4},{2,6},{4,0},{6,2},{8,12},{10,14},{12,8},{14,10},{16,20},{18,... | collective-permute-start | bytes 368648 | tf_op jit(solution)/shard_map/ppermute | solution.py:471
  47.5 8.5 %collective-permute-start.5 = (bf16[240,256]{1,0:T(8,128)(2,1)S(1)}, bf16[240,256]{1,0:T(8,128)(2,1)S(1)}, u32[]{:S(2)}, u32[]{:S(2)}) collective-permute-start(bf16[240,256]{1,0:T(8,128)(2,1)S(1)} %get-tuple-element.49), channel_id=1, source_target_pairs={{0,8},{2,10},{4,12},{6,14},{8,0},{10,2},{12,4},{14,6},{16,24},{18,... | collective-permute-start | bytes 368648 | tf_op jit(solution)/shard_map/ppermute | solution.py:471
  49.1 8.0 %collective-permute-start.6 = (bf16[240,256]{1,0:T(8,128)(2,1)S(1)}, bf16[240,256]{1,0:T(8,128)(2,1)S(1)}, u32[]{:S(2)}, u32[]{:S(2)}) collective-permute-start(bf16[240,256]{1,0:T(8,128)(2,1)S(1)} %get-tuple-element.50), channel_id=1, source_target_pairs={{0,12},{2,14},{4,8},{6,10},{8,4},{10,6},{12,0},{14,2},{16,28},{18,... | collective-permute-start | bytes 368648 | tf_op jit(solution)/shard_map/ppermute | solution.py:471
  58.1 5.1 %collective-permute-start.10 = (bf16[120,1280]{1,0:T(8,128)(2,1)S(1)}, bf16[120,1280]{1,0:T(8,128)(2,1)S(1)}, u32[]{:S(2)}, u32[]{:S(2)}) collective-permute-start(bf16[120,1280]{1,0:T(8,128)(2,1)S(1)} %get-tuple-element.53), channel_id=1, source_target_pairs={{0,2},{2,0},{4,6},{6,4},{8,10},{10,8},{12,14},{14,12},{16,18},{18,... | collective-permute-start | bytes 921608 | tf_op jit(solution)/shard_map/ppermute | solution.py:471
  58.1 14.5 %collective-permute-start.2 = (bf16[128,1280]{1,0:T(8,128)(2,1)S(1)}, bf16[128,1280]{1,0:T(8,128)(2,1)S(1)}, u32[]{:S(2)}, u32[]{:S(2)}) collective-permute-start(bf16[128,1280]{1,0:T(8,128)(2,1)S(1)} %get-tuple-element.38.own_ref), channel_id=1, source_target_pairs={{0,1},{1,0},{2,3},{3,2},{4,5},{5,4},{6,7},{7,6},{8,9},{9,8},{10,11... | collective-permute-start | bytes 983048 | tf_op jit(solution)/shard_map/ppermute | solution.py:468
  59.7 5.4 %collective-permute-start.11 = (bf16[240,256]{1,0:T(8,128)(2,1)S(1)}, bf16[240,256]{1,0:T(8,128)(2,1)S(1)}, u32[]{:S(2)}, u32[]{:S(2)}) collective-permute-start(bf16[240,256]{1,0:T(8,128)(2,1)S(1)} %get-tuple-element.55), channel_id=1, source_target_pairs={{0,4},{2,6},{4,0},{6,2},{8,12},{10,14},{12,8},{14,10},{16,20},{18,... | collective-permute-start | bytes 368648 | tf_op jit(solution)/shard_map/ppermute | solution.py:471
  61.2 6.2 %collective-permute-start.12 = (bf16[240,256]{1,0:T(8,128)(2,1)S(1)}, bf16[240,256]{1,0:T(8,128)(2,1)S(1)}, u32[]{:S(2)}, u32[]{:S(2)}) collective-permute-start(bf16[240,256]{1,0:T(8,128)(2,1)S(1)} %get-tuple-element.56), channel_id=1, source_target_pairs={{0,8},{2,10},{4,12},{6,14},{8,0},{10,2},{12,4},{14,6},{16,24},{18,... | collective-permute-start | bytes 368648 | tf_op jit(solution)/shard_map/ppermute | solution.py:471
  62.8 6.1 %collective-permute-start.13 = (bf16[240,256]{1,0:T(8,128)(2,1)S(1)}, bf16[240,256]{1,0:T(8,128)(2,1)S(1)}, u32[]{:S(2)}, u32[]{:S(2)}) collective-permute-start(bf16[240,256]{1,0:T(8,128)(2,1)S(1)} %get-tuple-element.57), channel_id=1, source_target_pairs={{0,12},{2,14},{4,8},{6,10},{8,4},{10,6},{12,0},{14,2},{16,28},{18,... | collective-permute-start | bytes 368648 | tf_op jit(solution)/shard_map/ppermute | solution.py:471
  69.8 4.8 %collective-permute-start.14 = (bf16[120,1280]{1,0:T(8,128)(2,1)S(1)}, bf16[120,1280]{1,0:T(8,128)(2,1)S(1)}, u32[]{:S(2)}, u32[]{:S(2)}) collective-permute-start(bf16[120,1280]{1,0:T(8,128)(2,1)S(1)} %get-tuple-element.59), channel_id=1, source_target_pairs={{0,2},{2,0},{4,6},{6,4},{8,10},{10,8},{12,14},{14,12},{16,18},{18,... | collective-permute-start | bytes 921608 | tf_op jit(solution)/shard_map/ppermute | solution.py:471
  69.9 17.2 %collective-permute-start.15 = (bf16[120,1280]{1,0:T(8,128)(2,1)S(1)}, bf16[120,1280]{1,0:T(8,128)(2,1)S(1)}, u32[]{:S(2)}, u32[]{:S(2)}) collective-permute-start(bf16[120,1280]{1,0:T(8,128)(2,1)S(1)} %add_convert_fusion._.refs_8_), channel_id=1, source_target_pairs={{0,16},{2,18},{4,20},{6,22},{8,24},{10,26},{12,28},{14,30},{16,0},... | collective-permute-start | bytes 921608 | tf_op jit(solution)/shard_map/ppermute | solution.py:471

commit v5 on v4

--- a/solution.py
+++ b/solution.py
@@ -184,39 +184,16 @@
     out_ref[...] = total.astype(out_ref.dtype)
 
 
-def prepare_kernel(
-    live_ref,
-    gain_hbm,
-    bias_hbm,
-    patches_hbm,
-    places_hbm,
-    grad_hbm,
-    normed_hbm,
-    send_hbm,
-    gain_ref,
-    bias_ref,
-    patches_ref,
-    places_ref,
-    grad_ref,
-    normed_ref,
-    send_ref,
-    sems,
-):
-    came = begin(
-        (gain_hbm, bias_hbm, patches_hbm, places_hbm, grad_hbm),
-        (gain_ref, bias_ref, patches_ref, places_ref, grad_ref),
-        sems,
-    )
-    for copy in came[:3]:
-        copy.wait()
-    normed_ref[...] = norm_low(patches_ref, gain_ref, bias_ref)
-    went = begin((normed_ref,), (normed_hbm,), sems, 5)
-    for copy in came[3:]:
+def pull_kernel(live_ref, places_hbm, grad_hbm, send_hbm, places_ref, grad_ref, send_ref, sems):
+    came = begin((places_hbm, grad_hbm), (places_ref, grad_ref), sems)
+    for copy in came:
         copy.wait()
     pull(live_ref, places_ref, grad_ref, send_ref, False)
-    went += begin((send_ref,), (send_hbm,), sems, 6)
-    for copy in went:
-        copy.wait()
+    begin((send_ref,), (send_hbm,), sems, 2)[0].wait()
+
+
+def norm_kernel(gain_ref, bias_ref, patches_ref, normed_ref):
+    normed_ref[...] = norm_low(patches_ref, gain_ref, bias_ref)
 
 
 def place_kernel(live_ref, places_ref, own_ref, other_ref, _, out_ref):
@@ -250,9 +227,7 @@
 def first_kernel(
     live_ref,
     b_ref,
-    gain_ref,
-    bias_ref,
-    patches_hbm,
+    normed_ref,
     w_hbm,
     proj_hbm,
     query_ref,
@@ -261,34 +236,30 @@
     wq_ref,
     probs_ref,
     send_ref,
-    patches_ref,
     w_ref,
     proj_ref,
     attended_ref,
-    normed_ref,
     sems,
 ):
     came = begin(
-        (patches_hbm, w_hbm.at[0], w_hbm.at[1], w_hbm.at[2], proj_hbm),
-        (patches_ref, wq_ref, w_ref.at[0], w_ref.at[1], proj_ref),
+        (w_hbm.at[0], w_hbm.at[1], w_hbm.at[2], proj_hbm),
+        (wq_ref, w_ref.at[0], w_ref.at[1], proj_ref),
         sems,
     )
-    came[0].wait()
-    normed_ref[...] = norm_low(patches_ref, gain_ref, bias_ref)
     half = send_ref.shape[0]
     start = half_start(half, False)
-    came[1].wait()
+    own_ref[...] = normed_ref[pl.ds(half_start(half, True), half), :]
+    came[0].wait()
     part = jnp.dot(
         normed_ref[pl.ds(start, half), :], wq_ref[...], preferred_element_type=jnp.float32
     )
     query_ref[...] = (part + b_ref[0:1, :]).astype(jnp.bfloat16)
-    own_ref[...] = normed_ref[pl.ds(half_start(half, True), half), :]
     for t in (1, 2):
-        came[1 + t].wait()
+        came[t].wait()
         part = jnp.dot(normed_ref[...], w_ref[t - 1], preferred_element_type=jnp.float32)
         pair_ref[t - 1] = (part + b_ref[t : t + 1, :]).astype(jnp.bfloat16)
     attend(live_ref, query_ref, pair_ref, probs_ref, attended_ref)
-    came[4].wait()
+    came[3].wait()
     send_ref[...] = jnp.dot(
         attended_ref[...], proj_ref[...], preferred_element_type=jnp.float32
     ).astype(jnp.bfloat16)
@@ -409,14 +380,20 @@
         out_ref[...] = slots_ref[k // 4, k % 4]
 
 
-def product_kernel(*refs):
-    t_refs, n_refs = refs[:4], refs[4:8]
+def product_kernel(t0, t1, t2, t3, n0, n1, n2, n3_low, n3_high, *refs):
     keep_ref, send_ref, sum_ref = refs[-3:]
     half = keep_ref.shape[0]
     core = lax.bitwise_and(lax.axis_index("clip"), 1)
+    cut = n3_low.shape[0]
     total = None
-    for t_ref, n_ref in zip(t_refs, n_refs, strict=True):
-        term = jnp.dot(t_ref[...], n_ref[...], preferred_element_type=jnp.float32)
+    for t, n in (
+        (t0[...], n0),
+        (t1[...], n1),
+        (t2[...], n2),
+        (t3[:, :cut], n3_low),
+        (t3[:, cut:], n3_high),
+    ):
+        term = jnp.dot(t, n[...], preferred_element_type=jnp.float32)
         total = term if total is None else total + term
     sum_ref[...] = total
     keep_ref[...] = sum_ref[pl.ds(pl.multiple_of(core * half, 8), half), :]
@@ -476,49 +453,42 @@
     query = shape((half, local), low)
     attended = pltpu.VMEM((half, local), low)
     block = 3 * local // 8
-    normed, up_send = call(
-        prepare_kernel,
-        (full, part),
-        "saaaaa",
-        8 * rows * share_rows * width,
-        (clip_tokens, norm_gain, norm_bias, patches, positions, grad_placed),
+    up_send = call(
+        pull_kernel,
+        part,
+        "saa",
+        4 * rows * share_rows * width,
+        (clip_tokens, positions, grad_placed),
         (
-            pltpu.VMEM(norm_gain.shape, jnp.float32),
-            pltpu.VMEM(norm_bias.shape, jnp.float32),
-            pltpu.VMEM((rows, width), low),
             pltpu.VMEM(positions.shape, jnp.int32),
             pltpu.VMEM(grad_placed.shape, low),
-            pltpu.VMEM((rows, width), low),
             pltpu.VMEM((half, width), low),
-            pltpu.SemaphoreType.DMA((7,)),
+            pltpu.SemaphoreType.DMA((3,)),
         ),
         limit=62,
         out_kind="a",
     )
     up_came = swap(up_send)
+    normed = call(norm_kernel, full, "vvv", 100 * rows * width, (norm_gain, norm_bias, patches))
     normed_of = [normed] + [flip(normed, q << 1) for q in (1, 2)]
-    normed_of += [flip(normed, 3 << 1)]
+    normed_of += [flip(normed_of[2][:half], 1 << 1), flip(normed_of[1][half:], 2 << 1)]
     other_query, pair, own_normed, w_query, other_probs, part_send = call(
         first_kernel,
         (query, shape((2, rows, local), low), part, shape((width, local), low), probs_half, part),
-        "svvvaaa",
+        "svvaa",
         7 * rows * width * local,
         (
             clip_tokens,
             b_qkv,
-            norm_gain,
-            norm_bias,
-            patches,
+            normed,
             jnp.transpose(w_qkv, (1, 0, 2)),
             w_proj,
         ),
         (
-            pltpu.VMEM((rows, width), low),
             pltpu.VMEM((2, width, local), low),
             pltpu.VMEM((local, width), low),
             attended,
-            pltpu.VMEM((rows, width), low),
-            pltpu.SemaphoreType.DMA((5,)),
+            pltpu.SemaphoreType.DMA((4,)),
         ),
         limit=49,
     )
@@ -589,13 +559,14 @@
     )
 
     def exchange(sent):
-        return [sent[0]] + [flip(sent[q], q << 1) for q in (1, 2, 3)]
+        diagonal = flip(sent[3], 3 << 1)
+        return [sent[0]] + [flip(sent[q], q << 1) for q in (1, 2)] + [diagonal]
 
     def product(taken, after=()):
         return call(
             product_kernel,
             (shape((block // 2, width), jnp.float32), shape((block // 2, width), low)),
-            "v" * 8 + "a" * len(after),
+            "v" * 9 + "a" * len(after),
             8 * block * rows * width,
             (*taken, *normed_of, *after),
             (pltpu.VMEM((block, width), jnp.float32),),

time: 88.5 us -> 93.1 us (1.052)
  Pallas kernels: 24.8 us -> 30.3 us
  waiting for transfers between devices: 30.4 us -> 27.5 us
  local copies, waits for them, and re-layouts: 10.6 us -> 12.5 us
    pallas_call x9 -> x10, Pallas kernels: 24.8 us -> 30.3 us  [call(): pl.pallas_call(kernel, out_shape=outs, in_specs=[spec[kind] for kind in k...]
    ppermute x12 -> x13, waiting for transfers between devices: 25.7 us -> 23.3 us  [flip(): return lax.ppermute(value, 'clip', [(i, i ^ bits) for i in range(n_clip)])]
    ppermute x4, starting transfers between devices: 6.5 us -> 4.26 us  [swap(): return lax.ppermute(value, 'seq', [(0, 1), (1, 0)])]
    ppermute x12 -> x13, starting transfers between devices: 13.4 us -> 15.5 us  [flip(): return lax.ppermute(value, 'clip', [(i, i ^ bits) for i in range(n_clip)])]
    slice x0 -> x2, local copies, waits for them, and re-layouts: none -> 1.99 us  [the longest x1 0.99 us: fast_body(): normed_of[1][half:]]
    unnamed x44 -> x42, local copies, waits for them, and re-layouts: 10.6 us -> 10.5 us
  transfers between devices with their start and end apart: 16 -> 17, of which waited for: 10 -> 8; matrix products, arithmetic and copies ran while one was open for 0% -> 2% of each run, Pallas kernels for 20% -> 28%
where the time goes in v5:
time: 93.1 us; the launch traced here: 92.5 us
  Pallas kernels  30.3 us (33%)
  waiting for transfers between devices  27.5 us (30%)
  starting transfers between devices  19.7 us (21%)
  local copies, waits for them, and re-layouts  12.5 us (13%)
  between operations  1.47 us (2%)
  other arithmetic  0.99 us (1%)
    pallas_call x10, Pallas kernels, call(): pl.pallas_call(kernel, out_shape=outs, in_specs=[spec[kind] for kind in k...  30.3 us
    ppermute x13, waiting for transfers between devices, flip(): return lax.ppermute(value, 'clip', [(i, i ^ bits) for i in range(n_clip)])  23.3 us
    ppermute x13, starting transfers between devices, flip(): return lax.ppermute(value, 'clip', [(i, i ^ bits) for i in range(n_clip)])  15.5 us
    unnamed x42, local copies, waits for them, and re-layouts  10.5 us
    ppermute x4, starting transfers between devices, swap(): return lax.ppermute(value, 'seq', [(0, 1), (1, 0)])  4.26 us
    ppermute x4, waiting for transfers between devices, swap(): return lax.ppermute(value, 'seq', [(0, 1), (1, 0)])  4.14 us
  transfers between devices with their start and end apart: 17, of which 8 were waited for; matrix products, arithmetic and copies ran while one was open for 2% of the time, Pallas kernels for 28%

profile of v5, /device:TPU:0, one launch (start us, length us, event | category | flops | bytes accessed | tf_op | source)
XLA Modules:
  0.0 92.5 jit_solution(4496206672621990542)
XLA Ops:
  0.6 0.0 copy-start.5
  0.6 1.1 %copy-done.5 = bf16[256,1280]{1,0:T(8,128)(2,1)S(1)} copy-done((bf16[256,1280]{1,0:T(8,128)(2,1)S(1)}, bf16[256,1280]{1,0:T(8,128)(2,1)}, u32[]{:S(2)}) %copy-start.5) | copy-done | bytes 655384
  1.7 0.7 copy-done.18
  2.4 0.7 copy-done.19
  3.1 1.3 %shard_map.131.normed_ref.n0 = bf16[256,1280]{1,0:T(8,128)(2,1)} custom-call(f32[1280]{0:T(1024)S(1)} %copy-done.18, f32[1280]{0:T(1024)S(1)} %copy-done.19, bf16[256,1280]{1,0:T(8,128)(2,1)S(1)} %copy-done.5), custom_call_target="tpu_custom_call" | custom-call | flops 32768000 | bytes 4000000 | tf_op jit(solution)/shard_map/pallas_call | solution.py:410
  4.4 3.0 %collective-permute-start.7 = (bf16[256,1280]{1,0:T(8,128)(2,1)}, bf16[256,1280]{1,0:T(8,128)(2,1)}, u32[]{:S(2)}, u32[]{:S(2)}) collective-permute-start(bf16[256,1280]{1,0:T(8,128)(2,1)} %shard_map.131.normed_ref.n0), channel_id=1, source_target_pairs={{0,4},{2,6},{4,0},{6,2},{8,12},{10,14},{12,8},{14,10},{16,20},{18,... | collective-permute-start | bytes 1966088 | tf_op jit(solution)/shard_map/ppermute | solution.py:448
  7.4 1.6 %collective-permute-start.8 = (bf16[256,1280]{1,0:T(8,128)(2,1)}, bf16[256,1280]{1,0:T(8,128)(2,1)}, u32[]{:S(2)}, u32[]{:S(2)}) collective-permute-start(bf16[256,1280]{1,0:T(8,128)(2,1)} %shard_map.131.normed_ref.n0), channel_id=1, source_target_pairs={{0,8},{2,10},{4,12},{6,14},{8,0},{10,2},{12,4},{14,6},{16,24},{18,... | collective-permute-start | bytes 1966088 | tf_op jit(solution)/shard_map/ppermute | solution.py:448
  9.6 0.0 copy-start.13
  9.7 0.7 copy-done.13
  10.3 6.7 %shard_map.132 = (bf16[128,640]{1,0:T(8,128)(2,1)S(1)}, bf16[2,256,640]{2,1,0:T(8,128)(2,1)S(1)}, bf16[128,1280]{1,0:T(8,128)(2,1)S(1)}, bf16[1280,640]{1,0:T(8,...) custom-call(s32[1]{0:T(128)S(6)} %copy.14.live_ref, f32[3,640]{1,0:T(4,128)S(1)} %copy-done.13, ...), custom_call_target="tpu_custom_call" | custom-call | flops 1468006400 | bytes 4000000 | tf_op jit(solution)/shard_map/pallas_call | solution.py:410
  17.1 0.8 copy-done.1
  17.9 1.2 %copy-done.7 = bf16[1280,640]{1,0:T(8,128)(2,1)} copy-done((bf16[1280,640]{1,0:T(8,128)(2,1)}, bf16[1280,640]{1,0:T(8,128)(2,1)S(1)}, u32[]{:S(2)}) %copy-start.7) | copy-done | bytes 1638424
  19.1 0.8 copy-done.9
  19.9 0.7 copy-done.11
  20.6 1.5 %collective-permute-start = (bf16[128,1280]{1,0:T(8,128)(2,1)}, bf16[128,1280]{1,0:T(8,128)(2,1)}, u32[]{:S(2)}, u32[]{:S(2)}) collective-permute-start(bf16[128,1280]{1,0:T(8,128)(2,1)} %get-tuple-element.33), channel_id=1, source_target_pairs={{0,1},{1,0},{2,3},{3,2},{4,5},{5,4},{6,7},{7,6},{8,9},{9,8},{10,11... | collective-permute-start | bytes 983048 | tf_op jit(solution)/shard_map/ppermute | solution.py:445
  22.0 2.8 %shard_map.134 = bf16[128,1280]{1,0:T(8,128)(2,1)} custom-call(s32[1]{0:T(128)S(6)} %copy.14.live_ref, s32[1,64]{1,0:T(1,128)} %places_ref.3, bf16[128,5120]{1,0:T(8,128)(2,1)} %grad_hbm.1), custom_call_target="tpu_custom_call" | custom-call | flops 167772160 | bytes 4000000 | tf_op jit(solution)/shard_map/pallas_call | solution.py:410
  24.8 0.6 collective-permute-start.1
  25.4 0.0 copy-done.14
  25.4 0.0 copy-done.20
  25.5 1.1 %copy-done.2 = bf16[2,256,640]{2,1,0:T(8,128)(2,1)S(1)} copy-done((bf16[2,256,640]{2,1,0:T(8,128)(2,1)S(1)}, bf16[2,256,640]{2,1,0:T(8,128)(2,1)}, u32[]{:S(2)}) %copy-start.2) | copy-done | bytes 655384
  26.5 1.3 %copy-done.4 = bf16[128,5120]{1,0:T(8,128)(2,1)S(1)} copy-done((bf16[128,5120]{1,0:T(8,128)(2,1)S(1)}, bf16[128,5120]{1,0:T(8,128)(2,1)}, u32[]{:S(2)}) %copy-start.4) | copy-done | bytes 1310744
  27.9 1.4 %copy-done.8 = bf16[1280,640]{1,0:T(8,128)(2,1)S(1)} copy-done((bf16[1280,640]{1,0:T(8,128)(2,1)S(1)}, bf16[1280,640]{1,0:T(8,128)(2,1)}, u32[]{:S(2)}) %copy-start.8) | copy-done | bytes 1638424
  29.3 3.3 %shard_map.133 = (bf16[128,640]{1,0:T(8,128)(2,1)S(1)}, bf16[8,128,256]{2,1,0:T(8,128)(2,1)S(1)}, f32[128,1280]{1,0:T(8,128)S(1)}, bf16[128,1280]{1,0:T(8,128)(2,1)S(1)}) custom-call(s32[1]{0:T(128)S(6)} %copy.14.live_ref, s32[1,64]{1,0:T(1,128)S(1)} %copy-done.20, bf16[128,5120]{1,0:T(8,128)(2,1)S(1)} %copy-done.4, f32[3,640]{1,0:T(4,128)S(1)} %copy-done.14, ...), custom_call_target="tpu_custom_call" | custom-call | flops 524288000 | bytes 4000000 | tf_op jit(solution)/shard_map/pallas_call | solution.py:410
  32.6 0.0 collective-permute-done.came_ref
  32.6 4.1 %collective-permute-done.1.up_came_ref = bf16[128,1280]{1,0:T(8,128)(2,1)S(1)} collective-permute-done((bf16[128,1280]{1,0:T(8,128)(2,1)}, bf16[128,1280]{1,0:T(8,128)(2,1)S(1)}, u32[]{:S(2)}, u32[]{:S(2)}) %collective-permute-start.1) | collective-permute-done | bytes 327712 | tf_op jit(solution)/shard_map/ppermute | solution.py:445
  36.7 0.0 copy-done.16
  36.7 1.6 %shard_map.135 = (bf16[128,1280]{1,0:T(8,128)(2,1)S(1)}, bf16[128,1280]{1,0:T(8,128)(2,1)S(1)}) custom-call(f32[1280]{0:T(1024)S(1)} %copy-done.15, f32[1280]{0:T(1024)S(1)} %copy-done.16, f32[1280]{0:T(1024)S(1)} %copy-done.17, f32[128,1280]{1,0:T(8,128)S(1)} %get-tuple-element.32.keep_ref, bf16[128,1280]{1,0:T(8,128)(2,1)} %collective-permute-done.came_ref, ...), custom_call_target="tpu_custom_call" | custom-call | flops 16384000 | bytes 4000000 | tf_op jit(solution)/shard_map/pallas_call | solution.py:410
  38.3 1.5 %collective-permute-start.3 = (bf16[128,1280]{1,0:T(8,128)(2,1)S(1)}, bf16[128,1280]{1,0:T(8,128)(2,1)S(1)}, u32[]{:S(2)}, u32[]{:S(2)}) collective-permute-start(bf16[128,1280]{1,0:T(8,128)(2,1)S(1)} %get-tuple-element.36.row_ref), channel_id=1, source_target_pairs={{0,1},{1,0},{2,3},{3,2},{4,5},{5,4},{6,7},{7,6},{8,9},{9,8},{10,11... | collective-permute-start | bytes 983048 | tf_op jit(solution)/shard_map/ppermute | solution.py:445
  39.9 0.0 collective-permute-done.7.n1
  39.9 1.0 %slice.9 = bf16[128,1280]{1,0:T(8,128)(2,1)S(1)} slice(bf16[256,1280]{1,0:T(8,128)(2,1)} %collective-permute-done.7.n1), slice={[128:256], [0:1280]} | slice | bytes 655360 | tf_op jit(solution)/shard_map/slice | solution.py:474
  40.9 0.5 collective-permute-start.10
  41.4 0.0 collective-permute-done.8.n2
  41.4 1.0 %slice.8 = bf16[128,1280]{1,0:T(8,128)(2,1)S(1)} slice(bf16[256,1280]{1,0:T(8,128)(2,1)} %collective-permute-done.8.n2), slice={[0:128], [0:1280]} | slice | bytes 655360 | tf_op jit(solution)/shard_map/slice | solution.py:474
  42.4 0.6 collective-permute-start.9
  43.0 3.5 %shard_map.136 = (bf16[640,128]{1,0:T(8,128)(2,1)S(1)}, f32[640,256]{1,0:T(8,128)S(1)}, f32[640,256]{1,0:T(8,128)S(1)}) custom-call(bf16[128,1280]{1,0:T(8,128)(2,1)S(1)} %get-tuple-element.36.row_ref, bf16[640,1280]{1,0:T(8,128)(2,1)S(1)} %copy-done, bf16[128,640]{1,0:T(8,128)(2,1)S(1)} %get-tuple-element.39.q_ref, bf16[2,256,640]{2,1,0:T(8,128)(2,1)S(1)} %copy-done.3, ...), custom_call_target="tpu_custom_call" | custom-call | flops 419430400 | bytes 4000000 | tf_op jit(solution)/shard_map/pallas_call | solution.py:410
  46.5 0.0 collective-permute-done.3.row_ref
  46.5 3.6 %shard_map.137 = (bf16[240,256]{1,0:T(8,128)(2,1)S(1)}, bf16[240,256]{1,0:T(8,128)(2,1)S(1)}, bf16[240,256]{1,0:T(8,128)(2,1)S(1)}, bf16[240,256]{1,0:T(8,128)(2...) custom-call(bf16[128,1280]{1,0:T(8,128)(2,1)S(1)} %collective-permut, ...), custom_call_target="tpu_custom_call" | custom-call | flops 419430400 | bytes 4000000 | tf_op jit(solution)/shard_map/pallas_call | solution.py:410
  50.2 1.6 %collective-permute-start.4 = (bf16[240,256]{1,0:T(8,128)(2,1)S(1)}, bf16[240,256]{1,0:T(8,128)(2,1)S(1)}, u32[]{:S(2)}, u32[]{:S(2)}) collective-permute-start(bf16[240,256]{1,0:T(8,128)(2,1)S(1)} %get-tuple-element.45), channel_id=1, source_target_pairs={{0,4},{2,6},{4,0},{6,2},{8,12},{10,14},{12,8},{14,10},{16,20},{18,... | collective-permute-start | bytes 368648 | tf_op jit(solution)/shard_map/ppermute | solution.py:448
  51.7 1.6 %collective-permute-start.5 = (bf16[240,256]{1,0:T(8,128)(2,1)S(1)}, bf16[240,256]{1,0:T(8,128)(2,1)S(1)}, u32[]{:S(2)}, u32[]{:S(2)}) collective-permute-start(bf16[240,256]{1,0:T(8,128)(2,1)S(1)} %get-tuple-element.46), channel_id=1, source_target_pairs={{0,8},{2,10},{4,12},{6,14},{8,0},{10,2},{12,4},{14,6},{16,24},{18,... | collective-permute-start | bytes 368648 | tf_op jit(solution)/shard_map/ppermute | solution.py:448
  53.3 0.4 collective-permute-start.6
  53.7 2.7 %collective-permute-done.4.t1 = bf16[240,256]{1,0:T(8,128)(2,1)S(1)} collective-permute-done((bf16[240,256]{1,0:T(8,128)(2,1)S(1)}, bf16[240,256]{1,0:T(8,128)(2,1)S(1)}, u32[]{:S(2)}, u32[]{:S(2)}) %collective-permute-start.4) | collective-permute-done | bytes 122912 | tf_op jit(solution)/shard_map/ppermute | solution.py:448
  56.4 0.2 collective-permute-done.5.t2
  56.6 2.5 %collective-permute-done.6.t3 = bf16[240,256]{1,0:T(8,128)(2,1)S(1)} collective-permute-done((bf16[240,256]{1,0:T(8,128)(2,1)S(1)}, bf16[240,256]{1,0:T(8,128)(2,1)S(1)}, u32[]{:S(2)}, u32[]{:S(2)}) %collective-permute-start.6) | collective-permute-done | bytes 122912 | tf_op jit(solution)/shard_map/ppermute | solution.py:448
  59.1 0.0 collective-permute-done.10.n3_high
  59.1 0.0 collective-permute-done.9.n3_low
  59.1 2.8 %shard_map.138 = (f32[120,1280]{1,0:T(8,128)S(1)}, bf16[120,1280]{1,0:T(8,128)(2,1)S(1)}) custom-call(bf16[240,256]{1,0:T(8,128)(2,1)S(1)} %get-tuple-element.44.t0, bf16[240,256]{1,0:T(8,128)(2,1)S(1)} %collective-permute-done.4.t1, bf16[240,256]{1,0:T(8,128)(2,1)S(1)} %collective-permute-done.5.t2, bf16[240,256]{1,0:T(8,128)(2,1)S(1)} %collective-permute-done.6.t3, ...), custom_call_target="tpu_custom_call" | custom-call | flops 629145600 | bytes 4000000 | tf_op jit(solution)/shard_map/pallas_call | solution.py:410
  61.9 0.1 collective-permute-start.11
  62.0 0.7 collective-permute-start.2
  62.7 0.5 collective-permute-start.12
  63.1 1.4 %collective-permute-start.13 = (bf16[240,256]{1,0:T(8,128)(2,1)S(1)}, bf16[240,256]{1,0:T(8,128)(2,1)S(1)}, u32[]{:S(2)}, u32[]{:S(2)}) collective-permute-start(bf16[240,256]{1,0:T(8,128)(2,1)S(1)} %get-tuple-element.52), channel_id=1, source_target_pairs={{0,8},{2,10},{4,12},{6,14},{8,0},{10,2},{12,4},{14,6},{16,24},{18,... | collective-permute-start | bytes 368648 | tf_op jit(solution)/shard_map/ppermute | solution.py:448
  64.5 1.6 %collective-permute-start.14 = (bf16[240,256]{1,0:T(8,128)(2,1)S(1)}, bf16[240,256]{1,0:T(8,128)(2,1)S(1)}, u32[]{:S(2)}, u32[]{:S(2)}) collective-permute-start(bf16[240,256]{1,0:T(8,128)(2,1)S(1)} %get-tuple-element.53), channel_id=1, source_target_pairs={{0,12},{2,14},{4,8},{6,10},{8,4},{10,6},{12,0},{14,2},{16,28},{18,... | collective-permute-start | bytes 368648 | tf_op jit(solution)/shard_map/ppermute | solution.py:448
  66.1 0.0 collective-permute-done.11
  66.2 0.1 add_convert_fusion._.refs_0_
  66.2 1.8 %collective-permute-done.12.t1 = bf16[240,256]{1,0:T(8,128)(2,1)S(1)} collective-permute-done((bf16[240,256]{1,0:T(8,128)(2,1)S(1)}, bf16[240,256]{1,0:T(8,128)(2,1)S(1)}, u32[]{:S(2)}, u32[]{:S(2)}) %collective-permute-start.12) | collective-permute-done | bytes 122912 | tf_op jit(solution)/shard_map/ppermute | solution.py:448
  68.0 1.3 %collective-permute-done.13.t2 = bf16[240,256]{1,0:T(8,128)(2,1)S(1)} collective-permute-done((bf16[240,256]{1,0:T(8,128)(2,1)S(1)}, bf16[240,256]{1,0:T(8,128)(2,1)S(1)}, u32[]{:S(2)}, u32[]{:S(2)}) %collective-permute-start.13) | collective-permute-done | bytes 122912 | tf_op jit(solution)/shard_map/ppermute | solution.py:448
  69.3 2.5 %collective-permute-done.14.t3 = bf16[240,256]{1,0:T(8,128)(2,1)S(1)} collective-permute-done((bf16[240,256]{1,0:T(8,128)(2,1)S(1)}, bf16[240,256]{1,0:T(8,128)(2,1)S(1)}, u32[]{:S(2)}, u32[]{:S(2)}) %collective-permute-start.14) | collective-permute-done | bytes 122912 | tf_op jit(solution)/shard_map/ppermute | solution.py:448
  71.9 2.6 %shard_map.140 = (f32[120,1280]{1,0:T(8,128)S(1)}, bf16[120,1280]{1,0:T(8,128)(2,1)S(1)}) custom-call(bf16[240,256]{1,0:T(8,128)(2,1)S(1)} %get-tuple-element.50.t0, bf16[240,256]{1,0:T(8,128)(2,1)S(1)} %collective-permute-done.12.t1, bf16[240,256]{1,0:T(8,128)(2,1)S(1)} %collective-permute-done.13.t2, bf16[240,256]{1,0:T(8,128)(2,1)S(1)} %collective-permute-done.14.t3, ...), custom_call_target="tpu_custom_call" | custom-call | flops 629145600 | bytes 4000000 | tf_op jit(solution)/shard_map/pallas_call | solution.py:410
  74.5 0.1 collective-permute-start.15
  74.5 2.6 %collective-permute-start.16 = (bf16[120,1280]{1,0:T(8,128)(2,1)S(1)}, bf16[120,1280]{1,0:T(8,128)(2,1)S(1)}, u32[]{:S(2)}, u32[]{:S(2)}) collective-permute-start(bf16[120,1280]{1,0:T(8,128)(2,1)S(1)} %add_convert_fusion._.refs_0_), channel_id=1, source_target_pairs={{0,16},{2,18},{4,20},{6,22},{8,24},{10,26},{12,28},{14,30},{16,0},... | collective-permute-start | bytes 921608 | tf_op jit(solution)/shard_map/ppermute | solution.py:448
  77.2 0.0 collective-permute-done.2.other_ref
  77.2 2.1 %shard_map.139 = bf16[128,5120]{1,0:T(8,128)(2,1)} custom-call(s32[1]{0:T(128)S(6)} %copy.14.live_ref, s32[1,64]{1,0:T(1,128)S(1)} %copy-done.20, bf16[128,1280]{1,0:T(8,128)(2,1)S(1)} %get-tuple-element.35.own_ref, bf16[128,1280]{1,0:T(8,128)(2,1)S(1)} %collective-permute-done.2.other_ref, bf16[120,1280]{1,0:T(8,128)(2,1)S(1)} %add_convert_fusion._.refs_0_), custom_call_target="tpu_custom_call" | custom-call | flops 335544320 | bytes 4000000 | tf_op jit(solution)/shard_map/pallas_call | solution.py:410
  79.2 0.0 collective-permute-done.15
  79.2 12.3 %collective-permute-done.16 = bf16[120,1280]{1,0:T(8,128)(2,1)S(1)} collective-permute-done((bf16[120,1280]{1,0:T(8,128)(2,1)S(1)}, bf16[120,1280]{1,0:T(8,128)(2,1)S(1)}, u32[]{:S(2)}, u32[]{:S(2)}) %collective-permute-start.16) | collective-permute-done | bytes 307232 | tf_op jit(solution)/shard_map/ppermute | solution.py:448
  91.6 0.9 add_bitcast_fusion
  (26 shorter events, 0.0 us)
Async XLA Ops:
  0.6 1.1 %copy-start.5 = (bf16[256,1280]{1,0:T(8,128)(2,1)S(1)}, bf16[256,1280]{1,0:T(8,128)(2,1)}, u32[]{:S(2)}) copy-start(bf16[256,1280]{1,0:T(8,128)(2,1)} %patches_ref.3) | copy-start | bytes 1966084
  1.7 0.7 copy-start.18
  2.4 0.7 copy-start.19
  4.4 35.4 %collective-permute-start.7 = (bf16[256,1280]{1,0:T(8,128)(2,1)}, bf16[256,1280]{1,0:T(8,128)(2,1)}, u32[]{:S(2)}, u32[]{:S(2)}) collective-permute-start(bf16[256,1280]{1,0:T(8,128)(2,1)} %shard_map.131.normed_ref.n0), channel_id=1, source_target_pairs={{0,4},{2,6},{4,0},{6,2},{8,12},{10,14},{12,8},{14,10},{16,20},{18,... | collective-permute-start | bytes 1966088 | tf_op jit(solution)/shard_map/ppermute | solution.py:448
  7.4 34.0 %collective-permute-start.8 = (bf16[256,1280]{1,0:T(8,128)(2,1)}, bf16[256,1280]{1,0:T(8,128)(2,1)}, u32[]{:S(2)}, u32[]{:S(2)}) collective-permute-start(bf16[256,1280]{1,0:T(8,128)(2,1)} %shard_map.131.normed_ref.n0), channel_id=1, source_target_pairs={{0,8},{2,10},{4,12},{6,14},{8,0},{10,2},{12,4},{14,6},{16,24},{18,... | collective-permute-start | bytes 1966088 | tf_op jit(solution)/shard_map/ppermute | solution.py:448
  9.6 0.7 copy-start.13
  10.3 15.1 %copy-start.14 = (f32[3,640]{1,0:T(4,128)S(1)}, f32[3,640]{1,0:T(4,128)}, u32[]{:S(2)}) copy-start(f32[3,640]{1,0:T(4,128)} %b_ref.4) | copy-start | bytes 23044
  17.1 0.8 copy-start.1
  17.9 1.2 %copy-start.7 = (bf16[1280,640]{1,0:T(8,128)(2,1)}, bf16[1280,640]{1,0:T(8,128)(2,1)S(1)}, u32[]{:S(2)}) copy-start(bf16[1280,640]{1,0:T(8,128)(2,1)S(1)} %get-tuple-element.30.w_ref) | copy-start | bytes 4915204
  19.1 0.8 copy-start.9
  19.9 0.7 copy-start.11
  20.5 4.9 %copy-start = (bf16[640,1280]{1,0:T(8,128)(2,1)S(1)}, bf16[640,1280]{1,0:T(8,128)(2,1)}, u32[]{:S(2)}) copy-start(bf16[640,1280]{1,0:T(8,128)(2,1)} %proj_ref.5) | copy-start | bytes 4915204
  20.5 4.9 %copy-start.20 = (s32[1,64]{1,0:T(1,128)S(1)}, s32[1,64]{1,0:T(1,128)}, u32[]{:S(2)}) copy-start(s32[1,64]{1,0:T(1,128)} %places_ref.3) | copy-start | bytes 772
  20.6 12.0 %collective-permute-start = (bf16[128,1280]{1,0:T(8,128)(2,1)}, bf16[128,1280]{1,0:T(8,128)(2,1)}, u32[]{:S(2)}, u32[]{:S(2)}) collective-permute-start(bf16[128,1280]{1,0:T(8,128)(2,1)} %get-tuple-element.33), channel_id=1, source_target_pairs={{0,1},{1,0},{2,3},{3,2},{4,5},{5,4},{6,7},{7,6},{8,9},{9,8},{10,11... | collective-permute-start | bytes 983048 | tf_op jit(solution)/shard_map/ppermute | solution.py:445
  24.8 11.9 %collective-permute-start.1 = (bf16[128,1280]{1,0:T(8,128)(2,1)}, bf16[128,1280]{1,0:T(8,128)(2,1)S(1)}, u32[]{:S(2)}, u32[]{:S(2)}) collective-permute-start(bf16[128,1280]{1,0:T(8,128)(2,1)} %shard_map.134), channel_id=1, source_target_pairs={{0,1},{1,0},{2,3},{3,2},{4,5},{5,4},{6,7},{7,6},{8,9},{9,8},{10,11... | collective-permute-start | bytes 983048 | tf_op jit(solution)/shard_map/ppermute | solution.py:445
  25.4 1.1 %copy-start.2 = (bf16[2,256,640]{2,1,0:T(8,128)(2,1)S(1)}, bf16[2,256,640]{2,1,0:T(8,128)(2,1)}, u32[]{:S(2)}) copy-start(bf16[2,256,640]{2,1,0:T(8,128)(2,1)} %copy-done.1) | copy-start | bytes 1966084
  26.5 1.3 %copy-start.4 = (bf16[128,5120]{1,0:T(8,128)(2,1)S(1)}, bf16[128,5120]{1,0:T(8,128)(2,1)}, u32[]{:S(2)}) copy-start(bf16[128,5120]{1,0:T(8,128)(2,1)} %grad_hbm.1) | copy-start | bytes 3932164
  27.9 1.4 %copy-start.8 = (bf16[1280,640]{1,0:T(8,128)(2,1)S(1)}, bf16[1280,640]{1,0:T(8,128)(2,1)}, u32[]{:S(2)}) copy-start(bf16[1280,640]{1,0:T(8,128)(2,1)} %copy-done.7) | copy-start | bytes 4915204
  29.3 7.4 %copy-start.6 = (bf16[256,1280]{1,0:T(8,128)(2,1)S(1)}, bf16[256,1280]{1,0:T(8,128)(2,1)}, u32[]{:S(2)}) copy-start(bf16[256,1280]{1,0:T(8,128)(2,1)} %patches_ref.3) | copy-start | bytes 1966084
  29.3 7.4 %copy-start.15 = (f32[1280]{0:T(1024)S(1)}, f32[1280]{0:T(1024)}, u32[]{:S(2)}) copy-start(f32[1280]{0:T(1024)} %b_ref.5) | copy-start | bytes 15364
  29.3 7.4 %copy-start.16 = (f32[1280]{0:T(1024)S(1)}, f32[1280]{0:T(1024)}, u32[]{:S(2)}) copy-start(f32[1280]{0:T(1024)} %gain_ref.3) | copy-start | bytes 15364
  29.3 7.4 %copy-start.17 = (f32[1280]{0:T(1024)S(1)}, f32[1280]{0:T(1024)}, u32[]{:S(2)}) copy-start(f32[1280]{0:T(1024)} %bias_ref.3) | copy-start | bytes 15364
  36.7 6.2 %copy-start.3 = (bf16[2,256,640]{2,1,0:T(8,128)(2,1)S(1)}, bf16[2,256,640]{2,1,0:T(8,128)(2,1)}, u32[]{:S(2)}) copy-start(bf16[2,256,640]{2,1,0:T(8,128)(2,1)} %copy-done.1) | copy-start | bytes 1966084
  38.3 8.2 %collective-permute-start.3 = (bf16[128,1280]{1,0:T(8,128)(2,1)S(1)}, bf16[128,1280]{1,0:T(8,128)(2,1)S(1)}, u32[]{:S(2)}, u32[]{:S(2)}) collective-permute-start(bf16[128,1280]{1,0:T(8,128)(2,1)S(1)} %get-tuple-element.36.row_ref), channel_id=1, source_target_pairs={{0,1},{1,0},{2,3},{3,2},{4,5},{5,4},{6,7},{7,6},{8,9},{9,8},{10,11... | collective-permute-start | bytes 983048 | tf_op jit(solution)/shard_map/ppermute | solution.py:445
  40.9 18.2 %collective-permute-start.10 = (bf16[128,1280]{1,0:T(8,128)(2,1)S(1)}, bf16[128,1280]{1,0:T(8,128)(2,1)S(1)}, u32[]{:S(2)}, u32[]{:S(2)}) collective-permute-start(bf16[128,1280]{1,0:T(8,128)(2,1)S(1)} %slice.9), channel_id=1, source_target_pairs={{0,8},{2,10},{4,12},{6,14},{8,0},{10,2},{12,4},{14,6},{16,24},{18,... | collective-permute-start | bytes 983048 | tf_op jit(solution)/shard_map/ppermute | solution.py:448
  42.4 16.7 %collective-permute-start.9 = (bf16[128,1280]{1,0:T(8,128)(2,1)S(1)}, bf16[128,1280]{1,0:T(8,128)(2,1)S(1)}, u32[]{:S(2)}, u32[]{:S(2)}) collective-permute-start(bf16[128,1280]{1,0:T(8,128)(2,1)S(1)} %slice.8), channel_id=1, source_target_pairs={{0,4},{2,6},{4,0},{6,2},{8,12},{10,14},{12,8},{14,10},{16,20},{18,... | collective-permute-start | bytes 983048 | tf_op jit(solution)/shard_map/ppermute | solution.py:448
  43.0 3.6 %copy-start.10 = (bf16[8,128,256]{2,1,0:T(8,128)(2,1)S(1)}, bf16[8,128,256]{2,1,0:T(8,128)(2,1)}, u32[]{:S(2)}) copy-start(bf16[8,128,256]{2,1,0:T(8,128)(2,1)} %copy-done.9) | copy-start | bytes 1572868
  43.0 3.6 %copy-start.12 = (bf16[128,640]{1,0:T(8,128)(2,1)S(1)}, bf16[128,640]{1,0:T(8,128)(2,1)}, u32[]{:S(2)}) copy-start(bf16[128,640]{1,0:T(8,128)(2,1)} %copy-done.11) | copy-start | bytes 491524
  50.2 6.3 %collective-permute-start.4 = (bf16[240,256]{1,0:T(8,128)(2,1)S(1)}, bf16[240,256]{1,0:T(8,128)(2,1)S(1)}, u32[]{:S(2)}, u32[]{:S(2)}) collective-permute-start(bf16[240,256]{1,0:T(8,128)(2,1)S(1)} %get-tuple-element.45), channel_id=1, source_target_pairs={{0,4},{2,6},{4,0},{6,2},{8,12},{10,14},{12,8},{14,10},{16,20},{18,... | collective-permute-start | bytes 368648 | tf_op jit(solution)/shard_map/ppermute | solution.py:448
  51.7 4.9 %collective-permute-start.5 = (bf16[240,256]{1,0:T(8,128)(2,1)S(1)}, bf16[240,256]{1,0:T(8,128)(2,1)S(1)}, u32[]{:S(2)}, u32[]{:S(2)}) collective-permute-start(bf16[240,256]{1,0:T(8,128)(2,1)S(1)} %get-tuple-element.46), channel_id=1, source_target_pairs={{0,8},{2,10},{4,12},{6,14},{8,0},{10,2},{12,4},{14,6},{16,24},{18,... | collective-permute-start | bytes 368648 | tf_op jit(solution)/shard_map/ppermute | solution.py:448
  53.3 5.8 %collective-permute-start.6 = (bf16[240,256]{1,0:T(8,128)(2,1)S(1)}, bf16[240,256]{1,0:T(8,128)(2,1)S(1)}, u32[]{:S(2)}, u32[]{:S(2)}) collective-permute-start(bf16[240,256]{1,0:T(8,128)(2,1)S(1)} %get-tuple-element.47), channel_id=1, source_target_pairs={{0,12},{2,14},{4,8},{6,10},{8,4},{10,6},{12,0},{14,2},{16,28},{18,... | collective-permute-start | bytes 368648 | tf_op jit(solution)/shard_map/ppermute | solution.py:448
  61.9 4.2 %collective-permute-start.11 = (bf16[120,1280]{1,0:T(8,128)(2,1)S(1)}, bf16[120,1280]{1,0:T(8,128)(2,1)S(1)}, u32[]{:S(2)}, u32[]{:S(2)}) collective-permute-start(bf16[120,1280]{1,0:T(8,128)(2,1)S(1)} %get-tuple-element.49), channel_id=1, source_target_pairs={{0,2},{2,0},{4,6},{6,4},{8,10},{10,8},{12,14},{14,12},{16,18},{18,... | collective-permute-start | bytes 921608 | tf_op jit(solution)/shard_map/ppermute | solution.py:448
  62.0 15.2 %collective-permute-start.2 = (bf16[128,1280]{1,0:T(8,128)(2,1)S(1)}, bf16[128,1280]{1,0:T(8,128)(2,1)S(1)}, u32[]{:S(2)}, u32[]{:S(2)}) collective-permute-start(bf16[128,1280]{1,0:T(8,128)(2,1)S(1)} %get-tuple-element.35.own_ref), channel_id=1, source_target_pairs={{0,1},{1,0},{2,3},{3,2},{4,5},{5,4},{6,7},{7,6},{8,9},{9,8},{10,11... | collective-permute-start | bytes 983048 | tf_op jit(solution)/shard_map/ppermute | solution.py:445
  62.7 5.4 %collective-permute-start.12 = (bf16[240,256]{1,0:T(8,128)(2,1)S(1)}, bf16[240,256]{1,0:T(8,128)(2,1)S(1)}, u32[]{:S(2)}, u32[]{:S(2)}) collective-permute-start(bf16[240,256]{1,0:T(8,128)(2,1)S(1)} %get-tuple-element.51), channel_id=1, source_target_pairs={{0,4},{2,6},{4,0},{6,2},{8,12},{10,14},{12,8},{14,10},{16,20},{18,... | collective-permute-start | bytes 368648 | tf_op jit(solution)/shard_map/ppermute | solution.py:448
  63.1 6.2 %collective-permute-start.13 = (bf16[240,256]{1,0:T(8,128)(2,1)S(1)}, bf16[240,256]{1,0:T(8,128)(2,1)S(1)}, u32[]{:S(2)}, u32[]{:S(2)}) collective-permute-start(bf16[240,256]{1,0:T(8,128)(2,1)S(1)} %get-tuple-element.52), channel_id=1, source_target_pairs={{0,8},{2,10},{4,12},{6,14},{8,0},{10,2},{12,4},{14,6},{16,24},{18,... | collective-permute-start | bytes 368648 | tf_op jit(solution)/shard_map/ppermute | solution.py:448
  64.5 7.3 %collective-permute-start.14 = (bf16[240,256]{1,0:T(8,128)(2,1)S(1)}, bf16[240,256]{1,0:T(8,128)(2,1)S(1)}, u32[]{:S(2)}, u32[]{:S(2)}) collective-permute-start(bf16[240,256]{1,0:T(8,128)(2,1)S(1)} %get-tuple-element.53), channel_id=1, source_target_pairs={{0,12},{2,14},{4,8},{6,10},{8,4},{10,6},{12,0},{14,2},{16,28},{18,... | collective-permute-start | bytes 368648 | tf_op jit(solution)/shard_map/ppermute | solution.py:448
  74.5 4.8 %collective-permute-start.15 = (bf16[120,1280]{1,0:T(8,128)(2,1)S(1)}, bf16[120,1280]{1,0:T(8,128)(2,1)S(1)}, u32[]{:S(2)}, u32[]{:S(2)}) collective-permute-start(bf16[120,1280]{1,0:T(8,128)(2,1)S(1)} %get-tuple-element.55), channel_id=1, source_target_pairs={{0,2},{2,0},{4,6},{6,4},{8,10},{10,8},{12,14},{14,12},{16,18},{18,... | collective-permute-start | bytes 921608 | tf_op jit(solution)/shard_map/ppermute | solution.py:448
  74.5 17.0 %collective-permute-start.16 = (bf16[120,1280]{1,0:T(8,128)(2,1)S(1)}, bf16[120,1280]{1,0:T(8,128)(2,1)S(1)}, u32[]{:S(2)}, u32[]{:S(2)}) collective-permute-start(bf16[120,1280]{1,0:T(8,128)(2,1)S(1)} %add_convert_fusion._.refs_0_), channel_id=1, source_target_pairs={{0,16},{2,18},{4,20},{6,22},{8,24},{10,26},{12,28},{14,30},{16,0},... | collective-permute-start | bytes 921608 | tf_op jit(solution)/shard_map/ppermute | solution.py:448

commit v6 on v5

--- a/solution.py
+++ b/solution.py
@@ -184,12 +184,26 @@
     out_ref[...] = total.astype(out_ref.dtype)
 
 
-def pull_kernel(live_ref, places_hbm, grad_hbm, send_hbm, places_ref, grad_ref, send_ref, sems):
-    came = begin((places_hbm, grad_hbm), (places_ref, grad_ref), sems)
-    for copy in came:
-        copy.wait()
-    pull(live_ref, places_ref, grad_ref, send_ref, False)
-    begin((send_ref,), (send_hbm,), sems, 2)[0].wait()
+def pull_kernel(live_ref, places_hbm, grad_hbm, send_ref, places_ref, grad_ref, sems):
+    half, width = send_ref.shape
+    came = begin((places_hbm,), (places_ref,), sems)
+    blocks = [slice(k * width, (k + 1) * width) for k in range(4)]
+    came += begin(
+        [grad_hbm.at[:, block] for block in blocks],
+        [grad_ref.at[:, block] for block in blocks],
+        sems,
+        1,
+    )
+    came[0].wait()
+    masks = place_masks(
+        live_ref, places_ref[...], grad_ref.shape[0], half, half_start(half, False)
+    )
+    total = None
+    for k in range(4):
+        came[1 + k].wait()
+        term = leading(masks[k], grad_ref[:, blocks[k]])
+        total = term if total is None else total + term
+    send_ref[...] = total.astype(send_ref.dtype)
 
 
 def norm_kernel(gain_ref, bias_ref, patches_ref, normed_ref):
@@ -381,19 +395,15 @@
 
 
 def product_kernel(t0, t1, t2, t3, n0, n1, n2, n3_low, n3_high, *refs):
-    keep_ref, send_ref, sum_ref = refs[-3:]
+    keep_ref, send_ref, sum_ref, n3 = refs[-4:]
     half = keep_ref.shape[0]
     core = lax.bitwise_and(lax.axis_index("clip"), 1)
     cut = n3_low.shape[0]
+    n3[:cut, :] = n3_low[...]
+    n3[cut:, :] = n3_high[...]
     total = None
-    for t, n in (
-        (t0[...], n0),
-        (t1[...], n1),
-        (t2[...], n2),
-        (t3[:, :cut], n3_low),
-        (t3[:, cut:], n3_high),
-    ):
-        term = jnp.dot(t, n[...], preferred_element_type=jnp.float32)
+    for t, n in ((t0, n0), (t1, n1), (t2, n2), (t3, n3)):
+        term = jnp.dot(t[...], n[...], preferred_element_type=jnp.float32)
         total = term if total is None else total + term
     sum_ref[...] = total
     keep_ref[...] = sum_ref[pl.ds(pl.multiple_of(core * half, 8), half), :]
@@ -401,7 +411,7 @@
     send_ref[...] = other.astype(jnp.bfloat16)
 
 
-def call(kernel, outs, kinds, flops, args, scratch=(), limit=30, out_kind="v"):
+def call(kernel, outs, kinds, flops, args, scratch=(), limit=30):
     spec = {
         "s": pl.BlockSpec(memory_space=pltpu.SMEM),
         "v": pl.BlockSpec(memory_space=pltpu.VMEM),
@@ -411,7 +421,7 @@
         kernel,
         out_shape=outs,
         in_specs=[spec[kind] for kind in kinds],
-        out_specs=jax.tree.map(lambda _: spec[out_kind], outs),
+        out_specs=jax.tree.map(lambda _: spec["v"], outs),
         scratch_shapes=list(scratch),
         cost_estimate=pl.CostEstimate(flops=flops, bytes_accessed=4_000_000, transcendentals=0),
         compiler_params=pltpu.CompilerParams(vmem_limit_bytes=limit * 1024 * 1024),
@@ -462,11 +472,9 @@
         (
             pltpu.VMEM(positions.shape, jnp.int32),
             pltpu.VMEM(grad_placed.shape, low),
-            pltpu.VMEM((half, width), low),
-            pltpu.SemaphoreType.DMA((3,)),
+            pltpu.SemaphoreType.DMA((5,)),
         ),
         limit=62,
-        out_kind="a",
     )
     up_came = swap(up_send)
     normed = call(norm_kernel, full, "vvv", 100 * rows * width, (norm_gain, norm_bias, patches))
@@ -569,7 +577,7 @@
             "v" * 9 + "a" * len(after),
             8 * block * rows * width,
             (*taken, *normed_of, *after),
-            (pltpu.VMEM((block, width), jnp.float32),),
+            (pltpu.VMEM((block, width), jnp.float32), pltpu.VMEM((rows, width), low)),
         )
 
     far_taken = exchange(sent[:4])

time: 93.1 us -> 92.7 us (level)
  no operation moved by 1% of the time
where the time goes in v6:
time: 92.7 us; the launch traced here: 92.1 us
  Pallas kernels  29.8 us (32%)
  waiting for transfers between devices  27.7 us (30%)
  starting transfers between devices  19.7 us (21%)
  local copies, waits for them, and re-layouts  12.5 us (13%)
  between operations  1.47 us (2%)
  other arithmetic  0.99 us (1%)
    pallas_call x10, Pallas kernels, call(): pl.pallas_call(kernel, out_shape=outs, in_specs=[spec[kind] for kind in k...  29.8 us
    ppermute x13, waiting for transfers between devices, flip(): return lax.ppermute(value, 'clip', [(i, i ^ bits) for i in range(n_clip)])  23.4 us
    ppermute x13, starting transfers between devices, flip(): return lax.ppermute(value, 'clip', [(i, i ^ bits) for i in range(n_clip)])  15.5 us
    unnamed x42, local copies, waits for them, and re-layouts  10.5 us
    ppermute x4, waiting for transfers between devices, swap(): return lax.ppermute(value, 'seq', [(0, 1), (1, 0)])  4.31 us
    ppermute x4, starting transfers between devices, swap(): return lax.ppermute(value, 'seq', [(0, 1), (1, 0)])  4.26 us
  transfers between devices with their start and end apart: 17, of which 8 were waited for; matrix products, arithmetic and copies ran while one was open for 2% of the time, Pallas kernels for 28%

profile of v6, /device:TPU:0, one launch (start us, length us, event | category | flops | bytes accessed | tf_op | source)
XLA Modules:
  0.0 92.1 jit_solution(1721239549572105708)
XLA Ops:
  0.6 0.0 copy-start.5
  0.6 1.1 %copy-done.5 = bf16[256,1280]{1,0:T(8,128)(2,1)S(1)} copy-done((bf16[256,1280]{1,0:T(8,128)(2,1)S(1)}, bf16[256,1280]{1,0:T(8,128)(2,1)}, u32[]{:S(2)}) %copy-start.5) | copy-done | bytes 655384
  1.7 0.7 copy-done.18
  2.4 0.7 copy-done.19
  3.1 1.3 %shard_map.131.normed_ref.n0 = bf16[256,1280]{1,0:T(8,128)(2,1)} custom-call(f32[1280]{0:T(1024)S(1)} %copy-done.18, f32[1280]{0:T(1024)S(1)} %copy-done.19, bf16[256,1280]{1,0:T(8,128)(2,1)S(1)} %copy-done.5), custom_call_target="tpu_custom_call" | custom-call | flops 32768000 | bytes 4000000 | tf_op jit(solution)/shard_map/pallas_call | solution.py:420
  4.4 3.0 %collective-permute-start.7 = (bf16[256,1280]{1,0:T(8,128)(2,1)}, bf16[256,1280]{1,0:T(8,128)(2,1)}, u32[]{:S(2)}, u32[]{:S(2)}) collective-permute-start(bf16[256,1280]{1,0:T(8,128)(2,1)} %shard_map.131.normed_ref.n0), channel_id=1, source_target_pairs={{0,4},{2,6},{4,0},{6,2},{8,12},{10,14},{12,8},{14,10},{16,20},{18,... | collective-permute-start | bytes 1966088 | tf_op jit(solution)/shard_map/ppermute | solution.py:458
  7.4 1.6 %collective-permute-start.8 = (bf16[256,1280]{1,0:T(8,128)(2,1)}, bf16[256,1280]{1,0:T(8,128)(2,1)}, u32[]{:S(2)}, u32[]{:S(2)}) collective-permute-start(bf16[256,1280]{1,0:T(8,128)(2,1)} %shard_map.131.normed_ref.n0), channel_id=1, source_target_pairs={{0,8},{2,10},{4,12},{6,14},{8,0},{10,2},{12,4},{14,6},{16,24},{18,... | collective-permute-start | bytes 1966088 | tf_op jit(solution)/shard_map/ppermute | solution.py:458
  9.6 0.0 copy-start.13
  9.7 0.7 copy-done.13
  10.3 6.7 %shard_map.132 = (bf16[128,640]{1,0:T(8,128)(2,1)S(1)}, bf16[2,256,640]{2,1,0:T(8,128)(2,1)S(1)}, bf16[128,1280]{1,0:T(8,128)(2,1)S(1)}, bf16[1280,640]{1,0:T(8,...) custom-call(s32[1]{0:T(128)S(6)} %copy.14.live_ref, f32[3,640]{1,0:T(4,128)S(1)} %copy-done.13, ...), custom_call_target="tpu_custom_call" | custom-call | flops 1468006400 | bytes 4000000 | tf_op jit(solution)/shard_map/pallas_call | solution.py:420
  17.1 0.0 copy-start.1
  17.1 0.8 copy-done.1
  17.9 1.2 %copy-done.7 = bf16[1280,640]{1,0:T(8,128)(2,1)} copy-done((bf16[1280,640]{1,0:T(8,128)(2,1)}, bf16[1280,640]{1,0:T(8,128)(2,1)S(1)}, u32[]{:S(2)}) %copy-start.7) | copy-done | bytes 1638424
  19.1 0.8 copy-done.9
  19.9 0.7 copy-done.11
  20.6 1.5 %collective-permute-start = (bf16[128,1280]{1,0:T(8,128)(2,1)}, bf16[128,1280]{1,0:T(8,128)(2,1)}, u32[]{:S(2)}, u32[]{:S(2)}) collective-permute-start(bf16[128,1280]{1,0:T(8,128)(2,1)} %get-tuple-element.33), channel_id=1, source_target_pairs={{0,1},{1,0},{2,3},{3,2},{4,5},{5,4},{6,7},{7,6},{8,9},{9,8},{10,11... | collective-permute-start | bytes 983048 | tf_op jit(solution)/shard_map/ppermute | solution.py:455
  22.0 2.6 %shard_map.134 = bf16[128,1280]{1,0:T(8,128)(2,1)} custom-call(s32[1]{0:T(128)S(6)} %copy.14.live_ref, s32[1,64]{1,0:T(1,128)} %places_ref.3, bf16[128,5120]{1,0:T(8,128)(2,1)} %grad_hbm.1), custom_call_target="tpu_custom_call" | custom-call | flops 167772160 | bytes 4000000 | tf_op jit(solution)/shard_map/pallas_call | solution.py:420
  24.7 0.6 collective-permute-start.1
  25.3 0.0 copy-done.14
  25.3 1.1 %copy-done.2 = bf16[2,256,640]{2,1,0:T(8,128)(2,1)S(1)} copy-done((bf16[2,256,640]{2,1,0:T(8,128)(2,1)S(1)}, bf16[2,256,640]{2,1,0:T(8,128)(2,1)}, u32[]{:S(2)}) %copy-start.2) | copy-done | bytes 655384
  26.4 1.3 %copy-done.4 = bf16[128,5120]{1,0:T(8,128)(2,1)S(1)} copy-done((bf16[128,5120]{1,0:T(8,128)(2,1)S(1)}, bf16[128,5120]{1,0:T(8,128)(2,1)}, u32[]{:S(2)}) %copy-start.4) | copy-done | bytes 1310744
  27.7 1.4 %copy-done.8 = bf16[1280,640]{1,0:T(8,128)(2,1)S(1)} copy-done((bf16[1280,640]{1,0:T(8,128)(2,1)S(1)}, bf16[1280,640]{1,0:T(8,128)(2,1)}, u32[]{:S(2)}) %copy-start.8) | copy-done | bytes 1638424
  29.1 3.3 %shard_map.133 = (bf16[128,640]{1,0:T(8,128)(2,1)S(1)}, bf16[8,128,256]{2,1,0:T(8,128)(2,1)S(1)}, f32[128,1280]{1,0:T(8,128)S(1)}, bf16[128,1280]{1,0:T(8,128)(2,1)S(1)}) custom-call(s32[1]{0:T(128)S(6)} %copy.14.live_ref, s32[1,64]{1,0:T(1,128)S(1)} %copy-done.20, bf16[128,5120]{1,0:T(8,128)(2,1)S(1)} %copy-done.4, f32[3,640]{1,0:T(4,128)S(1)} %copy-done.14, ...), custom_call_target="tpu_custom_call" | custom-call | flops 524288000 | bytes 4000000 | tf_op jit(solution)/shard_map/pallas_call | solution.py:420
  32.4 0.0 collective-permute-done.came_ref
  32.4 4.3 %collective-permute-done.1.up_came_ref = bf16[128,1280]{1,0:T(8,128)(2,1)S(1)} collective-permute-done((bf16[128,1280]{1,0:T(8,128)(2,1)}, bf16[128,1280]{1,0:T(8,128)(2,1)S(1)}, u32[]{:S(2)}, u32[]{:S(2)}) %collective-permute-start.1) | collective-permute-done | bytes 327712 | tf_op jit(solution)/shard_map/ppermute | solution.py:455
  36.7 0.0 copy-done.16
  36.7 1.6 %shard_map.135 = (bf16[128,1280]{1,0:T(8,128)(2,1)S(1)}, bf16[128,1280]{1,0:T(8,128)(2,1)S(1)}) custom-call(f32[1280]{0:T(1024)S(1)} %copy-done.15, f32[1280]{0:T(1024)S(1)} %copy-done.16, f32[1280]{0:T(1024)S(1)} %copy-done.17, f32[128,1280]{1,0:T(8,128)S(1)} %get-tuple-element.32.keep_ref, bf16[128,1280]{1,0:T(8,128)(2,1)} %collective-permute-done.came_ref, ...), custom_call_target="tpu_custom_call" | custom-call | flops 16384000 | bytes 4000000 | tf_op jit(solution)/shard_map/pallas_call | solution.py:420
  38.3 1.5 %collective-permute-start.3 = (bf16[128,1280]{1,0:T(8,128)(2,1)S(1)}, bf16[128,1280]{1,0:T(8,128)(2,1)S(1)}, u32[]{:S(2)}, u32[]{:S(2)}) collective-permute-start(bf16[128,1280]{1,0:T(8,128)(2,1)S(1)} %get-tuple-element.36.row_ref), channel_id=1, source_target_pairs={{0,1},{1,0},{2,3},{3,2},{4,5},{5,4},{6,7},{7,6},{8,9},{9,8},{10,11... | collective-permute-start | bytes 983048 | tf_op jit(solution)/shard_map/ppermute | solution.py:455
  39.9 0.0 collective-permute-done.7.n1
  39.9 1.0 %slice.9 = bf16[128,1280]{1,0:T(8,128)(2,1)S(1)} slice(bf16[256,1280]{1,0:T(8,128)(2,1)} %collective-permute-done.7.n1), slice={[128:256], [0:1280]} | slice | bytes 655360 | tf_op jit(solution)/shard_map/slice | solution.py:482
  40.9 0.5 collective-permute-start.10
  41.4 0.0 collective-permute-done.8.n2
  41.4 1.0 %slice.8 = bf16[128,1280]{1,0:T(8,128)(2,1)S(1)} slice(bf16[256,1280]{1,0:T(8,128)(2,1)} %collective-permute-done.8.n2), slice={[0:128], [0:1280]} | slice | bytes 655360 | tf_op jit(solution)/shard_map/slice | solution.py:482
  42.4 0.6 collective-permute-start.9
  43.0 3.5 %shard_map.136 = (bf16[640,128]{1,0:T(8,128)(2,1)S(1)}, f32[640,256]{1,0:T(8,128)S(1)}, f32[640,256]{1,0:T(8,128)S(1)}) custom-call(bf16[128,1280]{1,0:T(8,128)(2,1)S(1)} %get-tuple-element.36.row_ref, bf16[640,1280]{1,0:T(8,128)(2,1)S(1)} %copy-done, bf16[128,640]{1,0:T(8,128)(2,1)S(1)} %get-tuple-element.39.q_ref, bf16[2,256,640]{2,1,0:T(8,128)(2,1)S(1)} %copy-done.3, ...), custom_call_target="tpu_custom_call" | custom-call | flops 419430400 | bytes 4000000 | tf_op jit(solution)/shard_map/pallas_call | solution.py:420
  46.5 0.0 collective-permute-done.3.row_ref
  46.5 3.6 %shard_map.137 = (bf16[240,256]{1,0:T(8,128)(2,1)S(1)}, bf16[240,256]{1,0:T(8,128)(2,1)S(1)}, bf16[240,256]{1,0:T(8,128)(2,1)S(1)}, bf16[240,256]{1,0:T(8,128)(2...) custom-call(bf16[128,1280]{1,0:T(8,128)(2,1)S(1)} %collective-permut, ...), custom_call_target="tpu_custom_call" | custom-call | flops 419430400 | bytes 4000000 | tf_op jit(solution)/shard_map/pallas_call | solution.py:420
  50.2 1.6 %collective-permute-start.4 = (bf16[240,256]{1,0:T(8,128)(2,1)S(1)}, bf16[240,256]{1,0:T(8,128)(2,1)S(1)}, u32[]{:S(2)}, u32[]{:S(2)}) collective-permute-start(bf16[240,256]{1,0:T(8,128)(2,1)S(1)} %get-tuple-element.45), channel_id=1, source_target_pairs={{0,4},{2,6},{4,0},{6,2},{8,12},{10,14},{12,8},{14,10},{16,20},{18,... | collective-permute-start | bytes 368648 | tf_op jit(solution)/shard_map/ppermute | solution.py:458
  51.7 1.6 %collective-permute-start.5 = (bf16[240,256]{1,0:T(8,128)(2,1)S(1)}, bf16[240,256]{1,0:T(8,128)(2,1)S(1)}, u32[]{:S(2)}, u32[]{:S(2)}) collective-permute-start(bf16[240,256]{1,0:T(8,128)(2,1)S(1)} %get-tuple-element.46), channel_id=1, source_target_pairs={{0,8},{2,10},{4,12},{6,14},{8,0},{10,2},{12,4},{14,6},{16,24},{18,... | collective-permute-start | bytes 368648 | tf_op jit(solution)/shard_map/ppermute | solution.py:458
  53.3 0.4 collective-permute-start.6
  53.7 2.7 %collective-permute-done.4.t1 = bf16[240,256]{1,0:T(8,128)(2,1)S(1)} collective-permute-done((bf16[240,256]{1,0:T(8,128)(2,1)S(1)}, bf16[240,256]{1,0:T(8,128)(2,1)S(1)}, u32[]{:S(2)}, u32[]{:S(2)}) %collective-permute-start.4) | collective-permute-done | bytes 122912 | tf_op jit(solution)/shard_map/ppermute | solution.py:458
  56.4 0.2 collective-permute-done.5.t2
  56.6 2.5 %collective-permute-done.6.t3 = bf16[240,256]{1,0:T(8,128)(2,1)S(1)} collective-permute-done((bf16[240,256]{1,0:T(8,128)(2,1)S(1)}, bf16[240,256]{1,0:T(8,128)(2,1)S(1)}, u32[]{:S(2)}, u32[]{:S(2)}) %collective-permute-start.6) | collective-permute-done | bytes 122912 | tf_op jit(solution)/shard_map/ppermute | solution.py:458
  59.1 0.0 collective-permute-done.10.n3_high
  59.1 0.0 collective-permute-done.9.n3_low
  59.1 2.6 %shard_map.138 = (f32[120,1280]{1,0:T(8,128)S(1)}, bf16[120,1280]{1,0:T(8,128)(2,1)S(1)}) custom-call(bf16[240,256]{1,0:T(8,128)(2,1)S(1)} %get-tuple-element.44.t0, bf16[240,256]{1,0:T(8,128)(2,1)S(1)} %collective-permute-done.4.t1, bf16[240,256]{1,0:T(8,128)(2,1)S(1)} %collective-permute-done.5.t2, bf16[240,256]{1,0:T(8,128)(2,1)S(1)} %collective-permute-done.6.t3, ...), custom_call_target="tpu_custom_call" | custom-call | flops 629145600 | bytes 4000000 | tf_op jit(solution)/shard_map/pallas_call | solution.py:420
  61.7 0.1 collective-permute-start.11
  61.8 0.7 collective-permute-start.2
  62.4 0.5 collective-permute-start.12
  62.9 1.4 %collective-permute-start.13 = (bf16[240,256]{1,0:T(8,128)(2,1)S(1)}, bf16[240,256]{1,0:T(8,128)(2,1)S(1)}, u32[]{:S(2)}, u32[]{:S(2)}) collective-permute-start(bf16[240,256]{1,0:T(8,128)(2,1)S(1)} %get-tuple-element.52), channel_id=1, source_target_pairs={{0,8},{2,10},{4,12},{6,14},{8,0},{10,2},{12,4},{14,6},{16,24},{18,... | collective-permute-start | bytes 368648 | tf_op jit(solution)/shard_map/ppermute | solution.py:458
  64.3 1.6 %collective-permute-start.14 = (bf16[240,256]{1,0:T(8,128)(2,1)S(1)}, bf16[240,256]{1,0:T(8,128)(2,1)S(1)}, u32[]{:S(2)}, u32[]{:S(2)}) collective-permute-start(bf16[240,256]{1,0:T(8,128)(2,1)S(1)} %get-tuple-element.53), channel_id=1, source_target_pairs={{0,12},{2,14},{4,8},{6,10},{8,4},{10,6},{12,0},{14,2},{16,28},{18,... | collective-permute-start | bytes 368648 | tf_op jit(solution)/shard_map/ppermute | solution.py:458
  65.9 0.0 collective-permute-done.11
  65.9 0.1 add_convert_fusion._.refs_0_
  66.0 1.8 %collective-permute-done.12.t1 = bf16[240,256]{1,0:T(8,128)(2,1)S(1)} collective-permute-done((bf16[240,256]{1,0:T(8,128)(2,1)S(1)}, bf16[240,256]{1,0:T(8,128)(2,1)S(1)}, u32[]{:S(2)}, u32[]{:S(2)}) %collective-permute-start.12) | collective-permute-done | bytes 122912 | tf_op jit(solution)/shard_map/ppermute | solution.py:458
  67.8 1.3 %collective-permute-done.13.t2 = bf16[240,256]{1,0:T(8,128)(2,1)S(1)} collective-permute-done((bf16[240,256]{1,0:T(8,128)(2,1)S(1)}, bf16[240,256]{1,0:T(8,128)(2,1)S(1)}, u32[]{:S(2)}, u32[]{:S(2)}) %collective-permute-start.13) | collective-permute-done | bytes 122912 | tf_op jit(solution)/shard_map/ppermute | solution.py:458
  69.1 2.5 %collective-permute-done.14.t3 = bf16[240,256]{1,0:T(8,128)(2,1)S(1)} collective-permute-done((bf16[240,256]{1,0:T(8,128)(2,1)S(1)}, bf16[240,256]{1,0:T(8,128)(2,1)S(1)}, u32[]{:S(2)}, u32[]{:S(2)}) %collective-permute-start.14) | collective-permute-done | bytes 122912 | tf_op jit(solution)/shard_map/ppermute | solution.py:458
  71.6 2.4 %shard_map.140 = (f32[120,1280]{1,0:T(8,128)S(1)}, bf16[120,1280]{1,0:T(8,128)(2,1)S(1)}) custom-call(bf16[240,256]{1,0:T(8,128)(2,1)S(1)} %get-tuple-element.50.t0, bf16[240,256]{1,0:T(8,128)(2,1)S(1)} %collective-permute-done.12.t1, bf16[240,256]{1,0:T(8,128)(2,1)S(1)} %collective-permute-done.13.t2, bf16[240,256]{1,0:T(8,128)(2,1)S(1)} %collective-permute-done.14.t3, ...), custom_call_target="tpu_custom_call" | custom-call | flops 629145600 | bytes 4000000 | tf_op jit(solution)/shard_map/pallas_call | solution.py:420
  74.1 0.1 collective-permute-start.15
  74.2 2.6 %collective-permute-start.16 = (bf16[120,1280]{1,0:T(8,128)(2,1)S(1)}, bf16[120,1280]{1,0:T(8,128)(2,1)S(1)}, u32[]{:S(2)}, u32[]{:S(2)}) collective-permute-start(bf16[120,1280]{1,0:T(8,128)(2,1)S(1)} %add_convert_fusion._.refs_0_), channel_id=1, source_target_pairs={{0,16},{2,18},{4,20},{6,22},{8,24},{10,26},{12,28},{14,30},{16,0},... | collective-permute-start | bytes 921608 | tf_op jit(solution)/shard_map/ppermute | solution.py:458
  76.8 0.0 collective-permute-done.2.other_ref
  76.8 2.1 %shard_map.139 = bf16[128,5120]{1,0:T(8,128)(2,1)} custom-call(s32[1]{0:T(128)S(6)} %copy.14.live_ref, s32[1,64]{1,0:T(1,128)S(1)} %copy-done.20, bf16[128,1280]{1,0:T(8,128)(2,1)S(1)} %get-tuple-element.35.own_ref, bf16[128,1280]{1,0:T(8,128)(2,1)S(1)} %collective-permute-done.2.other_ref, bf16[120,1280]{1,0:T(8,128)(2,1)S(1)} %add_convert_fusion._.refs_0_), custom_call_target="tpu_custom_call" | custom-call | flops 335544320 | bytes 4000000 | tf_op jit(solution)/shard_map/pallas_call | solution.py:420
  78.8 0.0 collective-permute-done.15
  78.9 12.3 %collective-permute-done.16 = bf16[120,1280]{1,0:T(8,128)(2,1)S(1)} collective-permute-done((bf16[120,1280]{1,0:T(8,128)(2,1)S(1)}, bf16[120,1280]{1,0:T(8,128)(2,1)S(1)}, u32[]{:S(2)}, u32[]{:S(2)}) %collective-permute-start.16) | collective-permute-done | bytes 307232 | tf_op jit(solution)/shard_map/ppermute | solution.py:458
  91.2 0.9 add_bitcast_fusion
  (26 shorter events, 0.0 us)
Async XLA Ops:
  0.6 1.1 %copy-start.5 = (bf16[256,1280]{1,0:T(8,128)(2,1)S(1)}, bf16[256,1280]{1,0:T(8,128)(2,1)}, u32[]{:S(2)}) copy-start(bf16[256,1280]{1,0:T(8,128)(2,1)} %patches_ref.3) | copy-start | bytes 1966084
  1.7 0.7 copy-start.18
  2.4 0.7 copy-start.19
  4.4 35.4 %collective-permute-start.7 = (bf16[256,1280]{1,0:T(8,128)(2,1)}, bf16[256,1280]{1,0:T(8,128)(2,1)}, u32[]{:S(2)}, u32[]{:S(2)}) collective-permute-start(bf16[256,1280]{1,0:T(8,128)(2,1)} %shard_map.131.normed_ref.n0), channel_id=1, source_target_pairs={{0,4},{2,6},{4,0},{6,2},{8,12},{10,14},{12,8},{14,10},{16,20},{18,... | collective-permute-start | bytes 1966088 | tf_op jit(solution)/shard_map/ppermute | solution.py:458
  7.4 34.0 %collective-permute-start.8 = (bf16[256,1280]{1,0:T(8,128)(2,1)}, bf16[256,1280]{1,0:T(8,128)(2,1)}, u32[]{:S(2)}, u32[]{:S(2)}) collective-permute-start(bf16[256,1280]{1,0:T(8,128)(2,1)} %shard_map.131.normed_ref.n0), channel_id=1, source_target_pairs={{0,8},{2,10},{4,12},{6,14},{8,0},{10,2},{12,4},{14,6},{16,24},{18,... | collective-permute-start | bytes 1966088 | tf_op jit(solution)/shard_map/ppermute | solution.py:458
  9.6 0.7 copy-start.13
  10.3 14.9 %copy-start.14 = (f32[3,640]{1,0:T(4,128)S(1)}, f32[3,640]{1,0:T(4,128)}, u32[]{:S(2)}) copy-start(f32[3,640]{1,0:T(4,128)} %b_ref.4) | copy-start | bytes 23044
  17.1 0.8 copy-start.1
  17.9 1.2 %copy-start.7 = (bf16[1280,640]{1,0:T(8,128)(2,1)}, bf16[1280,640]{1,0:T(8,128)(2,1)S(1)}, u32[]{:S(2)}) copy-start(bf16[1280,640]{1,0:T(8,128)(2,1)S(1)} %get-tuple-element.30.w_ref) | copy-start | bytes 4915204
  19.1 0.8 copy-start.9
  19.9 0.7 copy-start.11
  20.5 4.7 %copy-start = (bf16[640,1280]{1,0:T(8,128)(2,1)S(1)}, bf16[640,1280]{1,0:T(8,128)(2,1)}, u32[]{:S(2)}) copy-start(bf16[640,1280]{1,0:T(8,128)(2,1)} %proj_ref.5) | copy-start | bytes 4915204
  20.5 4.7 %copy-start.20 = (s32[1,64]{1,0:T(1,128)S(1)}, s32[1,64]{1,0:T(1,128)}, u32[]{:S(2)}) copy-start(s32[1,64]{1,0:T(1,128)} %places_ref.3) | copy-start | bytes 772
  20.6 11.8 %collective-permute-start = (bf16[128,1280]{1,0:T(8,128)(2,1)}, bf16[128,1280]{1,0:T(8,128)(2,1)}, u32[]{:S(2)}, u32[]{:S(2)}) collective-permute-start(bf16[128,1280]{1,0:T(8,128)(2,1)} %get-tuple-element.33), channel_id=1, source_target_pairs={{0,1},{1,0},{2,3},{3,2},{4,5},{5,4},{6,7},{7,6},{8,9},{9,8},{10,11... | collective-permute-start | bytes 983048 | tf_op jit(solution)/shard_map/ppermute | solution.py:455
  24.7 12.0 %collective-permute-start.1 = (bf16[128,1280]{1,0:T(8,128)(2,1)}, bf16[128,1280]{1,0:T(8,128)(2,1)S(1)}, u32[]{:S(2)}, u32[]{:S(2)}) collective-permute-start(bf16[128,1280]{1,0:T(8,128)(2,1)} %shard_map.134), channel_id=1, source_target_pairs={{0,1},{1,0},{2,3},{3,2},{4,5},{5,4},{6,7},{7,6},{8,9},{9,8},{10,11... | collective-permute-start | bytes 983048 | tf_op jit(solution)/shard_map/ppermute | solution.py:455
  25.3 1.1 %copy-start.2 = (bf16[2,256,640]{2,1,0:T(8,128)(2,1)S(1)}, bf16[2,256,640]{2,1,0:T(8,128)(2,1)}, u32[]{:S(2)}) copy-start(bf16[2,256,640]{2,1,0:T(8,128)(2,1)} %copy-done.1) | copy-start | bytes 1966084
  26.4 1.3 %copy-start.4 = (bf16[128,5120]{1,0:T(8,128)(2,1)S(1)}, bf16[128,5120]{1,0:T(8,128)(2,1)}, u32[]{:S(2)}) copy-start(bf16[128,5120]{1,0:T(8,128)(2,1)} %grad_hbm.1) | copy-start | bytes 3932164
  27.7 1.4 %copy-start.8 = (bf16[1280,640]{1,0:T(8,128)(2,1)S(1)}, bf16[1280,640]{1,0:T(8,128)(2,1)}, u32[]{:S(2)}) copy-start(bf16[1280,640]{1,0:T(8,128)(2,1)} %copy-done.7) | copy-start | bytes 4915204
  29.1 7.6 %copy-start.6 = (bf16[256,1280]{1,0:T(8,128)(2,1)S(1)}, bf16[256,1280]{1,0:T(8,128)(2,1)}, u32[]{:S(2)}) copy-start(bf16[256,1280]{1,0:T(8,128)(2,1)} %patches_ref.3) | copy-start | bytes 1966084
  29.1 7.6 %copy-start.15 = (f32[1280]{0:T(1024)S(1)}, f32[1280]{0:T(1024)}, u32[]{:S(2)}) copy-start(f32[1280]{0:T(1024)} %b_ref.5) | copy-start | bytes 15364
  29.1 7.6 %copy-start.16 = (f32[1280]{0:T(1024)S(1)}, f32[1280]{0:T(1024)}, u32[]{:S(2)}) copy-start(f32[1280]{0:T(1024)} %gain_ref.3) | copy-start | bytes 15364
  29.1 7.6 %copy-start.17 = (f32[1280]{0:T(1024)S(1)}, f32[1280]{0:T(1024)}, u32[]{:S(2)}) copy-start(f32[1280]{0:T(1024)} %bias_ref.3) | copy-start | bytes 15364
  36.7 6.2 %copy-start.3 = (bf16[2,256,640]{2,1,0:T(8,128)(2,1)S(1)}, bf16[2,256,640]{2,1,0:T(8,128)(2,1)}, u32[]{:S(2)}) copy-start(bf16[2,256,640]{2,1,0:T(8,128)(2,1)} %copy-done.1) | copy-start | bytes 1966084
  38.3 8.2 %collective-permute-start.3 = (bf16[128,1280]{1,0:T(8,128)(2,1)S(1)}, bf16[128,1280]{1,0:T(8,128)(2,1)S(1)}, u32[]{:S(2)}, u32[]{:S(2)}) collective-permute-start(bf16[128,1280]{1,0:T(8,128)(2,1)S(1)} %get-tuple-element.36.row_ref), channel_id=1, source_target_pairs={{0,1},{1,0},{2,3},{3,2},{4,5},{5,4},{6,7},{7,6},{8,9},{9,8},{10,11... | collective-permute-start | bytes 983048 | tf_op jit(solution)/shard_map/ppermute | solution.py:455
  40.9 18.2 %collective-permute-start.10 = (bf16[128,1280]{1,0:T(8,128)(2,1)S(1)}, bf16[128,1280]{1,0:T(8,128)(2,1)S(1)}, u32[]{:S(2)}, u32[]{:S(2)}) collective-permute-start(bf16[128,1280]{1,0:T(8,128)(2,1)S(1)} %slice.9), channel_id=1, source_target_pairs={{0,8},{2,10},{4,12},{6,14},{8,0},{10,2},{12,4},{14,6},{16,24},{18,... | collective-permute-start | bytes 983048 | tf_op jit(solution)/shard_map/ppermute | solution.py:458
  42.4 16.7 %collective-permute-start.9 = (bf16[128,1280]{1,0:T(8,128)(2,1)S(1)}, bf16[128,1280]{1,0:T(8,128)(2,1)S(1)}, u32[]{:S(2)}, u32[]{:S(2)}) collective-permute-start(bf16[128,1280]{1,0:T(8,128)(2,1)S(1)} %slice.8), channel_id=1, source_target_pairs={{0,4},{2,6},{4,0},{6,2},{8,12},{10,14},{12,8},{14,10},{16,20},{18,... | collective-permute-start | bytes 983048 | tf_op jit(solution)/shard_map/ppermute | solution.py:458
  43.0 3.6 %copy-start.10 = (bf16[8,128,256]{2,1,0:T(8,128)(2,1)S(1)}, bf16[8,128,256]{2,1,0:T(8,128)(2,1)}, u32[]{:S(2)}) copy-start(bf16[8,128,256]{2,1,0:T(8,128)(2,1)} %copy-done.9) | copy-start | bytes 1572868
  43.0 3.6 %copy-start.12 = (bf16[128,640]{1,0:T(8,128)(2,1)S(1)}, bf16[128,640]{1,0:T(8,128)(2,1)}, u32[]{:S(2)}) copy-start(bf16[128,640]{1,0:T(8,128)(2,1)} %copy-done.11) | copy-start | bytes 491524
  50.2 6.3 %collective-permute-start.4 = (bf16[240,256]{1,0:T(8,128)(2,1)S(1)}, bf16[240,256]{1,0:T(8,128)(2,1)S(1)}, u32[]{:S(2)}, u32[]{:S(2)}) collective-permute-start(bf16[240,256]{1,0:T(8,128)(2,1)S(1)} %get-tuple-element.45), channel_id=1, source_target_pairs={{0,4},{2,6},{4,0},{6,2},{8,12},{10,14},{12,8},{14,10},{16,20},{18,... | collective-permute-start | bytes 368648 | tf_op jit(solution)/shard_map/ppermute | solution.py:458
  51.7 4.9 %collective-permute-start.5 = (bf16[240,256]{1,0:T(8,128)(2,1)S(1)}, bf16[240,256]{1,0:T(8,128)(2,1)S(1)}, u32[]{:S(2)}, u32[]{:S(2)}) collective-permute-start(bf16[240,256]{1,0:T(8,128)(2,1)S(1)} %get-tuple-element.46), channel_id=1, source_target_pairs={{0,8},{2,10},{4,12},{6,14},{8,0},{10,2},{12,4},{14,6},{16,24},{18,... | collective-permute-start | bytes 368648 | tf_op jit(solution)/shard_map/ppermute | solution.py:458
  53.3 5.8 %collective-permute-start.6 = (bf16[240,256]{1,0:T(8,128)(2,1)S(1)}, bf16[240,256]{1,0:T(8,128)(2,1)S(1)}, u32[]{:S(2)}, u32[]{:S(2)}) collective-permute-start(bf16[240,256]{1,0:T(8,128)(2,1)S(1)} %get-tuple-element.47), channel_id=1, source_target_pairs={{0,12},{2,14},{4,8},{6,10},{8,4},{10,6},{12,0},{14,2},{16,28},{18,... | collective-permute-start | bytes 368648 | tf_op jit(solution)/shard_map/ppermute | solution.py:458
  61.7 4.2 %collective-permute-start.11 = (bf16[120,1280]{1,0:T(8,128)(2,1)S(1)}, bf16[120,1280]{1,0:T(8,128)(2,1)S(1)}, u32[]{:S(2)}, u32[]{:S(2)}) collective-permute-start(bf16[120,1280]{1,0:T(8,128)(2,1)S(1)} %get-tuple-element.49), channel_id=1, source_target_pairs={{0,2},{2,0},{4,6},{6,4},{8,10},{10,8},{12,14},{14,12},{16,18},{18,... | collective-permute-start | bytes 921608 | tf_op jit(solution)/shard_map/ppermute | solution.py:458
  61.8 15.0 %collective-permute-start.2 = (bf16[128,1280]{1,0:T(8,128)(2,1)S(1)}, bf16[128,1280]{1,0:T(8,128)(2,1)S(1)}, u32[]{:S(2)}, u32[]{:S(2)}) collective-permute-start(bf16[128,1280]{1,0:T(8,128)(2,1)S(1)} %get-tuple-element.35.own_ref), channel_id=1, source_target_pairs={{0,1},{1,0},{2,3},{3,2},{4,5},{5,4},{6,7},{7,6},{8,9},{9,8},{10,11... | collective-permute-start | bytes 983048 | tf_op jit(solution)/shard_map/ppermute | solution.py:455
  62.4 5.4 %collective-permute-start.12 = (bf16[240,256]{1,0:T(8,128)(2,1)S(1)}, bf16[240,256]{1,0:T(8,128)(2,1)S(1)}, u32[]{:S(2)}, u32[]{:S(2)}) collective-permute-start(bf16[240,256]{1,0:T(8,128)(2,1)S(1)} %get-tuple-element.51), channel_id=1, source_target_pairs={{0,4},{2,6},{4,0},{6,2},{8,12},{10,14},{12,8},{14,10},{16,20},{18,... | collective-permute-start | bytes 368648 | tf_op jit(solution)/shard_map/ppermute | solution.py:458
  62.9 6.2 %collective-permute-start.13 = (bf16[240,256]{1,0:T(8,128)(2,1)S(1)}, bf16[240,256]{1,0:T(8,128)(2,1)S(1)}, u32[]{:S(2)}, u32[]{:S(2)}) collective-permute-start(bf16[240,256]{1,0:T(8,128)(2,1)S(1)} %get-tuple-element.52), channel_id=1, source_target_pairs={{0,8},{2,10},{4,12},{6,14},{8,0},{10,2},{12,4},{14,6},{16,24},{18,... | collective-permute-start | bytes 368648 | tf_op jit(solution)/shard_map/ppermute | solution.py:458
  64.3 7.3 %collective-permute-start.14 = (bf16[240,256]{1,0:T(8,128)(2,1)S(1)}, bf16[240,256]{1,0:T(8,128)(2,1)S(1)}, u32[]{:S(2)}, u32[]{:S(2)}) collective-permute-start(bf16[240,256]{1,0:T(8,128)(2,1)S(1)} %get-tuple-element.53), channel_id=1, source_target_pairs={{0,12},{2,14},{4,8},{6,10},{8,4},{10,6},{12,0},{14,2},{16,28},{18,... | collective-permute-start | bytes 368648 | tf_op jit(solution)/shard_map/ppermute | solution.py:458
  74.1 4.8 %collective-permute-start.15 = (bf16[120,1280]{1,0:T(8,128)(2,1)S(1)}, bf16[120,1280]{1,0:T(8,128)(2,1)S(1)}, u32[]{:S(2)}, u32[]{:S(2)}) collective-permute-start(bf16[120,1280]{1,0:T(8,128)(2,1)S(1)} %get-tuple-element.55), channel_id=1, source_target_pairs={{0,2},{2,0},{4,6},{6,4},{8,10},{10,8},{12,14},{14,12},{16,18},{18,... | collective-permute-start | bytes 921608 | tf_op jit(solution)/shard_map/ppermute | solution.py:458
  74.2 17.0 %collective-permute-start.16 = (bf16[120,1280]{1,0:T(8,128)(2,1)S(1)}, bf16[120,1280]{1,0:T(8,128)(2,1)S(1)}, u32[]{:S(2)}, u32[]{:S(2)}) collective-permute-start(bf16[120,1280]{1,0:T(8,128)(2,1)S(1)} %add_convert_fusion._.refs_0_), channel_id=1, source_target_pairs={{0,16},{2,18},{4,20},{6,22},{8,24},{10,26},{12,28},{14,30},{16,0},... | collective-permute-start | bytes 921608 | tf_op jit(solution)/shard_map/ppermute | solution.py:458

commit v7 on v6

--- a/solution.py
+++ b/solution.py
@@ -184,8 +184,11 @@
     out_ref[...] = total.astype(out_ref.dtype)
 
 
-def pull_kernel(live_ref, places_hbm, grad_hbm, send_ref, places_ref, grad_ref, sems):
+def pull_kernel(
+    live_hbm, places_hbm, grad_hbm, send_ref, live_ref, places_ref, grad_ref, sems
+):
     half, width = send_ref.shape
+    counted = begin((live_hbm,), (live_ref,), sems, 5)
     came = begin((places_hbm,), (places_ref,), sems)
     blocks = [slice(k * width, (k + 1) * width) for k in range(4)]
     came += begin(
@@ -194,6 +197,7 @@
         sems,
         1,
     )
+    counted[0].wait()
     came[0].wait()
     masks = place_masks(
         live_ref, places_ref[...], grad_ref.shape[0], half, half_start(half, False)
@@ -239,7 +243,7 @@
 
 
 def first_kernel(
-    live_ref,
+    live_hbm,
     b_ref,
     normed_ref,
     w_hbm,
@@ -250,14 +254,15 @@
     wq_ref,
     probs_ref,
     send_ref,
+    live_ref,
     w_ref,
     proj_ref,
     attended_ref,
     sems,
 ):
     came = begin(
-        (w_hbm.at[0], w_hbm.at[1], w_hbm.at[2], proj_hbm),
-        (wq_ref, w_ref.at[0], w_ref.at[1], proj_ref),
+        (w_hbm.at[0], w_hbm.at[1], w_hbm.at[2], proj_hbm, live_hbm),
+        (wq_ref, w_ref.at[0], w_ref.at[1], proj_ref, live_ref),
         sems,
     )
     half = send_ref.shape[0]
@@ -272,6 +277,7 @@
         came[t].wait()
         part = jnp.dot(normed_ref[...], w_ref[t - 1], preferred_element_type=jnp.float32)
         pair_ref[t - 1] = (part + b_ref[t : t + 1, :]).astype(jnp.bfloat16)
+    came[4].wait()
     attend(live_ref, query_ref, pair_ref, probs_ref, attended_ref)
     came[3].wait()
     send_ref[...] = jnp.dot(
@@ -457,6 +463,7 @@
     def flip(value, bits):
         return lax.ppermute(value, "clip", [(i, i ^ bits) for i in range(n_clip)])
 
+    counted = jnp.minimum(clip_tokens, rows // 4)
     half = rows // 2
     part, wide = shape((half, width), low), shape((half, width), jnp.float32)
     probs_half = shape((heads, half, rows), low)
@@ -466,13 +473,14 @@
     up_send = call(
         pull_kernel,
         part,
-        "saa",
+        "aaa",
         4 * rows * share_rows * width,
         (clip_tokens, positions, grad_placed),
         (
+            pltpu.SMEM((1,), jnp.int32),
             pltpu.VMEM(positions.shape, jnp.int32),
             pltpu.VMEM(grad_placed.shape, low),
-            pltpu.SemaphoreType.DMA((5,)),
+            pltpu.SemaphoreType.DMA((6,)),
         ),
         limit=62,
     )
@@ -483,7 +491,7 @@
     other_query, pair, own_normed, w_query, other_probs, part_send = call(
         first_kernel,
         (query, shape((2, rows, local), low), part, shape((width, local), low), probs_half, part),
-        "svvaa",
+        "avvaa",
         7 * rows * width * local,
         (
             clip_tokens,
@@ -493,10 +501,11 @@
             w_proj,
         ),
         (
+            pltpu.SMEM((1,), jnp.int32),
             pltpu.VMEM((2, width, local), low),
             pltpu.VMEM((local, width), low),
             attended,
-            pltpu.SemaphoreType.DMA((4,)),
+            pltpu.SemaphoreType.DMA((5,)),
         ),
         limit=49,
     )
@@ -507,7 +516,7 @@
         "svvvvvvv",
         5 * half * width * local,
         (
-            clip_tokens,
+            counted,
             positions,
             grad_placed,
             b_qkv,
@@ -593,7 +602,7 @@
         shape((share_rows, 4 * width), low),
         "svvva",
         8 * rows * share_rows * width,
-        (clip_tokens, positions, merged, other_merged, far_sum),
+        (counted, positions, merged, other_merged, far_sum),
     )
     summed = near_keep + near_came.astype(jnp.float32) + crossing.astype(jnp.float32)
     return (placed, summed[None])

time: 92.7 us -> 93.9 us (1.013)
  Pallas kernels: 29.8 us -> 31 us
    pallas_call x10, Pallas kernels: 29.8 us -> 31 us  [call(): pl.pallas_call(kernel, out_shape=outs, in_specs=[spec[kind] for kind in k...]
  transfers between devices with their start and end apart: 17 -> 17, of which waited for: 8 -> 8; matrix products, arithmetic and copies ran while one was open for 2% -> 2% of each run, Pallas kernels for 28% -> 29%
where the time goes in v7:
time: 93.9 us; the launch traced here: 93.3 us
  Pallas kernels  31 us (33%)
  waiting for transfers between devices  27.6 us (29%)
  starting transfers between devices  19.7 us (21%)
  local copies, waits for them, and re-layouts  12.5 us (13%)
  between operations  1.47 us (2%)
  other arithmetic  0.99 us (1%)
    pallas_call x10, Pallas kernels, call(): pl.pallas_call(kernel, out_shape=outs, in_specs=[spec[kind] for kind in k...  31 us
    ppermute x13, waiting for transfers between devices, flip(): return lax.ppermute(value, 'clip', [(i, i ^ bits) for i in range(n_clip)])  23.3 us
    ppermute x13, starting transfers between devices, flip(): return lax.ppermute(value, 'clip', [(i, i ^ bits) for i in range(n_clip)])  15.5 us
    unnamed x42, local copies, waits for them, and re-layouts  10.5 us
    ppermute x4, waiting for transfers between devices, swap(): return lax.ppermute(value, 'seq', [(0, 1), (1, 0)])  4.28 us
    ppermute x4, starting transfers between devices, swap(): return lax.ppermute(value, 'seq', [(0, 1), (1, 0)])  4.24 us
  transfers between devices with their start and end apart: 17, of which 8 were waited for; matrix products, arithmetic and copies ran while one was open for 2% of the time, Pallas kernels for 29%

profile of v7, /device:TPU:0, one launch (start us, length us, event | category | flops | bytes accessed | tf_op | source)
XLA Modules:
  0.0 93.3 jit_solution(15108023892034726837)
XLA Ops:
  0.6 0.0 copy-start.5
  0.6 1.1 %copy-done.5 = bf16[256,1280]{1,0:T(8,128)(2,1)S(1)} copy-done((bf16[256,1280]{1,0:T(8,128)(2,1)S(1)}, bf16[256,1280]{1,0:T(8,128)(2,1)}, u32[]{:S(2)}) %copy-start.5) | copy-done | bytes 655384
  1.7 0.7 copy-done.18
  2.4 0.7 copy-done.19
  3.1 1.3 %shard_map.131.normed_ref.n0 = bf16[256,1280]{1,0:T(8,128)(2,1)} custom-call(f32[1280]{0:T(1024)S(1)} %copy-done.18, f32[1280]{0:T(1024)S(1)} %copy-done.19, bf16[256,1280]{1,0:T(8,128)(2,1)S(1)} %copy-done.5), custom_call_target="tpu_custom_call" | custom-call | flops 32768000 | bytes 4000000 | tf_op jit(solution)/shard_map/pallas_call | solution.py:426
  4.4 3.0 %collective-permute-start.7 = (bf16[256,1280]{1,0:T(8,128)(2,1)}, bf16[256,1280]{1,0:T(8,128)(2,1)}, u32[]{:S(2)}, u32[]{:S(2)}) collective-permute-start(bf16[256,1280]{1,0:T(8,128)(2,1)} %shard_map.131.normed_ref.n0), channel_id=1, source_target_pairs={{0,4},{2,6},{4,0},{6,2},{8,12},{10,14},{12,8},{14,10},{16,20},{18,... | collective-permute-start | bytes 1966088 | tf_op jit(solution)/shard_map/ppermute | solution.py:464
  7.4 1.6 %collective-permute-start.8 = (bf16[256,1280]{1,0:T(8,128)(2,1)}, bf16[256,1280]{1,0:T(8,128)(2,1)}, u32[]{:S(2)}, u32[]{:S(2)}) collective-permute-start(bf16[256,1280]{1,0:T(8,128)(2,1)} %shard_map.131.normed_ref.n0), channel_id=1, source_target_pairs={{0,8},{2,10},{4,12},{6,14},{8,0},{10,2},{12,4},{14,6},{16,24},{18,... | collective-permute-start | bytes 1966088 | tf_op jit(solution)/shard_map/ppermute | solution.py:464
  9.6 0.0 copy-start.13
  9.7 0.7 copy-done.13
  10.3 7.9 %shard_map.132 = (bf16[128,640]{1,0:T(8,128)(2,1)S(1)}, bf16[2,256,640]{2,1,0:T(8,128)(2,1)S(1)}, bf16[128,1280]{1,0:T(8,128)(2,1)S(1)}, bf16[1280,640]{1,0:T(8,...) custom-call(s32[1]{0:T(128)S(6)} %copy.14.live_hbm, f32[3,640]{1,0:T(4,128)S(1)} %copy-done.13, ...), custom_call_target="tpu_custom_call" | custom-call | flops 1468006400 | bytes 4000000 | tf_op jit(solution)/shard_map/pallas_call | solution.py:426
  18.3 0.0 copy-start.1
  18.3 0.8 copy-done.1
  19.1 1.2 %copy-done.7 = bf16[1280,640]{1,0:T(8,128)(2,1)} copy-done((bf16[1280,640]{1,0:T(8,128)(2,1)}, bf16[1280,640]{1,0:T(8,128)(2,1)S(1)}, u32[]{:S(2)}) %copy-start.7) | copy-done | bytes 1638424
  20.3 0.8 copy-done.9
  21.1 0.7 copy-done.11
  21.8 1.5 %collective-permute-start = (bf16[128,1280]{1,0:T(8,128)(2,1)}, bf16[128,1280]{1,0:T(8,128)(2,1)}, u32[]{:S(2)}, u32[]{:S(2)}) collective-permute-start(bf16[128,1280]{1,0:T(8,128)(2,1)} %get-tuple-element.33), channel_id=1, source_target_pairs={{0,1},{1,0},{2,3},{3,2},{4,5},{5,4},{6,7},{7,6},{8,9},{9,8},{10,11... | collective-permute-start | bytes 983048 | tf_op jit(solution)/shard_map/ppermute | solution.py:461
  23.3 2.6 %shard_map.134 = bf16[128,1280]{1,0:T(8,128)(2,1)} custom-call(s32[1]{0:T(128)S(6)} %copy.14.live_hbm, s32[1,64]{1,0:T(1,128)} %places_ref.3, bf16[128,5120]{1,0:T(8,128)(2,1)} %grad_hbm.1), custom_call_target="tpu_custom_call" | custom-call | flops 167772160 | bytes 4000000 | tf_op jit(solution)/shard_map/pallas_call | solution.py:426
  25.9 0.6 collective-permute-start.1
  26.5 1.1 %copy-done.2 = bf16[2,256,640]{2,1,0:T(8,128)(2,1)S(1)} copy-done((bf16[2,256,640]{2,1,0:T(8,128)(2,1)S(1)}, bf16[2,256,640]{2,1,0:T(8,128)(2,1)}, u32[]{:S(2)}) %copy-start.2) | copy-done | bytes 655384
  27.6 1.3 %copy-done.4 = bf16[128,5120]{1,0:T(8,128)(2,1)S(1)} copy-done((bf16[128,5120]{1,0:T(8,128)(2,1)S(1)}, bf16[128,5120]{1,0:T(8,128)(2,1)}, u32[]{:S(2)}) %copy-start.4) | copy-done | bytes 1310744
  28.9 1.4 %copy-done.8 = bf16[1280,640]{1,0:T(8,128)(2,1)S(1)} copy-done((bf16[1280,640]{1,0:T(8,128)(2,1)S(1)}, bf16[1280,640]{1,0:T(8,128)(2,1)}, u32[]{:S(2)}) %copy-start.8) | copy-done | bytes 1638424
  30.4 3.3 %shard_map.133 = (bf16[128,640]{1,0:T(8,128)(2,1)S(1)}, bf16[8,128,256]{2,1,0:T(8,128)(2,1)S(1)}, f32[128,1280]{1,0:T(8,128)S(1)}, bf16[128,1280]{1,0:T(8,128)(2,1)S(1)}) custom-call(s32[1]{0:T(128)S(6)} %min.3.live_ref, s32[1,64]{1,0:T(1,128)S(1)} %copy-done.20, bf16[128,5120]{1,0:T(8,128)(2,1)S(1)} %copy-done.4, f32[3,640]{1,0:T(4,128)S(1)} %copy-done.14, ...), custom_call_target="tpu_custom_call" | custom-call | flops 524288000 | bytes 4000000 | tf_op jit(solution)/shard_map/pallas_call | solution.py:426
  33.6 0.0 collective-permute-done.came_ref
  33.6 4.3 %collective-permute-done.1.up_came_ref = bf16[128,1280]{1,0:T(8,128)(2,1)S(1)} collective-permute-done((bf16[128,1280]{1,0:T(8,128)(2,1)}, bf16[128,1280]{1,0:T(8,128)(2,1)S(1)}, u32[]{:S(2)}, u32[]{:S(2)}) %collective-permute-start.1) | collective-permute-done | bytes 327712 | tf_op jit(solution)/shard_map/ppermute | solution.py:461
  37.9 0.0 copy-done.6
  37.9 0.0 copy-done.16
  37.9 1.6 %shard_map.135 = (bf16[128,1280]{1,0:T(8,128)(2,1)S(1)}, bf16[128,1280]{1,0:T(8,128)(2,1)S(1)}) custom-call(f32[1280]{0:T(1024)S(1)} %copy-done.15, f32[1280]{0:T(1024)S(1)} %copy-done.16, f32[1280]{0:T(1024)S(1)} %copy-done.17, f32[128,1280]{1,0:T(8,128)S(1)} %get-tuple-element.32.keep_ref, bf16[128,1280]{1,0:T(8,128)(2,1)} %collective-permute-done.came_ref, ...), custom_call_target="tpu_custom_call" | custom-call | flops 16384000 | bytes 4000000 | tf_op jit(solution)/shard_map/pallas_call | solution.py:426
  39.5 1.6 %collective-permute-start.3 = (bf16[128,1280]{1,0:T(8,128)(2,1)S(1)}, bf16[128,1280]{1,0:T(8,128)(2,1)S(1)}, u32[]{:S(2)}, u32[]{:S(2)}) collective-permute-start(bf16[128,1280]{1,0:T(8,128)(2,1)S(1)} %get-tuple-element.36.row_ref), channel_id=1, source_target_pairs={{0,1},{1,0},{2,3},{3,2},{4,5},{5,4},{6,7},{7,6},{8,9},{9,8},{10,11... | collective-permute-start | bytes 983048 | tf_op jit(solution)/shard_map/ppermute | solution.py:461
  41.1 0.0 collective-permute-done.7.n1
  41.1 1.0 %slice.9 = bf16[128,1280]{1,0:T(8,128)(2,1)S(1)} slice(bf16[256,1280]{1,0:T(8,128)(2,1)} %collective-permute-done.7.n1), slice={[128:256], [0:1280]} | slice | bytes 655360 | tf_op jit(solution)/shard_map/slice | solution.py:490
  42.1 0.5 collective-permute-start.10
  42.6 0.0 collective-permute-done.8.n2
  42.6 1.0 %slice.8 = bf16[128,1280]{1,0:T(8,128)(2,1)S(1)} slice(bf16[256,1280]{1,0:T(8,128)(2,1)} %collective-permute-done.8.n2), slice={[0:128], [0:1280]} | slice | bytes 655360 | tf_op jit(solution)/shard_map/slice | solution.py:490
  43.6 0.6 collective-permute-start.9
  44.2 3.5 %shard_map.136 = (bf16[640,128]{1,0:T(8,128)(2,1)S(1)}, f32[640,256]{1,0:T(8,128)S(1)}, f32[640,256]{1,0:T(8,128)S(1)}) custom-call(bf16[128,1280]{1,0:T(8,128)(2,1)S(1)} %get-tuple-element.36.row_ref, bf16[640,1280]{1,0:T(8,128)(2,1)S(1)} %copy-done, bf16[128,640]{1,0:T(8,128)(2,1)S(1)} %get-tuple-element.39.q_ref, bf16[2,256,640]{2,1,0:T(8,128)(2,1)S(1)} %copy-done.3, ...), custom_call_target="tpu_custom_call" | custom-call | flops 419430400 | bytes 4000000 | tf_op jit(solution)/shard_map/pallas_call | solution.py:426
  47.7 0.0 collective-permute-done.3.row_ref
  47.8 3.8 %shard_map.137 = (bf16[240,256]{1,0:T(8,128)(2,1)S(1)}, bf16[240,256]{1,0:T(8,128)(2,1)S(1)}, bf16[240,256]{1,0:T(8,128)(2,1)S(1)}, bf16[240,256]{1,0:T(8,128)(2...) custom-call(bf16[128,1280]{1,0:T(8,128)(2,1)S(1)} %collective-permut, ...), custom_call_target="tpu_custom_call" | custom-call | flops 419430400 | bytes 4000000 | tf_op jit(solution)/shard_map/pallas_call | solution.py:426
  51.6 1.6 %collective-permute-start.4 = (bf16[240,256]{1,0:T(8,128)(2,1)S(1)}, bf16[240,256]{1,0:T(8,128)(2,1)S(1)}, u32[]{:S(2)}, u32[]{:S(2)}) collective-permute-start(bf16[240,256]{1,0:T(8,128)(2,1)S(1)} %get-tuple-element.45), channel_id=1, source_target_pairs={{0,4},{2,6},{4,0},{6,2},{8,12},{10,14},{12,8},{14,10},{16,20},{18,... | collective-permute-start | bytes 368648 | tf_op jit(solution)/shard_map/ppermute | solution.py:464
  53.2 1.6 %collective-permute-start.5 = (bf16[240,256]{1,0:T(8,128)(2,1)S(1)}, bf16[240,256]{1,0:T(8,128)(2,1)S(1)}, u32[]{:S(2)}, u32[]{:S(2)}) collective-permute-start(bf16[240,256]{1,0:T(8,128)(2,1)S(1)} %get-tuple-element.46), channel_id=1, source_target_pairs={{0,8},{2,10},{4,12},{6,14},{8,0},{10,2},{12,4},{14,6},{16,24},{18,... | collective-permute-start | bytes 368648 | tf_op jit(solution)/shard_map/ppermute | solution.py:464
  54.7 0.4 collective-permute-start.6
  55.1 2.7 %collective-permute-done.4.t1 = bf16[240,256]{1,0:T(8,128)(2,1)S(1)} collective-permute-done((bf16[240,256]{1,0:T(8,128)(2,1)S(1)}, bf16[240,256]{1,0:T(8,128)(2,1)S(1)}, u32[]{:S(2)}, u32[]{:S(2)}) %collective-permute-start.4) | collective-permute-done | bytes 122912 | tf_op jit(solution)/shard_map/ppermute | solution.py:464
  57.8 0.2 collective-permute-done.5.t2
  58.0 2.5 %collective-permute-done.6.t3 = bf16[240,256]{1,0:T(8,128)(2,1)S(1)} collective-permute-done((bf16[240,256]{1,0:T(8,128)(2,1)S(1)}, bf16[240,256]{1,0:T(8,128)(2,1)S(1)}, u32[]{:S(2)}, u32[]{:S(2)}) %collective-permute-start.6) | collective-permute-done | bytes 122912 | tf_op jit(solution)/shard_map/ppermute | solution.py:464
  60.5 0.0 collective-permute-done.10.n3_high
  60.5 0.0 collective-permute-done.9.n3_low
  60.5 2.4 %shard_map.138 = (f32[120,1280]{1,0:T(8,128)S(1)}, bf16[120,1280]{1,0:T(8,128)(2,1)S(1)}) custom-call(bf16[240,256]{1,0:T(8,128)(2,1)S(1)} %get-tuple-element.44.t0, bf16[240,256]{1,0:T(8,128)(2,1)S(1)} %collective-permute-done.4.t1, bf16[240,256]{1,0:T(8,128)(2,1)S(1)} %collective-permute-done.5.t2, bf16[240,256]{1,0:T(8,128)(2,1)S(1)} %collective-permute-done.6.t3, ...), custom_call_target="tpu_custom_call" | custom-call | flops 629145600 | bytes 4000000 | tf_op jit(solution)/shard_map/pallas_call | solution.py:426
  63.0 0.1 collective-permute-start.11
  63.0 0.6 collective-permute-start.2
  63.6 0.5 collective-permute-start.12
  64.1 1.4 %collective-permute-start.13 = (bf16[240,256]{1,0:T(8,128)(2,1)S(1)}, bf16[240,256]{1,0:T(8,128)(2,1)S(1)}, u32[]{:S(2)}, u32[]{:S(2)}) collective-permute-start(bf16[240,256]{1,0:T(8,128)(2,1)S(1)} %get-tuple-element.52), channel_id=1, source_target_pairs={{0,8},{2,10},{4,12},{6,14},{8,0},{10,2},{12,4},{14,6},{16,24},{18,... | collective-permute-start | bytes 368648 | tf_op jit(solution)/shard_map/ppermute | solution.py:464
  65.5 1.6 %collective-permute-start.14 = (bf16[240,256]{1,0:T(8,128)(2,1)S(1)}, bf16[240,256]{1,0:T(8,128)(2,1)S(1)}, u32[]{:S(2)}, u32[]{:S(2)}) collective-permute-start(bf16[240,256]{1,0:T(8,128)(2,1)S(1)} %get-tuple-element.53), channel_id=1, source_target_pairs={{0,12},{2,14},{4,8},{6,10},{8,4},{10,6},{12,0},{14,2},{16,28},{18,... | collective-permute-start | bytes 368648 | tf_op jit(solution)/shard_map/ppermute | solution.py:464
  67.1 0.0 collective-permute-done.11
  67.1 0.1 add_convert_fusion._.refs_0_
  67.2 1.8 %collective-permute-done.12.t1 = bf16[240,256]{1,0:T(8,128)(2,1)S(1)} collective-permute-done((bf16[240,256]{1,0:T(8,128)(2,1)S(1)}, bf16[240,256]{1,0:T(8,128)(2,1)S(1)}, u32[]{:S(2)}, u32[]{:S(2)}) %collective-permute-start.12) | collective-permute-done | bytes 122912 | tf_op jit(solution)/shard_map/ppermute | solution.py:464
  69.0 1.3 %collective-permute-done.13.t2 = bf16[240,256]{1,0:T(8,128)(2,1)S(1)} collective-permute-done((bf16[240,256]{1,0:T(8,128)(2,1)S(1)}, bf16[240,256]{1,0:T(8,128)(2,1)S(1)}, u32[]{:S(2)}, u32[]{:S(2)}) %collective-permute-start.13) | collective-permute-done | bytes 122912 | tf_op jit(solution)/shard_map/ppermute | solution.py:464
  70.3 2.5 %collective-permute-done.14.t3 = bf16[240,256]{1,0:T(8,128)(2,1)S(1)} collective-permute-done((bf16[240,256]{1,0:T(8,128)(2,1)S(1)}, bf16[240,256]{1,0:T(8,128)(2,1)S(1)}, u32[]{:S(2)}, u32[]{:S(2)}) %collective-permute-start.14) | collective-permute-done | bytes 122912 | tf_op jit(solution)/shard_map/ppermute | solution.py:464
  72.8 2.4 %shard_map.140 = (f32[120,1280]{1,0:T(8,128)S(1)}, bf16[120,1280]{1,0:T(8,128)(2,1)S(1)}) custom-call(bf16[240,256]{1,0:T(8,128)(2,1)S(1)} %get-tuple-element.50.t0, bf16[240,256]{1,0:T(8,128)(2,1)S(1)} %collective-permute-done.12.t1, bf16[240,256]{1,0:T(8,128)(2,1)S(1)} %collective-permute-done.13.t2, bf16[240,256]{1,0:T(8,128)(2,1)S(1)} %collective-permute-done.14.t3, ...), custom_call_target="tpu_custom_call" | custom-call | flops 629145600 | bytes 4000000 | tf_op jit(solution)/shard_map/pallas_call | solution.py:426
  75.3 0.1 collective-permute-start.15
  75.4 2.7 %collective-permute-start.16 = (bf16[120,1280]{1,0:T(8,128)(2,1)S(1)}, bf16[120,1280]{1,0:T(8,128)(2,1)S(1)}, u32[]{:S(2)}, u32[]{:S(2)}) collective-permute-start(bf16[120,1280]{1,0:T(8,128)(2,1)S(1)} %add_convert_fusion._.refs_0_), channel_id=1, source_target_pairs={{0,16},{2,18},{4,20},{6,22},{8,24},{10,26},{12,28},{14,30},{16,0},... | collective-permute-start | bytes 921608 | tf_op jit(solution)/shard_map/ppermute | solution.py:464
  78.0 0.0 collective-permute-done.2.other_ref
  78.0 2.1 %shard_map.139 = bf16[128,5120]{1,0:T(8,128)(2,1)} custom-call(s32[1]{0:T(128)S(6)} %min.3.live_ref, s32[1,64]{1,0:T(1,128)S(1)} %copy-done.20, bf16[128,1280]{1,0:T(8,128)(2,1)S(1)} %get-tuple-element.35.own_ref, bf16[128,1280]{1,0:T(8,128)(2,1)S(1)} %collective-permute-done.2.other_ref, bf16[120,1280]{1,0:T(8,128)(2,1)S(1)} %add_convert_fusion._.refs_0_), custom_call_target="tpu_custom_call" | custom-call | flops 335544320 | bytes 4000000 | tf_op jit(solution)/shard_map/pallas_call | solution.py:426
  80.1 0.0 collective-permute-done.15
  80.1 12.3 %collective-permute-done.16 = bf16[120,1280]{1,0:T(8,128)(2,1)S(1)} collective-permute-done((bf16[120,1280]{1,0:T(8,128)(2,1)S(1)}, bf16[120,1280]{1,0:T(8,128)(2,1)S(1)}, u32[]{:S(2)}, u32[]{:S(2)}) %collective-permute-start.16) | collective-permute-done | bytes 307232 | tf_op jit(solution)/shard_map/ppermute | solution.py:464
  92.4 0.9 add_bitcast_fusion
  (26 shorter events, 0.0 us)
Async XLA Ops:
  0.6 1.1 %copy-start.5 = (bf16[256,1280]{1,0:T(8,128)(2,1)S(1)}, bf16[256,1280]{1,0:T(8,128)(2,1)}, u32[]{:S(2)}) copy-start(bf16[256,1280]{1,0:T(8,128)(2,1)} %patches_ref.3) | copy-start | bytes 1966084
  1.7 0.7 copy-start.18
  2.4 0.7 copy-start.19
  4.4 36.7 %collective-permute-start.7 = (bf16[256,1280]{1,0:T(8,128)(2,1)}, bf16[256,1280]{1,0:T(8,128)(2,1)}, u32[]{:S(2)}, u32[]{:S(2)}) collective-permute-start(bf16[256,1280]{1,0:T(8,128)(2,1)} %shard_map.131.normed_ref.n0), channel_id=1, source_target_pairs={{0,4},{2,6},{4,0},{6,2},{8,12},{10,14},{12,8},{14,10},{16,20},{18,... | collective-permute-start | bytes 1966088 | tf_op jit(solution)/shard_map/ppermute | solution.py:464
  7.4 35.2 %collective-permute-start.8 = (bf16[256,1280]{1,0:T(8,128)(2,1)}, bf16[256,1280]{1,0:T(8,128)(2,1)}, u32[]{:S(2)}, u32[]{:S(2)}) collective-permute-start(bf16[256,1280]{1,0:T(8,128)(2,1)} %shard_map.131.normed_ref.n0), channel_id=1, source_target_pairs={{0,8},{2,10},{4,12},{6,14},{8,0},{10,2},{12,4},{14,6},{16,24},{18,... | collective-permute-start | bytes 1966088 | tf_op jit(solution)/shard_map/ppermute | solution.py:464
  9.6 0.7 copy-start.13
  10.3 16.2 %copy-start.20 = (s32[1,64]{1,0:T(1,128)S(1)}, s32[1,64]{1,0:T(1,128)}, u32[]{:S(2)}) copy-start(s32[1,64]{1,0:T(1,128)} %places_ref.3) | copy-start | bytes 772
  18.3 0.8 copy-start.1
  19.1 1.2 %copy-start.7 = (bf16[1280,640]{1,0:T(8,128)(2,1)}, bf16[1280,640]{1,0:T(8,128)(2,1)S(1)}, u32[]{:S(2)}) copy-start(bf16[1280,640]{1,0:T(8,128)(2,1)S(1)} %get-tuple-element.30.w_ref) | copy-start | bytes 4915204
  20.3 0.8 copy-start.9
  21.1 0.7 copy-start.11
  21.8 4.7 %copy-start = (bf16[640,1280]{1,0:T(8,128)(2,1)S(1)}, bf16[640,1280]{1,0:T(8,128)(2,1)}, u32[]{:S(2)}) copy-start(bf16[640,1280]{1,0:T(8,128)(2,1)} %proj_ref.5) | copy-start | bytes 4915204
  21.8 4.7 %copy-start.14 = (f32[3,640]{1,0:T(4,128)S(1)}, f32[3,640]{1,0:T(4,128)}, u32[]{:S(2)}) copy-start(f32[3,640]{1,0:T(4,128)} %b_ref.4) | copy-start | bytes 23044
  21.8 11.8 %collective-permute-start = (bf16[128,1280]{1,0:T(8,128)(2,1)}, bf16[128,1280]{1,0:T(8,128)(2,1)}, u32[]{:S(2)}, u32[]{:S(2)}) collective-permute-start(bf16[128,1280]{1,0:T(8,128)(2,1)} %get-tuple-element.33), channel_id=1, source_target_pairs={{0,1},{1,0},{2,3},{3,2},{4,5},{5,4},{6,7},{7,6},{8,9},{9,8},{10,11... | collective-permute-start | bytes 983048 | tf_op jit(solution)/shard_map/ppermute | solution.py:461
  25.9 12.0 %collective-permute-start.1 = (bf16[128,1280]{1,0:T(8,128)(2,1)}, bf16[128,1280]{1,0:T(8,128)(2,1)S(1)}, u32[]{:S(2)}, u32[]{:S(2)}) collective-permute-start(bf16[128,1280]{1,0:T(8,128)(2,1)} %shard_map.134), channel_id=1, source_target_pairs={{0,1},{1,0},{2,3},{3,2},{4,5},{5,4},{6,7},{7,6},{8,9},{9,8},{10,11... | collective-permute-start | bytes 983048 | tf_op jit(solution)/shard_map/ppermute | solution.py:461
  26.5 1.1 %copy-start.2 = (bf16[2,256,640]{2,1,0:T(8,128)(2,1)S(1)}, bf16[2,256,640]{2,1,0:T(8,128)(2,1)}, u32[]{:S(2)}) copy-start(bf16[2,256,640]{2,1,0:T(8,128)(2,1)} %copy-done.1) | copy-start | bytes 1966084
  27.6 1.3 %copy-start.4 = (bf16[128,5120]{1,0:T(8,128)(2,1)S(1)}, bf16[128,5120]{1,0:T(8,128)(2,1)}, u32[]{:S(2)}) copy-start(bf16[128,5120]{1,0:T(8,128)(2,1)} %grad_hbm.1) | copy-start | bytes 3932164
  28.9 1.4 %copy-start.8 = (bf16[1280,640]{1,0:T(8,128)(2,1)S(1)}, bf16[1280,640]{1,0:T(8,128)(2,1)}, u32[]{:S(2)}) copy-start(bf16[1280,640]{1,0:T(8,128)(2,1)} %copy-done.7) | copy-start | bytes 4915204
  30.3 7.6 %copy-start.6 = (bf16[256,1280]{1,0:T(8,128)(2,1)S(1)}, bf16[256,1280]{1,0:T(8,128)(2,1)}, u32[]{:S(2)}) copy-start(bf16[256,1280]{1,0:T(8,128)(2,1)} %patches_ref.3) | copy-start | bytes 1966084
  30.3 7.6 %copy-start.15 = (f32[1280]{0:T(1024)S(1)}, f32[1280]{0:T(1024)}, u32[]{:S(2)}) copy-start(f32[1280]{0:T(1024)} %b_ref.5) | copy-start | bytes 15364
  30.3 7.6 %copy-start.16 = (f32[1280]{0:T(1024)S(1)}, f32[1280]{0:T(1024)}, u32[]{:S(2)}) copy-start(f32[1280]{0:T(1024)} %gain_ref.3) | copy-start | bytes 15364
  30.4 7.6 %copy-start.17 = (f32[1280]{0:T(1024)S(1)}, f32[1280]{0:T(1024)}, u32[]{:S(2)}) copy-start(f32[1280]{0:T(1024)} %bias_ref.3) | copy-start | bytes 15364
  37.9 6.3 %copy-start.3 = (bf16[2,256,640]{2,1,0:T(8,128)(2,1)S(1)}, bf16[2,256,640]{2,1,0:T(8,128)(2,1)}, u32[]{:S(2)}) copy-start(bf16[2,256,640]{2,1,0:T(8,128)(2,1)} %copy-done.1) | copy-start | bytes 1966084
  39.5 8.2 %collective-permute-start.3 = (bf16[128,1280]{1,0:T(8,128)(2,1)S(1)}, bf16[128,1280]{1,0:T(8,128)(2,1)S(1)}, u32[]{:S(2)}, u32[]{:S(2)}) collective-permute-start(bf16[128,1280]{1,0:T(8,128)(2,1)S(1)} %get-tuple-element.36.row_ref), channel_id=1, source_target_pairs={{0,1},{1,0},{2,3},{3,2},{4,5},{5,4},{6,7},{7,6},{8,9},{9,8},{10,11... | collective-permute-start | bytes 983048 | tf_op jit(solution)/shard_map/ppermute | solution.py:461
  42.1 18.4 %collective-permute-start.10 = (bf16[128,1280]{1,0:T(8,128)(2,1)S(1)}, bf16[128,1280]{1,0:T(8,128)(2,1)S(1)}, u32[]{:S(2)}, u32[]{:S(2)}) collective-permute-start(bf16[128,1280]{1,0:T(8,128)(2,1)S(1)} %slice.9), channel_id=1, source_target_pairs={{0,8},{2,10},{4,12},{6,14},{8,0},{10,2},{12,4},{14,6},{16,24},{18,... | collective-permute-start | bytes 983048 | tf_op jit(solution)/shard_map/ppermute | solution.py:464
  43.6 16.9 %collective-permute-start.9 = (bf16[128,1280]{1,0:T(8,128)(2,1)S(1)}, bf16[128,1280]{1,0:T(8,128)(2,1)S(1)}, u32[]{:S(2)}, u32[]{:S(2)}) collective-permute-start(bf16[128,1280]{1,0:T(8,128)(2,1)S(1)} %slice.8), channel_id=1, source_target_pairs={{0,4},{2,6},{4,0},{6,2},{8,12},{10,14},{12,8},{14,10},{16,20},{18,... | collective-permute-start | bytes 983048 | tf_op jit(solution)/shard_map/ppermute | solution.py:464
  44.2 3.6 %copy-start.10 = (bf16[8,128,256]{2,1,0:T(8,128)(2,1)S(1)}, bf16[8,128,256]{2,1,0:T(8,128)(2,1)}, u32[]{:S(2)}) copy-start(bf16[8,128,256]{2,1,0:T(8,128)(2,1)} %copy-done.9) | copy-start | bytes 1572868
  44.2 3.6 %copy-start.12 = (bf16[128,640]{1,0:T(8,128)(2,1)S(1)}, bf16[128,640]{1,0:T(8,128)(2,1)}, u32[]{:S(2)}) copy-start(bf16[128,640]{1,0:T(8,128)(2,1)} %copy-done.11) | copy-start | bytes 491524
  51.6 6.3 %collective-permute-start.4 = (bf16[240,256]{1,0:T(8,128)(2,1)S(1)}, bf16[240,256]{1,0:T(8,128)(2,1)S(1)}, u32[]{:S(2)}, u32[]{:S(2)}) collective-permute-start(bf16[240,256]{1,0:T(8,128)(2,1)S(1)} %get-tuple-element.45), channel_id=1, source_target_pairs={{0,4},{2,6},{4,0},{6,2},{8,12},{10,14},{12,8},{14,10},{16,20},{18,... | collective-permute-start | bytes 368648 | tf_op jit(solution)/shard_map/ppermute | solution.py:464
  53.2 4.9 %collective-permute-start.5 = (bf16[240,256]{1,0:T(8,128)(2,1)S(1)}, bf16[240,256]{1,0:T(8,128)(2,1)S(1)}, u32[]{:S(2)}, u32[]{:S(2)}) collective-permute-start(bf16[240,256]{1,0:T(8,128)(2,1)S(1)} %get-tuple-element.46), channel_id=1, source_target_pairs={{0,8},{2,10},{4,12},{6,14},{8,0},{10,2},{12,4},{14,6},{16,24},{18,... | collective-permute-start | bytes 368648 | tf_op jit(solution)/shard_map/ppermute | solution.py:464
  54.7 5.8 %collective-permute-start.6 = (bf16[240,256]{1,0:T(8,128)(2,1)S(1)}, bf16[240,256]{1,0:T(8,128)(2,1)S(1)}, u32[]{:S(2)}, u32[]{:S(2)}) collective-permute-start(bf16[240,256]{1,0:T(8,128)(2,1)S(1)} %get-tuple-element.47), channel_id=1, source_target_pairs={{0,12},{2,14},{4,8},{6,10},{8,4},{10,6},{12,0},{14,2},{16,28},{18,... | collective-permute-start | bytes 368648 | tf_op jit(solution)/shard_map/ppermute | solution.py:464
  63.0 4.2 %collective-permute-start.11 = (bf16[120,1280]{1,0:T(8,128)(2,1)S(1)}, bf16[120,1280]{1,0:T(8,128)(2,1)S(1)}, u32[]{:S(2)}, u32[]{:S(2)}) collective-permute-start(bf16[120,1280]{1,0:T(8,128)(2,1)S(1)} %get-tuple-element.49), channel_id=1, source_target_pairs={{0,2},{2,0},{4,6},{6,4},{8,10},{10,8},{12,14},{14,12},{16,18},{18,... | collective-permute-start | bytes 921608 | tf_op jit(solution)/shard_map/ppermute | solution.py:464
  63.0 15.0 %collective-permute-start.2 = (bf16[128,1280]{1,0:T(8,128)(2,1)S(1)}, bf16[128,1280]{1,0:T(8,128)(2,1)S(1)}, u32[]{:S(2)}, u32[]{:S(2)}) collective-permute-start(bf16[128,1280]{1,0:T(8,128)(2,1)S(1)} %get-tuple-element.35.own_ref), channel_id=1, source_target_pairs={{0,1},{1,0},{2,3},{3,2},{4,5},{5,4},{6,7},{7,6},{8,9},{9,8},{10,11... | collective-permute-start | bytes 983048 | tf_op jit(solution)/shard_map/ppermute | solution.py:461
  63.6 5.4 %collective-permute-start.12 = (bf16[240,256]{1,0:T(8,128)(2,1)S(1)}, bf16[240,256]{1,0:T(8,128)(2,1)S(1)}, u32[]{:S(2)}, u32[]{:S(2)}) collective-permute-start(bf16[240,256]{1,0:T(8,128)(2,1)S(1)} %get-tuple-element.51), channel_id=1, source_target_pairs={{0,4},{2,6},{4,0},{6,2},{8,12},{10,14},{12,8},{14,10},{16,20},{18,... | collective-permute-start | bytes 368648 | tf_op jit(solution)/shard_map/ppermute | solution.py:464
  64.1 6.2 %collective-permute-start.13 = (bf16[240,256]{1,0:T(8,128)(2,1)S(1)}, bf16[240,256]{1,0:T(8,128)(2,1)S(1)}, u32[]{:S(2)}, u32[]{:S(2)}) collective-permute-start(bf16[240,256]{1,0:T(8,128)(2,1)S(1)} %get-tuple-element.52), channel_id=1, source_target_pairs={{0,8},{2,10},{4,12},{6,14},{8,0},{10,2},{12,4},{14,6},{16,24},{18,... | collective-permute-start | bytes 368648 | tf_op jit(solution)/shard_map/ppermute | solution.py:464
  65.5 7.3 %collective-permute-start.14 = (bf16[240,256]{1,0:T(8,128)(2,1)S(1)}, bf16[240,256]{1,0:T(8,128)(2,1)S(1)}, u32[]{:S(2)}, u32[]{:S(2)}) collective-permute-start(bf16[240,256]{1,0:T(8,128)(2,1)S(1)} %get-tuple-element.53), channel_id=1, source_target_pairs={{0,12},{2,14},{4,8},{6,10},{8,4},{10,6},{12,0},{14,2},{16,28},{18,... | collective-permute-start | bytes 368648 | tf_op jit(solution)/shard_map/ppermute | solution.py:464
  75.3 4.8 %collective-permute-start.15 = (bf16[120,1280]{1,0:T(8,128)(2,1)S(1)}, bf16[120,1280]{1,0:T(8,128)(2,1)S(1)}, u32[]{:S(2)}, u32[]{:S(2)}) collective-permute-start(bf16[120,1280]{1,0:T(8,128)(2,1)S(1)} %get-tuple-element.55), channel_id=1, source_target_pairs={{0,2},{2,0},{4,6},{6,4},{8,10},{10,8},{12,14},{14,12},{16,18},{18,... | collective-permute-start | bytes 921608 | tf_op jit(solution)/shard_map/ppermute | solution.py:464
  75.4 17.0 %collective-permute-start.16 = (bf16[120,1280]{1,0:T(8,128)(2,1)S(1)}, bf16[120,1280]{1,0:T(8,128)(2,1)S(1)}, u32[]{:S(2)}, u32[]{:S(2)}) collective-permute-start(bf16[120,1280]{1,0:T(8,128)(2,1)S(1)} %add_convert_fusion._.refs_0_), channel_id=1, source_target_pairs={{0,16},{2,18},{4,20},{6,22},{8,24},{10,26},{12,28},{14,30},{16,0},... | collective-permute-start | bytes 921608 | tf_op jit(solution)/shard_map/ppermute | solution.py:464

commit v8 on v7

--- a/solution.py
+++ b/solution.py
@@ -298,8 +298,10 @@
     probs_ref,
     keep_ref,
     up_ref,
+    turned_ref,
     attended_ref,
 ):
+    turned_ref[...] = proj_ref[...].T
     pull(live_ref, places_ref, grad_ref, up_ref, True)
     part = jnp.dot(own_ref[...], w_ref[...], preferred_element_type=jnp.float32)
     query_ref[...] = (part + b_ref[0:1, :]).astype(jnp.bfloat16)
@@ -333,8 +335,10 @@
     back_ref[...] = normalize_back(upstream, unit_rows, inverse, gain).astype(jnp.bfloat16)
 
 
-def attend_back(row_ref, proj_ref, query_ref, pair_ref, probs_ref, back_ref, put):
-    back_ref[...] = trailing(row_ref[...], proj_ref[...]).astype(jnp.bfloat16)
+def attend_back(row_ref, turned_ref, query_ref, pair_ref, probs_ref, back_ref, put):
+    back_ref[...] = jnp.dot(
+        row_ref[...], turned_ref[...], preferred_element_type=jnp.float32
+    ).astype(jnp.bfloat16)
     scaling = HEAD ** (-0.5)
     for h in range(probs_ref.shape[0]):
         cols = slice(h * HEAD, (h + 1) * HEAD)
@@ -344,18 +348,15 @@
         wide = weights.astype(jnp.float32)
         inner = jnp.sum(prob_grad * wide, axis=-1, keepdims=True)
         score_grad = (wide * (prob_grad - inner)).astype(jnp.bfloat16)
-        query_grad = lax.dot_general(
-            pair_ref[0, :, cols],
-            score_grad,
-            (((0,), (1,)), ((), ())),
-            preferred_element_type=jnp.float32,
+        query_grad = jnp.dot(
+            score_grad, pair_ref[0, :, cols], preferred_element_type=jnp.float32
         )
         key_grad = leading(query_ref[:, cols], score_grad)
-        put(h, query_grad * scaling, key_grad * scaling, leading(back, weights))
+        put(h, (query_grad * scaling).T, key_grad * scaling, leading(back, weights))
 
 
 def own_back_kernel(
-    row_ref, proj_ref, q_ref, pair_ref, probs_ref, query_ref, key_ref, value_ref, back_ref
+    row_ref, turned_ref, q_ref, pair_ref, probs_ref, query_ref, key_ref, value_ref, back_ref
 ):
     def put(h, query_grad, key_grad, value_grad):
         rows = slice(h * HEAD, (h + 1) * HEAD)
@@ -363,11 +364,11 @@
         key_ref[rows, :] = key_grad
         value_ref[rows, :] = value_grad
 
-    attend_back(row_ref, proj_ref, q_ref, pair_ref, probs_ref, back_ref, put)
+    attend_back(row_ref, turned_ref, q_ref, pair_ref, probs_ref, back_ref, put)
 
 
 def other_back_kernel(
-    row_ref, proj_ref, q_ref, pair_ref, probs_ref, query_ref, key_ref, value_ref, *refs
+    row_ref, turned_ref, q_ref, pair_ref, probs_ref, query_ref, key_ref, value_ref, *refs
 ):
     outs, (back_ref, slots_ref) = refs[:8], refs[8:]
     half = row_ref.shape[0]
@@ -395,7 +396,7 @@
         side, slot, place = where(2, h)
         slots_ref[side, slot, place, :] = (value_ref[rows, :] + value_grad).astype(jnp.bfloat16)
 
-    attend_back(row_ref, proj_ref, q_ref, pair_ref, probs_ref, back_ref, put)
+    attend_back(row_ref, turned_ref, q_ref, pair_ref, probs_ref, back_ref, put)
     for k, out_ref in enumerate(outs):
         out_ref[...] = slots_ref[k // 4, k % 4]
 
@@ -510,9 +511,9 @@
         limit=49,
     )
     part_came = swap(part_send)
-    own_query, own_probs, part_keep, up_keep = call(
+    own_query, own_probs, part_keep, up_keep, turned = call(
         second_kernel,
-        (query, probs_half, wide, part),
+        (query, probs_half, wide, part, shape((width, local), low)),
         "svvvvvvv",
         5 * half * width * local,
         (
@@ -554,7 +555,7 @@
         ),
         "vvvvv",
         4 * half * width * local,
-        (own_rows, w_proj, own_query, pair, own_probs),
+        (own_rows, turned, own_query, pair, own_probs),
         (attended,),
     )
     sent = call(
@@ -564,7 +565,7 @@
         4 * half * width * local,
         (
             other_rows,
-            w_proj,
+            turned,
             other_query,
             pair,
             other_probs,

time: 93.9 us -> 90.2 us (0.961)
  Pallas kernels: 31 us -> 27 us
  starting transfers between devices: 19.7 us -> 20.8 us
  waiting for transfers between devices: 27.6 us -> 26.6 us
    pallas_call x10, Pallas kernels: 31 us -> 27 us  [call(): pl.pallas_call(kernel, out_shape=outs, in_specs=[spec[kind] for kind in k...]
    unnamed x42 -> x40, local copies, waits for them, and re-layouts: 10.5 us -> 11.7 us
    ppermute x13, waiting for transfers between devices: 23.3 us -> 22.2 us  [flip(): return lax.ppermute(value, 'clip', [(i, i ^ bits) for i in range(n_clip)])]
    slice x1, local copies, waits for them, and re-layouts: 0.99 us -> 0.02 us  [fast_body(): normed_of[1][half:]]
    ppermute x4, starting transfers between devices: 4.24 us -> 5.21 us  [swap(): return lax.ppermute(value, 'seq', [(0, 1), (1, 0)])]
  transfers between devices with their start and end apart: 17 -> 17, of which waited for: 8 -> 9; matrix products, arithmetic and copies ran while one was open for 2% -> 1% of each run, Pallas kernels for 29% -> 27%
where the time goes in v8:
time: 90.2 us; the launch traced here: 89.6 us
  Pallas kernels  27 us (30%)
  waiting for transfers between devices  26.6 us (29%)
  starting transfers between devices  20.8 us (23%)
  local copies, waits for them, and re-layouts  12.8 us (14%)
  between operations  1.44 us (2%)
  other arithmetic  0.99 us (1%)
    pallas_call x10, Pallas kernels, call(): pl.pallas_call(kernel, out_shape=outs, in_specs=[spec[kind] for kind in k...  27 us
    ppermute x13, waiting for transfers between devices, flip(): return lax.ppermute(value, 'clip', [(i, i ^ bits) for i in range(n_clip)])  22.2 us
    ppermute x13, starting transfers between devices, flip(): return lax.ppermute(value, 'clip', [(i, i ^ bits) for i in range(n_clip)])  15.6 us
    unnamed x40, local copies, waits for them, and re-layouts  11.7 us
    ppermute x4, starting transfers between devices, swap(): return lax.ppermute(value, 'seq', [(0, 1), (1, 0)])  5.21 us
    ppermute x4, waiting for transfers between devices, swap(): return lax.ppermute(value, 'seq', [(0, 1), (1, 0)])  4.34 us
  transfers between devices with their start and end apart: 17, of which 9 were waited for; matrix products, arithmetic and copies ran while one was open for 1% of the time, Pallas kernels for 27%

profile of v8, /device:TPU:0, one launch (start us, length us, event | category | flops | bytes accessed | tf_op | source)
XLA Modules:
  0.0 89.6 jit_solution(9106260703999277479)
XLA Ops:
  0.6 0.0 copy-start.2
  0.6 1.1 %copy-done.2 = bf16[256,1280]{1,0:T(8,128)(2,1)S(1)} copy-done((bf16[256,1280]{1,0:T(8,128)(2,1)S(1)}, bf16[256,1280]{1,0:T(8,128)(2,1)}, u32[]{:S(2)}) %copy-start.2) | copy-done | bytes 655384
  1.7 0.7 copy-done.17
  2.4 0.7 copy-done.18
  3.1 0.5 shard_map.131.normed_ref.n0
  3.6 3.1 %collective-permute-start.7 = (bf16[256,1280]{1,0:T(8,128)(2,1)S(1)}, bf16[256,1280]{1,0:T(8,128)(2,1)S(1)}, u32[]{:S(2)}, u32[]{:S(2)}) collective-permute-start(bf16[256,1280]{1,0:T(8,128)(2,1)S(1)} %shard_map.131.normed_ref.n0), channel_id=1, source_target_pairs={{0,4},{2,6},{4,0},{6,2},{8,12},{10,14},{12,8},{14,10},{16,20},{18,... | collective-permute-start | bytes 1966088 | tf_op jit(solution)/shard_map/ppermute | solution.py:465
  6.6 1.6 %collective-permute-start.8 = (bf16[256,1280]{1,0:T(8,128)(2,1)S(1)}, bf16[256,1280]{1,0:T(8,128)(2,1)}, u32[]{:S(2)}, u32[]{:S(2)}) collective-permute-start(bf16[256,1280]{1,0:T(8,128)(2,1)S(1)} %shard_map.131.normed_ref.n0), channel_id=1, source_target_pairs={{0,8},{2,10},{4,12},{6,14},{8,0},{10,2},{12,4},{14,6},{16,24},{18,... | collective-permute-start | bytes 1966088 | tf_op jit(solution)/shard_map/ppermute | solution.py:465
  8.9 0.0 copy-start.12
  8.9 0.7 copy-done.12
  9.6 6.8 %shard_map.132 = (bf16[128,640]{1,0:T(8,128)(2,1)S(1)}, bf16[2,256,640]{2,1,0:T(8,128)(2,1)S(1)}, bf16[128,1280]{1,0:T(8,128)(2,1)S(1)}, bf16[1280,640]{1,0:T(8,...) custom-call(s32[1]{0:T(128)S(6)} %copy.14.live_hbm, f32[3,640]{1,0:T(4,128)S(1)} %copy-done.12, ...), custom_call_target="tpu_custom_call" | custom-call | flops 1468006400 | bytes 4000000 | tf_op jit(solution)/shard_map/pallas_call | solution.py:427
  16.4 0.0 copy-start.4
  16.4 1.2 %copy-done.4 = bf16[1280,640]{1,0:T(8,128)(2,1)} copy-done((bf16[1280,640]{1,0:T(8,128)(2,1)}, bf16[1280,640]{1,0:T(8,128)(2,1)S(1)}, u32[]{:S(2)}) %copy-start.4) | copy-done | bytes 1638424
  17.6 0.8 copy-done.6
  18.4 0.7 copy-done.8
  19.2 0.7 copy-done.10
  19.8 1.5 %collective-permute-start = (bf16[128,1280]{1,0:T(8,128)(2,1)}, bf16[128,1280]{1,0:T(8,128)(2,1)}, u32[]{:S(2)}, u32[]{:S(2)}) collective-permute-start(bf16[128,1280]{1,0:T(8,128)(2,1)} %get-tuple-element.34), channel_id=1, source_target_pairs={{0,1},{1,0},{2,3},{3,2},{4,5},{5,4},{6,7},{7,6},{8,9},{9,8},{10,11... | collective-permute-start | bytes 983048 | tf_op jit(solution)/shard_map/ppermute | solution.py:462
  21.3 2.6 %shard_map.134 = bf16[128,1280]{1,0:T(8,128)(2,1)} custom-call(s32[1]{0:T(128)S(6)} %copy.14.live_hbm, s32[1,64]{1,0:T(1,128)} %places_ref.3, bf16[128,5120]{1,0:T(8,128)(2,1)} %grad_hbm.1), custom_call_target="tpu_custom_call" | custom-call | flops 167772160 | bytes 4000000 | tf_op jit(solution)/shard_map/pallas_call | solution.py:427
  23.9 0.6 collective-permute-start.1
  24.5 0.0 copy-done.19
  24.5 1.4 %copy-done = bf16[640,1280]{1,0:T(8,128)(2,1)S(1)} copy-done((bf16[640,1280]{1,0:T(8,128)(2,1)S(1)}, bf16[640,1280]{1,0:T(8,128)(2,1)}, u32[]{:S(2)}) %copy-start) | copy-done | bytes 1638424
  26.0 1.3 %copy-done.1 = bf16[128,5120]{1,0:T(8,128)(2,1)S(1)} copy-done((bf16[128,5120]{1,0:T(8,128)(2,1)S(1)}, bf16[128,5120]{1,0:T(8,128)(2,1)}, u32[]{:S(2)}) %copy-start.1) | copy-done | bytes 1310744
  27.3 1.4 %copy-done.5 = bf16[1280,640]{1,0:T(8,128)(2,1)S(1)} copy-done((bf16[1280,640]{1,0:T(8,128)(2,1)S(1)}, bf16[1280,640]{1,0:T(8,128)(2,1)}, u32[]{:S(2)}) %copy-start.5) | copy-done | bytes 1638424
  28.7 1.0 %copy-done.9 = bf16[128,1280]{1,0:T(8,128)(2,1)S(1)} copy-done((bf16[128,1280]{1,0:T(8,128)(2,1)S(1)}, bf16[128,1280]{1,0:T(8,128)(2,1)}, u32[]{:S(2)}) %copy-start.9) | copy-done | bytes 327704
  29.7 3.5 %shard_map.133 = (bf16[128,640]{1,0:T(8,128)(2,1)S(1)}, bf16[8,128,256]{2,1,0:T(8,128)(2,1)S(1)}, f32[128,1280]{1,0:T(8,128)S(1)}, bf16[128,1280]{1,0:T(8,128)(2,1)S(1)}, bf16[1280,640]{1,0:T(8,128)(2,1)S(1)}) custom-call(s32[1]{0:T(128)S(6)} %min.3.live_ref, s32[1,64]{1,0:T(1,128)S(1)} %copy-done.19, bf16[128,5120]{1,0:T(8,128)(2,1)S(1)} %copy-done.1, ...), custom_call_target="tpu_custom_call" | custom-call | flops 524288000 | bytes 4000000 | tf_op jit(solution)/shard_map/pallas_call | solution.py:427
  33.2 0.0 collective-permute-done.came_ref
  33.2 2.7 %collective-permute-done.1.up_came_ref = bf16[128,1280]{1,0:T(8,128)(2,1)S(1)} collective-permute-done((bf16[128,1280]{1,0:T(8,128)(2,1)}, bf16[128,1280]{1,0:T(8,128)(2,1)S(1)}, u32[]{:S(2)}, u32[]{:S(2)}) %collective-permute-start.1) | collective-permute-done | bytes 327712 | tf_op jit(solution)/shard_map/ppermute | solution.py:462
  36.0 0.0 copy-done.15
  36.0 1.5 %shard_map.135 = (bf16[128,1280]{1,0:T(8,128)(2,1)S(1)}, bf16[128,1280]{1,0:T(8,128)(2,1)S(1)}) custom-call(f32[1280]{0:T(1024)S(1)} %copy-done.14, f32[1280]{0:T(1024)S(1)} %copy-done.15, f32[1280]{0:T(1024)S(1)} %copy-done.16, f32[128,1280]{1,0:T(8,128)S(1)} %get-tuple-element.33.keep_ref, bf16[128,1280]{1,0:T(8,128)(2,1)} %collective-permute-done.came_ref, ...), custom_call_target="tpu_custom_call" | custom-call | flops 16384000 | bytes 4000000 | tf_op jit(solution)/shard_map/pallas_call | solution.py:427
  37.5 1.6 %collective-permute-start.3 = (bf16[128,1280]{1,0:T(8,128)(2,1)S(1)}, bf16[128,1280]{1,0:T(8,128)(2,1)S(1)}, u32[]{:S(2)}, u32[]{:S(2)}) collective-permute-start(bf16[128,1280]{1,0:T(8,128)(2,1)S(1)} %get-tuple-element.37.row_ref), channel_id=1, source_target_pairs={{0,1},{1,0},{2,3},{3,2},{4,5},{5,4},{6,7},{7,6},{8,9},{9,8},{10,11... | collective-permute-start | bytes 983048 | tf_op jit(solution)/shard_map/ppermute | solution.py:462
  39.1 0.0 collective-permute-done.7.n1
  39.1 0.5 collective-permute-start.10
  39.6 0.0 collective-permute-done.8.n2
  39.6 1.0 %slice.8 = bf16[128,1280]{1,0:T(8,128)(2,1)S(1)} slice(bf16[256,1280]{1,0:T(8,128)(2,1)} %collective-permute-done.8.n2), slice={[0:128], [0:1280]} | slice | bytes 655360 | tf_op jit(solution)/shard_map/slice | solution.py:491
  40.6 0.6 collective-permute-start.9
  41.2 2.8 %shard_map.136 = (bf16[640,128]{1,0:T(8,128)(2,1)S(1)}, f32[640,256]{1,0:T(8,128)S(1)}, f32[640,256]{1,0:T(8,128)S(1)}) custom-call(bf16[128,1280]{1,0:T(8,128)(2,1)S(1)} %get-tuple-element.37.row_ref, bf16[1280,640]{1,0:T(8,128)(2,1)S(1)} %get-tuple-element.38.turned_ref, bf16[128,640]{1,0:T(8,128)(2,1)S(1)} %get-tuple-element.41.q_ref, ...), custom_call_target="tpu_custom_call" | custom-call | flops 419430400 | bytes 4000000 | tf_op jit(solution)/shard_map/pallas_call | solution.py:427
  44.0 1.6 %collective-permute-done.3.row_ref = bf16[128,1280]{1,0:T(8,128)(2,1)S(1)} collective-permute-done((bf16[128,1280]{1,0:T(8,128)(2,1)S(1)}, bf16[128,1280]{1,0:T(8,128)(2,1)S(1)}, u32[]{:S(2)}, u32[]{:S(2)}) %collective-permute-start.3) | collective-permute-done | bytes 327712 | tf_op jit(solution)/shard_map/ppermute | solution.py:462
  45.6 3.1 %shard_map.137 = (bf16[240,256]{1,0:T(8,128)(2,1)S(1)}, bf16[240,256]{1,0:T(8,128)(2,1)S(1)}, bf16[240,256]{1,0:T(8,128)(2,1)S(1)}, bf16[240,256]{1,0:T(8,128)(2...) custom-call(bf16[128,1280]{1,0:T(8,128)(2,1)S(1)} %collective-permut, ...), custom_call_target="tpu_custom_call" | custom-call | flops 419430400 | bytes 4000000 | tf_op jit(solution)/shard_map/pallas_call | solution.py:427
  48.7 0.6 collective-permute-start.4
  49.3 1.0 %collective-permute-start.5 = (bf16[240,256]{1,0:T(8,128)(2,1)S(1)}, bf16[240,256]{1,0:T(8,128)(2,1)S(1)}, u32[]{:S(2)}, u32[]{:S(2)}) collective-permute-start(bf16[240,256]{1,0:T(8,128)(2,1)S(1)} %get-tuple-element.48), channel_id=1, source_target_pairs={{0,8},{2,10},{4,12},{6,14},{8,0},{10,2},{12,4},{14,6},{16,24},{18,... | collective-permute-start | bytes 368648 | tf_op jit(solution)/shard_map/ppermute | solution.py:465
  50.3 2.0 %collective-permute-start.6 = (bf16[240,256]{1,0:T(8,128)(2,1)S(1)}, bf16[240,256]{1,0:T(8,128)(2,1)S(1)}, u32[]{:S(2)}, u32[]{:S(2)}) collective-permute-start(bf16[240,256]{1,0:T(8,128)(2,1)S(1)} %get-tuple-element.49), channel_id=1, source_target_pairs={{0,12},{2,14},{4,8},{6,10},{8,4},{10,6},{12,0},{14,2},{16,28},{18,... | collective-permute-start | bytes 368648 | tf_op jit(solution)/shard_map/ppermute | solution.py:465
  52.3 1.8 %collective-permute-done.4.t1 = bf16[240,256]{1,0:T(8,128)(2,1)S(1)} collective-permute-done((bf16[240,256]{1,0:T(8,128)(2,1)S(1)}, bf16[240,256]{1,0:T(8,128)(2,1)S(1)}, u32[]{:S(2)}, u32[]{:S(2)}) %collective-permute-start.4) | collective-permute-done | bytes 122912 | tf_op jit(solution)/shard_map/ppermute | solution.py:465
  54.1 0.1 collective-permute-done.5.t2
  54.2 2.3 %collective-permute-done.6.t3 = bf16[240,256]{1,0:T(8,128)(2,1)S(1)} collective-permute-done((bf16[240,256]{1,0:T(8,128)(2,1)S(1)}, bf16[240,256]{1,0:T(8,128)(2,1)S(1)}, u32[]{:S(2)}, u32[]{:S(2)}) %collective-permute-start.6) | collective-permute-done | bytes 122912 | tf_op jit(solution)/shard_map/ppermute | solution.py:465
  56.5 0.0 collective-permute-done.10.n3_high
  56.5 0.0 collective-permute-done.9.n3_low
  56.5 2.0 %shard_map.138 = (f32[120,1280]{1,0:T(8,128)S(1)}, bf16[120,1280]{1,0:T(8,128)(2,1)S(1)}) custom-call(bf16[240,256]{1,0:T(8,128)(2,1)S(1)} %get-tuple-element.46.t0, bf16[240,256]{1,0:T(8,128)(2,1)S(1)} %collective-permute-done.4.t1, bf16[240,256]{1,0:T(8,128)(2,1)S(1)} %collective-permute-done.5.t2, bf16[240,256]{1,0:T(8,128)(2,1)S(1)} %collective-permute-done.6.t3, ...), custom_call_target="tpu_custom_call" | custom-call | flops 629145600 | bytes 4000000 | tf_op jit(solution)/shard_map/pallas_call | solution.py:427
  58.5 0.1 collective-permute-start.11
  58.6 1.6 %collective-permute-start.2 = (bf16[128,1280]{1,0:T(8,128)(2,1)S(1)}, bf16[128,1280]{1,0:T(8,128)(2,1)S(1)}, u32[]{:S(2)}, u32[]{:S(2)}) collective-permute-start(bf16[128,1280]{1,0:T(8,128)(2,1)S(1)} %get-tuple-element.36.own_ref), channel_id=1, source_target_pairs={{0,1},{1,0},{2,3},{3,2},{4,5},{5,4},{6,7},{7,6},{8,9},{9,8},{10,11... | collective-permute-start | bytes 983048 | tf_op jit(solution)/shard_map/ppermute | solution.py:462
  60.2 0.6 collective-permute-start.12
  60.8 1.6 %collective-permute-start.13 = (bf16[240,256]{1,0:T(8,128)(2,1)S(1)}, bf16[240,256]{1,0:T(8,128)(2,1)S(1)}, u32[]{:S(2)}, u32[]{:S(2)}) collective-permute-start(bf16[240,256]{1,0:T(8,128)(2,1)S(1)} %get-tuple-element.54), channel_id=1, source_target_pairs={{0,8},{2,10},{4,12},{6,14},{8,0},{10,2},{12,4},{14,6},{16,24},{18,... | collective-permute-start | bytes 368648 | tf_op jit(solution)/shard_map/ppermute | solution.py:465
  62.3 1.3 %collective-permute-start.14 = (bf16[240,256]{1,0:T(8,128)(2,1)S(1)}, bf16[240,256]{1,0:T(8,128)(2,1)S(1)}, u32[]{:S(2)}, u32[]{:S(2)}) collective-permute-start(bf16[240,256]{1,0:T(8,128)(2,1)S(1)} %get-tuple-element.55), channel_id=1, source_target_pairs={{0,12},{2,14},{4,8},{6,10},{8,4},{10,6},{12,0},{14,2},{16,28},{18,... | collective-permute-start | bytes 368648 | tf_op jit(solution)/shard_map/ppermute | solution.py:465
  63.6 0.0 collective-permute-done.11
  63.7 0.1 add_convert_fusion._.refs_0_
  63.7 1.8 %collective-permute-done.12.t1 = bf16[240,256]{1,0:T(8,128)(2,1)S(1)} collective-permute-done((bf16[240,256]{1,0:T(8,128)(2,1)S(1)}, bf16[240,256]{1,0:T(8,128)(2,1)S(1)}, u32[]{:S(2)}, u32[]{:S(2)}) %collective-permute-start.12) | collective-permute-done | bytes 122912 | tf_op jit(solution)/shard_map/ppermute | solution.py:465
  65.5 1.4 %collective-permute-done.13.t2 = bf16[240,256]{1,0:T(8,128)(2,1)S(1)} collective-permute-done((bf16[240,256]{1,0:T(8,128)(2,1)S(1)}, bf16[240,256]{1,0:T(8,128)(2,1)S(1)}, u32[]{:S(2)}, u32[]{:S(2)}) %collective-permute-start.13) | collective-permute-done | bytes 122912 | tf_op jit(solution)/shard_map/ppermute | solution.py:465
  67.0 2.4 %collective-permute-done.14.t3 = bf16[240,256]{1,0:T(8,128)(2,1)S(1)} collective-permute-done((bf16[240,256]{1,0:T(8,128)(2,1)S(1)}, bf16[240,256]{1,0:T(8,128)(2,1)S(1)}, u32[]{:S(2)}, u32[]{:S(2)}) %collective-permute-start.14) | collective-permute-done | bytes 122912 | tf_op jit(solution)/shard_map/ppermute | solution.py:465
  69.4 2.0 %shard_map.140 = (f32[120,1280]{1,0:T(8,128)S(1)}, bf16[120,1280]{1,0:T(8,128)(2,1)S(1)}) custom-call(bf16[240,256]{1,0:T(8,128)(2,1)S(1)} %get-tuple-element.52.t0, bf16[240,256]{1,0:T(8,128)(2,1)S(1)} %collective-permute-done.12.t1, bf16[240,256]{1,0:T(8,128)(2,1)S(1)} %collective-permute-done.13.t2, bf16[240,256]{1,0:T(8,128)(2,1)S(1)} %collective-permute-done.14.t3, ...), custom_call_target="tpu_custom_call" | custom-call | flops 629145600 | bytes 4000000 | tf_op jit(solution)/shard_map/pallas_call | solution.py:427
  71.4 0.1 collective-permute-start.15
  71.5 2.7 %collective-permute-start.16 = (bf16[120,1280]{1,0:T(8,128)(2,1)S(1)}, bf16[120,1280]{1,0:T(8,128)(2,1)S(1)}, u32[]{:S(2)}, u32[]{:S(2)}) collective-permute-start(bf16[120,1280]{1,0:T(8,128)(2,1)S(1)} %add_convert_fusion._.refs_0_), channel_id=1, source_target_pairs={{0,16},{2,18},{4,20},{6,22},{8,24},{10,26},{12,28},{14,30},{16,0},... | collective-permute-start | bytes 921608 | tf_op jit(solution)/shard_map/ppermute | solution.py:465
  74.1 0.0 collective-permute-done.2.other_ref
  74.1 2.1 %shard_map.139 = bf16[128,5120]{1,0:T(8,128)(2,1)} custom-call(s32[1]{0:T(128)S(6)} %min.3.live_ref, s32[1,64]{1,0:T(1,128)S(1)} %copy-done.19, bf16[128,1280]{1,0:T(8,128)(2,1)S(1)} %get-tuple-element.36.own_ref, bf16[128,1280]{1,0:T(8,128)(2,1)S(1)} %collective-permute-done.2.other_ref, bf16[120,1280]{1,0:T(8,128)(2,1)S(1)} %add_convert_fusion._.refs_0_), custom_call_target="tpu_custom_call" | custom-call | flops 335544320 | bytes 4000000 | tf_op jit(solution)/shard_map/pallas_call | solution.py:427
  76.2 0.0 collective-permute-done.15
  76.2 12.4 %collective-permute-done.16 = bf16[120,1280]{1,0:T(8,128)(2,1)S(1)} collective-permute-done((bf16[120,1280]{1,0:T(8,128)(2,1)S(1)}, bf16[120,1280]{1,0:T(8,128)(2,1)S(1)}, u32[]{:S(2)}, u32[]{:S(2)}) %collective-permute-start.16) | collective-permute-done | bytes 307232 | tf_op jit(solution)/shard_map/ppermute | solution.py:465
  88.6 0.9 %add_bitcast_fusion = f32[1,120,1280]{2,1,0:T(8,128)} fusion(bf16[120,1280]{1,0:T(8,128)(2,1)S(1)} %collective-permute-done.16, f32[120,1280]{1,0:T(8,128)S(1)} %get-tuple-element.56, bf16[120,1280]{1,0:T(8,128)(2,1)S(1)} %collective-permute-done.15), kind=kLoop, calls=%fused_computation | loop fusion | flops 614400 | bytes 1843200 | tf_op jit(solution)/shard_map/broadcast_in_dim | solution.py:609
  (24 shorter events, 0.1 us)
Async XLA Ops:
  0.6 1.1 %copy-start.2 = (bf16[256,1280]{1,0:T(8,128)(2,1)S(1)}, bf16[256,1280]{1,0:T(8,128)(2,1)}, u32[]{:S(2)}) copy-start(bf16[256,1280]{1,0:T(8,128)(2,1)} %patches_ref.3) | copy-start | bytes 1966084
  1.7 0.7 copy-start.17
  2.4 0.7 copy-start.18
  3.6 35.5 %collective-permute-start.7 = (bf16[256,1280]{1,0:T(8,128)(2,1)S(1)}, bf16[256,1280]{1,0:T(8,128)(2,1)S(1)}, u32[]{:S(2)}, u32[]{:S(2)}) collective-permute-start(bf16[256,1280]{1,0:T(8,128)(2,1)S(1)} %shard_map.131.normed_ref.n0), channel_id=1, source_target_pairs={{0,4},{2,6},{4,0},{6,2},{8,12},{10,14},{12,8},{14,10},{16,20},{18,... | collective-permute-start | bytes 1966088 | tf_op jit(solution)/shard_map/ppermute | solution.py:465
  6.6 33.0 %collective-permute-start.8 = (bf16[256,1280]{1,0:T(8,128)(2,1)S(1)}, bf16[256,1280]{1,0:T(8,128)(2,1)}, u32[]{:S(2)}, u32[]{:S(2)}) collective-permute-start(bf16[256,1280]{1,0:T(8,128)(2,1)S(1)} %shard_map.131.normed_ref.n0), channel_id=1, source_target_pairs={{0,8},{2,10},{4,12},{6,14},{8,0},{10,2},{12,4},{14,6},{16,24},{18,... | collective-permute-start | bytes 1966088 | tf_op jit(solution)/shard_map/ppermute | solution.py:465
  8.9 0.7 copy-start.12
  16.4 1.2 %copy-start.4 = (bf16[1280,640]{1,0:T(8,128)(2,1)}, bf16[1280,640]{1,0:T(8,128)(2,1)S(1)}, u32[]{:S(2)}) copy-start(bf16[1280,640]{1,0:T(8,128)(2,1)S(1)} %get-tuple-element.31.w_ref) | copy-start | bytes 4915204
  17.6 0.8 copy-start.6
  18.4 0.7 copy-start.8
  19.2 0.7 copy-start.10
  19.8 4.7 %copy-start.13 = (f32[3,640]{1,0:T(4,128)S(1)}, f32[3,640]{1,0:T(4,128)}, u32[]{:S(2)}) copy-start(f32[3,640]{1,0:T(4,128)} %b_ref.4) | copy-start | bytes 23044
  19.8 4.7 %copy-start.19 = (s32[1,64]{1,0:T(1,128)S(1)}, s32[1,64]{1,0:T(1,128)}, u32[]{:S(2)}) copy-start(s32[1,64]{1,0:T(1,128)} %places_ref.3) | copy-start | bytes 772
  19.8 13.4 %collective-permute-start = (bf16[128,1280]{1,0:T(8,128)(2,1)}, bf16[128,1280]{1,0:T(8,128)(2,1)}, u32[]{:S(2)}, u32[]{:S(2)}) collective-permute-start(bf16[128,1280]{1,0:T(8,128)(2,1)} %get-tuple-element.34), channel_id=1, source_target_pairs={{0,1},{1,0},{2,3},{3,2},{4,5},{5,4},{6,7},{7,6},{8,9},{9,8},{10,11... | collective-permute-start | bytes 983048 | tf_op jit(solution)/shard_map/ppermute | solution.py:462
  23.9 12.0 %collective-permute-start.1 = (bf16[128,1280]{1,0:T(8,128)(2,1)}, bf16[128,1280]{1,0:T(8,128)(2,1)S(1)}, u32[]{:S(2)}, u32[]{:S(2)}) collective-permute-start(bf16[128,1280]{1,0:T(8,128)(2,1)} %shard_map.134), channel_id=1, source_target_pairs={{0,1},{1,0},{2,3},{3,2},{4,5},{5,4},{6,7},{7,6},{8,9},{9,8},{10,11... | collective-permute-start | bytes 983048 | tf_op jit(solution)/shard_map/ppermute | solution.py:462
  24.5 1.4 %copy-start = (bf16[640,1280]{1,0:T(8,128)(2,1)S(1)}, bf16[640,1280]{1,0:T(8,128)(2,1)}, u32[]{:S(2)}) copy-start(bf16[640,1280]{1,0:T(8,128)(2,1)} %proj_ref.1) | copy-start | bytes 4915204
  26.0 1.3 %copy-start.1 = (bf16[128,5120]{1,0:T(8,128)(2,1)S(1)}, bf16[128,5120]{1,0:T(8,128)(2,1)}, u32[]{:S(2)}) copy-start(bf16[128,5120]{1,0:T(8,128)(2,1)} %grad_hbm.1) | copy-start | bytes 3932164
  27.3 1.4 %copy-start.5 = (bf16[1280,640]{1,0:T(8,128)(2,1)S(1)}, bf16[1280,640]{1,0:T(8,128)(2,1)}, u32[]{:S(2)}) copy-start(bf16[1280,640]{1,0:T(8,128)(2,1)} %copy-done.4) | copy-start | bytes 4915204
  28.7 1.0 %copy-start.9 = (bf16[128,1280]{1,0:T(8,128)(2,1)S(1)}, bf16[128,1280]{1,0:T(8,128)(2,1)}, u32[]{:S(2)}) copy-start(bf16[128,1280]{1,0:T(8,128)(2,1)} %copy-done.8) | copy-start | bytes 983044
  29.7 6.3 %copy-start.3 = (bf16[256,1280]{1,0:T(8,128)(2,1)S(1)}, bf16[256,1280]{1,0:T(8,128)(2,1)}, u32[]{:S(2)}) copy-start(bf16[256,1280]{1,0:T(8,128)(2,1)} %patches_ref.3) | copy-start | bytes 1966084
  29.7 6.3 %copy-start.14 = (f32[1280]{0:T(1024)S(1)}, f32[1280]{0:T(1024)}, u32[]{:S(2)}) copy-start(f32[1280]{0:T(1024)} %b_ref.5) | copy-start | bytes 15364
  29.7 6.3 %copy-start.15 = (f32[1280]{0:T(1024)S(1)}, f32[1280]{0:T(1024)}, u32[]{:S(2)}) copy-start(f32[1280]{0:T(1024)} %gain_ref.3) | copy-start | bytes 15364
  29.7 6.3 %copy-start.16 = (f32[1280]{0:T(1024)S(1)}, f32[1280]{0:T(1024)}, u32[]{:S(2)}) copy-start(f32[1280]{0:T(1024)} %bias_ref.3) | copy-start | bytes 15364
  37.5 8.1 %collective-permute-start.3 = (bf16[128,1280]{1,0:T(8,128)(2,1)S(1)}, bf16[128,1280]{1,0:T(8,128)(2,1)S(1)}, u32[]{:S(2)}, u32[]{:S(2)}) collective-permute-start(bf16[128,1280]{1,0:T(8,128)(2,1)S(1)} %get-tuple-element.37.row_ref), channel_id=1, source_target_pairs={{0,1},{1,0},{2,3},{3,2},{4,5},{5,4},{6,7},{7,6},{8,9},{9,8},{10,11... | collective-permute-start | bytes 983048 | tf_op jit(solution)/shard_map/ppermute | solution.py:462
  39.1 17.4 %collective-permute-start.10 = (bf16[128,1280]{1,0:T(8,128)(2,1)S(1)}, bf16[128,1280]{1,0:T(8,128)(2,1)S(1)}, u32[]{:S(2)}, u32[]{:S(2)}) collective-permute-start(bf16[128,1280]{1,0:T(8,128)(2,1)S(1)} %slice.9), channel_id=1, source_target_pairs={{0,8},{2,10},{4,12},{6,14},{8,0},{10,2},{12,4},{14,6},{16,24},{18,... | collective-permute-start | bytes 983048 | tf_op jit(solution)/shard_map/ppermute | solution.py:465
  40.6 15.9 %collective-permute-start.9 = (bf16[128,1280]{1,0:T(8,128)(2,1)S(1)}, bf16[128,1280]{1,0:T(8,128)(2,1)S(1)}, u32[]{:S(2)}, u32[]{:S(2)}) collective-permute-start(bf16[128,1280]{1,0:T(8,128)(2,1)S(1)} %slice.8), channel_id=1, source_target_pairs={{0,4},{2,6},{4,0},{6,2},{8,12},{10,14},{12,8},{14,10},{16,20},{18,... | collective-permute-start | bytes 983048 | tf_op jit(solution)/shard_map/ppermute | solution.py:465
  41.2 4.4 %copy-start.7 = (bf16[8,128,256]{2,1,0:T(8,128)(2,1)S(1)}, bf16[8,128,256]{2,1,0:T(8,128)(2,1)}, u32[]{:S(2)}) copy-start(bf16[8,128,256]{2,1,0:T(8,128)(2,1)} %copy-done.6) | copy-start | bytes 1572868
  41.2 4.4 %copy-start.11 = (bf16[128,640]{1,0:T(8,128)(2,1)S(1)}, bf16[128,640]{1,0:T(8,128)(2,1)}, u32[]{:S(2)}) copy-start(bf16[128,640]{1,0:T(8,128)(2,1)} %copy-done.10) | copy-start | bytes 491524
  48.7 5.4 %collective-permute-start.4 = (bf16[240,256]{1,0:T(8,128)(2,1)S(1)}, bf16[240,256]{1,0:T(8,128)(2,1)S(1)}, u32[]{:S(2)}, u32[]{:S(2)}) collective-permute-start(bf16[240,256]{1,0:T(8,128)(2,1)S(1)} %get-tuple-element.47), channel_id=1, source_target_pairs={{0,4},{2,6},{4,0},{6,2},{8,12},{10,14},{12,8},{14,10},{16,20},{18,... | collective-permute-start | bytes 368648 | tf_op jit(solution)/shard_map/ppermute | solution.py:465
  49.3 4.9 %collective-permute-start.5 = (bf16[240,256]{1,0:T(8,128)(2,1)S(1)}, bf16[240,256]{1,0:T(8,128)(2,1)S(1)}, u32[]{:S(2)}, u32[]{:S(2)}) collective-permute-start(bf16[240,256]{1,0:T(8,128)(2,1)S(1)} %get-tuple-element.48), channel_id=1, source_target_pairs={{0,8},{2,10},{4,12},{6,14},{8,0},{10,2},{12,4},{14,6},{16,24},{18,... | collective-permute-start | bytes 368648 | tf_op jit(solution)/shard_map/ppermute | solution.py:465
  50.3 6.1 %collective-permute-start.6 = (bf16[240,256]{1,0:T(8,128)(2,1)S(1)}, bf16[240,256]{1,0:T(8,128)(2,1)S(1)}, u32[]{:S(2)}, u32[]{:S(2)}) collective-permute-start(bf16[240,256]{1,0:T(8,128)(2,1)S(1)} %get-tuple-element.49), channel_id=1, source_target_pairs={{0,12},{2,14},{4,8},{6,10},{8,4},{10,6},{12,0},{14,2},{16,28},{18,... | collective-permute-start | bytes 368648 | tf_op jit(solution)/shard_map/ppermute | solution.py:465
  58.5 5.1 %collective-permute-start.11 = (bf16[120,1280]{1,0:T(8,128)(2,1)S(1)}, bf16[120,1280]{1,0:T(8,128)(2,1)S(1)}, u32[]{:S(2)}, u32[]{:S(2)}) collective-permute-start(bf16[120,1280]{1,0:T(8,128)(2,1)S(1)} %get-tuple-element.51), channel_id=1, source_target_pairs={{0,2},{2,0},{4,6},{6,4},{8,10},{10,8},{12,14},{14,12},{16,18},{18,... | collective-permute-start | bytes 921608 | tf_op jit(solution)/shard_map/ppermute | solution.py:465
  58.6 15.5 %collective-permute-start.2 = (bf16[128,1280]{1,0:T(8,128)(2,1)S(1)}, bf16[128,1280]{1,0:T(8,128)(2,1)S(1)}, u32[]{:S(2)}, u32[]{:S(2)}) collective-permute-start(bf16[128,1280]{1,0:T(8,128)(2,1)S(1)} %get-tuple-element.36.own_ref), channel_id=1, source_target_pairs={{0,1},{1,0},{2,3},{3,2},{4,5},{5,4},{6,7},{7,6},{8,9},{9,8},{10,11... | collective-permute-start | bytes 983048 | tf_op jit(solution)/shard_map/ppermute | solution.py:462
  60.2 5.4 %collective-permute-start.12 = (bf16[240,256]{1,0:T(8,128)(2,1)S(1)}, bf16[240,256]{1,0:T(8,128)(2,1)S(1)}, u32[]{:S(2)}, u32[]{:S(2)}) collective-permute-start(bf16[240,256]{1,0:T(8,128)(2,1)S(1)} %get-tuple-element.53), channel_id=1, source_target_pairs={{0,4},{2,6},{4,0},{6,2},{8,12},{10,14},{12,8},{14,10},{16,20},{18,... | collective-permute-start | bytes 368648 | tf_op jit(solution)/shard_map/ppermute | solution.py:465
  60.8 6.2 %collective-permute-start.13 = (bf16[240,256]{1,0:T(8,128)(2,1)S(1)}, bf16[240,256]{1,0:T(8,128)(2,1)S(1)}, u32[]{:S(2)}, u32[]{:S(2)}) collective-permute-start(bf16[240,256]{1,0:T(8,128)(2,1)S(1)} %get-tuple-element.54), channel_id=1, source_target_pairs={{0,8},{2,10},{4,12},{6,14},{8,0},{10,2},{12,4},{14,6},{16,24},{18,... | collective-permute-start | bytes 368648 | tf_op jit(solution)/shard_map/ppermute | solution.py:465
  62.3 7.0 %collective-permute-start.14 = (bf16[240,256]{1,0:T(8,128)(2,1)S(1)}, bf16[240,256]{1,0:T(8,128)(2,1)S(1)}, u32[]{:S(2)}, u32[]{:S(2)}) collective-permute-start(bf16[240,256]{1,0:T(8,128)(2,1)S(1)} %get-tuple-element.55), channel_id=1, source_target_pairs={{0,12},{2,14},{4,8},{6,10},{8,4},{10,6},{12,0},{14,2},{16,28},{18,... | collective-permute-start | bytes 368648 | tf_op jit(solution)/shard_map/ppermute | solution.py:465
  71.4 4.8 %collective-permute-start.15 = (bf16[120,1280]{1,0:T(8,128)(2,1)S(1)}, bf16[120,1280]{1,0:T(8,128)(2,1)S(1)}, u32[]{:S(2)}, u32[]{:S(2)}) collective-permute-start(bf16[120,1280]{1,0:T(8,128)(2,1)S(1)} %get-tuple-element.57), channel_id=1, source_target_pairs={{0,2},{2,0},{4,6},{6,4},{8,10},{10,8},{12,14},{14,12},{16,18},{18,... | collective-permute-start | bytes 921608 | tf_op jit(solution)/shard_map/ppermute | solution.py:465
  71.5 17.2 %collective-permute-start.16 = (bf16[120,1280]{1,0:T(8,128)(2,1)S(1)}, bf16[120,1280]{1,0:T(8,128)(2,1)S(1)}, u32[]{:S(2)}, u32[]{:S(2)}) collective-permute-start(bf16[120,1280]{1,0:T(8,128)(2,1)S(1)} %add_convert_fusion._.refs_0_), channel_id=1, source_target_pairs={{0,16},{2,18},{4,20},{6,22},{8,24},{10,26},{12,28},{14,30},{16,0},... | collective-permute-start | bytes 921608 | tf_op jit(solution)/shard_map/ppermute | solution.py:465

commit v9 on v8

--- a/solution.py
+++ b/solution.py
@@ -184,11 +184,8 @@
     out_ref[...] = total.astype(out_ref.dtype)
 
 
-def pull_kernel(
-    live_hbm, places_hbm, grad_hbm, send_ref, live_ref, places_ref, grad_ref, sems
-):
+def pull_kernel(live_ref, places_hbm, grad_hbm, send_ref, places_ref, grad_ref, sems):
     half, width = send_ref.shape
-    counted = begin((live_hbm,), (live_ref,), sems, 5)
     came = begin((places_hbm,), (places_ref,), sems)
     blocks = [slice(k * width, (k + 1) * width) for k in range(4)]
     came += begin(
@@ -197,7 +194,6 @@
         sems,
         1,
     )
-    counted[0].wait()
     came[0].wait()
     masks = place_masks(
         live_ref, places_ref[...], grad_ref.shape[0], half, half_start(half, False)
@@ -243,7 +239,7 @@
 
 
 def first_kernel(
-    live_hbm,
+    live_ref,
     b_ref,
     normed_ref,
     w_hbm,
@@ -254,15 +250,14 @@
     wq_ref,
     probs_ref,
     send_ref,
-    live_ref,
     w_ref,
     proj_ref,
     attended_ref,
     sems,
 ):
     came = begin(
-        (w_hbm.at[0], w_hbm.at[1], w_hbm.at[2], proj_hbm, live_hbm),
-        (wq_ref, w_ref.at[0], w_ref.at[1], proj_ref, live_ref),
+        (w_hbm.at[0], w_hbm.at[1], w_hbm.at[2], proj_hbm),
+        (wq_ref, w_ref.at[0], w_ref.at[1], proj_ref),
         sems,
     )
     half = send_ref.shape[0]
@@ -277,7 +272,6 @@
         came[t].wait()
         part = jnp.dot(normed_ref[...], w_ref[t - 1], preferred_element_type=jnp.float32)
         pair_ref[t - 1] = (part + b_ref[t : t + 1, :]).astype(jnp.bfloat16)
-    came[4].wait()
     attend(live_ref, query_ref, pair_ref, probs_ref, attended_ref)
     came[3].wait()
     send_ref[...] = jnp.dot(
@@ -464,7 +458,6 @@
     def flip(value, bits):
         return lax.ppermute(value, "clip", [(i, i ^ bits) for i in range(n_clip)])
 
-    counted = jnp.minimum(clip_tokens, rows // 4)
     half = rows // 2
     part, wide = shape((half, width), low), shape((half, width), jnp.float32)
     probs_half = shape((heads, half, rows), low)
@@ -474,14 +467,13 @@
     up_send = call(
         pull_kernel,
         part,
-        "aaa",
+        "saa",
         4 * rows * share_rows * width,
         (clip_tokens, positions, grad_placed),
         (
-            pltpu.SMEM((1,), jnp.int32),
             pltpu.VMEM(positions.shape, jnp.int32),
             pltpu.VMEM(grad_placed.shape, low),
-            pltpu.SemaphoreType.DMA((6,)),
+            pltpu.SemaphoreType.DMA((5,)),
         ),
         limit=62,
     )
@@ -492,7 +484,7 @@
     other_query, pair, own_normed, w_query, other_probs, part_send = call(
         first_kernel,
         (query, shape((2, rows, local), low), part, shape((width, local), low), probs_half, part),
-        "avvaa",
+        "svvaa",
         7 * rows * width * local,
         (
             clip_tokens,
@@ -502,11 +494,10 @@
             w_proj,
         ),
         (
-            pltpu.SMEM((1,), jnp.int32),
             pltpu.VMEM((2, width, local), low),
             pltpu.VMEM((local, width), low),
             attended,
-            pltpu.SemaphoreType.DMA((5,)),
+            pltpu.SemaphoreType.DMA((4,)),
         ),
         limit=49,
     )
@@ -517,7 +508,7 @@
         "svvvvvvv",
         5 * half * width * local,
         (
-            counted,
+            clip_tokens,
             positions,
             grad_placed,
             b_qkv,
@@ -578,7 +569,8 @@
 
     def exchange(sent):
         diagonal = flip(sent[3], 3 << 1)
-        return [sent[0]] + [flip(sent[q], q << 1) for q in (1, 2)] + [diagonal]
+        high = flip(sent[2], 2 << 1)
+        return [sent[0], flip(sent[1], 1 << 1), high, diagonal]
 
     def product(taken, after=()):
         return call(
@@ -603,7 +595,7 @@
         shape((share_rows, 4 * width), low),
         "svvva",
         8 * rows * share_rows * width,
-        (counted, positions, merged, other_merged, far_sum),
+        (clip_tokens, positions, merged, other_merged, far_sum),
     )
     summed = near_keep + near_came.astype(jnp.float32) + crossing.astype(jnp.float32)
     return (placed, summed[None])

time: 90.2 us -> 88.7 us (0.983)
  Pallas kernels: 27 us -> 25.5 us
    pallas_call x10, Pallas kernels: 27 us -> 25.5 us  [call(): pl.pallas_call(kernel, out_shape=outs, in_specs=[spec[kind] for kind in k...]
  transfers between devices with their start and end apart: 17 -> 17, of which waited for: 9 -> 9; matrix products, arithmetic and copies ran while one was open for 1% -> 1% of each run, Pallas kernels for 27% -> 26%
where the time goes in v9:
time: 88.7 us; the launch traced here: 88.1 us
  waiting for transfers between devices  26.6 us (30%)
  Pallas kernels  25.5 us (29%)
  starting transfers between devices  20.8 us (23%)
  local copies, waits for them, and re-layouts  12.8 us (14%)
  between operations  1.44 us (2%)
  other arithmetic  0.98 us (1%)
    pallas_call x10, Pallas kernels, call(): pl.pallas_call(kernel, out_shape=outs, in_specs=[spec[kind] for kind in k...  25.5 us
    ppermute x13, waiting for transfers between devices, flip(): return lax.ppermute(value, 'clip', [(i, i ^ bits) for i in range(n_clip)])  22.3 us
    ppermute x13, starting transfers between devices, flip(): return lax.ppermute(value, 'clip', [(i, i ^ bits) for i in range(n_clip)])  15.6 us
    unnamed x40, local copies, waits for them, and re-layouts  11.7 us
    ppermute x4, starting transfers between devices, swap(): return lax.ppermute(value, 'seq', [(0, 1), (1, 0)])  5.2 us
    ppermute x4, waiting for transfers between devices, swap(): return lax.ppermute(value, 'seq', [(0, 1), (1, 0)])  4.39 us
  transfers between devices with their start and end apart: 17, of which 9 were waited for; matrix products, arithmetic and copies ran while one was open for 1% of the time, Pallas kernels for 26%

profile of v9, /device:TPU:0, one launch (start us, length us, event | category | flops | bytes accessed | tf_op | source)
XLA Modules:
  0.0 88.1 jit_solution(7459061563150594552)
XLA Ops:
  0.6 0.0 copy-start.2
  0.6 1.1 %copy-done.2 = bf16[256,1280]{1,0:T(8,128)(2,1)S(1)} copy-done((bf16[256,1280]{1,0:T(8,128)(2,1)S(1)}, bf16[256,1280]{1,0:T(8,128)(2,1)}, u32[]{:S(2)}) %copy-start.2) | copy-done | bytes 655384
  1.7 0.7 copy-done.17
  2.4 0.7 copy-done.18
  3.1 0.5 shard_map.131.normed_ref.n0
  3.6 3.1 %collective-permute-start.7 = (bf16[256,1280]{1,0:T(8,128)(2,1)S(1)}, bf16[256,1280]{1,0:T(8,128)(2,1)S(1)}, u32[]{:S(2)}, u32[]{:S(2)}) collective-permute-start(bf16[256,1280]{1,0:T(8,128)(2,1)S(1)} %shard_map.131.normed_ref.n0), channel_id=1, source_target_pairs={{0,4},{2,6},{4,0},{6,2},{8,12},{10,14},{12,8},{14,10},{16,20},{18,... | collective-permute-start | bytes 1966088 | tf_op jit(solution)/shard_map/ppermute | solution.py:459
  6.6 1.6 %collective-permute-start.8 = (bf16[256,1280]{1,0:T(8,128)(2,1)S(1)}, bf16[256,1280]{1,0:T(8,128)(2,1)}, u32[]{:S(2)}, u32[]{:S(2)}) collective-permute-start(bf16[256,1280]{1,0:T(8,128)(2,1)S(1)} %shard_map.131.normed_ref.n0), channel_id=1, source_target_pairs={{0,8},{2,10},{4,12},{6,14},{8,0},{10,2},{12,4},{14,6},{16,24},{18,... | collective-permute-start | bytes 1966088 | tf_op jit(solution)/shard_map/ppermute | solution.py:459
  8.9 0.0 copy-start.12
  8.9 0.7 copy-done.12
  9.6 5.6 %shard_map.132 = (bf16[128,640]{1,0:T(8,128)(2,1)S(1)}, bf16[2,256,640]{2,1,0:T(8,128)(2,1)S(1)}, bf16[128,1280]{1,0:T(8,128)(2,1)S(1)}, bf16[1280,640]{1,0:T(8,...) custom-call(s32[1]{0:T(128)S(6)} %copy.14.live_ref, f32[3,640]{1,0:T(4,128)S(1)} %copy-done.12, ...), custom_call_target="tpu_custom_call" | custom-call | flops 1468006400 | bytes 4000000 | tf_op jit(solution)/shard_map/pallas_call | solution.py:421
  15.2 0.0 copy-start.4
  15.2 1.2 %copy-done.4 = bf16[1280,640]{1,0:T(8,128)(2,1)} copy-done((bf16[1280,640]{1,0:T(8,128)(2,1)}, bf16[1280,640]{1,0:T(8,128)(2,1)S(1)}, u32[]{:S(2)}) %copy-start.4) | copy-done | bytes 1638424
  16.4 0.8 copy-done.6
  17.2 0.7 copy-done.8
  17.9 0.7 copy-done.10
  18.6 1.5 %collective-permute-start = (bf16[128,1280]{1,0:T(8,128)(2,1)}, bf16[128,1280]{1,0:T(8,128)(2,1)}, u32[]{:S(2)}, u32[]{:S(2)}) collective-permute-start(bf16[128,1280]{1,0:T(8,128)(2,1)} %get-tuple-element.34), channel_id=1, source_target_pairs={{0,1},{1,0},{2,3},{3,2},{4,5},{5,4},{6,7},{7,6},{8,9},{9,8},{10,11... | collective-permute-start | bytes 983048 | tf_op jit(solution)/shard_map/ppermute | solution.py:456
  20.1 2.6 %shard_map.134 = bf16[128,1280]{1,0:T(8,128)(2,1)} custom-call(s32[1]{0:T(128)S(6)} %copy.14.live_ref, s32[1,64]{1,0:T(1,128)} %places_ref.3, bf16[128,5120]{1,0:T(8,128)(2,1)} %grad_hbm.1), custom_call_target="tpu_custom_call" | custom-call | flops 167772160 | bytes 4000000 | tf_op jit(solution)/shard_map/pallas_call | solution.py:421
  22.7 0.6 collective-permute-start.1
  23.3 0.0 copy-done.13
  23.3 0.0 copy-done.19
  23.3 1.4 %copy-done = bf16[640,1280]{1,0:T(8,128)(2,1)S(1)} copy-done((bf16[640,1280]{1,0:T(8,128)(2,1)S(1)}, bf16[640,1280]{1,0:T(8,128)(2,1)}, u32[]{:S(2)}) %copy-start) | copy-done | bytes 1638424
  24.7 1.3 %copy-done.1 = bf16[128,5120]{1,0:T(8,128)(2,1)S(1)} copy-done((bf16[128,5120]{1,0:T(8,128)(2,1)S(1)}, bf16[128,5120]{1,0:T(8,128)(2,1)}, u32[]{:S(2)}) %copy-start.1) | copy-done | bytes 1310744
  26.0 1.4 %copy-done.5 = bf16[1280,640]{1,0:T(8,128)(2,1)S(1)} copy-done((bf16[1280,640]{1,0:T(8,128)(2,1)S(1)}, bf16[1280,640]{1,0:T(8,128)(2,1)}, u32[]{:S(2)}) %copy-start.5) | copy-done | bytes 1638424
  27.5 1.0 %copy-done.9 = bf16[128,1280]{1,0:T(8,128)(2,1)S(1)} copy-done((bf16[128,1280]{1,0:T(8,128)(2,1)S(1)}, bf16[128,1280]{1,0:T(8,128)(2,1)}, u32[]{:S(2)}) %copy-start.9) | copy-done | bytes 327704
  28.4 3.5 %shard_map.133 = (bf16[128,640]{1,0:T(8,128)(2,1)S(1)}, bf16[8,128,256]{2,1,0:T(8,128)(2,1)S(1)}, f32[128,1280]{1,0:T(8,128)S(1)}, bf16[128,1280]{1,0:T(8,128)(2,1)S(1)}, bf16[1280,640]{1,0:T(8,128)(2,1)S(1)}) custom-call(s32[1]{0:T(128)S(6)} %copy.14.live_ref, s32[1,64]{1,0:T(1,128)S(1)} %copy-done.19, bf16[128,5120]{1,0:T(8,128)(2,1)S(1)} %copy-done.1, ...), custom_call_target="tpu_custom_call" | custom-call | flops 524288000 | bytes 4000000 | tf_op jit(solution)/shard_map/pallas_call | solution.py:421
  31.9 0.0 collective-permute-done.came_ref
  31.9 2.8 %collective-permute-done.1.up_came_ref = bf16[128,1280]{1,0:T(8,128)(2,1)S(1)} collective-permute-done((bf16[128,1280]{1,0:T(8,128)(2,1)}, bf16[128,1280]{1,0:T(8,128)(2,1)S(1)}, u32[]{:S(2)}, u32[]{:S(2)}) %collective-permute-start.1) | collective-permute-done | bytes 327712 | tf_op jit(solution)/shard_map/ppermute | solution.py:456
  34.7 1.5 %shard_map.135 = (bf16[128,1280]{1,0:T(8,128)(2,1)S(1)}, bf16[128,1280]{1,0:T(8,128)(2,1)S(1)}) custom-call(f32[1280]{0:T(1024)S(1)} %copy-done.14, f32[1280]{0:T(1024)S(1)} %copy-done.15, f32[1280]{0:T(1024)S(1)} %copy-done.16, f32[128,1280]{1,0:T(8,128)S(1)} %get-tuple-element.33.keep_ref, bf16[128,1280]{1,0:T(8,128)(2,1)} %collective-permute-done.came_ref, ...), custom_call_target="tpu_custom_call" | custom-call | flops 16384000 | bytes 4000000 | tf_op jit(solution)/shard_map/pallas_call | solution.py:421
  36.3 1.6 %collective-permute-start.3 = (bf16[128,1280]{1,0:T(8,128)(2,1)S(1)}, bf16[128,1280]{1,0:T(8,128)(2,1)S(1)}, u32[]{:S(2)}, u32[]{:S(2)}) collective-permute-start(bf16[128,1280]{1,0:T(8,128)(2,1)S(1)} %get-tuple-element.37.row_ref), channel_id=1, source_target_pairs={{0,1},{1,0},{2,3},{3,2},{4,5},{5,4},{6,7},{7,6},{8,9},{9,8},{10,11... | collective-permute-start | bytes 983048 | tf_op jit(solution)/shard_map/ppermute | solution.py:456
  37.8 0.0 collective-permute-done.7.n1
  37.9 0.5 collective-permute-start.10
  38.4 0.0 collective-permute-done.8.n2
  38.4 1.0 %slice.8 = bf16[128,1280]{1,0:T(8,128)(2,1)S(1)} slice(bf16[256,1280]{1,0:T(8,128)(2,1)} %collective-permute-done.8.n2), slice={[0:128], [0:1280]} | slice | bytes 655360 | tf_op jit(solution)/shard_map/slice | solution.py:483
  39.4 0.6 collective-permute-start.9
  39.9 2.8 %shard_map.136 = (bf16[640,128]{1,0:T(8,128)(2,1)S(1)}, f32[640,256]{1,0:T(8,128)S(1)}, f32[640,256]{1,0:T(8,128)S(1)}) custom-call(bf16[128,1280]{1,0:T(8,128)(2,1)S(1)} %get-tuple-element.37.row_ref, bf16[1280,640]{1,0:T(8,128)(2,1)S(1)} %get-tuple-element.38.turned_ref, bf16[128,640]{1,0:T(8,128)(2,1)S(1)} %get-tuple-element.41.q_ref, ...), custom_call_target="tpu_custom_call" | custom-call | flops 419430400 | bytes 4000000 | tf_op jit(solution)/shard_map/pallas_call | solution.py:421
  42.8 1.6 %collective-permute-done.3.row_ref = bf16[128,1280]{1,0:T(8,128)(2,1)S(1)} collective-permute-done((bf16[128,1280]{1,0:T(8,128)(2,1)S(1)}, bf16[128,1280]{1,0:T(8,128)(2,1)S(1)}, u32[]{:S(2)}, u32[]{:S(2)}) %collective-permute-start.3) | collective-permute-done | bytes 327712 | tf_op jit(solution)/shard_map/ppermute | solution.py:456
  44.4 2.9 %shard_map.137 = (bf16[240,256]{1,0:T(8,128)(2,1)S(1)}, bf16[240,256]{1,0:T(8,128)(2,1)S(1)}, bf16[240,256]{1,0:T(8,128)(2,1)S(1)}, bf16[240,256]{1,0:T(8,128)(2...) custom-call(bf16[128,1280]{1,0:T(8,128)(2,1)S(1)} %collective-permut, ...), custom_call_target="tpu_custom_call" | custom-call | flops 419430400 | bytes 4000000 | tf_op jit(solution)/shard_map/pallas_call | solution.py:421
  47.3 0.6 collective-permute-start.4
  47.9 1.0 %collective-permute-start.5 = (bf16[240,256]{1,0:T(8,128)(2,1)S(1)}, bf16[240,256]{1,0:T(8,128)(2,1)S(1)}, u32[]{:S(2)}, u32[]{:S(2)}) collective-permute-start(bf16[240,256]{1,0:T(8,128)(2,1)S(1)} %get-tuple-element.48), channel_id=1, source_target_pairs={{0,8},{2,10},{4,12},{6,14},{8,0},{10,2},{12,4},{14,6},{16,24},{18,... | collective-permute-start | bytes 368648 | tf_op jit(solution)/shard_map/ppermute | solution.py:459
  48.9 2.0 %collective-permute-start.6 = (bf16[240,256]{1,0:T(8,128)(2,1)S(1)}, bf16[240,256]{1,0:T(8,128)(2,1)S(1)}, u32[]{:S(2)}, u32[]{:S(2)}) collective-permute-start(bf16[240,256]{1,0:T(8,128)(2,1)S(1)} %get-tuple-element.49), channel_id=1, source_target_pairs={{0,12},{2,14},{4,8},{6,10},{8,4},{10,6},{12,0},{14,2},{16,28},{18,... | collective-permute-start | bytes 368648 | tf_op jit(solution)/shard_map/ppermute | solution.py:459
  50.9 1.8 %collective-permute-done.4.t1 = bf16[240,256]{1,0:T(8,128)(2,1)S(1)} collective-permute-done((bf16[240,256]{1,0:T(8,128)(2,1)S(1)}, bf16[240,256]{1,0:T(8,128)(2,1)S(1)}, u32[]{:S(2)}, u32[]{:S(2)}) %collective-permute-start.4) | collective-permute-done | bytes 122912 | tf_op jit(solution)/shard_map/ppermute | solution.py:459
  52.6 0.1 collective-permute-done.5.t2
  52.8 2.3 %collective-permute-done.6.t3 = bf16[240,256]{1,0:T(8,128)(2,1)S(1)} collective-permute-done((bf16[240,256]{1,0:T(8,128)(2,1)S(1)}, bf16[240,256]{1,0:T(8,128)(2,1)S(1)}, u32[]{:S(2)}, u32[]{:S(2)}) %collective-permute-start.6) | collective-permute-done | bytes 122912 | tf_op jit(solution)/shard_map/ppermute | solution.py:459
  55.0 0.0 collective-permute-done.10.n3_high
  55.0 0.0 collective-permute-done.9.n3_low
  55.0 2.0 %shard_map.138 = (f32[120,1280]{1,0:T(8,128)S(1)}, bf16[120,1280]{1,0:T(8,128)(2,1)S(1)}) custom-call(bf16[240,256]{1,0:T(8,128)(2,1)S(1)} %get-tuple-element.46.t0, bf16[240,256]{1,0:T(8,128)(2,1)S(1)} %collective-permute-done.4.t1, bf16[240,256]{1,0:T(8,128)(2,1)S(1)} %collective-permute-done.5.t2, bf16[240,256]{1,0:T(8,128)(2,1)S(1)} %collective-permute-done.6.t3, ...), custom_call_target="tpu_custom_call" | custom-call | flops 629145600 | bytes 4000000 | tf_op jit(solution)/shard_map/pallas_call | solution.py:421
  57.1 0.1 collective-permute-start.11
  57.2 1.6 %collective-permute-start.2 = (bf16[128,1280]{1,0:T(8,128)(2,1)S(1)}, bf16[128,1280]{1,0:T(8,128)(2,1)S(1)}, u32[]{:S(2)}, u32[]{:S(2)}) collective-permute-start(bf16[128,1280]{1,0:T(8,128)(2,1)S(1)} %get-tuple-element.36.own_ref), channel_id=1, source_target_pairs={{0,1},{1,0},{2,3},{3,2},{4,5},{5,4},{6,7},{7,6},{8,9},{9,8},{10,11... | collective-permute-start | bytes 983048 | tf_op jit(solution)/shard_map/ppermute | solution.py:456
  58.7 0.6 collective-permute-start.12
  59.3 1.6 %collective-permute-start.13 = (bf16[240,256]{1,0:T(8,128)(2,1)S(1)}, bf16[240,256]{1,0:T(8,128)(2,1)S(1)}, u32[]{:S(2)}, u32[]{:S(2)}) collective-permute-start(bf16[240,256]{1,0:T(8,128)(2,1)S(1)} %get-tuple-element.54), channel_id=1, source_target_pairs={{0,8},{2,10},{4,12},{6,14},{8,0},{10,2},{12,4},{14,6},{16,24},{18,... | collective-permute-start | bytes 368648 | tf_op jit(solution)/shard_map/ppermute | solution.py:459
  60.9 1.3 %collective-permute-start.14 = (bf16[240,256]{1,0:T(8,128)(2,1)S(1)}, bf16[240,256]{1,0:T(8,128)(2,1)S(1)}, u32[]{:S(2)}, u32[]{:S(2)}) collective-permute-start(bf16[240,256]{1,0:T(8,128)(2,1)S(1)} %get-tuple-element.55), channel_id=1, source_target_pairs={{0,12},{2,14},{4,8},{6,10},{8,4},{10,6},{12,0},{14,2},{16,28},{18,... | collective-permute-start | bytes 368648 | tf_op jit(solution)/shard_map/ppermute | solution.py:459
  62.2 0.0 collective-permute-done.11
  62.2 0.1 add_convert_fusion._.refs_0_
  62.3 1.8 %collective-permute-done.12.t1 = bf16[240,256]{1,0:T(8,128)(2,1)S(1)} collective-permute-done((bf16[240,256]{1,0:T(8,128)(2,1)S(1)}, bf16[240,256]{1,0:T(8,128)(2,1)S(1)}, u32[]{:S(2)}, u32[]{:S(2)}) %collective-permute-start.12) | collective-permute-done | bytes 122912 | tf_op jit(solution)/shard_map/ppermute | solution.py:459
  64.1 1.4 %collective-permute-done.13.t2 = bf16[240,256]{1,0:T(8,128)(2,1)S(1)} collective-permute-done((bf16[240,256]{1,0:T(8,128)(2,1)S(1)}, bf16[240,256]{1,0:T(8,128)(2,1)S(1)}, u32[]{:S(2)}, u32[]{:S(2)}) %collective-permute-start.13) | collective-permute-done | bytes 122912 | tf_op jit(solution)/shard_map/ppermute | solution.py:459
  65.5 2.4 %collective-permute-done.14.t3 = bf16[240,256]{1,0:T(8,128)(2,1)S(1)} collective-permute-done((bf16[240,256]{1,0:T(8,128)(2,1)S(1)}, bf16[240,256]{1,0:T(8,128)(2,1)S(1)}, u32[]{:S(2)}, u32[]{:S(2)}) %collective-permute-start.14) | collective-permute-done | bytes 122912 | tf_op jit(solution)/shard_map/ppermute | solution.py:459
  67.9 2.0 %shard_map.140 = (f32[120,1280]{1,0:T(8,128)S(1)}, bf16[120,1280]{1,0:T(8,128)(2,1)S(1)}) custom-call(bf16[240,256]{1,0:T(8,128)(2,1)S(1)} %get-tuple-element.52.t0, bf16[240,256]{1,0:T(8,128)(2,1)S(1)} %collective-permute-done.12.t1, bf16[240,256]{1,0:T(8,128)(2,1)S(1)} %collective-permute-done.13.t2, bf16[240,256]{1,0:T(8,128)(2,1)S(1)} %collective-permute-done.14.t3, ...), custom_call_target="tpu_custom_call" | custom-call | flops 629145600 | bytes 4000000 | tf_op jit(solution)/shard_map/pallas_call | solution.py:421
  69.9 0.1 collective-permute-start.15
  70.0 2.7 %collective-permute-start.16 = (bf16[120,1280]{1,0:T(8,128)(2,1)S(1)}, bf16[120,1280]{1,0:T(8,128)(2,1)S(1)}, u32[]{:S(2)}, u32[]{:S(2)}) collective-permute-start(bf16[120,1280]{1,0:T(8,128)(2,1)S(1)} %add_convert_fusion._.refs_0_), channel_id=1, source_target_pairs={{0,16},{2,18},{4,20},{6,22},{8,24},{10,26},{12,28},{14,30},{16,0},... | collective-permute-start | bytes 921608 | tf_op jit(solution)/shard_map/ppermute | solution.py:459
  72.7 0.0 collective-permute-done.2.other_ref
  72.7 2.1 %shard_map.139 = bf16[128,5120]{1,0:T(8,128)(2,1)} custom-call(s32[1]{0:T(128)S(6)} %copy.14.live_ref, s32[1,64]{1,0:T(1,128)S(1)} %copy-done.19, bf16[128,1280]{1,0:T(8,128)(2,1)S(1)} %get-tuple-element.36.own_ref, bf16[128,1280]{1,0:T(8,128)(2,1)S(1)} %collective-permute-done.2.other_ref, bf16[120,1280]{1,0:T(8,128)(2,1)S(1)} %add_convert_fusion._.refs_0_), custom_call_target="tpu_custom_call" | custom-call | flops 335544320 | bytes 4000000 | tf_op jit(solution)/shard_map/pallas_call | solution.py:421
  74.8 0.0 collective-permute-done.15
  74.8 12.4 %collective-permute-done.16 = bf16[120,1280]{1,0:T(8,128)(2,1)S(1)} collective-permute-done((bf16[120,1280]{1,0:T(8,128)(2,1)S(1)}, bf16[120,1280]{1,0:T(8,128)(2,1)S(1)}, u32[]{:S(2)}, u32[]{:S(2)}) %collective-permute-start.16) | collective-permute-done | bytes 307232 | tf_op jit(solution)/shard_map/ppermute | solution.py:459
  87.2 0.9 %add_bitcast_fusion = f32[1,120,1280]{2,1,0:T(8,128)} fusion(bf16[120,1280]{1,0:T(8,128)(2,1)S(1)} %collective-permute-done.16, f32[120,1280]{1,0:T(8,128)S(1)} %get-tuple-element.56, bf16[120,1280]{1,0:T(8,128)(2,1)S(1)} %collective-permute-done.15), kind=kLoop, calls=%fused_computation | loop fusion | flops 614400 | bytes 1843200 | tf_op jit(solution)/shard_map/broadcast_in_dim | solution.py:601
  (24 shorter events, 0.1 us)
Async XLA Ops:
  0.6 1.1 %copy-start.2 = (bf16[256,1280]{1,0:T(8,128)(2,1)S(1)}, bf16[256,1280]{1,0:T(8,128)(2,1)}, u32[]{:S(2)}) copy-start(bf16[256,1280]{1,0:T(8,128)(2,1)} %patches_ref.3) | copy-start | bytes 1966084
  1.7 0.7 copy-start.17
  2.4 0.7 copy-start.18
  3.6 34.2 %collective-permute-start.7 = (bf16[256,1280]{1,0:T(8,128)(2,1)S(1)}, bf16[256,1280]{1,0:T(8,128)(2,1)S(1)}, u32[]{:S(2)}, u32[]{:S(2)}) collective-permute-start(bf16[256,1280]{1,0:T(8,128)(2,1)S(1)} %shard_map.131.normed_ref.n0), channel_id=1, source_target_pairs={{0,4},{2,6},{4,0},{6,2},{8,12},{10,14},{12,8},{14,10},{16,20},{18,... | collective-permute-start | bytes 1966088 | tf_op jit(solution)/shard_map/ppermute | solution.py:459
  6.6 31.7 %collective-permute-start.8 = (bf16[256,1280]{1,0:T(8,128)(2,1)S(1)}, bf16[256,1280]{1,0:T(8,128)(2,1)}, u32[]{:S(2)}, u32[]{:S(2)}) collective-permute-start(bf16[256,1280]{1,0:T(8,128)(2,1)S(1)} %shard_map.131.normed_ref.n0), channel_id=1, source_target_pairs={{0,8},{2,10},{4,12},{6,14},{8,0},{10,2},{12,4},{14,6},{16,24},{18,... | collective-permute-start | bytes 1966088 | tf_op jit(solution)/shard_map/ppermute | solution.py:459
  8.9 0.7 copy-start.12
  15.2 1.2 %copy-start.4 = (bf16[1280,640]{1,0:T(8,128)(2,1)}, bf16[1280,640]{1,0:T(8,128)(2,1)S(1)}, u32[]{:S(2)}) copy-start(bf16[1280,640]{1,0:T(8,128)(2,1)S(1)} %get-tuple-element.31.w_ref) | copy-start | bytes 4915204
  16.4 0.8 copy-start.6
  17.2 0.7 copy-start.8
  17.9 0.7 copy-start.10
  18.6 4.7 %copy-start.13 = (f32[3,640]{1,0:T(4,128)S(1)}, f32[3,640]{1,0:T(4,128)}, u32[]{:S(2)}) copy-start(f32[3,640]{1,0:T(4,128)} %b_ref.4) | copy-start | bytes 23044
  18.6 4.7 %copy-start.19 = (s32[1,64]{1,0:T(1,128)S(1)}, s32[1,64]{1,0:T(1,128)}, u32[]{:S(2)}) copy-start(s32[1,64]{1,0:T(1,128)} %places_ref.3) | copy-start | bytes 772
  18.6 13.3 %collective-permute-start = (bf16[128,1280]{1,0:T(8,128)(2,1)}, bf16[128,1280]{1,0:T(8,128)(2,1)}, u32[]{:S(2)}, u32[]{:S(2)}) collective-permute-start(bf16[128,1280]{1,0:T(8,128)(2,1)} %get-tuple-element.34), channel_id=1, source_target_pairs={{0,1},{1,0},{2,3},{3,2},{4,5},{5,4},{6,7},{7,6},{8,9},{9,8},{10,11... | collective-permute-start | bytes 983048 | tf_op jit(solution)/shard_map/ppermute | solution.py:456
  22.7 12.0 %collective-permute-start.1 = (bf16[128,1280]{1,0:T(8,128)(2,1)}, bf16[128,1280]{1,0:T(8,128)(2,1)S(1)}, u32[]{:S(2)}, u32[]{:S(2)}) collective-permute-start(bf16[128,1280]{1,0:T(8,128)(2,1)} %shard_map.134), channel_id=1, source_target_pairs={{0,1},{1,0},{2,3},{3,2},{4,5},{5,4},{6,7},{7,6},{8,9},{9,8},{10,11... | collective-permute-start | bytes 983048 | tf_op jit(solution)/shard_map/ppermute | solution.py:456
  23.3 1.4 %copy-start = (bf16[640,1280]{1,0:T(8,128)(2,1)S(1)}, bf16[640,1280]{1,0:T(8,128)(2,1)}, u32[]{:S(2)}) copy-start(bf16[640,1280]{1,0:T(8,128)(2,1)} %proj_ref.1) | copy-start | bytes 4915204
  24.7 1.3 %copy-start.1 = (bf16[128,5120]{1,0:T(8,128)(2,1)S(1)}, bf16[128,5120]{1,0:T(8,128)(2,1)}, u32[]{:S(2)}) copy-start(bf16[128,5120]{1,0:T(8,128)(2,1)} %grad_hbm.1) | copy-start | bytes 3932164
  26.0 1.4 %copy-start.5 = (bf16[1280,640]{1,0:T(8,128)(2,1)S(1)}, bf16[1280,640]{1,0:T(8,128)(2,1)}, u32[]{:S(2)}) copy-start(bf16[1280,640]{1,0:T(8,128)(2,1)} %copy-done.4) | copy-start | bytes 4915204
  27.5 1.0 %copy-start.9 = (bf16[128,1280]{1,0:T(8,128)(2,1)S(1)}, bf16[128,1280]{1,0:T(8,128)(2,1)}, u32[]{:S(2)}) copy-start(bf16[128,1280]{1,0:T(8,128)(2,1)} %copy-done.8) | copy-start | bytes 983044
  28.4 6.3 %copy-start.3 = (bf16[256,1280]{1,0:T(8,128)(2,1)S(1)}, bf16[256,1280]{1,0:T(8,128)(2,1)}, u32[]{:S(2)}) copy-start(bf16[256,1280]{1,0:T(8,128)(2,1)} %patches_ref.3) | copy-start | bytes 1966084
  28.4 6.3 %copy-start.14 = (f32[1280]{0:T(1024)S(1)}, f32[1280]{0:T(1024)}, u32[]{:S(2)}) copy-start(f32[1280]{0:T(1024)} %b_ref.5) | copy-start | bytes 15364
  28.4 6.3 %copy-start.15 = (f32[1280]{0:T(1024)S(1)}, f32[1280]{0:T(1024)}, u32[]{:S(2)}) copy-start(f32[1280]{0:T(1024)} %gain_ref.3) | copy-start | bytes 15364
  28.4 6.3 %copy-start.16 = (f32[1280]{0:T(1024)S(1)}, f32[1280]{0:T(1024)}, u32[]{:S(2)}) copy-start(f32[1280]{0:T(1024)} %bias_ref.3) | copy-start | bytes 15364
  36.3 8.1 %collective-permute-start.3 = (bf16[128,1280]{1,0:T(8,128)(2,1)S(1)}, bf16[128,1280]{1,0:T(8,128)(2,1)S(1)}, u32[]{:S(2)}, u32[]{:S(2)}) collective-permute-start(bf16[128,1280]{1,0:T(8,128)(2,1)S(1)} %get-tuple-element.37.row_ref), channel_id=1, source_target_pairs={{0,1},{1,0},{2,3},{3,2},{4,5},{5,4},{6,7},{7,6},{8,9},{9,8},{10,11... | collective-permute-start | bytes 983048 | tf_op jit(solution)/shard_map/ppermute | solution.py:456
  37.9 17.2 %collective-permute-start.10 = (bf16[128,1280]{1,0:T(8,128)(2,1)S(1)}, bf16[128,1280]{1,0:T(8,128)(2,1)S(1)}, u32[]{:S(2)}, u32[]{:S(2)}) collective-permute-start(bf16[128,1280]{1,0:T(8,128)(2,1)S(1)} %slice.9), channel_id=1, source_target_pairs={{0,8},{2,10},{4,12},{6,14},{8,0},{10,2},{12,4},{14,6},{16,24},{18,... | collective-permute-start | bytes 983048 | tf_op jit(solution)/shard_map/ppermute | solution.py:459
  39.4 15.7 %collective-permute-start.9 = (bf16[128,1280]{1,0:T(8,128)(2,1)S(1)}, bf16[128,1280]{1,0:T(8,128)(2,1)S(1)}, u32[]{:S(2)}, u32[]{:S(2)}) collective-permute-start(bf16[128,1280]{1,0:T(8,128)(2,1)S(1)} %slice.8), channel_id=1, source_target_pairs={{0,4},{2,6},{4,0},{6,2},{8,12},{10,14},{12,8},{14,10},{16,20},{18,... | collective-permute-start | bytes 983048 | tf_op jit(solution)/shard_map/ppermute | solution.py:459
  39.9 4.4 %copy-start.7 = (bf16[8,128,256]{2,1,0:T(8,128)(2,1)S(1)}, bf16[8,128,256]{2,1,0:T(8,128)(2,1)}, u32[]{:S(2)}) copy-start(bf16[8,128,256]{2,1,0:T(8,128)(2,1)} %copy-done.6) | copy-start | bytes 1572868
  39.9 4.4 %copy-start.11 = (bf16[128,640]{1,0:T(8,128)(2,1)S(1)}, bf16[128,640]{1,0:T(8,128)(2,1)}, u32[]{:S(2)}) copy-start(bf16[128,640]{1,0:T(8,128)(2,1)} %copy-done.10) | copy-start | bytes 491524
  47.3 5.3 %collective-permute-start.4 = (bf16[240,256]{1,0:T(8,128)(2,1)S(1)}, bf16[240,256]{1,0:T(8,128)(2,1)S(1)}, u32[]{:S(2)}, u32[]{:S(2)}) collective-permute-start(bf16[240,256]{1,0:T(8,128)(2,1)S(1)} %get-tuple-element.47), channel_id=1, source_target_pairs={{0,4},{2,6},{4,0},{6,2},{8,12},{10,14},{12,8},{14,10},{16,20},{18,... | collective-permute-start | bytes 368648 | tf_op jit(solution)/shard_map/ppermute | solution.py:459
  47.9 4.9 %collective-permute-start.5 = (bf16[240,256]{1,0:T(8,128)(2,1)S(1)}, bf16[240,256]{1,0:T(8,128)(2,1)S(1)}, u32[]{:S(2)}, u32[]{:S(2)}) collective-permute-start(bf16[240,256]{1,0:T(8,128)(2,1)S(1)} %get-tuple-element.48), channel_id=1, source_target_pairs={{0,8},{2,10},{4,12},{6,14},{8,0},{10,2},{12,4},{14,6},{16,24},{18,... | collective-permute-start | bytes 368648 | tf_op jit(solution)/shard_map/ppermute | solution.py:459
  48.9 6.1 %collective-permute-start.6 = (bf16[240,256]{1,0:T(8,128)(2,1)S(1)}, bf16[240,256]{1,0:T(8,128)(2,1)S(1)}, u32[]{:S(2)}, u32[]{:S(2)}) collective-permute-start(bf16[240,256]{1,0:T(8,128)(2,1)S(1)} %get-tuple-element.49), channel_id=1, source_target_pairs={{0,12},{2,14},{4,8},{6,10},{8,4},{10,6},{12,0},{14,2},{16,28},{18,... | collective-permute-start | bytes 368648 | tf_op jit(solution)/shard_map/ppermute | solution.py:459
  57.1 5.1 %collective-permute-start.11 = (bf16[120,1280]{1,0:T(8,128)(2,1)S(1)}, bf16[120,1280]{1,0:T(8,128)(2,1)S(1)}, u32[]{:S(2)}, u32[]{:S(2)}) collective-permute-start(bf16[120,1280]{1,0:T(8,128)(2,1)S(1)} %get-tuple-element.51), channel_id=1, source_target_pairs={{0,2},{2,0},{4,6},{6,4},{8,10},{10,8},{12,14},{14,12},{16,18},{18,... | collective-permute-start | bytes 921608 | tf_op jit(solution)/shard_map/ppermute | solution.py:459
  57.2 15.5 %collective-permute-start.2 = (bf16[128,1280]{1,0:T(8,128)(2,1)S(1)}, bf16[128,1280]{1,0:T(8,128)(2,1)S(1)}, u32[]{:S(2)}, u32[]{:S(2)}) collective-permute-start(bf16[128,1280]{1,0:T(8,128)(2,1)S(1)} %get-tuple-element.36.own_ref), channel_id=1, source_target_pairs={{0,1},{1,0},{2,3},{3,2},{4,5},{5,4},{6,7},{7,6},{8,9},{9,8},{10,11... | collective-permute-start | bytes 983048 | tf_op jit(solution)/shard_map/ppermute | solution.py:456
  58.7 5.4 %collective-permute-start.12 = (bf16[240,256]{1,0:T(8,128)(2,1)S(1)}, bf16[240,256]{1,0:T(8,128)(2,1)S(1)}, u32[]{:S(2)}, u32[]{:S(2)}) collective-permute-start(bf16[240,256]{1,0:T(8,128)(2,1)S(1)} %get-tuple-element.53), channel_id=1, source_target_pairs={{0,4},{2,6},{4,0},{6,2},{8,12},{10,14},{12,8},{14,10},{16,20},{18,... | collective-permute-start | bytes 368648 | tf_op jit(solution)/shard_map/ppermute | solution.py:459
  59.3 6.2 %collective-permute-start.13 = (bf16[240,256]{1,0:T(8,128)(2,1)S(1)}, bf16[240,256]{1,0:T(8,128)(2,1)S(1)}, u32[]{:S(2)}, u32[]{:S(2)}) collective-permute-start(bf16[240,256]{1,0:T(8,128)(2,1)S(1)} %get-tuple-element.54), channel_id=1, source_target_pairs={{0,8},{2,10},{4,12},{6,14},{8,0},{10,2},{12,4},{14,6},{16,24},{18,... | collective-permute-start | bytes 368648 | tf_op jit(solution)/shard_map/ppermute | solution.py:459
  60.9 7.0 %collective-permute-start.14 = (bf16[240,256]{1,0:T(8,128)(2,1)S(1)}, bf16[240,256]{1,0:T(8,128)(2,1)S(1)}, u32[]{:S(2)}, u32[]{:S(2)}) collective-permute-start(bf16[240,256]{1,0:T(8,128)(2,1)S(1)} %get-tuple-element.55), channel_id=1, source_target_pairs={{0,12},{2,14},{4,8},{6,10},{8,4},{10,6},{12,0},{14,2},{16,28},{18,... | collective-permute-start | bytes 368648 | tf_op jit(solution)/shard_map/ppermute | solution.py:459
  69.9 4.8 %collective-permute-start.15 = (bf16[120,1280]{1,0:T(8,128)(2,1)S(1)}, bf16[120,1280]{1,0:T(8,128)(2,1)S(1)}, u32[]{:S(2)}, u32[]{:S(2)}) collective-permute-start(bf16[120,1280]{1,0:T(8,128)(2,1)S(1)} %get-tuple-element.57), channel_id=1, source_target_pairs={{0,2},{2,0},{4,6},{6,4},{8,10},{10,8},{12,14},{14,12},{16,18},{18,... | collective-permute-start | bytes 921608 | tf_op jit(solution)/shard_map/ppermute | solution.py:459
  70.0 17.2 %collective-permute-start.16 = (bf16[120,1280]{1,0:T(8,128)(2,1)S(1)}, bf16[120,1280]{1,0:T(8,128)(2,1)S(1)}, u32[]{:S(2)}, u32[]{:S(2)}) collective-permute-start(bf16[120,1280]{1,0:T(8,128)(2,1)S(1)} %add_convert_fusion._.refs_0_), channel_id=1, source_target_pairs={{0,16},{2,18},{4,20},{6,22},{8,24},{10,26},{12,28},{14,30},{16,0},... | collective-permute-start | bytes 921608 | tf_op jit(solution)/shard_map/ppermute | solution.py:459
